TPU v7x, 16 devices: a whole 2x2x2 slice. The times are simulated.
16 devices in a mesh: ep: 2 (over z), dp: 8 (over y, x, core).
Axes of the slice: x: 2, y: 2, z: 2, core: 2. Of those that a mesh axis runs over, the one named last changes fastest.
Arguments:
- tokens: bfloat16 [16384, 512], P(('dp', 'ep'))
- d_out: bfloat16 [16384, 512], P(('dp', 'ep'))
- expert_ids: int32 [2, 16384, 8], P(None, ('dp', 'ep'))
- gate_vals: float32 [2, 16384, 8], P(None, ('dp', 'ep'))
- w_mix: bfloat16 [2, 512, 512], replicated
- w_gate: bfloat16 [2, 128, 512, 192], P(None, 'ep')
- w_up: bfloat16 [2, 128, 512, 192], P(None, 'ep')
- w_down: bfloat16 [2, 128, 192, 512], P(None, 'ep')
Outputs:
- output 1: bfloat16 [16384, 512], P(('dp', 'ep'))
- output 2: bfloat16 [16384, 512], P(('dp', 'ep'))
- output 3: bfloat16 [2, 512, 512], replicated
- output 4: bfloat16 [2, 128, 512, 192], P(None, 'ep')
- output 5: bfloat16 [2, 128, 512, 192], P(None, 'ep')
- output 6: bfloat16 [2, 128, 192, 512], P(None, 'ep')
All inputs are finite; a program needn't handle non-finite values.
Results may differ from a plain program's by a relative error of at most 0.0179442.
Values are sent between devices in bfloat16 or wider.
A program may use at most 1 GiB of HBM per device.

v0:
```python
import jax
import jax.numpy as jnp
from jax import lax
from jax.sharding import PartitionSpec as P

CAP_FACTOR = 3


def silu_parts(pre_gate):
    sig_val = jax.nn.sigmoid(pre_gate)
    return pre_gate * sig_val, sig_val * (1.0 + pre_gate * (1.0 - sig_val))


def route_tables(expert_ids, n_experts, capacity):
    flat_ids = expert_ids.reshape(-1)
    n_copies = flat_ids.shape[0]
    sort_order = jnp.argsort(flat_ids, stable=True)
    counts = jnp.bincount(flat_ids, length=n_experts)
    starts = jnp.cumsum(counts) - counts
    slot_pos = jnp.arange(capacity)
    src_copy = sort_order[jnp.minimum(starts[:, None] + slot_pos[None, :], n_copies - 1)]
    is_valid = slot_pos[None, :] < counts[:, None]
    sorted_ids = flat_ids[sort_order]
    rows_sorted = sorted_ids * capacity + jnp.arange(n_copies) - starts[sorted_ids]
    copy_row = jnp.zeros_like(flat_ids).at[sort_order].set(rows_sorted)
    return src_copy, is_valid, copy_row


def layer_forward(x_in, expert_ids, gate_vals, w_mix, w_gate, w_up, w_down, n_experts, capacity):
    tok_local, d_model = x_in.shape
    top_k = expert_ids.shape[1]
    n_local = w_gate.shape[0]
    mixed = x_in.astype(jnp.float32) + jnp.dot(x_in, w_mix, preferred_element_type=jnp.float32)
    u_act = mixed.astype(jnp.bfloat16)
    src_copy, is_valid, copy_row = route_tables(expert_ids, n_experts, capacity)
    send_buf = jnp.where(is_valid[:, :, None], u_act[src_copy // top_k], 0)
    send_buf = send_buf.reshape(n_experts // n_local, n_local, capacity, d_model)
    recv_buf = lax.all_to_all(send_buf, 'ep', 0, 0, tiled=True)
    pre_gate = jnp.einsum('secd,edf->secf', recv_buf, w_gate, preferred_element_type=jnp.float32)
    pre_up = jnp.einsum('secd,edf->secf', recv_buf, w_up, preferred_element_type=jnp.float32)
    act, _ = silu_parts(pre_gate)
    hidden = (act * pre_up).astype(jnp.bfloat16)
    out_buf = jnp.einsum('secf,efd->secd', hidden, w_down, preferred_element_type=jnp.float32).astype(jnp.bfloat16)
    back_buf = lax.all_to_all(out_buf, 'ep', 0, 0, tiled=True).reshape(n_experts * capacity, d_model)
    out_copy = back_buf[copy_row].reshape(tok_local, top_k, d_model)
    y_out = u_act.astype(jnp.float32) + jnp.sum(gate_vals[:, :, None] * out_copy.astype(jnp.float32), axis=1)
    saved = (x_in, src_copy, is_valid, copy_row, recv_buf, pre_gate, pre_up, hidden)
    return y_out.astype(jnp.bfloat16), saved


def layer_backward(saved, d_y, gate_vals, w_mix, w_gate, w_up, w_down):
    x_in, src_copy, is_valid, copy_row, recv_buf, pre_gate, pre_up, hidden = saved
    tok_local, d_model = d_y.shape
    top_k = gate_vals.shape[1]
    n_experts, capacity = is_valid.shape
    g_dy = (gate_vals[:, :, None] * d_y.astype(jnp.float32)[:, None, :]).astype(jnp.bfloat16)
    g_dy = g_dy.reshape(tok_local * top_k, d_model)
    send_grad = jnp.where(is_valid[:, :, None], g_dy[src_copy], 0).reshape(recv_buf.shape)
    recv_grad = lax.all_to_all(send_grad, 'ep', 0, 0, tiled=True)
    d_hidden = jnp.einsum('secd,efd->secf', recv_grad, w_down, preferred_element_type=jnp.float32)
    act, act_slope = silu_parts(pre_gate)
    d_pre_gate = (d_hidden * pre_up * act_slope).astype(jnp.bfloat16)
    d_pre_up = (d_hidden * act).astype(jnp.bfloat16)
    d_recv = (jnp.einsum('secf,edf->secd', d_pre_gate, w_gate, preferred_element_type=jnp.float32)
              + jnp.einsum('secf,edf->secd', d_pre_up, w_up, preferred_element_type=jnp.float32)).astype(jnp.bfloat16)
    g_gate = jnp.einsum('secd,secf->edf', recv_buf, d_pre_gate, preferred_element_type=jnp.float32).astype(jnp.bfloat16)
    g_up = jnp.einsum('secd,secf->edf', recv_buf, d_pre_up, preferred_element_type=jnp.float32).astype(jnp.bfloat16)
    g_down = jnp.einsum('secf,secd->efd', hidden, recv_grad, preferred_element_type=jnp.float32).astype(jnp.bfloat16)
    g_gate = lax.psum(g_gate, 'dp')
    g_up = lax.psum(g_up, 'dp')
    g_down = lax.psum(g_down, 'dp')
    d_back = lax.all_to_all(d_recv, 'ep', 0, 0, tiled=True).reshape(n_experts * capacity, d_model)
    d_copy = d_back[copy_row].reshape(tok_local, top_k, d_model)
    d_u = (d_y.astype(jnp.float32)
           + jnp.sum(gate_vals[:, :, None] * d_copy.astype(jnp.float32), axis=1)).astype(jnp.bfloat16)
    g_mix = jnp.einsum('td,te->de', x_in, d_u, preferred_element_type=jnp.float32).astype(jnp.bfloat16)
    g_mix = lax.psum(g_mix, ('dp', 'ep'))
    d_x = (d_u.astype(jnp.float32)
           + jnp.einsum('te,de->td', d_u, w_mix, preferred_element_type=jnp.float32)).astype(jnp.bfloat16)
    return d_x, (g_mix, g_gate, g_up, g_down)


def stack_part(grads, index):
    return jnp.stack([entry[index] for entry in grads])


def solution(mesh):
    ep_size = mesh.shape['ep']
    tok_spec = P(('dp', 'ep'), None)
    route_spec = P(None, ('dp', 'ep'), None)
    whole_spec = P(None, None, None)
    expert_spec = P(None, 'ep', None, None)

    def device_step(tokens, d_out, expert_ids, gate_vals, w_mix, w_gate, w_up, w_down):
        n_layers = w_mix.shape[0]
        n_experts = w_gate.shape[1] * ep_size
        tok_local = tokens.shape[0]
        top_k = expert_ids.shape[2]
        capacity = (CAP_FACTOR * tok_local * top_k + n_experts - 1) // n_experts
        layer_in = tokens
        saved_all = []
        for layer in range(n_layers):
            layer_in, saved = layer_forward(layer_in, expert_ids[layer], gate_vals[layer], w_mix[layer],
                                            w_gate[layer], w_up[layer], w_down[layer], n_experts, capacity)
            saved_all.append(saved)
        d_y = d_out
        grads = []
        for layer in reversed(range(n_layers)):
            d_y, grad_set = layer_backward(saved_all[layer], d_y, gate_vals[layer], w_mix[layer],
                                           w_gate[layer], w_up[layer], w_down[layer])
            grads.insert(0, grad_set)
        return (layer_in, d_y, stack_part(grads, 0), stack_part(grads, 1),
                stack_part(grads, 2), stack_part(grads, 3))

    return jax.shard_map(device_step, mesh=mesh,
                         in_specs=(tok_spec, tok_spec, route_spec, route_spec, whole_spec,
                                   expert_spec, expert_spec, expert_spec),
                         out_specs=(tok_spec, tok_spec, whole_spec, expert_spec, expert_spec, expert_spec),
                         check_vma=False)
```

profile of v0, /device:TPU:0, one launch (start us, length us, event | category | flops | bytes accessed | tf_op | source)
XLA Modules:
  0.0 4486.2 jit_solution(12706518709288586127)
XLA Ops:
  9.1 57.0 %scatter_custom_fusion = s32[128]{0:T(128)S(1)} fusion(s32[8192]{0:T(1024)S(1)} %reshape.560, s32[8192]{0:T(1024)S(1)} %broadcast.375, s32[]{:T(128)} %constant.39.clone.1), kind=kCustom, calls=%fused_computation.207 | custom fusion | flops 8192 | bytes 516 | tf_op jit(solution)/shard_map/scatter-add | solution.py:18
  74.7 135.5 %gather_fusion = s32[24576]{0:T(1024)S(1)} fusion(s32[8192]{0:T(1024)S(1)} %get-tuple-element.8, s32[24576]{0:T(1024)S(1)} %broadcast_clamp_fusion.5), kind=kCustom, calls=%fused_computation | custom fusion | bytes 294912 | tf_op jit(solution)/shard_map/gather | solution.py:21
  211.9 99.1 %gather_fusion.1 = bf16[24576,512]{1,0:T(8,128)(2,1)} fusion(bf16[1024,512]{1,0:T(8,128)(2,1)S(1)} %add_convert_fusion.9, s32[24576]{0:T(1024)S(1)} %broadcast_clamp_fusion.1), kind=kCustom, calls=%fused_computation.1 | custom fusion | bytes 50429952 | tf_op jit(solution)/shard_map/gather | solution.py:36
  324.2 280.8 %all_to_all.40 = bf16[2,64,192,512]{3,2,1,0:T(8,128)(2,1)} all-to-all(bf16[2,64,192,512]{3,2,1,0:T(8,128)(2,1)S(1)} %broadcast_select_fusion.3), channel_id=1, replica_groups=mesh['ep'=2,'dp'=8] {'ep'}, dimensions={0} | all-to-all | bytes 50331648 | tf_op jit(solution)/shard_map/all_to_all | solution.py:38
  605.1 23.7 fusion.34
  628.8 34.7 fusion.14
  663.5 20.2 convert_bitcast_fusion.1
  683.6 20.9 copy.62
  718.2 57.4 %scatter_custom_fusion.2 = s32[128]{0:T(128)S(1)} fusion(s32[8192]{0:T(1024)S(1)} %reshape.576, s32[8192]{0:T(1024)} %copy-done.37, s32[]{:T(128)} %constant.39.clone.1), kind=kCustom, calls=%fused_computation.205 | custom fusion | flops 8192 | bytes 1024 | tf_op jit(solution)/shard_map/scatter-add | solution.py:18
  784.7 135.5 %gather_fusion.5 = s32[24576]{0:T(1024)S(1)} fusion(s32[8192]{0:T(1024)S(1)} %get-tuple-element.9, s32[24576]{0:T(1024)S(1)} %broadcast_clamp_fusion.4), kind=kCustom, calls=%fused_computation.5 | custom fusion | bytes 294912 | tf_op jit(solution)/shard_map/gather | solution.py:21
  920.7 45.5 %gather_fusion.2 = s32[8192]{0:T(1024)S(1)} fusion(s32[8192]{0:T(1024)S(1)} %copy-done.16, s32[8192]{0:T(1024)S(1)} %get-tuple-element.59), kind=kCustom, calls=%fused_computation.2 | custom fusion | bytes 98304 | tf_op jit(solution)/shard_map/gather | solution.py:23
  966.3 48.9 %gather_fusion.3 = s32[8192]{0:T(1024)S(1)} fusion(s32[128]{0:T(128)S(1)} %copy-done.3, s32[8192]{0:T(1024)S(1)} %broadcast_clamp_fusion.8), kind=kCustom, calls=%fused_computation.3 | custom fusion | bytes 98304 | tf_op jit(solution)/shard_map/gather | solution.py:24
  1016.7 30.9 scatter_custom_fusion.1
  1051.7 103.9 %gather_fusion.10 = bf16[24576,512]{1,0:T(8,128)(2,1)} fusion(bf16[8192,512]{1,0:T(8,128)(2,1)} %fusion.41, s32[24576]{0:T(1024)S(1)} %broadcast_clamp_fusion.3), kind=kCustom, calls=%fused_computation.10 | custom fusion | bytes 50429952 | tf_op jit(solution)/shard_map/gather | solution.py:58
  1155.7 45.4 %gather_fusion.4 = bf16[8192,512]{1,0:T(8,128)(2,1)} fusion(bf16[24576,512]{1,0:T(8,128)(2,1)} %bitcast.16, s32[8192]{0:T(1024)S(1)} %fusion.109), kind=kCustom, calls=%fused_computation.4 | custom fusion | bytes 16809984 | tf_op jit(solution)/shard_map/gather | solution.py:45
  1212.2 99.1 %gather_fusion.6 = bf16[24576,512]{1,0:T(8,128)(2,1)} fusion(bf16[1024,512]{1,0:T(8,128)(2,1)S(1)} %add_convert_fusion.7, s32[24576]{0:T(1024)S(1)} %broadcast_clamp_fusion), kind=kCustom, calls=%fused_computation.6 | custom fusion | bytes 50429952 | tf_op jit(solution)/shard_map/gather | solution.py:36
  1311.3 34.3 broadcast_select_fusion.1
  1345.7 296.8 %all_to_all.41 = bf16[2,64,192,512]{3,2,1,0:T(8,128)(2,1)} all-to-all(bf16[2,64,192,512]{3,2,1,0:T(8,128)(2,1)} %get-tuple-element.58), channel_id=1, replica_groups=mesh['ep'=2,'dp'=8] {'ep'}, dimensions={0} | all-to-all | bytes 50331648 | tf_op jit(solution)/shard_map/all_to_all | solution.py:59
  1654.4 23.6 fusion.26
  1678.0 247.2 %all-to-all-done.2 = bf16[2,64,192,512]{3,2,1,0:T(8,128)(2,1)} async-done(((bf16[2,64,192,512]{3,2,1,0:T(8,128)(2,1)}), bf16[2,64,192,512]{3,2,1,0:T(8,128)(2,1)}, u32[]{:S(2)}, u32[]{:S(2)}) %all-to-all-start.2) | async-done | bytes 25165856 | tf_op jit(solution)/shard_map/all_to_all | solution.py:38
  1925.2 23.7 fusion.30
  1948.9 43.2 fusion.8
  1992.1 20.2 convert_bitcast_fusion
  2012.3 20.9 copy.69
  2044.8 26.0 fusion.65
  2070.9 33.1 fusion
  2103.9 20.9 copy.72
  2124.8 190.1 %all-to-all-done.3 = bf16[2,64,192,512]{3,2,1,0:T(8,128)(2,1)} async-done(((bf16[2,64,192,512]{3,2,1,0:T(8,128)(2,1)}), bf16[2,64,192,512]{3,2,1,0:T(8,128)(2,1)}, u32[]{:S(2)}, u32[]{:S(2)}) %all-to-all-start.3) | async-done | bytes 25165856 | tf_op jit(solution)/shard_map/all_to_all | solution.py:44
  2327.7 45.5 %gather_fusion.7 = s32[8192]{0:T(1024)S(1)} fusion(s32[8192]{0:T(1024)S(1)} %copy-done.14, s32[8192]{0:T(1024)S(1)} %get-tuple-element.55), kind=kCustom, calls=%fused_computation.7 | custom fusion | bytes 98304 | tf_op jit(solution)/shard_map/gather | solution.py:23
  2373.3 48.9 %gather_fusion.8 = s32[8192]{0:T(1024)S(1)} fusion(s32[128]{0:T(128)S(1)} %copy-done.1, s32[8192]{0:T(1024)S(1)} %broadcast_clamp_fusion.6), kind=kCustom, calls=%fused_computation.8 | custom fusion | bytes 98304 | tf_op jit(solution)/shard_map/gather | solution.py:24
  2422.3 30.5 scatter_custom_fusion.3
  2452.8 45.5 %gather_fusion.9 = bf16[8192,512]{1,0:T(8,128)(2,1)} fusion(bf16[24576,512]{1,0:T(8,128)(2,1)} %bitcast.36, s32[8192]{0:T(1024)S(1)} %fusion.110), kind=kCustom, calls=%fused_computation.9 | custom fusion | bytes 16809984 | tf_op jit(solution)/shard_map/gather | solution.py:45
  2498.3 98.0 %all-to-all-done.5 = bf16[2,64,192,512]{3,2,1,0:T(8,128)(2,1)} async-done(((bf16[2,64,192,512]{3,2,1,0:T(8,128)(2,1)}), bf16[2,64,192,512]{3,2,1,0:T(8,128)(2,1)}, u32[]{:S(2)}, u32[]{:S(2)}) %all-to-all-start.5) | async-done | bytes 25165856 | tf_op jit(solution)/shard_map/all_to_all | solution.py:72
  2596.3 45.5 %gather_fusion.11 = bf16[8192,512]{1,0:T(8,128)(2,1)} fusion(bf16[24576,512]{1,0:T(8,128)(2,1)} %bitcast.47, s32[8192]{0:T(1024)S(1)} %fusion.110), kind=kCustom, calls=%fused_computation.11 | custom fusion | bytes 16809984 | tf_op jit(solution)/shard_map/gather | solution.py:73
  2663.3 104.1 %gather_fusion.12 = bf16[24576,512]{1,0:T(8,128)(2,1)} fusion(bf16[8192,512]{1,0:T(8,128)(2,1)} %fusion.40, s32[24576]{0:T(1024)S(1)} %broadcast_clamp_fusion.2), kind=kCustom, calls=%fused_computation.12 | custom fusion | bytes 50429952 | tf_op jit(solution)/shard_map/gather | solution.py:58
  2780.7 276.1 %all_to_all.42 = bf16[2,64,192,512]{3,2,1,0:T(8,128)(2,1)} all-to-all(bf16[2,64,192,512]{3,2,1,0:T(8,128)(2,1)S(1)} %broadcast_select_fusion.2), channel_id=1, replica_groups=mesh['ep'=2,'dp'=8] {'ep'}, dimensions={0} | all-to-all | bytes 50331648 | tf_op jit(solution)/shard_map/all_to_all | solution.py:59
  3056.8 38.5 fusion.4
  3095.3 26.0 fusion.58
  3121.3 33.1 fusion.1
  3154.3 20.9 copy.75
  3225.1 19.1 fusion.47
  3266.7 19.1 fusion.46
  3285.8 169.0 %all-to-all-done.7 = bf16[2,64,192,512]{3,2,1,0:T(8,128)(2,1)} async-done(((bf16[2,64,192,512]{3,2,1,0:T(8,128)(2,1)}), bf16[2,64,192,512]{3,2,1,0:T(8,128)(2,1)}, u32[]{:S(2)}, u32[]{:S(2)}) %all-to-all-start.7) | async-done | bytes 25165856 | tf_op jit(solution)/shard_map/all_to_all | solution.py:72
  3454.8 45.5 %gather_fusion.13 = bf16[8192,512]{1,0:T(8,128)(2,1)} fusion(bf16[24576,512]{1,0:T(8,128)(2,1)} %bitcast.56, s32[8192]{0:T(1024)S(1)} %copy-done.29), kind=kCustom, calls=%fused_computation.13 | custom fusion | bytes 16809984 | tf_op jit(solution)/shard_map/gather | solution.py:73
  3538.3 40.5 all-reduce.5.cloned.1.call-done
  3581.4 843.5 %all-reduce.7.cloned.1.call-done = (bf16[1,64,512,192]{2,3,1,0:T(8,128)(2,1)}, bf16[1,64,512,192]{2,3,1,0:T(8,128)(2,1)}, bf16[1,64,512,192]{2,3,1,0:T(8,128)(2,...) async-done(((bf16[1,64,512,192]{2,3,1,0:T(8,128)(2,1)}, bf16[1,64,512,192]{2,3,1,0:T(8,128)(2,1)}, ...) | async-done | bytes 75497488 | tf_op jit(solution)/shard_map/psum | solution.py:69
  4425.0 20.6 pad_maximum_fusion.2
  4445.5 33.6 pad_maximum_fusion
  (175 shorter events, 249.2 us)
Async XLA Ops:
  9.0 58.2 %copy-start.37 = (s32[8192]{0:T(1024)}, s32[8192]{0:T(1024)S(1)}, u32[]{:S(2)}) copy-start(s32[8192]{0:T(1024)S(1)} %broadcast.375) | copy-start | bytes 98308
  66.2 244.8 %copy-start.30 = (pred[2,64,192]{2,1,0:T(8,128)(4,1)}, pred[2,64,192]{2,1,0:T(8,128)(4,1)S(1)}, u32[]{:S(2)}) copy-start(pred[2,64,192]{2,1,0:T(8,128)(4,1)S(1)} %iota_compare_fusion.1) | copy-start | bytes 73732
  66.6 0.5 copy-start.2
  67.9 142.3 %copy-start.15 = (s32[8192]{0:T(1024)}, s32[8192]{0:T(1024)S(1)}, u32[]{:S(2)}) copy-start(s32[8192]{0:T(1024)S(1)} %reshape_squeeze.6) | copy-start | bytes 98308
  74.7 135.6 %copy-start.6 = (s32[8192]{0:T(1024)}, s32[8192]{0:T(1024)S(1)}, u32[]{:S(2)}) copy-start(s32[8192]{0:T(1024)S(1)} %get-tuple-element.8) | copy-start | bytes 98308
  74.7 136.5 %copy-start.38 = (bf16[1024,512]{1,0:T(8,128)(2,1)S(1)}, bf16[1024,512]{1,0:T(8,128)(2,1)}, u32[]{:S(2)}) copy-start(bf16[1024,512]{1,0:T(8,128)(2,1)} %param.8) | copy-start | bytes 3145732
  74.7 136.5 %copy-start.39 = (bf16[2,512,512]{2,1,0:T(8,128)(2,1)S(1)}, bf16[2,512,512]{2,1,0:T(8,128)(2,1)}, u32[]{:S(2)}) copy-start(bf16[2,512,512]{2,1,0:T(8,128)(2,1)} %param.12) | copy-start | bytes 3145732
  211.9 99.1 %copy-start.8 = (bf16[1024,512]{1,0:T(8,128)(2,1)}, bf16[1024,512]{1,0:T(8,128)(2,1)S(1)}, u32[]{:S(2)}) copy-start(bf16[1024,512]{1,0:T(8,128)(2,1)S(1)} %add_convert_fusion.9) | copy-start | bytes 3145732
  704.5 11.9 copy-start.36
  704.5 13.2 copy-start.35
  704.5 72.3 %copy-start.34 = (s32[1,1024,8]{1,2,0:T(8,128)S(1)}, s32[1,1024,8]{1,2,0:T(8,128)}, u32[]{:S(2)}) copy-start(s32[1,1024,8]{1,2,0:T(8,128)} %get-tuple-element.53) | copy-start | bytes 98308
  704.5 451.2 %all-to-all-start.1 = ((bf16[2,64,192,512]{3,2,1,0:T(8,128)(2,1)}), bf16[2,64,192,512]{3,2,1,0:T(8,128)(2,1)}, u32[]{:S(2)}, u32[]{:S(2)}) async-start(bf16[2,64,192,512]{3,2,1,0:T(8,128)(2,1)} %copy.62), calls=%async_computation.1 | async-start | bytes 50331648 | tf_op jit(solution)/shard_map/all_to_all | solution.py:44
  717.3 483.8 %copy-start.23 = (f32[1024,8]{1,0:T(8,128)}, f32[1024,8]{1,0:T(8,128)S(1)}, u32[]{:S(2)}) copy-start(f32[1024,8]{1,0:T(8,128)S(1)} %copy.56) | copy-start | bytes 98308
  776.1 0.5 copy-start
  777.3 6.8 copy-start.13
  784.1 0.6 copy-start.4
  784.7 136.0 %copy-start.7 = (s32[8192]{0:T(1024)S(1)}, s32[8192]{0:T(1024)}, u32[]{:S(2)}) copy-start(s32[8192]{0:T(1024)} %copy-done.6) | copy-start | bytes 98308
  784.7 136.0 %copy-start.16 = (s32[8192]{0:T(1024)S(1)}, s32[8192]{0:T(1024)}, u32[]{:S(2)}) copy-start(s32[8192]{0:T(1024)} %copy-done.15) | copy-start | bytes 98308
  920.2 46.1 %copy-start.3 = (s32[128]{0:T(128)S(1)}, s32[128]{0:T(128)}, u32[]{:S(2)}) copy-start(s32[128]{0:T(128)} %copy-done.2) | copy-start | bytes 1540
  1155.7 45.5 %copy-start.28 = (s32[8192]{0:T(1024)}, s32[8192]{0:T(1024)S(1)}, u32[]{:S(2)}) copy-start(s32[8192]{0:T(1024)S(1)} %fusion.109) | copy-start | bytes 98308
  1155.7 54.8 %copy-start.9 = (bf16[1024,512]{1,0:T(8,128)(2,1)S(1)}, bf16[1024,512]{1,0:T(8,128)(2,1)}, u32[]{:S(2)}) copy-start(bf16[1024,512]{1,0:T(8,128)(2,1)} %copy-done.8) | copy-start | bytes 3145732
  1209.1 1.4 copy-start.19
  1212.2 99.1 %copy-start.11 = (bf16[1024,512]{1,0:T(8,128)(2,1)}, bf16[1024,512]{1,0:T(8,128)(2,1)S(1)}, u32[]{:S(2)}) copy-start(bf16[1024,512]{1,0:T(8,128)(2,1)S(1)} %add_convert_fusion.7) | copy-start | bytes 3145732
  1642.5 282.7 %all-to-all-start.2 = ((bf16[2,64,192,512]{3,2,1,0:T(8,128)(2,1)}), bf16[2,64,192,512]{3,2,1,0:T(8,128)(2,1)}, u32[]{:S(2)}, u32[]{:S(2)}) async-start(bf16[2,64,192,512]{3,2,1,0:T(8,128)(2,1)} %get-tuple-element.57), calls=%async_computation.2 | async-start | bytes 50331648 | tf_op jit(solution)/shard_map/all_to_all | solution.py:38
  2033.1 281.8 %all-to-all-start.3 = ((bf16[2,64,192,512]{3,2,1,0:T(8,128)(2,1)}), bf16[2,64,192,512]{3,2,1,0:T(8,128)(2,1)}, u32[]{:S(2)}, u32[]{:S(2)}) async-start(bf16[2,64,192,512]{3,2,1,0:T(8,128)(2,1)} %copy.69), calls=%async_computation.3 | async-start | bytes 50331648 | tf_op jit(solution)/shard_map/all_to_all | solution.py:44
  2124.8 202.2 %copy-start.33 = (f32[1,1024,8]{1,2,0:T(8,128)S(1)}, f32[1,1024,8]{1,2,0:T(8,128)}, u32[]{:S(2)}) copy-start(f32[1,1024,8]{1,2,0:T(8,128)} %get-tuple-element.47) | copy-start | bytes 98308
  2124.8 202.6 %copy-start.32 = (f32[1024,8]{0,1:T(8,128)S(1)}, f32[1024,8]{0,1:T(8,128)}, u32[]{:S(2)}) copy-start(f32[1024,8]{0,1:T(8,128)} %get-tuple-element.49) | copy-start | bytes 98308
  2124.8 202.8 %copy-start.5 = (s32[8192]{0:T(1024)S(1)}, s32[8192]{0:T(1024)}, u32[]{:S(2)}) copy-start(s32[8192]{0:T(1024)} %copy-done.4) | copy-start | bytes 98308
  2124.8 202.9 %copy-start.14 = (s32[8192]{0:T(1024)S(1)}, s32[8192]{0:T(1024)}, u32[]{:S(2)}) copy-start(s32[8192]{0:T(1024)} %copy-done.13) | copy-start | bytes 98308
  2314.9 281.4 %all-to-all-start.5 = ((bf16[2,64,192,512]{3,2,1,0:T(8,128)(2,1)}), bf16[2,64,192,512]{3,2,1,0:T(8,128)(2,1)}, u32[]{:S(2)}, u32[]{:S(2)}) async-start(bf16[2,64,192,512]{3,2,1,0:T(8,128)(2,1)} %copy.72), calls=%async_computation.5 | async-start | bytes 50331648 | tf_op jit(solution)/shard_map/all_to_all | solution.py:72
  2327.0 46.3 %copy-start.1 = (s32[128]{0:T(128)S(1)}, s32[128]{0:T(128)}, u32[]{:S(2)}) copy-start(s32[128]{0:T(128)} %copy-done) | copy-start | bytes 1540
  2373.2 49.0 %copy-start.27 = (s32[128,192,1]{1,0,2:T(8,128)S(1)}, s32[128,192,1]{1,0,2:T(8,128)}, u32[]{:S(2)}) copy-start(s32[128,192,1]{1,0,2:T(8,128)} %get-tuple-element.43) | copy-start | bytes 294916
  2596.3 60.9 %copy-start.25 = (bf16[1024,512]{1,0:T(8,128)(2,1)S(1)}, bf16[1024,512]{1,0:T(8,128)(2,1)}, u32[]{:S(2)}) copy-start(bf16[1024,512]{1,0:T(8,128)(2,1)} %param.9) | copy-start | bytes 3145732
  2596.3 60.9 %copy-start.40 = (bf16[2,512,512]{2,1,0:T(8,128)(2,1)S(1)}, bf16[2,512,512]{2,1,0:T(8,128)(2,1)}, u32[]{:S(2)}) copy-start(bf16[2,512,512]{2,1,0:T(8,128)(2,1)} %param.12) | copy-start | bytes 3145732
  2655.8 1.4 copy-start.22
  2657.9 1.4 copy-start.17
  2663.3 104.2 %copy-start.31 = (pred[2,64,192]{2,1,0:T(8,128)(4,1)S(1)}, pred[2,64,192]{2,1,0:T(8,128)(4,1)}, u32[]{:S(2)}) copy-start(pred[2,64,192]{2,1,0:T(8,128)(4,1)} %copy-done.30) | copy-start | bytes 73732
  3175.3 279.6 %all-to-all-start.7 = ((bf16[2,64,192,512]{3,2,1,0:T(8,128)(2,1)}), bf16[2,64,192,512]{3,2,1,0:T(8,128)(2,1)}, u32[]{:S(2)}, u32[]{:S(2)}) async-start(bf16[2,64,192,512]{3,2,1,0:T(8,128)(2,1)} %copy.75), calls=%async_computation.7 | async-start | bytes 50331648 | tf_op jit(solution)/shard_map/all_to_all | solution.py:72
  3187.0 391.8 %all-reduce.5.cloned.1.call-start = ((), (), s32[]{:S(2)}) async-start(), calls=%async_computation.8 | async-start | bytes 2097152 | tf_op jit(solution)/shard_map/psum | solution.py:77
  3225.1 19.1 copy-start.10
  3225.1 19.1 copy-start.20
  3266.7 188.1 %copy-start.29 = (s32[8192]{0:T(1024)S(1)}, s32[8192]{0:T(1024)}, u32[]{:S(2)}) copy-start(s32[8192]{0:T(1024)} %copy-done.28) | copy-start | bytes 98308
  3454.8 45.5 %copy-start.24 = (f32[1024,8]{1,0:T(8,128)S(1)}, f32[1024,8]{1,0:T(8,128)}, u32[]{:S(2)}) copy-start(f32[1024,8]{1,0:T(8,128)} %copy-done.23) | copy-start | bytes 98308
  3454.8 53.5 %copy-start.18 = (f32[1024,512]{1,0:T(8,128)S(1)}, f32[1024,512]{1,0:T(8,128)}, u32[]{:S(2)}) copy-start(f32[1024,512]{1,0:T(8,128)} %copy-done.17) | copy-start | bytes 6291460
  3508.8 1.0 copy-start.26
  3512.6 912.4 %all-reduce.7.cloned.1.call-start = ((), (), s32[]{:S(2)}) async-start(), calls=%async_computation.9 | async-start | bytes 150994944 | tf_op jit(solution)/shard_map/psum | solution.py:69
  3531.6 1.2 copy-start.12
  3531.6 1.9 copy-start.21
Sparse Core Ops, SparseCore 0:
  3512.7 66.0 all-reduce.4
  3584.2 840.6 all-reduce.6
where the time goes:
time: 4490 us
  waiting for transfers between devices  1590 us (35%)
  local copies, waits for them, and re-layouts  1210 us (27%)
  blocking collectives  854 us (19%)
  matrix products  473 us (11%)
  other arithmetic  289 us (6%)
  starting transfers between devices  59.4 us (1%)
    psum x1, waiting for transfers between devices, layer_backward(): g_gate = lax.psum(g_gate, 'dp')  844 us
    all_to_all x2, blocking collectives, layer_backward(): recv_grad = lax.all_to_all(send_grad, 'ep', 0, 0, tiled=True)  573 us
    all_to_all x1, blocking collectives, layer_forward(): recv_buf = lax.all_to_all(send_buf, 'ep', 0, 0, tiled=True)  281 us
    gather x4, local copies, waits for them, and re-layouts, route_tables(): sort_order[jnp.minimum(starts[:, None] + slot_pos[None, :], n_copies - 1)]  271 us
    all_to_all x2, waiting for transfers between devices, layer_backward(): lax.all_to_all(d_recv, 'ep', 0, 0, tiled=True)  267 us
    all_to_all x1, waiting for transfers between devices, layer_forward(): recv_buf = lax.all_to_all(send_buf, 'ep', 0, 0, tiled=True)  247 us
    gather x2, local copies, waits for them, and re-layouts, layer_backward(): g_dy[src_copy]  208 us
    gather x2, local copies, waits for them, and re-layouts, layer_forward(): send_buf = jnp.where(is_valid[:, :, None], u_act[src_copy // top_k], 0)  198 us
  transfers between devices with their start and end apart: 7, of which 6 were waited for; matrix products, arithmetic and copies ran while one was open for 19% of the time, Pallas kernels for 0%

commit v1 on v0

v1 whole, which is shorter than its diff:
```python
import functools

import jax
import jax.numpy as jnp
from jax import lax
from jax.experimental import pallas as pl
from jax.experimental.pallas import tpu as pltpu
from jax.sharding import PartitionSpec as P

CAP_FACTOR = 3
LANES = 128
TILE = 128
WTILE = 256
BATCH = 16
UNROLL = 16
PAGE = 1024
VMEM_LIMIT = 62 * 2**20


def cdiv(a, b):
    return (a + b - 1) // b


def nt_dot(a, b):
    return lax.dot_general(a, b, (((1,), (1,)), ((), ())), preferred_element_type=jnp.float32)


def tn_dot(a, b):
    return lax.dot_general(a, b, (((0,), (0,)), ((), ())), preferred_element_type=jnp.float32)


def nn_dot(a, b):
    return lax.dot_general(a, b, (((1,), (0,)), ((), ())), preferred_element_type=jnp.float32)


def load_rows(ref, start, rows, parts):
    cols = [ref[pl.ds(start * parts + k, rows, stride=parts), :] for k in range(parts)]
    return jnp.concatenate(cols, axis=1).astype(jnp.bfloat16)


def store_rows(ref, start, vals, parts):
    rows = vals.shape[0]
    for k in range(parts):
        ref[pl.ds(start * parts + k, rows, stride=parts), :] = vals[:, k * LANES:(k + 1) * LANES]


def fetch_pair(first, other, dst, sem, ep, tok):
    copies = (pltpu.make_async_copy(first, dst.at[pl.ds(ep * tok, tok)], sem.at[0]),
              pltpu.make_async_copy(other, dst.at[pl.ds((1 - ep) * tok, tok)], sem.at[1]))
    return copies


def add_rows(acc, vals_ref, idx, gat, row, parts):
    for b in range(0, TILE, BATCH):
        toks = [idx[row + b + r] for r in range(BATCH)]
        gates = [gat[row + b + r] for r in range(BATCH)]
        vals = [acc[pl.ds(toks[r] * parts, parts), :] + gates[r] * vals_ref[pl.ds((b + r) * parts, parts), :]
                for r in range(BATCH)]
        for r in reversed(range(BATCH)):
            acc[pl.ds(toks[r] * parts, parts), :] = vals[r]


def write_sums(acc, own_ref, other_ref, ep, tok, parts):
    step = min(32, tok)

    def copy_out(q, carry):
        r0 = pl.multiple_of(q * step, step)
        for k in range(parts):
            cols = slice(k * LANES, (k + 1) * LANES)
            own_ref[pl.ds(r0, step), cols] = acc[pl.ds((ep * tok + r0) * parts + k, step, stride=parts), :]
            other_ref[pl.ds(r0, step), cols] = acc[pl.ds(((1 - ep) * tok + r0) * parts + k, step, stride=parts), :]
        return carry

    lax.fori_loop(0, tok // step, copy_out, 0)


def expert_copies(weights, buf, sem, layer, e):
    slot = lax.rem(e, 2)
    ff = weights[0].shape[2]
    return [pltpu.make_async_copy(w.at[layer, e], buf.at[slot, pl.ds(k * ff, ff)], sem.at[slot])
            for k, w in enumerate(weights)]


def run_tiles(step, weights, wbuf, wsem, tile_e, tile_first, n_steps, layer, copies):
    n_local = weights[0].shape[1]
    ahead = list(copies) + expert_copies(weights, wbuf, wsem, layer, 0)
    for c in ahead:
        c.start()
    for c in expert_copies(weights, wbuf, wsem, layer, 1):
        c.start()
    for c in ahead:
        c.wait()

    def one(i, carry):
        e = tile_e[i + 1]

        @pl.when(tile_first[i + 1] == 1)
        def _():
            for c in expert_copies(weights, wbuf, wsem, layer, e):
                c.wait()

            @pl.when(e + 1 < n_local)
            def _():
                for c in expert_copies(weights, wbuf, wsem, layer, e + 1):
                    c.start()

        step(i, lax.rem(e, 2))
        return carry

    lax.fori_loop(0, n_steps, one, 0)


def forward_body(te, tf, tr, tn, nt, idx, gat, epr, u_own, u_oth, g_ref, up_ref, w_ref, own_ref, other_ref,
                 usc, ut, ot, acc, wbuf, sem, wsem, *, layer, tok, parts):
    ff = g_ref.shape[2]
    ep = epr[0]
    acc[...] = jnp.zeros_like(acc)
    ot[...] = jnp.zeros_like(ot)
    ut[...] = jnp.zeros_like(ut)

    def step(i, slot):
        u = load_rows(ut, 0, TILE, parts)
        ab = nt_dot(wbuf[slot, :2 * ff], u)
        add_rows(acc, ot, idx, gat, tr[i], parts)
        row = tr[i + 2]
        for r in range(TILE):
            ut[pl.ds(parts * r, parts), :] = usc[idx[row + r]].astype(jnp.float32)
        a, b = ab[:ff], ab[ff:]
        h = (a * jax.nn.sigmoid(a) * b).astype(jnp.bfloat16)
        o = tn_dot(h, wbuf[slot, 2 * ff:]).astype(jnp.bfloat16).astype(jnp.float32)
        live = lax.broadcasted_iota(jnp.int32, o.shape, 0) < tn[i + 1]
        store_rows(ot, 0, jnp.where(live, o, 0.0), parts)

    run_tiles(step, (g_ref, up_ref, w_ref), wbuf, wsem, te, tf, nt[0] + 2, layer,
              fetch_pair(u_own, u_oth, usc, sem, ep, tok))
    write_sums(acc, own_ref, other_ref, ep, tok, parts)


def backward_body(te, tf, tr, tn, nt, idx, gat, epr, u_own, u_oth, d_own, d_oth, g_ref, up_ref, w_ref, own_ref, other_ref,
                  usc, dsc, ut, ct, vt, acc, wbuf, sem, wsem, *, layer, tok, parts):
    ff = g_ref.shape[2]
    ep = epr[0]
    acc[...] = jnp.zeros_like(acc)
    vt[...] = jnp.zeros_like(vt)
    ut[...] = jnp.zeros_like(ut)
    ct[...] = jnp.zeros_like(ct)

    def step(i, slot):
        u = load_rows(ut, 0, TILE, parts)
        c = load_rows(ct, 0, TILE, parts)
        gu = wbuf[slot, :2 * ff]
        ab = nt_dot(gu, u)
        dh = nt_dot(wbuf[slot, 2 * ff:], c)
        add_rows(acc, vt, idx, gat, tr[i], parts)
        row = tr[i + 2]
        for r in range(TILE):
            t = idx[row + r]
            ut[pl.ds(parts * r, parts), :] = usc[t].astype(jnp.float32)
            ct[pl.ds(parts * r, parts), :] = gat[row + r] * dsc[t].astype(jnp.float32)
        a, b = ab[:ff], ab[ff:]
        s = jax.nn.sigmoid(a)
        da = (dh * b * (s * (1.0 + a * (1.0 - s)))).astype(jnp.bfloat16)
        db = (dh * (a * s)).astype(jnp.bfloat16)
        v = tn_dot(jnp.concatenate([da, db], axis=0), gu).astype(jnp.bfloat16).astype(jnp.float32)
        live = lax.broadcasted_iota(jnp.int32, v.shape, 0) < tn[i + 1]
        store_rows(vt, 0, jnp.where(live, v, 0.0), parts)

    run_tiles(step, (g_ref, up_ref, w_ref), wbuf, wsem, te, tf, nt[0] + 2, layer,
              fetch_pair(u_own, u_oth, usc, sem.at[0], ep, tok) + fetch_pair(d_own, d_oth, dsc, sem.at[1], ep, tok))
    write_sums(acc, own_ref, other_ref, ep, tok, parts)


def token_kernel(body, name, layer, tables, ep, slabs, weights):
    tok, parts, _ = slabs[0].shape
    n_layers, n_local, ff, d_model = weights[0].shape
    n_pairs = len(slabs) // 2
    rows_spec = pl.BlockSpec((tok, d_model), lambda i, *_: (0, 0))
    any_spec = pl.BlockSpec(memory_space=pl.ANY)
    sem_shape = (2,) if n_pairs == 1 else (2, 2)
    copies = 8 * tok
    return pl.pallas_call(
        functools.partial(body, layer=layer, tok=tok, parts=parts),
        grid_spec=pltpu.PrefetchScalarGridSpec(
            num_scalar_prefetch=len(tables) + 1,
            grid=(1,),
            in_specs=[any_spec] * (len(slabs) + 3),
            out_specs=[rows_spec] * 2,
            scratch_shapes=[pltpu.VMEM((2 * tok, parts, LANES), jnp.bfloat16)] * n_pairs
            + [pltpu.VMEM((TILE * parts, LANES), jnp.float32)] * (n_pairs + 1)
            + [pltpu.VMEM((2 * tok * parts, LANES), jnp.float32), pltpu.VMEM((2, 3 * ff, d_model), jnp.bfloat16),
               pltpu.SemaphoreType.DMA(sem_shape), pltpu.SemaphoreType.DMA((2,))],
        ),
        out_shape=[jax.ShapeDtypeStruct((tok, d_model), jnp.float32)] * 2,
        compiler_params=pltpu.CompilerParams(dimension_semantics=("arbitrary",), vmem_limit_bytes=VMEM_LIMIT),
        cost_estimate=pl.CostEstimate(flops=(3 + 3 * (n_pairs - 1)) * 2 * copies * d_model * ff * 4,
                                      bytes_accessed=3 * n_local * ff * d_model * 2, transcendentals=0),
        name=name,
    )(*tables, ep, *slabs, *weights)


def weight_grad_body(st, core, u_all, d_all, idx_all, gat_all, *refs, rows, src, page_rows, parts, n_exp, n_alias, max_rows):
    g_ref, up_ref, w_ref = refs[:3]
    dg_ref, du_ref, dw_ref, og_ref, ou_ref, ow_ref, usc, dsc, ut, ct, gacc, wacc, idx_s, gat_s, sem, tsem = refs[3 + n_alias:]
    e = pl.program_id(0)
    ff = g_ref.shape[2]
    base = core[0] * n_exp
    per_slot = src * page_rows

    def table_copies(exp, slot):
        out = []
        for d in range(src):
            first = st[d * LANES + base + exp]
            at = pl.multiple_of(lax.div(first, PAGE) * PAGE + d * rows, PAGE)
            to = pl.multiple_of(slot * per_slot + d * page_rows, PAGE)
            out.append(pltpu.make_async_copy(idx_all.at[pl.ds(at, page_rows)], idx_s.at[pl.ds(to, page_rows)], tsem.at[0]))
            out.append(pltpu.make_async_copy(gat_all.at[pl.ds(at, page_rows)], gat_s.at[pl.ds(to, page_rows)], tsem.at[1]))
        return out

    slot = lax.rem(e, 2)

    @pl.when(e == 0)
    def _():
        cu = pltpu.make_async_copy(u_all, usc, sem.at[0])
        cd = pltpu.make_async_copy(d_all, dsc, sem.at[1])
        cu.start()
        cd.start()
        for c in table_copies(0, 0):
            c.start()

        def clear(q, carry):
            ut[pl.ds(pl.multiple_of(q * 256, 256), 256), :] = jnp.zeros((256, LANES), jnp.float32)
            return carry

        lax.fori_loop(0, ut.shape[0] // 256, clear, 0)
        cu.wait()
        cd.wait()

    for c in table_copies(e, slot):
        c.wait()

    @pl.when(e + 1 < n_exp)
    def _():
        for c in table_copies(e + 1, 1 - slot):
            c.start()

    off = 0
    for d in range(src):
        first = st[d * LANES + base + e]
        count = st[d * LANES + base + e + 1] - first
        p0 = slot * per_slot + d * page_rows + lax.rem(first, PAGE)

        def gather(q, carry, p0=p0, off=off):
            p = p0 + q * UNROLL
            o = (off + q * UNROLL) * parts
            for r in range(UNROLL):
                t = idx_s[p + r]
                ut[pl.ds(o + r * parts, parts), :] = usc[t].astype(jnp.float32)
                ct[pl.ds(o + r * parts, parts), :] = gat_s[p + r] * dsc[t].astype(jnp.float32)
            return carry

        lax.fori_loop(0, lax.div(count + UNROLL - 1, UNROLL), gather, 0)
        off = off + count
    tiles = lax.div(off + WTILE - 1, WTILE)

    def clear_tail(q, carry):
        ct[pl.ds((off + q * 8) * parts, 8 * parts), :] = jnp.zeros((8 * parts, LANES), jnp.float32)
        return carry

    lax.fori_loop(0, lax.div(tiles * WTILE - off + 7, 8), clear_tail, 0)
    gacc[...] = jnp.zeros_like(gacc)
    wacc[...] = jnp.zeros_like(wacc)

    def tile(j, carry):
        u = load_rows(ut, j * WTILE, WTILE, parts)
        c = load_rows(ct, j * WTILE, WTILE, parts)
        ab = nt_dot(jnp.concatenate([g_ref[0, 0], up_ref[0, 0]], axis=0), u)
        dh = nt_dot(w_ref[0, 0], c)
        a, b = ab[:ff], ab[ff:]
        s = jax.nn.sigmoid(a)
        act = a * s
        h = (act * b).astype(jnp.bfloat16)
        da = (dh * b * (s * (1.0 + a * (1.0 - s)))).astype(jnp.bfloat16)
        db = (dh * act).astype(jnp.bfloat16)
        gacc[...] += nn_dot(jnp.concatenate([da, db], axis=0), u)
        wacc[...] += nn_dot(h, c)
        return carry

    lax.fori_loop(0, tiles, tile, 0)
    dg = gacc[:ff].astype(jnp.bfloat16)
    du = gacc[ff:].astype(jnp.bfloat16)
    dw = wacc[...].astype(jnp.bfloat16)
    dg_ref[0, 0], du_ref[0, 0], dw_ref[0, 0] = dg, du, dw
    og_ref[0], ou_ref[0], ow_ref[0] = dg, du, dw


def weight_grads(layer, starts, core, u_all, d_all, idx_all, gat_all, weights, full, cap):
    n_tok, parts, _ = u_all.shape
    n_layers, n_local, ff, d_model = weights[0].shape
    n_exp = n_local // 2
    src = starts.shape[0] // LANES
    rows = idx_all.shape[0] // src
    page_rows = cdiv(PAGE - 1 + 2 * cap + UNROLL, PAGE) * PAGE
    max_rows = cdiv(src * 2 * cap, WTILE) * WTILE + max(UNROLL, 8)
    max_rows = cdiv(max_rows, 64) * 64
    any_spec = pl.BlockSpec(memory_space=pl.ANY)
    mine = pl.BlockSpec((1, 1, ff, d_model), lambda e, st, core: (layer, core[0] * n_exp + e, 0, 0))
    half = pl.BlockSpec((1, ff, d_model), lambda e, st, core: (e, 0, 0))
    aliased = list(full) if full is not None else []
    outs = pl.pallas_call(
        functools.partial(weight_grad_body, rows=rows, src=src, page_rows=page_rows, parts=parts, n_exp=n_exp,
                          n_alias=len(aliased), max_rows=max_rows),
        grid_spec=pltpu.PrefetchScalarGridSpec(
            num_scalar_prefetch=2,
            grid=(n_exp,),
            in_specs=[any_spec] * 4 + [mine] * 3 + [any_spec] * len(aliased),
            out_specs=[mine] * 3 + [half] * 3,
            scratch_shapes=[pltpu.VMEM((n_tok, parts, LANES), jnp.bfloat16)] * 2
            + [pltpu.VMEM((max_rows * parts, LANES), jnp.float32)] * 2
            + [pltpu.VMEM((2 * ff, d_model), jnp.float32), pltpu.VMEM((ff, d_model), jnp.float32),
               pltpu.SMEM((2 * src * page_rows,), jnp.int32), pltpu.SMEM((2 * src * page_rows,), jnp.float32),
               pltpu.SemaphoreType.DMA((2,)), pltpu.SemaphoreType.DMA((2,))],
        ),
        out_shape=[jax.ShapeDtypeStruct((n_layers, n_local, ff, d_model), jnp.bfloat16)] * 3
        + [jax.ShapeDtypeStruct((n_exp, ff, d_model), jnp.bfloat16)] * 3,
        input_output_aliases={9 + k: k for k in range(len(aliased))},
        compiler_params=pltpu.CompilerParams(dimension_semantics=("arbitrary",), vmem_limit_bytes=VMEM_LIMIT),
        cost_estimate=pl.CostEstimate(flops=6 * 2 * n_tok * 2 * d_model * ff * 4,
                                      bytes_accessed=n_tok * d_model * 4 + 9 * n_exp * ff * d_model * 2, transcendentals=0),
        name="weight_grads",
    )(starts, core, u_all, d_all, idx_all, gat_all, *weights, *aliased)
    return outs[:3], outs[3:]


def merge_body(core, a, b, c, f0, f1, f2, o0, o1, o2):
    o0[0, 0], o1[0, 0], o2[0, 0] = a[0], b[0], c[0]


def merge_half(layer, core, half, full):
    n_layers, n_local, ff, d_model = full[0].shape
    n_exp = n_local // 2
    any_spec = pl.BlockSpec(memory_space=pl.ANY)
    part = pl.BlockSpec((1, ff, d_model), lambda e, core: (e, 0, 0))
    place = pl.BlockSpec((1, 1, ff, d_model), lambda e, core: (layer, (1 - core[0]) * n_exp + e, 0, 0))
    return pl.pallas_call(
        merge_body,
        grid_spec=pltpu.PrefetchScalarGridSpec(
            num_scalar_prefetch=1, grid=(n_exp,), in_specs=[part] * 3 + [any_spec] * 3, out_specs=[place] * 3),
        out_shape=[jax.ShapeDtypeStruct(x.shape, x.dtype) for x in full],
        input_output_aliases={4: 0, 5: 1, 6: 2},
        compiler_params=pltpu.CompilerParams(dimension_semantics=("arbitrary",)),
        cost_estimate=pl.CostEstimate(flops=0, bytes_accessed=6 * n_exp * ff * d_model * 2, transcendentals=0),
        name="merge_half",
    )(core, *half, *full)


def route_tables(ids, gates, ep, n_local):
    n_src, top_k, tok = ids.shape
    n = n_src * top_k * tok
    local = ids - ep * n_local
    here = (local >= 0) & (local < n_local)
    group = jnp.where(here, local, n_local).reshape(-1)
    key, gate = lax.sort((group * n + jnp.arange(n, dtype=jnp.int32), gates.reshape(-1)), num_keys=1, is_stable=False)
    copy = key % n
    token = copy // (top_k * tok) * tok + copy % tok
    counts = jnp.sum((group[:, None] == jnp.arange(n_local)[None, :]).astype(jnp.int32), axis=0)
    ends = jnp.cumsum(counts)
    starts = ends - counts
    n_tiles = jnp.maximum((counts + TILE - 1) // TILE, 1)
    tile_end = jnp.cumsum(n_tiles)
    tile_id = jnp.arange(n // TILE + n_local + 4, dtype=jnp.int32) - 2
    tile_e = jnp.minimum(jnp.sum((tile_end[None, :] <= tile_id[:, None]).astype(jnp.int32), axis=1), n_local - 1)
    pick = (tile_e[:, None] == jnp.arange(n_local)[None, :]).astype(jnp.int32)
    inside = (tile_id - jnp.sum(pick * (tile_end - n_tiles)[None, :], axis=1)) * TILE
    real = (tile_id >= 0) & (tile_id < tile_end[-1])
    tile_row = jnp.where(real, jnp.sum(pick * starts[None, :], axis=1) + inside, 0)
    tile_first = (real & (inside == 0) & (tile_e > 0)).astype(jnp.int32)
    tile_n = jnp.where(real, jnp.clip(jnp.sum(pick * counts[None, :], axis=1) - inside, 0, TILE), 0)
    pad = cdiv(2 * PAGE, TILE) * TILE
    token = jnp.pad(token, (0, pad))
    gate = jnp.pad(gate, (0, pad))
    bounds = jnp.concatenate([jnp.zeros((1,), jnp.int32), ends, jnp.full((LANES - 1 - n_local,), ends[-1], jnp.int32)])
    return (tile_e, tile_first, tile_row, tile_n, tile_end[-1:], token, gate), bounds


def solution(mesh):
    ep_size = mesh.shape['ep']
    dp_size = mesh.shape['dp']
    tok_spec = P(('dp', 'ep'), None)
    route_spec = P(None, ('dp', 'ep'), None)
    whole_spec = P(None, None, None)
    expert_spec = P(None, 'ep', None, None)
    ep_pairs = [(i, 1 - i) for i in range(ep_size)]
    core_pairs = [(i, i ^ 1) for i in range(dp_size)]

    def device_step(tokens, d_out, expert_ids, gate_vals, w_mix, w_gate, w_up, w_down):
        n_layers = w_mix.shape[0]
        n_local = w_gate.shape[1]
        n_experts = n_local * ep_size
        tok, d_model = tokens.shape
        top_k = expert_ids.shape[2]
        parts = d_model // LANES
        cap = cdiv(CAP_FACTOR * tok * top_k, n_experts)
        ep_id = lax.axis_index('ep').astype(jnp.int32)
        dp_id = lax.axis_index('dp').astype(jnp.int32)
        ep = ep_id.reshape(1)
        core = (dp_id % 2).reshape(1)
        weights = (jnp.swapaxes(w_gate, 2, 3), jnp.swapaxes(w_up, 2, 3), w_down)

        def swap(x):
            return lax.ppermute(x, 'ep', ep_pairs)

        def spread(x):
            return lax.all_gather(x, ('dp', 'ep'), axis=0, tiled=True)

        def slab(x):
            return x.reshape(tok, parts, LANES)

        def mixed(x, layer):
            return (x.astype(jnp.float32) + jnp.dot(x, w_mix[layer], preferred_element_type=jnp.float32)).astype(jnp.bfloat16)

        ids = jnp.swapaxes(expert_ids, 1, 2)
        gates = jnp.swapaxes(gate_vals, 1, 2)
        mine = jnp.stack([ids.astype(jnp.float32), gates])
        theirs = swap(mine)
        both = jnp.where(ep_id == 0, jnp.stack([mine, theirs], 2), jnp.stack([theirs, mine], 2))
        both_ids = both[0].astype(jnp.int32)
        tables, packed = [], []
        for layer in range(n_layers):
            table, bounds = route_tables(both_ids[layer], both[1, layer], ep_id, n_local)
            tables.append(table)
            token, gate = table[5], table[6]
            packed.append(jnp.stack([jnp.concatenate([token + dp_id * (2 * tok), jnp.pad(bounds, (0, PAGE - LANES))])
                                     .astype(jnp.float32), jnp.pad(gate, (0, PAGE))]))
        rows = packed[0].shape[1]
        shared = lax.all_gather(jnp.stack(packed), 'dp', axis=2)
        shared = shared.reshape(n_layers, 2, dp_size, rows)

        d_slab = slab(d_out)
        d_other = swap(d_slab)
        d_spread = spread(d_slab)

        x_in, u_slabs, u_others, xs, u_spreads = tokens, [], [], [], []
        for layer in range(n_layers):
            u = mixed(x_in, layer)
            u_slab = slab(u)
            u_other = swap(u_slab)
            own, other = token_kernel(forward_body, "experts_forward", layer, tables[layer], ep, (u_slab, u_other), weights)
            xs.append(x_in)
            u_slabs.append(u_slab)
            u_others.append(u_other)
            u_spreads.append(spread(u_slab))
            x_in = (u.astype(jnp.float32) + own + swap(other)).astype(jnp.bfloat16)
        layer_out = x_in

        d_y, full = d_out, None
        d_mix = [None] * n_layers
        for layer in reversed(range(n_layers)):
            own, other = token_kernel(backward_body, "experts_backward", layer, tables[layer], ep,
                                      (u_slabs[layer], u_others[layer], d_slab, d_other), weights)
            d_u = (d_y.astype(jnp.float32) + own + swap(other)).astype(jnp.bfloat16)
            ids_all = shared[layer, 0].astype(jnp.int32)
            starts = ids_all[:, rows - PAGE:rows - PAGE + LANES].reshape(-1)
            full, half = weight_grads(layer, starts, core, u_spreads[layer], d_spread, ids_all.reshape(-1),
                                      shared[layer, 1].reshape(-1), weights, full, cap)
            full = merge_half(layer, core, [lax.ppermute(x, 'dp', core_pairs) for x in half], full)
            d_mix[layer] = lax.psum(jnp.einsum('td,te->de', xs[layer], d_u, preferred_element_type=jnp.float32)
                                    .astype(jnp.bfloat16), ('dp', 'ep'))
            d_y = (d_u.astype(jnp.float32)
                   + jnp.einsum('te,de->td', d_u, w_mix[layer], preferred_element_type=jnp.float32)).astype(jnp.bfloat16)
            if layer:
                d_slab = slab(d_y)
                d_other = swap(d_slab)
                d_spread = spread(d_slab)
        return (layer_out, d_y, jnp.stack(d_mix), jnp.swapaxes(full[0], 2, 3), jnp.swapaxes(full[1], 2, 3), full[2])

    return jax.shard_map(device_step, mesh=mesh,
                         in_specs=(tok_spec, tok_spec, route_spec, route_spec, whole_spec,
                                   expert_spec, expert_spec, expert_spec),
                         out_specs=(tok_spec, tok_spec, whole_spec, expert_spec, expert_spec, expert_spec),
                         check_vma=False)
```

time: 4490 us -> 1220 us (0.27)
  waiting for transfers between devices: 1590 us -> 255 us
  local copies, waits for them, and re-layouts: 1210 us -> 22.5 us
  blocking collectives: 854 us -> 0 us
  Pallas kernels: 0 us -> 826 us
  matrix products: 473 us -> 9.22 us
  other arithmetic: 289 us -> 37.6 us
    gather x16 -> x0, local copies, waits for them, and re-layouts: 1050 us -> none  [the longest x4 271 us: route_tables(): sort_order[jnp.minimum(starts[:, None] + slot_pos[None, :], n_copies - 1)]]
    psum x2 -> x1, waiting for transfers between devices: 884 us -> 21.4 us  [device_step(): lax.psum(jnp.einsum('td,te->de', xs[layer], d_u, preferred_element_type=j...]
    all_to_all x3 -> x0, blocking collectives: 854 us -> none  [the longest x2 573 us: layer_backward(): recv_grad = lax.all_to_all(send_grad, 'ep', 0, 0, tiled=True)]
    pallas_call x0 -> x8, Pallas kernels: none -> 826 us  [the longest x2 418 us: weight_grads(): pl.pallas_call(functools.partial(weight_grad_body, rows=rows, src=src, pa...]
    all_to_all x5 -> x0, waiting for transfers between devices: 704 us -> none  [the longest x2 267 us: layer_backward(): lax.all_to_all(d_recv, 'ep', 0, 0, tiled=True)]
    dot_general x24 -> x6, matrix products: 473 us -> 9.22 us  [the longest x2 4.31 us: device_step(): jnp.einsum('td,te->de', xs[layer], d_u, preferred_element_type=jnp.float32)]
    ppermute x0 -> x15, waiting for transfers between devices: none -> 233 us  [the longest x9 231 us: swap(): return lax.ppermute(x, 'ep', ep_pairs)]
    scatter-add x2 -> x0, other arithmetic: 114 us -> none  [route_tables(): counts = jnp.bincount(flat_ids, length=n_experts)]
  transfers between devices with their start and end apart: 7 -> 21, of which waited for: 6 -> 9; matrix products, arithmetic and copies ran while one was open for 19% -> 4% of each run, Pallas kernels for 0% -> 67%
where the time goes in v1:
time: 1220 us; the launch traced here: 1200 us
  Pallas kernels  826 us (68%)
  waiting for transfers between devices  255 us (21%)
  other arithmetic  37.6 us (3%)
  starting transfers between devices  35.3 us (3%)
  local copies, waits for them, and re-layouts  22.5 us (2%)
  between operations  14.7 us (1%)
    pallas_call x2, Pallas kernels, weight_grads(): pl.pallas_call(functools.partial(weight_grad_body, rows=rows, src=src, pa...  418 us
    pallas_call x4, Pallas kernels, token_kernel(): pl.pallas_call(functools.partial(body, layer=layer, tok=tok, parts=parts)...  362 us
    ppermute x9, waiting for transfers between devices, swap(): return lax.ppermute(x, 'ep', ep_pairs)  231 us
    pallas_call x2, Pallas kernels, merge_half(): pl.pallas_call(merge_body, grid_spec=pltpu.PrefetchScalarGridSpec(num_sca...  46.1 us
    ppermute x9, starting transfers between devices, swap(): return lax.ppermute(x, 'ep', ep_pairs)  33.9 us
  transfers between devices with their start and end apart: 21, of which 9 were waited for; matrix products, arithmetic and copies ran while one was open for 4% of the time, Pallas kernels for 67%

profile of v1, /device:TPU:0, one launch (start us, length us, event | category | flops | bytes accessed | tf_op | source)
XLA Modules:
  0.0 1200.4 jit_solution(2538369369514504526)
XLA Ops:
  8.9 3.3 collective-permute-start
  12.3 3.5 collective-permute-done
  18.7 6.4 sort.30
  25.2 6.4 sort.31
  36.0 1.1 reshape.350.d_own
  37.2 1.8 add_convert_fusion.7
  39.2 1.8 collective-permute-start.1
  42.4 1.2 and_convert_fusion.1.tf
  43.5 1.1 clamp_select_fusion.1
  44.6 18.9 %collective-permute-done.1.u_oth = bf16[1024,4,128]{2,1,0:T(4,128)(2,1)} collective-permute-done((bf16[1024,4,128]{2,1,0:T(4,128)(2,1)S(1)}, bf16[1024,4,128]{2,1,0:T(4,128)(2,1)}, u32[]{:S(2)}, u32[]{:S(2)}) %collective-permute-start.1) | collective-permute-done | bytes 1048608 | tf_op jit(solution)/shard_map/ppermute | solution.py:410
  63.6 86.9 %experts_forward.2 = (f32[1024,512]{1,0:T(8,128)}, f32[1024,512]{1,0:T(8,128)}) custom-call(s32[196]{0:T(256)} %copy-done.22, s32[196]{0:T(256)} %and_convert_fusion.1.tf, s32[196]{0:T(256)} %get-tuple-element.121.tr, s32[196]{0:T(256)} %get-tuple-element.120.tn, s32[1]{0:T(128)} %bitcast.9.nt, s32[18432]{0:T(1024)} %get-tuple-element.113.idx, ...), custom_call_target="tpu_custom_call" | custom-call | flops 19327352832 | bytes 37748736 | tf_op jit(solution)/shard_map/experts_forward/pallas_call | solution.py:181
  150.6 46.0 %collective-permute-done.2 = f32[1024,512]{1,0:T(8,128)S(1)} collective-permute-done((f32[1024,512]{1,0:T(8,128)}, f32[1024,512]{1,0:T(8,128)S(1)}, u32[]{:S(2)}, u32[]{:S(2)}) %collective-permute-start.2) | collective-permute-done | bytes 2097184 | tf_op jit(solution)/shard_map/ppermute | solution.py:410
  196.6 2.6 add_convert_fusion.6
  200.9 1.1 reshape.349.u_own
  203.3 1.6 collective-permute-start.3
  205.5 1.2 and_convert_fusion.tf
  206.8 1.2 clamp_select_fusion
  207.9 32.1 %collective-permute-done.5.d_oth = bf16[1024,4,128]{2,1,0:T(4,128)(2,1)S(1)} collective-permute-done((bf16[1024,4,128]{2,1,0:T(4,128)(2,1)S(1)}, bf16[1024,4,128]{2,1,0:T(4,128)(2,1)S(1)}, u32[]{:S(2)}, u32[]{:S(2)}) %collective-permute-start.5) | collective-permute-done | bytes 1048608 | tf_op jit(solution)/shard_map/ppermute | solution.py:410
  240.1 34.3 %collective-permute-done.3.u_oth = bf16[1024,4,128]{2,1,0:T(4,128)(2,1)S(1)} collective-permute-done((bf16[1024,4,128]{2,1,0:T(4,128)(2,1)S(1)}, bf16[1024,4,128]{2,1,0:T(4,128)(2,1)S(1)}, u32[]{:S(2)}, u32[]{:S(2)}) %collective-permute-start.3) | collective-permute-done | bytes 1048608 | tf_op jit(solution)/shard_map/ppermute | solution.py:410
  274.3 1.0 copy-done.14
  275.3 93.7 %experts_backward.2 = (f32[1024,512]{1,0:T(8,128)}, f32[1024,512]{1,0:T(8,128)}) custom-call(s32[196]{0:T(256)} %copy-done.23, s32[196]{0:T(256)} %and_convert_fusion.tf, s32[196]{0:T(256)} %get-tuple-element.123.tr, s32[196]{0:T(256)} %get-tuple-element.122.tn, s32[1]{0:T(128)} %bitcast.16.nt, s32[18432]{0:T(1024)} %get-tuple-element.115.idx, ...), custom_call_target="tpu_custom_call" | custom-call | flops 38654705664 | bytes 37748736 | tf_op jit(solution)/shard_map/experts_backward/pallas_call | solution.py:181
  369.0 1.4 collective-permute-start.6
  370.4 53.2 %collective-permute-done.6 = f32[1024,512]{1,0:T(8,128)S(1)} collective-permute-done((f32[1024,512]{1,0:T(8,128)}, f32[1024,512]{1,0:T(8,128)S(1)}, u32[]{:S(2)}, u32[]{:S(2)}) %collective-permute-start.6) | collective-permute-done | bytes 2097184 | tf_op jit(solution)/shard_map/ppermute | solution.py:410
  423.7 2.3 add_convert_fusion.3
  426.0 1.0 copy-done.17
  427.7 1.3 reshape.351.d_own
  429.2 3.5 reshape.355
  432.6 1.3 slice_bitcast_fusion
  434.0 1.0 copy.70
  436.5 197.8 %weight_grads.2 = (bf16[2,64,192,512]{3,2,1,0:T(8,128)(2,1)}, bf16[2,64,192,512]{3,2,1,0:T(8,128)(2,1)}, bf16[2,64,192,512]{3,2,1,0:T(8,128)(2,1)}, bf16[32,192,...) custom-call(s32[1024]{0:T(1024)} %slice_bitcast_fusion.4.st, s32[1]{0:T(128)} %bitcast.20.core, ...), custom_call_target="tpu_custom_call" | custom-call | flops 154618822656 | bytes 90177536 | tf_op jit(solution)/shard_map/weight_grads/pallas_call | solution.py:309
  636.8 1.3 slice_bitcast_fusion.5.st
  638.1 22.9 %collective-permute-start.7 = (bf16[1024,4,128]{2,1,0:T(4,128)(2,1)}, bf16[1024,4,128]{2,1,0:T(4,128)(2,1)}, u32[]{:S(2)}, u32[]{:S(2)}) collective-permute-start(bf16[1024,4,128]{2,1,0:T(4,128)(2,1)} %reshape.351.d_own), channel_id=1, source_target_pairs={{0,8},{8,0},{1,9},{9,1},{2,10},{10,2},{3,11},{11,3},{4,12},{12,4},... | collective-permute-start | bytes 3145736 | tf_op jit(solution)/shard_map/ppermute | solution.py:410
  661.0 1.4 collective-permute-done.11.c
  662.5 23.0 %merge_half.2 = (bf16[2,64,192,512]{3,2,1,0:T(8,128)(2,1)}, bf16[2,64,192,512]{3,2,1,0:T(8,128)(2,1)}, bf16[2,64,192,512]{3,2,1,0:T(8,128)(2,1)}) custom-call(s32[1]{0:T(128)} %bitcast.20.core, bf16[32,192,512]{2,1,0:T(8,128)(2,1)} %collective-permute-done.9.a, ...), custom_call_target="tpu_custom_call", output_to_operand_aliasing={{0}: (4, {}), {1}: (5, {}), {2}: (6, {})} | custom-call | bytes 37748736 | tf_op jit(solution)/shard_map/merge_half/pallas_call | solution.py:344
  685.5 220.3 %weight_grads.3 = (bf16[2,64,192,512]{3,2,1,0:T(8,128)(2,1)}, bf16[2,64,192,512]{3,2,1,0:T(8,128)(2,1)}, bf16[2,64,192,512]{3,2,1,0:T(8,128)(2,1)}, bf16[32,192,...) custom-call(s32[1024]{0:T(1024)} %slice_bitcast_fusion.5.st, ...), custom_call_target="tpu_custom_call", output_to_operand_aliasing={{0}: (9, {}), {1}: (10, {}), {2}: (11, {})} | custom-call | flops 154618822656 | bytes 90177536 | tf_op jit(solution)/shard_map/weight_grads/pallas_call | solution.py:309
  906.4 95.1 %experts_backward.3 = (f32[1024,512]{1,0:T(8,128)}, f32[1024,512]{1,0:T(8,128)}) custom-call(s32[196]{0:T(256)} %copy-done.22, s32[196]{0:T(256)} %and_convert_fusion.1.tf, s32[196]{0:T(256)} %get-tuple-element.121.tr, s32[196]{0:T(256)} %get-tuple-element.120.tn, s32[1]{0:T(128)} %bitcast.9.nt, s32[18432]{0:T(1024)} %get-tuple-element.113.idx, ...), custom_call_target="tpu_custom_call" | custom-call | flops 38654705664 | bytes 37748736 | tf_op jit(solution)/shard_map/experts_backward/pallas_call | solution.py:181
  1001.5 86.4 %experts_forward.3 = (f32[1024,512]{1,0:T(8,128)}, f32[1024,512]{1,0:T(8,128)}) custom-call(s32[196]{0:T(256)} %copy-done.23, s32[196]{0:T(256)} %and_convert_fusion.tf, s32[196]{0:T(256)} %get-tuple-element.123.tr, s32[196]{0:T(256)} %get-tuple-element.122.tn, s32[1]{0:T(128)} %bitcast.16.nt, s32[18432]{0:T(1024)} %get-tuple-element.115.idx, ...), custom_call_target="tpu_custom_call" | custom-call | flops 19327352832 | bytes 37748736 | tf_op jit(solution)/shard_map/experts_forward/pallas_call | solution.py:181
  1087.9 2.5 collective-permute-start.4
  1090.4 2.8 fusion.1
  1093.2 2.3 add_convert_fusion.1
  1096.5 1.5 fusion
  1098.1 43.3 %collective-permute-done.4 = f32[1024,512]{1,0:T(8,128)} collective-permute-done((f32[1024,512]{1,0:T(8,128)}, f32[1024,512]{1,0:T(8,128)}, u32[]{:S(2)}, u32[]{:S(2)}) %collective-permute-start.4) | collective-permute-done | bytes 2097184 | tf_op jit(solution)/shard_map/ppermute | solution.py:410
  1141.4 3.3 add_convert_fusion.4
  1144.7 1.7 add_convert_fusion
  1146.4 21.4 %all-reduce.11.cloned.1.call-done = (bf16[1,512,512]{1,2,0:T(8,128)(2,1)}, bf16[1,512,512]{1,2,0:T(8,128)(2,1)}) async-done(((bf16[1,512,512]{1,2,0:T(8,128)(2,1)}, bf16[1,512,512]{1,2,0:T(8,128)(2,1)}), (bf16[1,512,512]{1,2,0:T(8,128)(2,1)}, bf16[1,512,512]{1,2,0:T(8,128)(2,1)})) %all-reduce.11.cloned.1.call-update) | async-done | bytes 1048592 | tf_op jit(solution)/shard_map/psum | solution.py:466
  1167.8 1.3 pad_maximum_fusion
  1169.1 1.3 copy.58
  1170.5 23.1 %merge_half.3 = (bf16[2,64,192,512]{3,2,1,0:T(8,128)(2,1)}, bf16[2,64,192,512]{3,2,1,0:T(8,128)(2,1)}, bf16[2,64,192,512]{3,2,1,0:T(8,128)(2,1)}) custom-call(s32[1]{0:T(128)} %bitcast.20.core, bf16[32,192,512]{2,1,0:T(8,128)(2,1)} %collective-permute-done.12.a, ...), custom_call_target="tpu_custom_call", output_to_operand_aliasing={{0}: (4, {}), {1}: (5, {}), {2}: (6, {})} | custom-call | bytes 37748736 | tf_op jit(solution)/shard_map/merge_half/pallas_call | solution.py:344
  (156 shorter events, 20.7 us)
Async XLA Ops:
  7.2 422.0 %all-gather.15.cloned.1.call-start = ((), (), s32[]{:S(2)}) async-start(), calls=%async_computation.4 | async-start | bytes 2801664 | tf_op jit(solution)/shard_map/all_gather | solution.py:435
  8.9 6.8 collective-permute-start
  17.3 18.7 %copy-start.3 = (bf16[1024,512]{1,0:T(8,128)(2,1)S(1)}, bf16[1024,512]{1,0:T(8,128)(2,1)}, u32[]{:S(2)}) copy-start(bf16[1024,512]{1,0:T(8,128)(2,1)} %param.9) | copy-start | bytes 3145732
  33.2 3.9 copy-start.20
  33.2 3.8 copy-start.21
  35.0 2.2 copy-start.24
  35.9 400.6 %all-gather.13.cloned.1.call-start = ((), (), s32[]{:S(2)}) async-start(), calls=%async_computation.3 | async-start | bytes 17825792 | tf_op jit(solution)/shard_map/all_gather | solution.py:413
  37.1 399.4 %all-gather.11.cloned.1.call-start = ((), (), s32[]{:S(2)}) async-start(), calls=%async_computation.2 | async-start | bytes 17825792 | tf_op jit(solution)/shard_map/all_gather | solution.py:413
  38.9 24.7 %copy-start.9 = (bf16[1024,512]{1,0:T(8,128)(2,1)}, bf16[1024,512]{1,0:T(8,128)(2,1)S(1)}, u32[]{:S(2)}) copy-start(bf16[1024,512]{1,0:T(8,128)(2,1)S(1)} %add_convert_fusion.7) | copy-start | bytes 3145732
  39.2 24.4 %copy-start = (bf16[1024,4,128]{2,1,0:T(4,128)(2,1)}, bf16[1024,4,128]{2,1,0:T(4,128)(2,1)S(1)}, u32[]{:S(2)}) copy-start(bf16[1024,4,128]{2,1,0:T(4,128)(2,1)S(1)} %reshape.347.u_own) | copy-start | bytes 3145732
  39.2 24.4 %collective-permute-start.1 = (bf16[1024,4,128]{2,1,0:T(4,128)(2,1)S(1)}, bf16[1024,4,128]{2,1,0:T(4,128)(2,1)}, u32[]{:S(2)}, u32[]{:S(2)}) collective-permute-start(bf16[1024,4,128]{2,1,0:T(4,128)(2,1)S(1)} %reshape.347.u_own), channel_id=1, source_target_pairs={{0,8},{8,0},{1,9},{9,1},{2,10},{10,2},{3,11},{11,3},{4,12},{12,4},... | collective-permute-start | bytes 3145736 | tf_op jit(solution)/shard_map/ppermute | solution.py:410
  42.2 21.3 %copy-start.22 = (s32[196]{0:T(256)}, s32[196]{0:T(256)S(1)}, u32[]{:S(2)}) copy-start(s32[196]{0:T(256)S(1)} %broadcast_minimum_fusion.1.te) | copy-start | bytes 2356
  150.5 46.1 %collective-permute-start.2 = (f32[1024,512]{1,0:T(8,128)}, f32[1024,512]{1,0:T(8,128)S(1)}, u32[]{:S(2)}, u32[]{:S(2)}) collective-permute-start(f32[1024,512]{1,0:T(8,128)} %get-tuple-element.39), channel_id=1, source_target_pairs={{0,8},{8,0},{1,9},{9,1},{2,10},{10,2},{3,11},{11,3},{4,12},{12,4},... | collective-permute-start | bytes 6291464 | tf_op jit(solution)/shard_map/ppermute | solution.py:410
  196.6 3.6 copy-start.26
  200.9 1.7 copy-start.5
  200.9 2.0 copy-start.2
  202.0 1.3 copy-start.1
  202.0 483.5 %all-gather.7.cloned.1.call-start = ((), (), s32[]{:S(2)}) async-start(), calls=%async_computation | async-start | bytes 17825792 | tf_op jit(solution)/shard_map/all_gather | solution.py:413
  202.6 482.9 %all-gather.9.cloned.1.call-start = ((), (), s32[]{:S(2)}) async-start(), calls=%async_computation.1 | async-start | bytes 17825792 | tf_op jit(solution)/shard_map/all_gather | solution.py:413
  202.9 37.2 %collective-permute-start.5 = (bf16[1024,4,128]{2,1,0:T(4,128)(2,1)S(1)}, bf16[1024,4,128]{2,1,0:T(4,128)(2,1)S(1)}, u32[]{:S(2)}, u32[]{:S(2)}) collective-permute-start(bf16[1024,4,128]{2,1,0:T(4,128)(2,1)S(1)} %copy-done.2), channel_id=1, source_target_pairs={{0,8},{8,0},{1,9},{9,1},{2,10},{10,2},{3,11},{11,3},{4,12},{12,4},... | collective-permute-start | bytes 3145736 | tf_op jit(solution)/shard_map/ppermute | solution.py:410
  203.3 71.0 %collective-permute-start.3 = (bf16[1024,4,128]{2,1,0:T(4,128)(2,1)S(1)}, bf16[1024,4,128]{2,1,0:T(4,128)(2,1)S(1)}, u32[]{:S(2)}, u32[]{:S(2)}) collective-permute-start(bf16[1024,4,128]{2,1,0:T(4,128)(2,1)S(1)} %copy-done.1), channel_id=1, source_target_pairs={{0,8},{8,0},{1,9},{9,1},{2,10},{10,2},{3,11},{11,3},{4,12},{12,4},... | collective-permute-start | bytes 3145736 | tf_op jit(solution)/shard_map/ppermute | solution.py:410
  205.4 69.9 %copy-start.23 = (s32[196]{0:T(256)}, s32[196]{0:T(256)S(1)}, u32[]{:S(2)}) copy-start(s32[196]{0:T(256)S(1)} %broadcast_minimum_fusion.te) | copy-start | bytes 2356
  240.1 34.3 %copy-start.29 = (bf16[1024,4,128]{2,1,0:T(4,128)(2,1)}, bf16[1024,4,128]{2,1,0:T(4,128)(2,1)S(1)}, u32[]{:S(2)}) copy-start(bf16[1024,4,128]{2,1,0:T(4,128)(2,1)S(1)} %collective-permute-done.5.d_oth) | copy-start | bytes 3145732
  275.3 148.4 %copy-start.4 = (bf16[1024,512]{1,0:T(8,128)(2,1)S(1)}, bf16[1024,512]{1,0:T(8,128)(2,1)}, u32[]{:S(2)}) copy-start(bf16[1024,512]{1,0:T(8,128)(2,1)} %param.9) | copy-start | bytes 3145732
  369.0 54.6 %collective-permute-start.6 = (f32[1024,512]{1,0:T(8,128)}, f32[1024,512]{1,0:T(8,128)S(1)}, u32[]{:S(2)}, u32[]{:S(2)}) collective-permute-start(f32[1024,512]{1,0:T(8,128)} %get-tuple-element.45), channel_id=1, source_target_pairs={{0,8},{8,0},{1,9},{9,1},{2,10},{10,2},{3,11},{11,3},{4,12},{12,4},... | collective-permute-start | bytes 6291464 | tf_op jit(solution)/shard_map/ppermute | solution.py:410
  423.7 3.3 copy-start.27
  426.0 1.0 copy-start.17
  427.7 1.4 copy-start.7
  429.1 738.7 %all-reduce.11.cloned.1.call-start = ((), (), s32[]{:S(2)}) async-start(), calls=%async_computation.5 | async-start | bytes 2097152 | tf_op jit(solution)/shard_map/psum | solution.py:466
  436.5 198.4 %copy-start.11 = (s32[1,152,8,128]{3,2,1,0:T(8,128)S(1)}, s32[1,152,8,128]{3,2,1,0:T(8,128)}, u32[]{:S(2)}) copy-start(s32[1,152,8,128]{3,2,1,0:T(8,128)} %get-tuple-element.102) | copy-start | bytes 1867780
  436.5 199.4 %copy-start.10 = (f32[1,152,8,128]{3,2,1,0:T(8,128)S(1)}, f32[1,152,8,128]{3,2,1,0:T(8,128)}, u32[]{:S(2)}) copy-start(f32[1,152,8,128]{3,2,1,0:T(8,128)} %get-tuple-element.104) | copy-start | bytes 1867780
  634.3 26.7 %collective-permute-start.9 = (bf16[32,192,512]{2,1,0:T(8,128)(2,1)}, bf16[32,192,512]{2,1,0:T(8,128)(2,1)}, u32[]{:S(2)}, u32[]{:S(2)}) collective-permute-start(bf16[32,192,512]{2,1,0:T(8,128)(2,1)} %get-tuple-element.48), channel_id=1, source_target_pairs={{0,1},{1,0},{2,3},{3,2},{4,5},{5,4},{6,7},{7,6},{8,9},{9,8},{10,11... | collective-permute-start | bytes 18874376 | tf_op jit(solution)/shard_map/ppermute | solution.py:465
  634.4 26.6 %collective-permute-start.10 = (bf16[32,192,512]{2,1,0:T(8,128)(2,1)}, bf16[32,192,512]{2,1,0:T(8,128)(2,1)}, u32[]{:S(2)}, u32[]{:S(2)}) collective-permute-start(bf16[32,192,512]{2,1,0:T(8,128)(2,1)} %get-tuple-element.49), channel_id=1, source_target_pairs={{0,1},{1,0},{2,3},{3,2},{4,5},{5,4},{6,7},{7,6},{8,9},{9,8},{10,11... | collective-permute-start | bytes 18874376 | tf_op jit(solution)/shard_map/ppermute | solution.py:465
  634.9 27.6 %collective-permute-start.11 = (bf16[32,192,512]{2,1,0:T(8,128)(2,1)}, bf16[32,192,512]{2,1,0:T(8,128)(2,1)}, u32[]{:S(2)}, u32[]{:S(2)}) collective-permute-start(bf16[32,192,512]{2,1,0:T(8,128)(2,1)} %get-tuple-element.50), channel_id=1, source_target_pairs={{0,1},{1,0},{2,3},{3,2},{4,5},{5,4},{6,7},{7,6},{8,9},{9,8},{10,11... | collective-permute-start | bytes 18874376 | tf_op jit(solution)/shard_map/ppermute | solution.py:465
  638.1 268.3 %collective-permute-start.7 = (bf16[1024,4,128]{2,1,0:T(4,128)(2,1)}, bf16[1024,4,128]{2,1,0:T(4,128)(2,1)}, u32[]{:S(2)}, u32[]{:S(2)}) collective-permute-start(bf16[1024,4,128]{2,1,0:T(4,128)(2,1)} %reshape.351.d_own), channel_id=1, source_target_pairs={{0,8},{8,0},{1,9},{9,1},{2,10},{10,2},{3,11},{11,3},{4,12},{12,4},... | collective-permute-start | bytes 3145736 | tf_op jit(solution)/shard_map/ppermute | solution.py:410
  905.8 264.7 %collective-permute-start.12 = (bf16[32,192,512]{2,1,0:T(8,128)(2,1)}, bf16[32,192,512]{2,1,0:T(8,128)(2,1)}, u32[]{:S(2)}, u32[]{:S(2)}) collective-permute-start(bf16[32,192,512]{2,1,0:T(8,128)(2,1)} %get-tuple-element.57), channel_id=1, source_target_pairs={{0,1},{1,0},{2,3},{3,2},{4,5},{5,4},{6,7},{7,6},{8,9},{9,8},{10,11... | collective-permute-start | bytes 18874376 | tf_op jit(solution)/shard_map/ppermute | solution.py:465
  905.8 264.6 %collective-permute-start.13 = (bf16[32,192,512]{2,1,0:T(8,128)(2,1)}, bf16[32,192,512]{2,1,0:T(8,128)(2,1)}, u32[]{:S(2)}, u32[]{:S(2)}) collective-permute-start(bf16[32,192,512]{2,1,0:T(8,128)(2,1)} %get-tuple-element.58), channel_id=1, source_target_pairs={{0,1},{1,0},{2,3},{3,2},{4,5},{5,4},{6,7},{7,6},{8,9},{9,8},{10,11... | collective-permute-start | bytes 18874376 | tf_op jit(solution)/shard_map/ppermute | solution.py:465
  906.3 264.1 %collective-permute-start.14 = (bf16[32,192,512]{2,1,0:T(8,128)(2,1)}, bf16[32,192,512]{2,1,0:T(8,128)(2,1)}, u32[]{:S(2)}, u32[]{:S(2)}) collective-permute-start(bf16[32,192,512]{2,1,0:T(8,128)(2,1)} %get-tuple-element.59), channel_id=1, source_target_pairs={{0,1},{1,0},{2,3},{3,2},{4,5},{5,4},{6,7},{7,6},{8,9},{9,8},{10,11... | collective-permute-start | bytes 18874376 | tf_op jit(solution)/shard_map/ppermute | solution.py:465
  1001.5 88.9 %copy-start.16 = (bf16[1024,512]{1,0:T(8,128)(2,1)S(1)}, bf16[1024,512]{1,0:T(8,128)(2,1)}, u32[]{:S(2)}) copy-start(bf16[1024,512]{1,0:T(8,128)(2,1)} %copy-done.15) | copy-start | bytes 3145732
  1001.5 91.7 %collective-permute-start.8 = (f32[1024,512]{1,0:T(8,128)}, f32[1024,512]{1,0:T(8,128)}, u32[]{:S(2)}, u32[]{:S(2)}) collective-permute-start(f32[1024,512]{1,0:T(8,128)} %get-tuple-element.47), channel_id=1, source_target_pairs={{0,8},{8,0},{1,9},{9,1},{2,10},{10,2},{3,11},{11,3},{4,12},{12,4},... | collective-permute-start | bytes 6291464 | tf_op jit(solution)/shard_map/ppermute | solution.py:410
  1087.9 5.3 copy-start.8
  1087.9 5.3 copy-start.13
  1087.9 53.4 %collective-permute-start.4 = (f32[1024,512]{1,0:T(8,128)}, f32[1024,512]{1,0:T(8,128)}, u32[]{:S(2)}, u32[]{:S(2)}) collective-permute-start(f32[1024,512]{1,0:T(8,128)} %get-tuple-element.43), channel_id=1, source_target_pairs={{0,8},{8,0},{1,9},{9,1},{2,10},{10,2},{3,11},{11,3},{4,12},{12,4},... | collective-permute-start | bytes 6291464 | tf_op jit(solution)/shard_map/ppermute | solution.py:410
  1093.2 3.3 copy-start.25
  1096.5 44.8 %copy-start.6 = (bf16[1024,512]{1,0:T(8,128)(2,1)S(1)}, bf16[1024,512]{1,0:T(8,128)(2,1)}, u32[]{:S(2)}) copy-start(bf16[1024,512]{1,0:T(8,128)(2,1)} %copy-done.5) | copy-start | bytes 3145732
  1096.5 44.8 %copy-start.12 = (f32[1024,512]{1,0:T(8,128)S(1)}, f32[1024,512]{1,0:T(8,128)}, u32[]{:S(2)}) copy-start(f32[1024,512]{1,0:T(8,128)} %get-tuple-element.42) | copy-start | bytes 6291460
  1141.4 3.3 copy-start.19
  1141.4 3.3 copy-start.28
  (3 other events, 2.9 us)
Sparse Core Ops, SparseCore 0:
  36.0 26.6 all-gather.14
  65.5 76.0 all-gather.12
  202.1 100.8 all-gather.10
  305.8 87.4 all-gather.6
  429.2 76.0 all-gather.8
  1098.2 69.5 all-reduce.10

commit v2 on v1

--- a/solution.py
+++ b/solution.py
@@ -7,12 +7,14 @@
 from jax.experimental.pallas import tpu as pltpu
 from jax.sharding import PartitionSpec as P
 
+
 CAP_FACTOR = 3
 LANES = 128
 TILE = 128
 WTILE = 256
 BATCH = 16
 UNROLL = 16
+SLOTS = 4
 PAGE = 1024
 VMEM_LIMIT = 62 * 2**20
 
@@ -75,7 +77,7 @@
 
 
 def expert_copies(weights, buf, sem, layer, e):
-    slot = lax.rem(e, 2)
+    slot = lax.rem(e, SLOTS)
     ff = weights[0].shape[2]
     return [pltpu.make_async_copy(w.at[layer, e], buf.at[slot, pl.ds(k * ff, ff)], sem.at[slot])
             for k, w in enumerate(weights)]
@@ -86,8 +88,9 @@
     ahead = list(copies) + expert_copies(weights, wbuf, wsem, layer, 0)
     for c in ahead:
         c.start()
-    for c in expert_copies(weights, wbuf, wsem, layer, 1):
-        c.start()
+    for e in range(1, min(SLOTS - 1, n_local)):
+        for c in expert_copies(weights, wbuf, wsem, layer, e):
+            c.start()
     for c in ahead:
         c.wait()
 
@@ -99,12 +102,12 @@
             for c in expert_copies(weights, wbuf, wsem, layer, e):
                 c.wait()
 
-            @pl.when(e + 1 < n_local)
-            def _():
-                for c in expert_copies(weights, wbuf, wsem, layer, e + 1):
-                    c.start()
-
-        step(i, lax.rem(e, 2))
+        @pl.when((tile_first[i + 1] == 1) & (e + SLOTS - 2 < n_local))
+        def _():
+            for c in expert_copies(weights, wbuf, wsem, layer, e + SLOTS - 2):
+                c.start()
+
+        step(i, lax.rem(e, SLOTS))
         return carry
 
     lax.fori_loop(0, n_steps, one, 0)
@@ -170,9 +173,9 @@
     write_sums(acc, own_ref, other_ref, ep, tok, parts)
 
 
-def token_kernel(body, name, layer, tables, ep, slabs, weights):
+def token_kernel(body, layer, tables, ep, slabs, weights):
     tok, parts, _ = slabs[0].shape
-    n_layers, n_local, ff, d_model = weights[0].shape
+    _, n_local, ff, d_model = weights[0].shape
     n_pairs = len(slabs) // 2
     rows_spec = pl.BlockSpec((tok, d_model), lambda i, *_: (0, 0))
     any_spec = pl.BlockSpec(memory_space=pl.ANY)
@@ -187,29 +190,27 @@
             out_specs=[rows_spec] * 2,
             scratch_shapes=[pltpu.VMEM((2 * tok, parts, LANES), jnp.bfloat16)] * n_pairs
             + [pltpu.VMEM((TILE * parts, LANES), jnp.float32)] * (n_pairs + 1)
-            + [pltpu.VMEM((2 * tok * parts, LANES), jnp.float32), pltpu.VMEM((2, 3 * ff, d_model), jnp.bfloat16),
-               pltpu.SemaphoreType.DMA(sem_shape), pltpu.SemaphoreType.DMA((2,))],
+            + [pltpu.VMEM((2 * tok * parts, LANES), jnp.float32), pltpu.VMEM((SLOTS, 3 * ff, d_model), jnp.bfloat16),
+               pltpu.SemaphoreType.DMA(sem_shape), pltpu.SemaphoreType.DMA((SLOTS,))],
         ),
         out_shape=[jax.ShapeDtypeStruct((tok, d_model), jnp.float32)] * 2,
         compiler_params=pltpu.CompilerParams(dimension_semantics=("arbitrary",), vmem_limit_bytes=VMEM_LIMIT),
         cost_estimate=pl.CostEstimate(flops=(3 + 3 * (n_pairs - 1)) * 2 * copies * d_model * ff * 4,
                                       bytes_accessed=3 * n_local * ff * d_model * 2, transcendentals=0),
-        name=name,
     )(*tables, ep, *slabs, *weights)
 
 
-def weight_grad_body(st, core, u_all, d_all, idx_all, gat_all, *refs, rows, src, page_rows, parts, n_exp, n_alias, max_rows):
+def weight_grad_body(st, exps, u_all, d_all, idx_all, gat_all, *refs, rows, src, page_rows, parts, n_exp, n_alias):
     g_ref, up_ref, w_ref = refs[:3]
     dg_ref, du_ref, dw_ref, og_ref, ou_ref, ow_ref, usc, dsc, ut, ct, gacc, wacc, idx_s, gat_s, sem, tsem = refs[3 + n_alias:]
     e = pl.program_id(0)
     ff = g_ref.shape[2]
-    base = core[0] * n_exp
     per_slot = src * page_rows
 
     def table_copies(exp, slot):
         out = []
         for d in range(src):
-            first = st[d * LANES + base + exp]
+            first = st[d * LANES + exps[exp]]
             at = pl.multiple_of(lax.div(first, PAGE) * PAGE + d * rows, PAGE)
             to = pl.multiple_of(slot * per_slot + d * page_rows, PAGE)
             out.append(pltpu.make_async_copy(idx_all.at[pl.ds(at, page_rows)], idx_s.at[pl.ds(to, page_rows)], tsem.at[0]))
@@ -245,8 +246,8 @@
 
     off = 0
     for d in range(src):
-        first = st[d * LANES + base + e]
-        count = st[d * LANES + base + e + 1] - first
+        first = st[d * LANES + exps[e]]
+        count = st[d * LANES + exps[e] + 1] - first
         p0 = slot * per_slot + d * page_rows + lax.rem(first, PAGE)
 
         def gather(q, carry, p0=p0, off=off):
@@ -293,7 +294,7 @@
     og_ref[0], ou_ref[0], ow_ref[0] = dg, du, dw
 
 
-def weight_grads(layer, starts, core, u_all, d_all, idx_all, gat_all, weights, full, cap):
+def weight_grads(layer, starts, exps, u_all, d_all, idx_all, gat_all, weights, full, cap):
     n_tok, parts, _ = u_all.shape
     n_layers, n_local, ff, d_model = weights[0].shape
     n_exp = n_local // 2
@@ -303,12 +304,12 @@
     max_rows = cdiv(src * 2 * cap, WTILE) * WTILE + max(UNROLL, 8)
     max_rows = cdiv(max_rows, 64) * 64
     any_spec = pl.BlockSpec(memory_space=pl.ANY)
-    mine = pl.BlockSpec((1, 1, ff, d_model), lambda e, st, core: (layer, core[0] * n_exp + e, 0, 0))
-    half = pl.BlockSpec((1, ff, d_model), lambda e, st, core: (e, 0, 0))
+    mine = pl.BlockSpec((1, 1, ff, d_model), lambda e, st, exps: (layer, exps[e], 0, 0))
+    half = pl.BlockSpec((1, ff, d_model), lambda e, st, exps: (e, 0, 0))
     aliased = list(full) if full is not None else []
     outs = pl.pallas_call(
         functools.partial(weight_grad_body, rows=rows, src=src, page_rows=page_rows, parts=parts, n_exp=n_exp,
-                          n_alias=len(aliased), max_rows=max_rows),
+                          n_alias=len(aliased)),
         grid_spec=pltpu.PrefetchScalarGridSpec(
             num_scalar_prefetch=2,
             grid=(n_exp,),
@@ -327,20 +328,20 @@
         cost_estimate=pl.CostEstimate(flops=6 * 2 * n_tok * 2 * d_model * ff * 4,
                                       bytes_accessed=n_tok * d_model * 4 + 9 * n_exp * ff * d_model * 2, transcendentals=0),
         name="weight_grads",
-    )(starts, core, u_all, d_all, idx_all, gat_all, *weights, *aliased)
+    )(starts, exps, u_all, d_all, idx_all, gat_all, *weights, *aliased)
     return outs[:3], outs[3:]
 
 
-def merge_body(core, a, b, c, f0, f1, f2, o0, o1, o2):
+def merge_body(exps, a, b, c, f0, f1, f2, o0, o1, o2):
     o0[0, 0], o1[0, 0], o2[0, 0] = a[0], b[0], c[0]
 
 
-def merge_half(layer, core, half, full):
-    n_layers, n_local, ff, d_model = full[0].shape
+def merge_half(layer, exps, half, full):
+    _, n_local, ff, d_model = full[0].shape
     n_exp = n_local // 2
     any_spec = pl.BlockSpec(memory_space=pl.ANY)
-    part = pl.BlockSpec((1, ff, d_model), lambda e, core: (e, 0, 0))
-    place = pl.BlockSpec((1, 1, ff, d_model), lambda e, core: (layer, (1 - core[0]) * n_exp + e, 0, 0))
+    part = pl.BlockSpec((1, ff, d_model), lambda e, exps: (e, 0, 0))
+    place = pl.BlockSpec((1, 1, ff, d_model), lambda e, exps: (layer, exps[e], 0, 0))
     return pl.pallas_call(
         merge_body,
         grid_spec=pltpu.PrefetchScalarGridSpec(
@@ -350,7 +351,7 @@
         compiler_params=pltpu.CompilerParams(dimension_semantics=("arbitrary",)),
         cost_estimate=pl.CostEstimate(flops=0, bytes_accessed=6 * n_exp * ff * d_model * 2, transcendentals=0),
         name="merge_half",
-    )(core, *half, *full)
+    )(exps, *half, *full)
 
 
 def route_tables(ids, gates, ep, n_local):
@@ -382,6 +383,25 @@
     return (tile_e, tile_first, tile_row, tile_n, tile_end[-1:], token, gate), bounds
 
 
+def split_experts(bounds, core):
+    n_local = bounds.shape[1] - 1
+    load = jnp.sum(bounds[:, 1:] - bounds[:, :-1], axis=0)
+    ids = jnp.arange(n_local, dtype=jnp.int32)
+    ahead = (load[None, :] > load[:, None]) | ((load[None, :] == load[:, None]) & (ids[None, :] < ids[:, None]))
+    rank = jnp.sum(ahead.astype(jnp.int32), axis=1)
+    turn = jnp.arange(n_local // 2, dtype=jnp.int32)
+
+    def dealt(which):
+        want = 2 * turn + (which + turn) % 2
+        return jnp.sum((rank[None, :] == want[:, None]).astype(jnp.int32) * ids[None, :], axis=1)
+
+    return dealt(core), dealt(1 - core)
+
+
+def after(x, *earlier):
+    return lax.optimization_barrier((x, *earlier))[0]
+
+
 def solution(mesh):
     ep_size = mesh.shape['ep']
     dp_size = mesh.shape['dp']
@@ -392,7 +412,7 @@
     ep_pairs = [(i, 1 - i) for i in range(ep_size)]
     core_pairs = [(i, i ^ 1) for i in range(dp_size)]
 
-    def device_step(tokens, d_out, expert_ids, gate_vals, w_mix, w_gate, w_up, w_down):
+    def device_body(tokens, d_out, expert_ids, gate_vals, w_mix, w_gate, w_up, w_down):
         n_layers = w_mix.shape[0]
         n_local = w_gate.shape[1]
         n_experts = n_local * ep_size
@@ -403,7 +423,6 @@
         ep_id = lax.axis_index('ep').astype(jnp.int32)
         dp_id = lax.axis_index('dp').astype(jnp.int32)
         ep = ep_id.reshape(1)
-        core = (dp_id % 2).reshape(1)
         weights = (jnp.swapaxes(w_gate, 2, 3), jnp.swapaxes(w_up, 2, 3), w_down)
 
         def swap(x):
@@ -439,41 +458,49 @@
         d_other = swap(d_slab)
         d_spread = spread(d_slab)
 
+        top = n_layers - 1
         x_in, u_slabs, u_others, xs, u_spreads = tokens, [], [], [], []
         for layer in range(n_layers):
             u = mixed(x_in, layer)
-            u_slab = slab(u)
-            u_other = swap(u_slab)
-            own, other = token_kernel(forward_body, "experts_forward", layer, tables[layer], ep, (u_slab, u_other), weights)
+            u_slabs.append(slab(u))
+            u_others.append(swap(u_slabs[layer]))
             xs.append(x_in)
-            u_slabs.append(u_slab)
-            u_others.append(u_other)
-            u_spreads.append(spread(u_slab))
-            x_in = (u.astype(jnp.float32) + own + swap(other)).astype(jnp.bfloat16)
-        layer_out = x_in
+            u_spreads.append(spread(u_slabs[layer]))
+            if layer < top:
+                own, other = token_kernel(forward_body, layer, tables[layer], ep,
+                                          (u_slabs[layer], u_others[layer]), weights)
+                x_in = (u.astype(jnp.float32) + own + swap(other)).astype(jnp.bfloat16)
 
         d_y, full = d_out, None
         d_mix = [None] * n_layers
         for layer in reversed(range(n_layers)):
-            own, other = token_kernel(backward_body, "experts_backward", layer, tables[layer], ep,
+            own, other = token_kernel(backward_body, layer, tables[layer], ep,
                                       (u_slabs[layer], u_others[layer], d_slab, d_other), weights)
             d_u = (d_y.astype(jnp.float32) + own + swap(other)).astype(jnp.bfloat16)
-            ids_all = shared[layer, 0].astype(jnp.int32)
-            starts = ids_all[:, rows - PAGE:rows - PAGE + LANES].reshape(-1)
-            full, half = weight_grads(layer, starts, core, u_spreads[layer], d_spread, ids_all.reshape(-1),
-                                      shared[layer, 1].reshape(-1), weights, full, cap)
-            full = merge_half(layer, core, [lax.ppermute(x, 'dp', core_pairs) for x in half], full)
-            d_mix[layer] = lax.psum(jnp.einsum('td,te->de', xs[layer], d_u, preferred_element_type=jnp.float32)
-                                    .astype(jnp.bfloat16), ('dp', 'ep'))
+            last = other
+            if layer == top:
+                y_own, y_other = token_kernel(forward_body, top, tables[top], ep,
+                                              (after(u_slabs[top], other), u_others[top]), weights)
+                layer_out = (u.astype(jnp.float32) + y_own + swap(y_other)).astype(jnp.bfloat16)
+                last = y_other
+            shared_l, _ = lax.optimization_barrier((shared[layer], last))
+            ids_all = shared_l[0].astype(jnp.int32)
+            starts = ids_all[:, rows - PAGE:rows - PAGE + LANES]
+            mine_e, theirs_e = split_experts(starts[:, :n_local + 1], dp_id % 2)
+            full, half = weight_grads(layer, starts.reshape(-1), mine_e, u_spreads[layer], d_spread, ids_all.reshape(-1),
+                                      shared_l[1].reshape(-1), weights, full, cap)
+            full = merge_half(layer, theirs_e, [lax.ppermute(x, 'dp', core_pairs) for x in half], full)
+            d_mix[layer] = jnp.einsum('td,te->de', xs[layer], d_u, preferred_element_type=jnp.float32).astype(jnp.bfloat16)
             d_y = (d_u.astype(jnp.float32)
                    + jnp.einsum('te,de->td', d_u, w_mix[layer], preferred_element_type=jnp.float32)).astype(jnp.bfloat16)
             if layer:
                 d_slab = slab(d_y)
                 d_other = swap(d_slab)
                 d_spread = spread(d_slab)
-        return (layer_out, d_y, jnp.stack(d_mix), jnp.swapaxes(full[0], 2, 3), jnp.swapaxes(full[1], 2, 3), full[2])
-
-    return jax.shard_map(device_step, mesh=mesh,
+        d_mix = lax.psum(jnp.stack(d_mix), ('dp', 'ep'))
+        return (layer_out, d_y, d_mix, jnp.swapaxes(full[0], 2, 3), jnp.swapaxes(full[1], 2, 3), full[2])
+
+    return jax.shard_map(device_body, mesh=mesh,
                          in_specs=(tok_spec, tok_spec, route_spec, route_spec, whole_spec,
                                    expert_spec, expert_spec, expert_spec),
                          out_specs=(tok_spec, tok_spec, whole_spec, expert_spec, expert_spec, expert_spec),

time: 1220 us -> 1150 us (0.943); the launches traced: 1200 us -> 1150 us
  Pallas kernels: 826 us -> 728 us
  waiting for transfers between devices: 255 us -> 313 us
    pallas_call x4, Pallas kernels: 362 us -> 286 us  [token_kernel(): pl.pallas_call(functools.partial(body, layer=layer, tok=tok, parts=parts)...]
    ppermute x9, waiting for transfers between devices: 231 us -> 270 us  [swap(): return lax.ppermute(x, 'ep', ep_pairs)]
    pallas_call x2, Pallas kernels: 418 us -> 395 us  [weight_grads(): pl.pallas_call(functools.partial(weight_grad_body, rows=rows, src=src, pa...]
    ppermute x6, waiting for transfers between devices: 1.45 us -> 24.5 us  [device_body(): lax.ppermute(x, 'dp', core_pairs)]
    ppermute x9, starting transfers between devices: 33.9 us -> 13.4 us  [swap(): return lax.ppermute(x, 'ep', ep_pairs)]
  transfers between devices with their start and end apart: 21 -> 21, of which waited for: 9 -> 13; matrix products, arithmetic and copies ran while one was open for 4% -> 4% of each run, Pallas kernels for 67% -> 43%
where the time goes in v2:
time: 1150 us
  Pallas kernels  728 us (63%)
  waiting for transfers between devices  313 us (27%)
  other arithmetic  37.9 us (3%)
  starting transfers between devices  23.8 us (2%)
  local copies, waits for them, and re-layouts  23.8 us (2%)
  between operations  14.7 us (1%)
    pallas_call x2, Pallas kernels, weight_grads(): pl.pallas_call(functools.partial(weight_grad_body, rows=rows, src=src, pa...  395 us
    pallas_call x4, Pallas kernels, token_kernel(): pl.pallas_call(functools.partial(body, layer=layer, tok=tok, parts=parts)...  286 us
    ppermute x9, waiting for transfers between devices, swap(): return lax.ppermute(x, 'ep', ep_pairs)  270 us
    pallas_call x2, Pallas kernels, merge_half(): pl.pallas_call(merge_body, grid_spec=pltpu.PrefetchScalarGridSpec(num_sca...  47.5 us
    ppermute x6, waiting for transfers between devices, device_body(): lax.ppermute(x, 'dp', core_pairs)  24.5 us
  transfers between devices with their start and end apart: 21, of which 13 were waited for; matrix products, arithmetic and copies ran while one was open for 4% of the time, Pallas kernels for 43%

profile of v2, /device:TPU:0, one launch (start us, length us, event | category | flops | bytes accessed | tf_op | source)
XLA Modules:
  0.0 1149.4 jit_solution(175626235632388518)
XLA Ops:
  8.9 3.3 collective-permute-start
  12.2 3.5 collective-permute-done
  18.6 6.4 sort.30
  25.2 6.4 sort.31
  35.9 1.1 reshape.388.d_own
  37.1 1.7 add_convert_fusion.7
  39.2 1.8 collective-permute-start.1
  42.4 1.3 and_convert_fusion.1.tf
  43.7 1.3 clamp_select_fusion.1
  44.9 18.7 %collective-permute-done.1.u_oth = bf16[1024,4,128]{2,1,0:T(4,128)(2,1)} collective-permute-done((bf16[1024,4,128]{2,1,0:T(4,128)(2,1)S(1)}, bf16[1024,4,128]{2,1,0:T(4,128)(2,1)}, u32[]{:S(2)}, u32[]{:S(2)}) %collective-permute-start.1) | collective-permute-done | bytes 1048608 | tf_op jit(solution)/shard_map/ppermute | solution.py:429
  63.6 62.7 %shard_map.127 = (f32[1024,512]{1,0:T(8,128)}, f32[1024,512]{1,0:T(8,128)}) custom-call(s32[196]{0:T(256)} %copy-done.24, s32[196]{0:T(256)} %and_convert_fusion.1.tf, s32[196]{0:T(256)} %get-tuple-element.131.tr, s32[196]{0:T(256)} %get-tuple-element.130.tn, s32[1]{0:T(128)} %bitcast.9.nt, s32[18432]{0:T(1024)} %get-tuple-element.123.idx, ...), custom_call_target="tpu_custom_call" | custom-call | flops 19327352832 | bytes 37748736 | tf_op jit(solution)/shard_map/pallas_call | solution.py:184
  126.4 58.1 %collective-permute-done.2 = f32[1024,512]{1,0:T(8,128)S(1)} collective-permute-done((f32[1024,512]{1,0:T(8,128)}, f32[1024,512]{1,0:T(8,128)S(1)}, u32[]{:S(2)}, u32[]{:S(2)}) %collective-permute-start.2) | collective-permute-done | bytes 2097184 | tf_op jit(solution)/shard_map/ppermute | solution.py:429
  184.5 2.6 add_convert_fusion.6
  187.1 1.0 copy-done.16
  188.8 1.0 copy-done.6
  189.8 1.1 reshape.387.u_own
  192.2 1.4 collective-permute-start.3
  194.4 1.2 and_convert_fusion.tf
  195.6 1.2 clamp_select_fusion
  196.8 31.7 %collective-permute-done.4.d_oth = bf16[1024,4,128]{2,1,0:T(4,128)(2,1)S(1)} collective-permute-done((bf16[1024,4,128]{2,1,0:T(4,128)(2,1)S(1)}, bf16[1024,4,128]{2,1,0:T(4,128)(2,1)S(1)}, u32[]{:S(2)}, u32[]{:S(2)}) %collective-permute-start.4) | collective-permute-done | bytes 1048608 | tf_op jit(solution)/shard_map/ppermute | solution.py:429
  228.6 37.3 %collective-permute-done.3.u_oth = bf16[1024,4,128]{2,1,0:T(4,128)(2,1)S(1)} collective-permute-done((bf16[1024,4,128]{2,1,0:T(4,128)(2,1)S(1)}, bf16[1024,4,128]{2,1,0:T(4,128)(2,1)S(1)}, u32[]{:S(2)}, u32[]{:S(2)}) %collective-permute-start.3) | collective-permute-done | bytes 1048608 | tf_op jit(solution)/shard_map/ppermute | solution.py:429
  266.9 79.4 %shard_map.128 = (f32[1024,512]{1,0:T(8,128)}, f32[1024,512]{1,0:T(8,128)}) custom-call(s32[196]{0:T(256)} %copy-done.25, s32[196]{0:T(256)} %and_convert_fusion.tf, s32[196]{0:T(256)} %get-tuple-element.133.tr, s32[196]{0:T(256)} %get-tuple-element.132.tn, s32[1]{0:T(128)} %bitcast.16.nt, s32[18432]{0:T(1024)} %get-tuple-element.125.idx, f32[18432]{0:T(1024)} %copy-done.22, ...), custom_call_target="tpu_custom_call" | custom-call | flops 38654705664 | bytes 37748736 | tf_op jit(solution)/shard_map/pallas_call | solution.py:184
  346.3 4.0 collective-permute-start.6
  350.3 58.9 %shard_map.129 = (f32[1024,512]{1,0:T(8,128)}, f32[1024,512]{1,0:T(8,128)}) custom-call(s32[196]{0:T(256)} %copy-done.25, s32[196]{0:T(256)} %and_convert_fusion.tf, s32[196]{0:T(256)} %get-tuple-element.133.tr, s32[196]{0:T(256)} %get-tuple-element.132.tn, s32[1]{0:T(128)} %bitcast.16.nt, s32[18432]{0:T(1024)} %get-tuple-element.125.idx, f32[18432]{0:T(1024)} %copy-done.22, ...), custom_call_target="tpu_custom_call" | custom-call | flops 19327352832 | bytes 37748736 | tf_op jit(solution)/shard_map/pallas_call | solution.py:184
  409.2 5.8 collective-permute-done.6
  415.1 2.9 add_convert_fusion.3
  421.1 1.8 fusion.49
  426.6 24.5 %collective-permute-done.7.d_oth = bf16[1024,4,128]{2,1,0:T(4,128)(2,1)} collective-permute-done((bf16[1024,4,128]{2,1,0:T(4,128)(2,1)S(1)}, bf16[1024,4,128]{2,1,0:T(4,128)(2,1)}, u32[]{:S(2)}, u32[]{:S(2)}) %collective-permute-start.7) | collective-permute-done | bytes 1048608 | tf_op jit(solution)/shard_map/ppermute | solution.py:429
  451.0 84.8 %shard_map.130 = (f32[1024,512]{1,0:T(8,128)}, f32[1024,512]{1,0:T(8,128)}) custom-call(s32[196]{0:T(256)} %copy-done.24, s32[196]{0:T(256)} %and_convert_fusion.1.tf, s32[196]{0:T(256)} %get-tuple-element.131.tr, s32[196]{0:T(256)} %get-tuple-element.130.tn, s32[1]{0:T(128)} %bitcast.9.nt, s32[18432]{0:T(1024)} %get-tuple-element.123.idx, ...), custom_call_target="tpu_custom_call" | custom-call | flops 38654705664 | bytes 37748736 | tf_op jit(solution)/shard_map/pallas_call | solution.py:184
  535.8 1.2 slice_bitcast_fusion.1
  538.9 186.4 %weight_grads.2 = (bf16[2,64,192,512]{3,2,1,0:T(8,128)(2,1)}, bf16[2,64,192,512]{3,2,1,0:T(8,128)(2,1)}, bf16[2,64,192,512]{3,2,1,0:T(8,128)(2,1)}, bf16[32,192,...) custom-call(s32[1024]{0:T(1024)} %slice_bitcast_fusion.4.st, ...), custom_call_target="tpu_custom_call" | custom-call | flops 154618822656 | bytes 90177536 | tf_op jit(solution)/shard_map/weight_grads/pallas_call | solution.py:310
  725.3 8.7 collective-permute-start.9
  736.4 1.3 slice_bitcast_fusion.5.st
  737.7 6.5 collective-permute-done.9.a
  744.1 9.0 collective-permute-done.10.b
  753.1 9.0 collective-permute-done.11.c
  762.1 23.7 %merge_half.2 = (bf16[2,64,192,512]{3,2,1,0:T(8,128)(2,1)}, bf16[2,64,192,512]{3,2,1,0:T(8,128)(2,1)}, bf16[2,64,192,512]{3,2,1,0:T(8,128)(2,1)}) custom-call(s32[32]{0:T(128)} %get-tuple-element.107.exps, bf16[32,192,512]{2,1,0:T(8,128)(2,1)} %collective-permute-done.9.a, ...), custom_call_target="tpu_custom_call", output_to_operand_aliasing={{0}: (4, {}), {1}: (5, {}), {2}: (6, {})} | custom-call | bytes 37748736 | tf_op jit(solution)/shard_map/merge_half/pallas_call | solution.py:345
  785.9 208.6 %weight_grads.3 = (bf16[2,64,192,512]{3,2,1,0:T(8,128)(2,1)}, bf16[2,64,192,512]{3,2,1,0:T(8,128)(2,1)}, bf16[2,64,192,512]{3,2,1,0:T(8,128)(2,1)}, bf16[32,192,...) custom-call(s32[1024]{0:T(1024)} %slice_bitcast_fusion.5.st, ...), custom_call_target="tpu_custom_call", output_to_operand_aliasing={{0}: (9, {}), {1}: (10, {}), {2}: (11, {})} | custom-call | flops 154618822656 | bytes 90177536 | tf_op jit(solution)/shard_map/weight_grads/pallas_call | solution.py:310
  995.4 2.0 collective-permute-start.5
  997.4 2.0 fusion.1
  999.4 44.7 %collective-permute-done.8 = f32[1024,512]{1,0:T(8,128)S(1)} collective-permute-done((f32[1024,512]{1,0:T(8,128)}, f32[1024,512]{1,0:T(8,128)S(1)}, u32[]{:S(2)}, u32[]{:S(2)}) %collective-permute-start.8) | collective-permute-done | bytes 2097184 | tf_op jit(solution)/shard_map/ppermute | solution.py:429
  1046.3 1.1 pad_maximum_fusion
  1047.4 45.9 %collective-permute-done.5 = f32[1024,512]{1,0:T(8,128)} collective-permute-done((f32[1024,512]{1,0:T(8,128)}, f32[1024,512]{1,0:T(8,128)}, u32[]{:S(2)}, u32[]{:S(2)}) %collective-permute-start.5) | collective-permute-done | bytes 2097184 | tf_op jit(solution)/shard_map/ppermute | solution.py:429
  1093.3 3.4 add_convert_fusion.4
  1096.7 1.7 add_convert_fusion
  1098.4 18.1 %all-reduce.10.cloned.1.call-done = bf16[2,512,512]{1,2,0:T(8,128)(2,1)} async-done(((bf16[2,512,512]{1,2,0:T(8,128)(2,1)}), bf16[2,512,512]{1,2,0:T(8,128)(2,1)}) %all-reduce.10.cloned.1.call-update) | async-done | bytes 1048592 | tf_op jit(solution)/shard_map/psum | solution.py:500
  1116.5 2.3 copy.58
  1118.8 23.7 %merge_half.3 = (bf16[2,64,192,512]{3,2,1,0:T(8,128)(2,1)}, bf16[2,64,192,512]{3,2,1,0:T(8,128)(2,1)}, bf16[2,64,192,512]{3,2,1,0:T(8,128)(2,1)}) custom-call(s32[32]{0:T(128)} %get-tuple-element.106.exps, bf16[32,192,512]{2,1,0:T(8,128)(2,1)} %collective-permute-done.12.a, ...), custom_call_target="tpu_custom_call", output_to_operand_aliasing={{0}: (4, {}), {1}: (5, {}), {2}: (6, {})} | custom-call | bytes 37748736 | tf_op jit(solution)/shard_map/merge_half/pallas_call | solution.py:345
  (169 shorter events, 28.5 us)
Async XLA Ops:
  7.2 413.9 %all-gather.15.cloned.1.call-start = ((), (), s32[]{:S(2)}) async-start(), calls=%async_computation.5 | async-start | bytes 2801664 | tf_op jit(solution)/shard_map/all_gather | solution.py:454
  8.9 6.8 collective-permute-start
  17.2 18.7 %copy-start.4 = (bf16[1024,512]{1,0:T(8,128)(2,1)S(1)}, bf16[1024,512]{1,0:T(8,128)(2,1)}, u32[]{:S(2)}) copy-start(bf16[1024,512]{1,0:T(8,128)(2,1)} %param.9) | copy-start | bytes 3145732
  33.2 3.8 copy-start.22
  33.2 3.8 copy-start.21
  34.9 2.1 copy-start.26
  35.8 503.1 %all-gather.13.cloned.1.call-start = ((), (), s32[]{:S(2)}) async-start(), calls=%async_computation.4 | async-start | bytes 17825792 | tf_op jit(solution)/shard_map/all_gather | solution.py:432
  37.0 501.9 %all-gather.11.cloned.1.call-start = ((), (), s32[]{:S(2)}) async-start(), calls=%async_computation.3 | async-start | bytes 17825792 | tf_op jit(solution)/shard_map/all_gather | solution.py:432
  38.8 24.8 %copy-start.10 = (bf16[1024,512]{1,0:T(8,128)(2,1)}, bf16[1024,512]{1,0:T(8,128)(2,1)S(1)}, u32[]{:S(2)}) copy-start(bf16[1024,512]{1,0:T(8,128)(2,1)S(1)} %add_convert_fusion.7) | copy-start | bytes 3145732
  39.1 24.5 %copy-start = (bf16[1024,4,128]{2,1,0:T(4,128)(2,1)}, bf16[1024,4,128]{2,1,0:T(4,128)(2,1)S(1)}, u32[]{:S(2)}) copy-start(bf16[1024,4,128]{2,1,0:T(4,128)(2,1)S(1)} %reshape.385.u_own) | copy-start | bytes 3145732
  39.2 24.5 %collective-permute-start.1 = (bf16[1024,4,128]{2,1,0:T(4,128)(2,1)S(1)}, bf16[1024,4,128]{2,1,0:T(4,128)(2,1)}, u32[]{:S(2)}, u32[]{:S(2)}) collective-permute-start(bf16[1024,4,128]{2,1,0:T(4,128)(2,1)S(1)} %reshape.385.u_own), channel_id=1, source_target_pairs={{0,8},{8,0},{1,9},{9,1},{2,10},{10,2},{3,11},{11,3},{4,12},{12,4},... | collective-permute-start | bytes 3145736 | tf_op jit(solution)/shard_map/ppermute | solution.py:429
  42.3 21.4 %copy-start.24 = (s32[196]{0:T(256)}, s32[196]{0:T(256)S(1)}, u32[]{:S(2)}) copy-start(s32[196]{0:T(256)S(1)} %broadcast_minimum_fusion.1.te) | copy-start | bytes 2356
  126.4 58.1 %collective-permute-start.2 = (f32[1024,512]{1,0:T(8,128)}, f32[1024,512]{1,0:T(8,128)S(1)}, u32[]{:S(2)}, u32[]{:S(2)}) collective-permute-start(f32[1024,512]{1,0:T(8,128)} %get-tuple-element.42), channel_id=1, source_target_pairs={{0,8},{8,0},{1,9},{9,1},{2,10},{10,2},{3,11},{11,3},{4,12},{12,4},... | collective-permute-start | bytes 6291464 | tf_op jit(solution)/shard_map/ppermute | solution.py:429
  184.5 3.6 copy-start.28
  187.1 1.0 copy-start.16
  189.8 1.7 copy-start.2
  190.9 1.3 copy-start.1
  190.9 594.9 %all-gather.7.cloned.1.call-start = ((), (), s32[]{:S(2)}) async-start(), calls=%async_computation.1 | async-start | bytes 17825792 | tf_op jit(solution)/shard_map/all_gather | solution.py:432
  191.5 594.4 %all-gather.9.cloned.1.call-start = ((), (), s32[]{:S(2)}) async-start(), calls=%async_computation.2 | async-start | bytes 17825792 | tf_op jit(solution)/shard_map/all_gather | solution.py:432
  191.6 37.0 %collective-permute-start.4 = (bf16[1024,4,128]{2,1,0:T(4,128)(2,1)S(1)}, bf16[1024,4,128]{2,1,0:T(4,128)(2,1)S(1)}, u32[]{:S(2)}, u32[]{:S(2)}) collective-permute-start(bf16[1024,4,128]{2,1,0:T(4,128)(2,1)S(1)} %copy-done.2), channel_id=1, source_target_pairs={{0,8},{8,0},{1,9},{9,1},{2,10},{10,2},{3,11},{11,3},{4,12},{12,4},... | collective-permute-start | bytes 3145736 | tf_op jit(solution)/shard_map/ppermute | solution.py:429
  192.2 73.7 %collective-permute-start.3 = (bf16[1024,4,128]{2,1,0:T(4,128)(2,1)S(1)}, bf16[1024,4,128]{2,1,0:T(4,128)(2,1)S(1)}, u32[]{:S(2)}, u32[]{:S(2)}) collective-permute-start(bf16[1024,4,128]{2,1,0:T(4,128)(2,1)S(1)} %copy-done.1), channel_id=1, source_target_pairs={{0,8},{8,0},{1,9},{9,1},{2,10},{10,2},{3,11},{11,3},{4,12},{12,4},... | collective-permute-start | bytes 3145736 | tf_op jit(solution)/shard_map/ppermute | solution.py:429
  194.2 71.7 %copy-start.25 = (s32[196]{0:T(256)}, s32[196]{0:T(256)S(1)}, u32[]{:S(2)}) copy-start(s32[196]{0:T(256)S(1)} %broadcast_minimum_fusion.te) | copy-start | bytes 2356
  228.6 37.4 %copy-start.31 = (bf16[1024,4,128]{2,1,0:T(4,128)(2,1)}, bf16[1024,4,128]{2,1,0:T(4,128)(2,1)S(1)}, u32[]{:S(2)}) copy-start(bf16[1024,4,128]{2,1,0:T(4,128)(2,1)S(1)} %collective-permute-done.4.d_oth) | copy-start | bytes 3145732
  346.3 68.8 %collective-permute-start.6 = (f32[1024,512]{1,0:T(8,128)}, f32[1024,512]{1,0:T(8,128)}, u32[]{:S(2)}, u32[]{:S(2)}) collective-permute-start(f32[1024,512]{1,0:T(8,128)} %get-tuple-element.45), channel_id=1, source_target_pairs={{0,8},{8,0},{1,9},{9,1},{2,10},{10,2},{3,11},{11,3},{4,12},{12,4},... | collective-permute-start | bytes 6291464 | tf_op jit(solution)/shard_map/ppermute | solution.py:429
  350.3 64.8 %copy-start.5 = (bf16[1024,512]{1,0:T(8,128)(2,1)S(1)}, bf16[1024,512]{1,0:T(8,128)(2,1)}, u32[]{:S(2)}) copy-start(bf16[1024,512]{1,0:T(8,128)(2,1)} %param.9) | copy-start | bytes 3145732
  415.1 3.9 copy-start.29
  419.7 3.2 copy-start.8
  420.0 1.0 copy-start.3
  420.0 31.0 %collective-permute-start.7 = (bf16[1024,4,128]{2,1,0:T(4,128)(2,1)S(1)}, bf16[1024,4,128]{2,1,0:T(4,128)(2,1)}, u32[]{:S(2)}, u32[]{:S(2)}) collective-permute-start(bf16[1024,4,128]{2,1,0:T(4,128)(2,1)S(1)} %reshape.389.d_own), channel_id=1, source_target_pairs={{0,8},{8,0},{1,9},{9,1},{2,10},{10,2},{3,11},{11,3},{4,12},{12,4},... | collective-permute-start | bytes 3145736 | tf_op jit(solution)/shard_map/ppermute | solution.py:429
  421.0 695.4 %all-reduce.10.cloned.1.call-start = ((), (), s32[]{:S(2)}) async-start(), calls=%async_computation | async-start | bytes 2097152 | tf_op jit(solution)/shard_map/psum | solution.py:500
  538.9 195.6 %copy-start.12 = (f32[1,152,8,128]{3,2,1,0:T(8,128)S(1)}, f32[1,152,8,128]{3,2,1,0:T(8,128)}, u32[]{:S(2)}) copy-start(f32[1,152,8,128]{3,2,1,0:T(8,128)} %get-tuple-element.113) | copy-start | bytes 1867780
  538.9 196.6 %copy-start.11 = (s32[1,152,8,128]{3,2,1,0:T(8,128)S(1)}, s32[1,152,8,128]{3,2,1,0:T(8,128)}, u32[]{:S(2)}) copy-start(s32[1,152,8,128]{3,2,1,0:T(8,128)} %get-tuple-element.114) | copy-start | bytes 1867780
  725.3 18.9 %collective-permute-start.9 = (bf16[32,192,512]{2,1,0:T(8,128)(2,1)}, bf16[32,192,512]{2,1,0:T(8,128)(2,1)}, u32[]{:S(2)}, u32[]{:S(2)}) collective-permute-start(bf16[32,192,512]{2,1,0:T(8,128)(2,1)} %get-tuple-element.54), channel_id=1, source_target_pairs={{0,1},{1,0},{2,3},{3,2},{4,5},{5,4},{6,7},{7,6},{8,9},{9,8},{10,11... | collective-permute-start | bytes 18874376 | tf_op jit(solution)/shard_map/ppermute | solution.py:492
  734.0 19.1 %collective-permute-start.10 = (bf16[32,192,512]{2,1,0:T(8,128)(2,1)}, bf16[32,192,512]{2,1,0:T(8,128)(2,1)}, u32[]{:S(2)}, u32[]{:S(2)}) collective-permute-start(bf16[32,192,512]{2,1,0:T(8,128)(2,1)} %get-tuple-element.55), channel_id=1, source_target_pairs={{0,1},{1,0},{2,3},{3,2},{4,5},{5,4},{6,7},{7,6},{8,9},{9,8},{10,11... | collective-permute-start | bytes 18874376 | tf_op jit(solution)/shard_map/ppermute | solution.py:492
  734.1 28.1 %collective-permute-start.11 = (bf16[32,192,512]{2,1,0:T(8,128)(2,1)}, bf16[32,192,512]{2,1,0:T(8,128)(2,1)}, u32[]{:S(2)}, u32[]{:S(2)}) collective-permute-start(bf16[32,192,512]{2,1,0:T(8,128)(2,1)} %get-tuple-element.56), channel_id=1, source_target_pairs={{0,1},{1,0},{2,3},{3,2},{4,5},{5,4},{6,7},{7,6},{8,9},{9,8},{10,11... | collective-permute-start | bytes 18874376 | tf_op jit(solution)/shard_map/ppermute | solution.py:492
  785.9 211.5 %copy-start.17 = (bf16[1024,512]{1,0:T(8,128)(2,1)S(1)}, bf16[1024,512]{1,0:T(8,128)(2,1)}, u32[]{:S(2)}) copy-start(bf16[1024,512]{1,0:T(8,128)(2,1)} %copy-done.16) | copy-start | bytes 3145732
  994.4 124.3 %collective-permute-start.12 = (bf16[32,192,512]{2,1,0:T(8,128)(2,1)}, bf16[32,192,512]{2,1,0:T(8,128)(2,1)}, u32[]{:S(2)}, u32[]{:S(2)}) collective-permute-start(bf16[32,192,512]{2,1,0:T(8,128)(2,1)} %get-tuple-element.63), channel_id=1, source_target_pairs={{0,1},{1,0},{2,3},{3,2},{4,5},{5,4},{6,7},{7,6},{8,9},{9,8},{10,11... | collective-permute-start | bytes 18874376 | tf_op jit(solution)/shard_map/ppermute | solution.py:492
  994.9 123.9 %collective-permute-start.13 = (bf16[32,192,512]{2,1,0:T(8,128)(2,1)}, bf16[32,192,512]{2,1,0:T(8,128)(2,1)}, u32[]{:S(2)}, u32[]{:S(2)}) collective-permute-start(bf16[32,192,512]{2,1,0:T(8,128)(2,1)} %get-tuple-element.64), channel_id=1, source_target_pairs={{0,1},{1,0},{2,3},{3,2},{4,5},{5,4},{6,7},{7,6},{8,9},{9,8},{10,11... | collective-permute-start | bytes 18874376 | tf_op jit(solution)/shard_map/ppermute | solution.py:492
  995.0 49.1 %copy-start.9 = (bf16[1024,512]{1,0:T(8,128)(2,1)S(1)}, bf16[1024,512]{1,0:T(8,128)(2,1)}, u32[]{:S(2)}) copy-start(bf16[1024,512]{1,0:T(8,128)(2,1)} %copy-done.8) | copy-start | bytes 3145732
  995.0 49.1 %copy-start.14 = (f32[1024,512]{1,0:T(8,128)S(1)}, f32[1024,512]{1,0:T(8,128)}, u32[]{:S(2)}) copy-start(f32[1024,512]{1,0:T(8,128)} %get-tuple-element.50) | copy-start | bytes 6291460
  995.0 123.8 %collective-permute-start.14 = (bf16[32,192,512]{2,1,0:T(8,128)(2,1)}, bf16[32,192,512]{2,1,0:T(8,128)(2,1)}, u32[]{:S(2)}, u32[]{:S(2)}) collective-permute-start(bf16[32,192,512]{2,1,0:T(8,128)(2,1)} %get-tuple-element.65), channel_id=1, source_target_pairs={{0,1},{1,0},{2,3},{3,2},{4,5},{5,4},{6,7},{7,6},{8,9},{9,8},{10,11... | collective-permute-start | bytes 18874376 | tf_op jit(solution)/shard_map/ppermute | solution.py:492
  995.4 48.7 %collective-permute-start.8 = (f32[1024,512]{1,0:T(8,128)}, f32[1024,512]{1,0:T(8,128)S(1)}, u32[]{:S(2)}, u32[]{:S(2)}) collective-permute-start(f32[1024,512]{1,0:T(8,128)} %get-tuple-element.51), channel_id=1, source_target_pairs={{0,8},{8,0},{1,9},{9,1},{2,10},{10,2},{3,11},{11,3},{4,12},{12,4},... | collective-permute-start | bytes 6291464 | tf_op jit(solution)/shard_map/ppermute | solution.py:429
  995.4 97.9 %collective-permute-start.5 = (f32[1024,512]{1,0:T(8,128)}, f32[1024,512]{1,0:T(8,128)}, u32[]{:S(2)}, u32[]{:S(2)}) collective-permute-start(f32[1024,512]{1,0:T(8,128)} %get-tuple-element.48), channel_id=1, source_target_pairs={{0,8},{8,0},{1,9},{9,1},{2,10},{10,2},{3,11},{11,3},{4,12},{12,4},... | collective-permute-start | bytes 6291464 | tf_op jit(solution)/shard_map/ppermute | solution.py:429
  1044.1 1.2 copy-start.27
  1046.3 47.0 %copy-start.7 = (bf16[1024,512]{1,0:T(8,128)(2,1)S(1)}, bf16[1024,512]{1,0:T(8,128)(2,1)}, u32[]{:S(2)}) copy-start(bf16[1024,512]{1,0:T(8,128)(2,1)} %copy-done.6) | copy-start | bytes 3145732
  1046.3 47.0 %copy-start.13 = (f32[1024,512]{1,0:T(8,128)S(1)}, f32[1024,512]{1,0:T(8,128)}, u32[]{:S(2)}) copy-start(f32[1024,512]{1,0:T(8,128)} %get-tuple-element.47) | copy-start | bytes 6291460
  1093.3 3.4 copy-start.20
  1093.3 3.4 copy-start.30
  (5 other events, 4.7 us)
Sparse Core Ops, SparseCore 0:
  35.9 26.9 all-gather.14
  65.7 87.8 all-gather.12
  191.1 102.4 all-gather.10
  296.2 98.3 all-gather.6
  421.2 84.5 all-gather.8
  1047.5 68.9 all-reduce.9

commit v3 on v2

--- a/solution.py
+++ b/solution.py
@@ -13,7 +13,6 @@
 TILE = 128
 WTILE = 256
 BATCH = 16
-UNROLL = 16
 SLOTS = 4
 PAGE = 1024
 VMEM_LIMIT = 62 * 2**20
@@ -46,10 +45,10 @@
         ref[pl.ds(start * parts + k, rows, stride=parts), :] = vals[:, k * LANES:(k + 1) * LANES]
 
 
-def fetch_pair(first, other, dst, sem, ep, tok):
-    copies = (pltpu.make_async_copy(first, dst.at[pl.ds(ep * tok, tok)], sem.at[0]),
-              pltpu.make_async_copy(other, dst.at[pl.ds((1 - ep) * tok, tok)], sem.at[1]))
-    return copies
+def fetch_pair(own, other, dst, sem):
+    n = own.shape[0]
+    return (pltpu.make_async_copy(own, dst.at[pl.ds(0, n)], sem.at[0]),
+            pltpu.make_async_copy(other, dst.at[pl.ds(n, n)], sem.at[1]))
 
 
 def add_rows(acc, vals_ref, idx, gat, row, parts):
@@ -62,15 +61,15 @@
             acc[pl.ds(toks[r] * parts, parts), :] = vals[r]
 
 
-def write_sums(acc, own_ref, other_ref, ep, tok, parts):
+def write_sums(acc, own_ref, other_ref, tok, parts):
     step = min(32, tok)
 
     def copy_out(q, carry):
         r0 = pl.multiple_of(q * step, step)
         for k in range(parts):
             cols = slice(k * LANES, (k + 1) * LANES)
-            own_ref[pl.ds(r0, step), cols] = acc[pl.ds((ep * tok + r0) * parts + k, step, stride=parts), :]
-            other_ref[pl.ds(r0, step), cols] = acc[pl.ds(((1 - ep) * tok + r0) * parts + k, step, stride=parts), :]
+            own_ref[pl.ds(r0, step), cols] = acc[pl.ds(r0 * parts + k, step, stride=parts), :]
+            other_ref[pl.ds(r0, step), cols] = acc[pl.ds((tok + r0) * parts + k, step, stride=parts), :]
         return carry
 
     lax.fori_loop(0, tok // step, copy_out, 0)
@@ -113,10 +112,9 @@
     lax.fori_loop(0, n_steps, one, 0)
 
 
-def forward_body(te, tf, tr, tn, nt, idx, gat, epr, u_own, u_oth, g_ref, up_ref, w_ref, own_ref, other_ref,
+def forward_body(te, tf, tr, tn, nt, idx, gat, u_own, u_oth, g_ref, up_ref, w_ref, own_ref, other_ref,
                  usc, ut, ot, acc, wbuf, sem, wsem, *, layer, tok, parts):
     ff = g_ref.shape[2]
-    ep = epr[0]
     acc[...] = jnp.zeros_like(acc)
     ot[...] = jnp.zeros_like(ot)
     ut[...] = jnp.zeros_like(ut)
@@ -135,14 +133,13 @@
         store_rows(ot, 0, jnp.where(live, o, 0.0), parts)
 
     run_tiles(step, (g_ref, up_ref, w_ref), wbuf, wsem, te, tf, nt[0] + 2, layer,
-              fetch_pair(u_own, u_oth, usc, sem, ep, tok))
-    write_sums(acc, own_ref, other_ref, ep, tok, parts)
-
-
-def backward_body(te, tf, tr, tn, nt, idx, gat, epr, u_own, u_oth, d_own, d_oth, g_ref, up_ref, w_ref, own_ref, other_ref,
+              fetch_pair(u_own, u_oth, usc, sem))
+    write_sums(acc, own_ref, other_ref, tok, parts)
+
+
+def backward_body(te, tf, tr, tn, nt, idx, gat, u_own, u_oth, d_own, d_oth, g_ref, up_ref, w_ref, own_ref, other_ref,
                   usc, dsc, ut, ct, vt, acc, wbuf, sem, wsem, *, layer, tok, parts):
     ff = g_ref.shape[2]
-    ep = epr[0]
     acc[...] = jnp.zeros_like(acc)
     vt[...] = jnp.zeros_like(vt)
     ut[...] = jnp.zeros_like(ut)
@@ -169,11 +166,11 @@
         store_rows(vt, 0, jnp.where(live, v, 0.0), parts)
 
     run_tiles(step, (g_ref, up_ref, w_ref), wbuf, wsem, te, tf, nt[0] + 2, layer,
-              fetch_pair(u_own, u_oth, usc, sem.at[0], ep, tok) + fetch_pair(d_own, d_oth, dsc, sem.at[1], ep, tok))
-    write_sums(acc, own_ref, other_ref, ep, tok, parts)
-
-
-def token_kernel(body, layer, tables, ep, slabs, weights):
+              fetch_pair(u_own, u_oth, usc, sem.at[0]) + fetch_pair(d_own, d_oth, dsc, sem.at[1]))
+    write_sums(acc, own_ref, other_ref, tok, parts)
+
+
+def token_kernel(body, layer, tables, slabs, weights):
     tok, parts, _ = slabs[0].shape
     _, n_local, ff, d_model = weights[0].shape
     n_pairs = len(slabs) // 2
@@ -184,7 +181,7 @@
     return pl.pallas_call(
         functools.partial(body, layer=layer, tok=tok, parts=parts),
         grid_spec=pltpu.PrefetchScalarGridSpec(
-            num_scalar_prefetch=len(tables) + 1,
+            num_scalar_prefetch=len(tables),
             grid=(1,),
             in_specs=[any_spec] * (len(slabs) + 3),
             out_specs=[rows_spec] * 2,
@@ -197,96 +194,135 @@
         compiler_params=pltpu.CompilerParams(dimension_semantics=("arbitrary",), vmem_limit_bytes=VMEM_LIMIT),
         cost_estimate=pl.CostEstimate(flops=(3 + 3 * (n_pairs - 1)) * 2 * copies * d_model * ff * 4,
                                       bytes_accessed=3 * n_local * ff * d_model * 2, transcendentals=0),
-    )(*tables, ep, *slabs, *weights)
-
-
-def weight_grad_body(st, exps, u_all, d_all, idx_all, gat_all, *refs, rows, src, page_rows, parts, n_exp, n_alias):
+    )(*tables, *slabs, *weights)
+
+
+def merge_tables_body(st, exps, table, idx_ref, gate_ref, buf, *, src, n_exp, src_rows, out_rows):
+    layer, e = pl.program_id(0), pl.program_id(1)
+    exp = exps[layer * n_exp + e]
+    buf[...] = jnp.zeros_like(buf)
+    row = lax.broadcasted_iota(jnp.int32, (8, LANES), 0)
+    lane = lax.broadcasted_iota(jnp.int32, (8, LANES), 1)
+    off = 0
+    for d in range(src):
+        at = (layer * src + d) * LANES + exp
+        first = st[at]
+        count = st[at + 1] - first
+        to = lax.rem(off, LANES) + LANES
+        shift = to - lax.rem(first, LANES)
+        over = lax.rem(shift, LANES)
+        start = lax.div(off, LANES)
+        place = row * LANES + lane
+        take = (place >= to) & (place < to + count)
+        for kind in range(2):
+            x = table[0, kind, pl.ds(d * src_rows + lax.div(first, LANES), 8), :]
+            x = pltpu.roll(pltpu.roll(x, over, 1), lax.div(shift, LANES), 0)
+            x = jnp.where(lane >= over, x, pltpu.roll(x, 1, 0))
+            old = buf[kind, pl.ds(start, 8), :]
+            buf[kind, pl.ds(start, 8), :] = jnp.where(take, x, old)
+        off = off + count
+    idx_ref[0, 0] = buf[0, pl.ds(1, out_rows), :].astype(jnp.int32)
+    gate_ref[0, 0] = buf[1, pl.ds(1, out_rows), :]
+
+
+def merge_tables(shared, starts, exps, out_rows):
+    n_layers, _, src, rows = shared.shape
+    n_exp = exps.shape[1]
+    exps = exps.reshape(-1)
+    src_rows = rows // LANES
+    out = pl.BlockSpec((1, 1, out_rows, LANES), lambda l, e, *_: (l, e, 0, 0))
+    return pl.pallas_call(
+        functools.partial(merge_tables_body, src=src, n_exp=n_exp, src_rows=src_rows, out_rows=out_rows),
+        grid_spec=pltpu.PrefetchScalarGridSpec(
+            num_scalar_prefetch=2,
+            grid=(n_layers, n_exp),
+            in_specs=[pl.BlockSpec((1, 2, src * src_rows, LANES), lambda l, e, *_: (l, 0, 0, 0))],
+            out_specs=[out] * 2,
+            scratch_shapes=[pltpu.VMEM((2, out_rows + 16, LANES), jnp.float32)],
+        ),
+        out_shape=[jax.ShapeDtypeStruct((n_layers, n_exp, out_rows, LANES), jnp.int32),
+                   jax.ShapeDtypeStruct((n_layers, n_exp, out_rows, LANES), jnp.float32)],
+        compiler_params=pltpu.CompilerParams(dimension_semantics=("arbitrary", "arbitrary")),
+        cost_estimate=pl.CostEstimate(flops=10**9, bytes_accessed=4 * shared.size, transcendentals=0),
+        name="merge_tables",
+    )(starts, exps, shared.reshape(n_layers, 2, src * src_rows, LANES))
+
+
+def weight_grad_body(exps, tiles, u_own, u_oth, d_own, d_oth, idx_all, gate_ref, *refs, parts, n_exp, n_alias, layer, page):
     g_ref, up_ref, w_ref = refs[:3]
-    dg_ref, du_ref, dw_ref, og_ref, ou_ref, ow_ref, usc, dsc, ut, ct, gacc, wacc, idx_s, gat_s, sem, tsem = refs[3 + n_alias:]
+    (dg_ref, du_ref, dw_ref, og_ref, ou_ref, ow_ref,
+     usc, dsc, ut, dt, ub, cb, gacc, wacc, idx_s, sem, tsem) = refs[3 + n_alias:]
     e = pl.program_id(0)
     ff = g_ref.shape[2]
-    per_slot = src * page_rows
-
-    def table_copies(exp, slot):
-        out = []
-        for d in range(src):
-            first = st[d * LANES + exps[exp]]
-            at = pl.multiple_of(lax.div(first, PAGE) * PAGE + d * rows, PAGE)
-            to = pl.multiple_of(slot * per_slot + d * page_rows, PAGE)
-            out.append(pltpu.make_async_copy(idx_all.at[pl.ds(at, page_rows)], idx_s.at[pl.ds(to, page_rows)], tsem.at[0]))
-            out.append(pltpu.make_async_copy(gat_all.at[pl.ds(at, page_rows)], gat_s.at[pl.ds(to, page_rows)], tsem.at[1]))
-        return out
-
-    slot = lax.rem(e, 2)
+    slots = 3
+
+    def table_copy(exp):
+        slot = lax.rem(exp, slots)
+        at = pl.multiple_of((layer * n_exp + exp) * page, PAGE)
+        to = pl.multiple_of(slot * page, PAGE)
+        return pltpu.make_async_copy(idx_all.at[pl.ds(at, page)], idx_s.at[pl.ds(to, page)], tsem.at[slot])
+
+    def gather_row(at, r):
+        t = idx_s[at]
+        ut[pl.ds(r * parts, parts), :] = usc[t].astype(jnp.float32)
+        dt[pl.ds(r * parts, parts), :] = dsc[t].astype(jnp.float32)
 
     @pl.when(e == 0)
     def _():
-        cu = pltpu.make_async_copy(u_all, usc, sem.at[0])
-        cd = pltpu.make_async_copy(d_all, dsc, sem.at[1])
-        cu.start()
-        cd.start()
-        for c in table_copies(0, 0):
+        copies = fetch_pair(u_own, u_oth, usc, sem.at[0]) + fetch_pair(d_own, d_oth, dsc, sem.at[1])
+        for c in copies:
             c.start()
-
-        def clear(q, carry):
-            ut[pl.ds(pl.multiple_of(q * 256, 256), 256), :] = jnp.zeros((256, LANES), jnp.float32)
+        table_copy(0).start()
+        table_copy(1).start()
+        table_copy(0).wait()
+        for c in copies:
+            c.wait()
+
+        def first_rows(q, carry):
+            for r in range(16):
+                gather_row(q * 16 + r, q * 16 + r)
             return carry
 
-        lax.fori_loop(0, ut.shape[0] // 256, clear, 0)
-        cu.wait()
-        cd.wait()
-
-    for c in table_copies(e, slot):
-        c.wait()
+        lax.fori_loop(0, WTILE // 16, first_rows, 0)
 
     @pl.when(e + 1 < n_exp)
     def _():
-        for c in table_copies(e + 1, 1 - slot):
-            c.start()
-
-    off = 0
-    for d in range(src):
-        first = st[d * LANES + exps[e]]
-        count = st[d * LANES + exps[e] + 1] - first
-        p0 = slot * per_slot + d * page_rows + lax.rem(first, PAGE)
-
-        def gather(q, carry, p0=p0, off=off):
-            p = p0 + q * UNROLL
-            o = (off + q * UNROLL) * parts
-            for r in range(UNROLL):
-                t = idx_s[p + r]
-                ut[pl.ds(o + r * parts, parts), :] = usc[t].astype(jnp.float32)
-                ct[pl.ds(o + r * parts, parts), :] = gat_s[p + r] * dsc[t].astype(jnp.float32)
-            return carry
-
-        lax.fori_loop(0, lax.div(count + UNROLL - 1, UNROLL), gather, 0)
-        off = off + count
-    tiles = lax.div(off + WTILE - 1, WTILE)
-
-    def clear_tail(q, carry):
-        ct[pl.ds((off + q * 8) * parts, 8 * parts), :] = jnp.zeros((8 * parts, LANES), jnp.float32)
-        return carry
-
-    lax.fori_loop(0, lax.div(tiles * WTILE - off + 7, 8), clear_tail, 0)
+        table_copy(e + 1).wait()
+
+    @pl.when(e + 2 < n_exp)
+    def _():
+        table_copy(e + 2).start()
+
     gacc[...] = jnp.zeros_like(gacc)
     wacc[...] = jnp.zeros_like(wacc)
+    here = lax.rem(e, slots) * page
+    there = lax.rem(jnp.minimum(e + 1, n_exp - 1), slots) * page
+    n_tiles = tiles[layer * n_exp + e]
+    gate_rows = WTILE // LANES
 
     def tile(j, carry):
-        u = load_rows(ut, j * WTILE, WTILE, parts)
-        c = load_rows(ct, j * WTILE, WTILE, parts)
-        ab = nt_dot(jnp.concatenate([g_ref[0, 0], up_ref[0, 0]], axis=0), u)
-        dh = nt_dot(w_ref[0, 0], c)
+        ub[...] = load_rows(ut, 0, WTILE, parts)
+        gates = [jnp.broadcast_to(gate_ref[0, 0, pl.ds(j * gate_rows + q, 1), :], (LANES, LANES)).T for q in range(gate_rows)]
+        for k in range(parts):
+            for q in range(gate_rows):
+                d = dt[pl.ds(q * LANES * parts + k, LANES, stride=parts), :]
+                cb[q * LANES:(q + 1) * LANES, k * LANES:(k + 1) * LANES] = (d * gates[q]).astype(jnp.bfloat16)
+        ab = nt_dot(jnp.concatenate([g_ref[0, 0], up_ref[0, 0]], axis=0), ub[...])
+        dh = nt_dot(w_ref[0, 0], cb[...])
+        nxt = jnp.where(j + 1 < n_tiles, here + (j + 1) * WTILE, there)
+        for r in range(WTILE):
+            gather_row(nxt + r, r)
         a, b = ab[:ff], ab[ff:]
         s = jax.nn.sigmoid(a)
         act = a * s
         h = (act * b).astype(jnp.bfloat16)
         da = (dh * b * (s * (1.0 + a * (1.0 - s)))).astype(jnp.bfloat16)
         db = (dh * act).astype(jnp.bfloat16)
-        gacc[...] += nn_dot(jnp.concatenate([da, db], axis=0), u)
-        wacc[...] += nn_dot(h, c)
+        gacc[...] += nn_dot(jnp.concatenate([da, db], axis=0), ub[...])
+        wacc[...] += nn_dot(h, cb[...])
         return carry
 
-    lax.fori_loop(0, tiles, tile, 0)
+    lax.fori_loop(0, n_tiles, tile, 0)
     dg = gacc[:ff].astype(jnp.bfloat16)
     du = gacc[ff:].astype(jnp.bfloat16)
     dw = wacc[...].astype(jnp.bfloat16)
@@ -294,41 +330,39 @@
     og_ref[0], ou_ref[0], ow_ref[0] = dg, du, dw
 
 
-def weight_grads(layer, starts, exps, u_all, d_all, idx_all, gat_all, weights, full, cap):
-    n_tok, parts, _ = u_all.shape
+def weight_grads(layer, exps, tiles, u_alls, d_alls, idx_all, gates, weights, full):
+    n_src, parts, _ = u_alls[0].shape
+    n_tok = 2 * n_src
     n_layers, n_local, ff, d_model = weights[0].shape
     n_exp = n_local // 2
-    src = starts.shape[0] // LANES
-    rows = idx_all.shape[0] // src
-    page_rows = cdiv(PAGE - 1 + 2 * cap + UNROLL, PAGE) * PAGE
-    max_rows = cdiv(src * 2 * cap, WTILE) * WTILE + max(UNROLL, 8)
-    max_rows = cdiv(max_rows, 64) * 64
+    out_rows = gates.shape[2]
+    page = out_rows * LANES
     any_spec = pl.BlockSpec(memory_space=pl.ANY)
-    mine = pl.BlockSpec((1, 1, ff, d_model), lambda e, st, exps: (layer, exps[e], 0, 0))
-    half = pl.BlockSpec((1, ff, d_model), lambda e, st, exps: (e, 0, 0))
+    mine = pl.BlockSpec((1, 1, ff, d_model), lambda e, exps, tiles: (layer, exps[e], 0, 0))
+    half = pl.BlockSpec((1, ff, d_model), lambda e, *_: (e, 0, 0))
+    gate_spec = pl.BlockSpec((1, 1, out_rows, LANES), lambda e, *_: (layer, e, 0, 0))
     aliased = list(full) if full is not None else []
     outs = pl.pallas_call(
-        functools.partial(weight_grad_body, rows=rows, src=src, page_rows=page_rows, parts=parts, n_exp=n_exp,
-                          n_alias=len(aliased)),
+        functools.partial(weight_grad_body, parts=parts, n_exp=n_exp, n_alias=len(aliased), layer=layer, page=page),
         grid_spec=pltpu.PrefetchScalarGridSpec(
             num_scalar_prefetch=2,
             grid=(n_exp,),
-            in_specs=[any_spec] * 4 + [mine] * 3 + [any_spec] * len(aliased),
+            in_specs=[any_spec] * 5 + [gate_spec] + [mine] * 3 + [any_spec] * len(aliased),
             out_specs=[mine] * 3 + [half] * 3,
             scratch_shapes=[pltpu.VMEM((n_tok, parts, LANES), jnp.bfloat16)] * 2
-            + [pltpu.VMEM((max_rows * parts, LANES), jnp.float32)] * 2
+            + [pltpu.VMEM((WTILE * parts, LANES), jnp.float32)] * 2
+            + [pltpu.VMEM((WTILE, d_model), jnp.bfloat16)] * 2
             + [pltpu.VMEM((2 * ff, d_model), jnp.float32), pltpu.VMEM((ff, d_model), jnp.float32),
-               pltpu.SMEM((2 * src * page_rows,), jnp.int32), pltpu.SMEM((2 * src * page_rows,), jnp.float32),
-               pltpu.SemaphoreType.DMA((2,)), pltpu.SemaphoreType.DMA((2,))],
+               pltpu.SMEM((3 * page,), jnp.int32), pltpu.SemaphoreType.DMA((2, 2)), pltpu.SemaphoreType.DMA((3,))],
         ),
         out_shape=[jax.ShapeDtypeStruct((n_layers, n_local, ff, d_model), jnp.bfloat16)] * 3
         + [jax.ShapeDtypeStruct((n_exp, ff, d_model), jnp.bfloat16)] * 3,
-        input_output_aliases={9 + k: k for k in range(len(aliased))},
+        input_output_aliases={11 + k: k for k in range(len(aliased))},
         compiler_params=pltpu.CompilerParams(dimension_semantics=("arbitrary",), vmem_limit_bytes=VMEM_LIMIT),
         cost_estimate=pl.CostEstimate(flops=6 * 2 * n_tok * 2 * d_model * ff * 4,
                                       bytes_accessed=n_tok * d_model * 4 + 9 * n_exp * ff * d_model * 2, transcendentals=0),
         name="weight_grads",
-    )(starts, exps, u_all, d_all, idx_all, gat_all, *weights, *aliased)
+    )(exps, tiles, *u_alls, *d_alls, idx_all, gates, *weights, *aliased)
     return outs[:3], outs[3:]
 
 
@@ -393,9 +427,11 @@
 
     def dealt(which):
         want = 2 * turn + (which + turn) % 2
-        return jnp.sum((rank[None, :] == want[:, None]).astype(jnp.int32) * ids[None, :], axis=1)
-
-    return dealt(core), dealt(1 - core)
+        return (rank[None, :] == want[:, None]).astype(jnp.int32)
+
+    mine, theirs = dealt(core), dealt(1 - core)
+    tiles = jnp.maximum((jnp.sum(mine * load[None, :], axis=1) + WTILE - 1) // WTILE, 1)
+    return jnp.sum(mine * ids[None, :], axis=1), jnp.sum(theirs * ids[None, :], axis=1), tiles
 
 
 def after(x, *earlier):
@@ -422,14 +458,13 @@
         cap = cdiv(CAP_FACTOR * tok * top_k, n_experts)
         ep_id = lax.axis_index('ep').astype(jnp.int32)
         dp_id = lax.axis_index('dp').astype(jnp.int32)
-        ep = ep_id.reshape(1)
         weights = (jnp.swapaxes(w_gate, 2, 3), jnp.swapaxes(w_up, 2, 3), w_down)
 
         def swap(x):
             return lax.ppermute(x, 'ep', ep_pairs)
 
         def spread(x):
-            return lax.all_gather(x, ('dp', 'ep'), axis=0, tiled=True)
+            return lax.all_gather(x, 'dp', axis=0, tiled=True)
 
         def slab(x):
             return x.reshape(tok, parts, LANES)
@@ -441,22 +476,29 @@
         gates = jnp.swapaxes(gate_vals, 1, 2)
         mine = jnp.stack([ids.astype(jnp.float32), gates])
         theirs = swap(mine)
-        both = jnp.where(ep_id == 0, jnp.stack([mine, theirs], 2), jnp.stack([theirs, mine], 2))
+        both = jnp.stack([mine, theirs], 2)
         both_ids = both[0].astype(jnp.int32)
         tables, packed = [], []
         for layer in range(n_layers):
             table, bounds = route_tables(both_ids[layer], both[1, layer], ep_id, n_local)
             tables.append(table)
             token, gate = table[5], table[6]
-            packed.append(jnp.stack([jnp.concatenate([token + dp_id * (2 * tok), jnp.pad(bounds, (0, PAGE - LANES))])
+            spot = lax.div(token, tok) * (dp_size * tok) + dp_id * tok + lax.rem(token, tok)
+            packed.append(jnp.stack([jnp.concatenate([spot, jnp.pad(bounds, (0, PAGE - LANES))])
                                      .astype(jnp.float32), jnp.pad(gate, (0, PAGE))]))
         rows = packed[0].shape[1]
         shared = lax.all_gather(jnp.stack(packed), 'dp', axis=2)
         shared = shared.reshape(n_layers, 2, dp_size, rows)
+        starts = shared[:, 0, :, rows - PAGE:rows - PAGE + LANES].astype(jnp.int32)
+        split = [split_experts(starts[layer, :, :n_local + 1], dp_id % 2) for layer in range(n_layers)]
+        mine_e, theirs_e, tiles = (jnp.stack(x) for x in zip(*split))
+        list_rows = cdiv(cdiv(dp_size * 2 * cap, LANES), 8) * 8 + 8
+        idx_all, gate_all = merge_tables(shared, starts.reshape(-1), mine_e, list_rows)
+        idx_all = idx_all.reshape(-1)
 
         d_slab = slab(d_out)
         d_other = swap(d_slab)
-        d_spread = spread(d_slab)
+        d_spread = (spread(d_slab), spread(d_other))
 
         top = n_layers - 1
         x_in, u_slabs, u_others, xs, u_spreads = tokens, [], [], [], []
@@ -465,38 +507,34 @@
             u_slabs.append(slab(u))
             u_others.append(swap(u_slabs[layer]))
             xs.append(x_in)
-            u_spreads.append(spread(u_slabs[layer]))
+            u_spreads.append((spread(u_slabs[layer]), spread(u_others[layer])))
             if layer < top:
-                own, other = token_kernel(forward_body, layer, tables[layer], ep,
+                own, other = token_kernel(forward_body, layer, tables[layer],
                                           (u_slabs[layer], u_others[layer]), weights)
                 x_in = (u.astype(jnp.float32) + own + swap(other)).astype(jnp.bfloat16)
 
         d_y, full = d_out, None
         d_mix = [None] * n_layers
         for layer in reversed(range(n_layers)):
-            own, other = token_kernel(backward_body, layer, tables[layer], ep,
+            own, other = token_kernel(backward_body, layer, tables[layer],
                                       (u_slabs[layer], u_others[layer], d_slab, d_other), weights)
             d_u = (d_y.astype(jnp.float32) + own + swap(other)).astype(jnp.bfloat16)
             last = other
             if layer == top:
-                y_own, y_other = token_kernel(forward_body, top, tables[top], ep,
+                y_own, y_other = token_kernel(forward_body, top, tables[top],
                                               (after(u_slabs[top], other), u_others[top]), weights)
                 layer_out = (u.astype(jnp.float32) + y_own + swap(y_other)).astype(jnp.bfloat16)
                 last = y_other
-            shared_l, _ = lax.optimization_barrier((shared[layer], last))
-            ids_all = shared_l[0].astype(jnp.int32)
-            starts = ids_all[:, rows - PAGE:rows - PAGE + LANES]
-            mine_e, theirs_e = split_experts(starts[:, :n_local + 1], dp_id % 2)
-            full, half = weight_grads(layer, starts.reshape(-1), mine_e, u_spreads[layer], d_spread, ids_all.reshape(-1),
-                                      shared_l[1].reshape(-1), weights, full, cap)
-            full = merge_half(layer, theirs_e, [lax.ppermute(x, 'dp', core_pairs) for x in half], full)
+            full, half = weight_grads(layer, mine_e[layer], after(tiles, last).reshape(-1), u_spreads[layer], d_spread,
+                                      idx_all, gate_all, weights, full)
+            full = merge_half(layer, theirs_e[layer], [lax.ppermute(x, 'dp', core_pairs) for x in half], full)
             d_mix[layer] = jnp.einsum('td,te->de', xs[layer], d_u, preferred_element_type=jnp.float32).astype(jnp.bfloat16)
             d_y = (d_u.astype(jnp.float32)
                    + jnp.einsum('te,de->td', d_u, w_mix[layer], preferred_element_type=jnp.float32)).astype(jnp.bfloat16)
             if layer:
                 d_slab = slab(d_y)
                 d_other = swap(d_slab)
-                d_spread = spread(d_slab)
+                d_spread = (spread(d_slab), spread(d_other))
         d_mix = lax.psum(jnp.stack(d_mix), ('dp', 'ep'))
         return (layer_out, d_y, d_mix, jnp.swapaxes(full[0], 2, 3), jnp.swapaxes(full[1], 2, 3), full[2])
 

time: 1150 us -> 1020 us (0.89)
  Pallas kernels: 728 us -> 647 us
  waiting for transfers between devices: 313 us -> 262 us
    pallas_call x2 -> x3, Pallas kernels: 395 us -> 314 us  [the longest x2 287 us: weight_grads(): pl.pallas_call(functools.partial(weight_grad_body, parts=parts, n_exp=n_e...]
    ppermute x9, waiting for transfers between devices: 270 us -> 245 us  [swap(): return lax.ppermute(x, 'ep', ep_pairs)]
    ppermute x6, waiting for transfers between devices: 24.5 us -> 0.02 us  [device_body(): lax.ppermute(x, 'dp', core_pairs)]
  transfers between devices with their start and end apart: 21 -> 25, of which waited for: 13 -> 9; matrix products, arithmetic and copies ran while one was open for 4% -> 4% of each run, Pallas kernels for 43% -> 46%
where the time goes in v3:
time: 1020 us
  Pallas kernels  647 us (63%)
  waiting for transfers between devices  262 us (26%)
  other arithmetic  37.7 us (4%)
  local copies, waits for them, and re-layouts  27.7 us (3%)
  starting transfers between devices  21.8 us (2%)
  between operations  15.9 us (2%)
    pallas_call x2, Pallas kernels, weight_grads(): pl.pallas_call(functools.partial(weight_grad_body, parts=parts, n_exp=n_e...  287 us
    pallas_call x4, Pallas kernels, token_kernel(): pl.pallas_call(functools.partial(body, layer=layer, tok=tok, parts=parts)...  286 us
    ppermute x9, waiting for transfers between devices, swap(): return lax.ppermute(x, 'ep', ep_pairs)  245 us
    pallas_call x2, Pallas kernels, merge_half(): pl.pallas_call(merge_body, grid_spec=pltpu.PrefetchScalarGridSpec(num_sca...  47.5 us
    pallas_call x1, Pallas kernels, merge_tables(): pl.pallas_call(functools.partial(merge_tables_body, src=src, n_exp=n_exp,...  27.6 us
  transfers between devices with their start and end apart: 25, of which 9 were waited for; matrix products, arithmetic and copies ran while one was open for 4% of the time, Pallas kernels for 46%

profile of v3, /device:TPU:0, one launch (start us, length us, event | category | flops | bytes accessed | tf_op | source)
XLA Modules:
  0.0 1020.1 jit_solution(10823867757675402549)
XLA Ops:
  9.8 3.3 collective-permute-start
  13.1 3.5 collective-permute-done
  19.4 6.4 sort.30
  26.0 6.4 sort.31
  36.7 1.1 reshape.503.d_own
  37.9 1.8 collective-permute-start.4
  39.7 22.8 %collective-permute-done.4.d_oth = bf16[1024,4,128]{2,1,0:T(4,128)(2,1)S(1)} collective-permute-done((bf16[1024,4,128]{2,1,0:T(4,128)(2,1)}, bf16[1024,4,128]{2,1,0:T(4,128)(2,1)S(1)}, u32[]{:S(2)}, u32[]{:S(2)}) %collective-permute-start.4) | collective-permute-done | bytes 1048608 | tf_op jit(solution)/shard_map/ppermute | solution.py:464
  62.5 1.0 copy-done.14
  63.5 1.7 add_convert_fusion.7
  66.3 1.5 collective-permute-start.1
  69.2 1.2 and_convert_fusion.1.tf
  70.4 1.3 clamp_select_fusion.1
  71.7 18.1 %collective-permute-done.1.u_oth = bf16[1024,4,128]{2,1,0:T(4,128)(2,1)S(1)} collective-permute-done((bf16[1024,4,128]{2,1,0:T(4,128)(2,1)S(1)}, bf16[1024,4,128]{2,1,0:T(4,128)(2,1)S(1)}, u32[]{:S(2)}, u32[]{:S(2)}) %collective-permute-start.1) | collective-permute-done | bytes 1048608 | tf_op jit(solution)/shard_map/ppermute | solution.py:464
  90.8 62.5 %shard_map.127 = (f32[1024,512]{1,0:T(8,128)}, f32[1024,512]{1,0:T(8,128)}) custom-call(s32[196]{0:T(256)} %copy-done.22, s32[196]{0:T(256)} %and_convert_fusion.1.tf, s32[196]{0:T(256)} %get-tuple-element.137.tr, s32[196]{0:T(256)} %get-tuple-element.136.tn, s32[1]{0:T(128)} %bitcast.9.nt, s32[18432]{0:T(1024)} %get-tuple-element.127.idx, ...), custom_call_target="tpu_custom_call" | custom-call | flops 19327352832 | bytes 37748736 | tf_op jit(solution)/shard_map/pallas_call | solution.py:181
  153.4 45.3 %collective-permute-done.2 = f32[1024,512]{1,0:T(8,128)S(1)} collective-permute-done((f32[1024,512]{1,0:T(8,128)}, f32[1024,512]{1,0:T(8,128)S(1)}, u32[]{:S(2)}, u32[]{:S(2)}) %collective-permute-start.2) | collective-permute-done | bytes 2097184 | tf_op jit(solution)/shard_map/ppermute | solution.py:464
  198.8 2.6 add_convert_fusion.6
  201.4 1.0 copy-done.15
  203.1 1.3 reshape.502.u_own
  204.8 21.7 %collective-permute-done.3.u_oth = bf16[1024,4,128]{2,1,0:T(4,128)(2,1)S(1)} collective-permute-done((bf16[1024,4,128]{2,1,0:T(4,128)(2,1)}, bf16[1024,4,128]{2,1,0:T(4,128)(2,1)S(1)}, u32[]{:S(2)}, u32[]{:S(2)}) %collective-permute-start.3) | collective-permute-done | bytes 1048608 | tf_op jit(solution)/shard_map/ppermute | solution.py:464
  229.5 1.1 and_convert_fusion.tf
  230.6 1.1 clamp_select_fusion
  231.8 79.4 %shard_map.128 = (f32[1024,512]{1,0:T(8,128)}, f32[1024,512]{1,0:T(8,128)}) custom-call(s32[196]{0:T(256)} %copy-done.23, s32[196]{0:T(256)} %and_convert_fusion.tf, s32[196]{0:T(256)} %get-tuple-element.139.tr, s32[196]{0:T(256)} %get-tuple-element.138.tn, s32[1]{0:T(128)} %bitcast.15.nt, s32[18432]{0:T(1024)} %get-tuple-element.129.idx, f32[18432]{0:T(1024)} %copy-done.21, ...), custom_call_target="tpu_custom_call" | custom-call | flops 38654705664 | bytes 37748736 | tf_op jit(solution)/shard_map/pallas_call | solution.py:181
  311.2 4.0 collective-permute-start.6
  315.2 42.2 %collective-permute-done.6 = f32[1024,512]{1,0:T(8,128)S(1)} collective-permute-done((f32[1024,512]{1,0:T(8,128)}, f32[1024,512]{1,0:T(8,128)S(1)}, u32[]{:S(2)}, u32[]{:S(2)}) %collective-permute-start.6) | collective-permute-done | bytes 2097184 | tf_op jit(solution)/shard_map/ppermute | solution.py:464
  357.4 2.3 add_convert_fusion.3
  361.5 1.0 copy-done.9
  362.5 1.1 reshape.504.d_own
  363.7 59.1 %shard_map.129 = (f32[1024,512]{1,0:T(8,128)}, f32[1024,512]{1,0:T(8,128)}) custom-call(s32[196]{0:T(256)} %copy-done.23, s32[196]{0:T(256)} %and_convert_fusion.tf, s32[196]{0:T(256)} %get-tuple-element.139.tr, s32[196]{0:T(256)} %get-tuple-element.138.tn, s32[1]{0:T(128)} %bitcast.15.nt, s32[18432]{0:T(1024)} %get-tuple-element.129.idx, f32[18432]{0:T(1024)} %copy-done.21, ...), custom_call_target="tpu_custom_call" | custom-call | flops 19327352832 | bytes 37748736 | tf_op jit(solution)/shard_map/pallas_call | solution.py:181
  422.9 4.6 reshape.510
  427.5 1.3 fusion.52
  429.1 4.2 collective-permute-start.7
  436.8 3.2 reshape.507.table
  440.0 27.6 %merge_tables.1 = (s32[2,32,32,128]{3,2,1,0:T(8,128)}, f32[2,32,32,128]{3,2,1,0:T(8,128)}) custom-call(s32[2048]{0:T(1024)} %get-tuple-element.118.st, s32[64]{0:T(128)} %reshape.506.exps, f32[2,2,1216,128]{3,2,1,0:T(8,128)} %reshape.507.table), custom_call_target="tpu_custom_call" | custom-call | flops 1000000000 | bytes 2490368 | tf_op jit(solution)/shard_map/merge_tables/pallas_call | solution.py:234
  467.7 135.7 %weight_grads.2 = (bf16[2,64,192,512]{3,2,1,0:T(8,128)(2,1)}, bf16[2,64,192,512]{3,2,1,0:T(8,128)(2,1)}, bf16[2,64,192,512]{3,2,1,0:T(8,128)(2,1)}, bf16[32,192,...) custom-call(s32[32]{0:T(128)} %copy-done.25, s32[64]{0:T(128)} %reshape.509.tiles, ...), custom_call_target="tpu_custom_call" | custom-call | flops 154618822656 | bytes 90177536 | tf_op jit(solution)/shard_map/weight_grads/pallas_call | solution.py:345
  603.4 3.2 collective-permute-start.9
  607.1 84.7 %shard_map.130 = (f32[1024,512]{1,0:T(8,128)}, f32[1024,512]{1,0:T(8,128)}) custom-call(s32[196]{0:T(256)} %copy-done.22, s32[196]{0:T(256)} %and_convert_fusion.1.tf, s32[196]{0:T(256)} %get-tuple-element.137.tr, s32[196]{0:T(256)} %get-tuple-element.136.tn, s32[1]{0:T(128)} %bitcast.9.nt, s32[18432]{0:T(1024)} %get-tuple-element.127.idx, ...), custom_call_target="tpu_custom_call" | custom-call | flops 38654705664 | bytes 37748736 | tf_op jit(solution)/shard_map/pallas_call | solution.py:181
  692.4 23.7 %merge_half.2 = (bf16[2,64,192,512]{3,2,1,0:T(8,128)(2,1)}, bf16[2,64,192,512]{3,2,1,0:T(8,128)(2,1)}, bf16[2,64,192,512]{3,2,1,0:T(8,128)(2,1)}) custom-call(s32[32]{0:T(128)} %get-tuple-element.112.exps, bf16[32,192,512]{2,1,0:T(8,128)(2,1)} %collective-permute-done.9.a, ...), custom_call_target="tpu_custom_call", output_to_operand_aliasing={{0}: (4, {}), {1}: (5, {}), {2}: (6, {})} | custom-call | bytes 37748736 | tf_op jit(solution)/shard_map/merge_half/pallas_call | solution.py:379
  716.2 151.0 %weight_grads.3 = (bf16[2,64,192,512]{3,2,1,0:T(8,128)(2,1)}, bf16[2,64,192,512]{3,2,1,0:T(8,128)(2,1)}, bf16[2,64,192,512]{3,2,1,0:T(8,128)(2,1)}, bf16[32,192,...) custom-call(s32[32]{0:T(128)} %copy-done.24, ...), custom_call_target="tpu_custom_call", output_to_operand_aliasing={{0}: (11, {}), {1}: (12, {}), {2}: (13, {})} | custom-call | flops 154618822656 | bytes 90177536 | tf_op jit(solution)/shard_map/weight_grads/pallas_call | solution.py:345
  867.9 2.0 collective-permute-start.5
  869.9 2.0 fusion.1
  871.9 44.7 %collective-permute-done.8 = f32[1024,512]{1,0:T(8,128)S(1)} collective-permute-done((f32[1024,512]{1,0:T(8,128)}, f32[1024,512]{1,0:T(8,128)S(1)}, u32[]{:S(2)}, u32[]{:S(2)}) %collective-permute-start.8) | collective-permute-done | bytes 2097184 | tf_op jit(solution)/shard_map/ppermute | solution.py:464
  918.8 1.0 pad_maximum_fusion
  919.8 46.3 %collective-permute-done.5 = f32[1024,512]{1,0:T(8,128)} collective-permute-done((f32[1024,512]{1,0:T(8,128)}, f32[1024,512]{1,0:T(8,128)}, u32[]{:S(2)}, u32[]{:S(2)}) %collective-permute-start.5) | collective-permute-done | bytes 2097184 | tf_op jit(solution)/shard_map/ppermute | solution.py:464
  966.1 3.3 add_convert_fusion.4
  969.5 1.7 add_convert_fusion
  971.2 15.7 %all-reduce.10.cloned.1.call-done = bf16[2,512,512]{1,2,0:T(8,128)(2,1)} async-done(((bf16[2,512,512]{1,2,0:T(8,128)(2,1)}), bf16[2,512,512]{1,2,0:T(8,128)(2,1)}) %all-reduce.10.cloned.1.call-update) | async-done | bytes 1048592 | tf_op jit(solution)/shard_map/psum | solution.py:538
  986.9 2.3 copy.58
  989.2 23.7 %merge_half.3 = (bf16[2,64,192,512]{3,2,1,0:T(8,128)(2,1)}, bf16[2,64,192,512]{3,2,1,0:T(8,128)(2,1)}, bf16[2,64,192,512]{3,2,1,0:T(8,128)(2,1)}) custom-call(s32[32]{0:T(128)} %get-tuple-element.113.exps, bf16[32,192,512]{2,1,0:T(8,128)(2,1)} %collective-permute-done.12.a, ...), custom_call_target="tpu_custom_call", output_to_operand_aliasing={{0}: (4, {}), {1}: (5, {}), {2}: (6, {})} | custom-call | bytes 37748736 | tf_op jit(solution)/shard_map/merge_half/pallas_call | solution.py:379
  (183 shorter events, 26.0 us)
Async XLA Ops:
  8.0 414.9 %all-gather.27.cloned.1.call-start = ((), (), s32[]{:S(2)}) async-start(), calls=%async_computation.9 | async-start | bytes 2801664 | tf_op jit(solution)/shard_map/all_gather | solution.py:490
  9.8 6.8 collective-permute-start
  16.6 20.1 %copy-start.5 = (bf16[1024,512]{1,0:T(8,128)(2,1)S(1)}, bf16[1024,512]{1,0:T(8,128)(2,1)}, u32[]{:S(2)}) copy-start(bf16[1024,512]{1,0:T(8,128)(2,1)} %param.9) | copy-start | bytes 3145732
  34.0 3.9 copy-start.21
  34.0 3.9 copy-start.20
  35.7 27.8 %copy-start.28 = (bf16[1024,512]{1,0:T(8,128)(2,1)S(1)}, bf16[1024,512]{1,0:T(8,128)(2,1)}, u32[]{:S(2)}) copy-start(bf16[1024,512]{1,0:T(8,128)(2,1)} %param.8) | copy-start | bytes 3145732
  36.6 431.0 %all-gather.23.cloned.1.call-start = ((), (), s32[]{:S(2)}) async-start(), calls=%async_computation.7 | async-start | bytes 9437184 | tf_op jit(solution)/shard_map/all_gather | solution.py:467
  37.8 429.8 %all-gather.25.cloned.1.call-start = ((), (), s32[]{:S(2)}) async-start(), calls=%async_computation.8 | async-start | bytes 9437184 | tf_op jit(solution)/shard_map/all_gather | solution.py:467
  37.9 24.6 %collective-permute-start.4 = (bf16[1024,4,128]{2,1,0:T(4,128)(2,1)}, bf16[1024,4,128]{2,1,0:T(4,128)(2,1)S(1)}, u32[]{:S(2)}, u32[]{:S(2)}) collective-permute-start(bf16[1024,4,128]{2,1,0:T(4,128)(2,1)} %reshape.503.d_own), channel_id=1, source_target_pairs={{0,8},{8,0},{1,9},{9,1},{2,10},{10,2},{3,11},{11,3},{4,12},{12,4},... | collective-permute-start | bytes 3145736 | tf_op jit(solution)/shard_map/ppermute | solution.py:464
  63.5 404.2 %all-gather.19.cloned.1.call-start = ((), (), s32[]{:S(2)}) async-start(), calls=%async_computation.5 | async-start | bytes 9437184 | tf_op jit(solution)/shard_map/all_gather | solution.py:467
  65.6 25.2 %copy-start.1 = (bf16[1024,4,128]{2,1,0:T(4,128)(2,1)}, bf16[1024,4,128]{2,1,0:T(4,128)(2,1)S(1)}, u32[]{:S(2)}) copy-start(bf16[1024,4,128]{2,1,0:T(4,128)(2,1)S(1)} %reshape.500.u_own) | copy-start | bytes 3145732
  66.3 23.6 %collective-permute-start.1 = (bf16[1024,4,128]{2,1,0:T(4,128)(2,1)S(1)}, bf16[1024,4,128]{2,1,0:T(4,128)(2,1)S(1)}, u32[]{:S(2)}, u32[]{:S(2)}) collective-permute-start(bf16[1024,4,128]{2,1,0:T(4,128)(2,1)S(1)} %reshape.500.u_own), channel_id=1, source_target_pairs={{0,8},{8,0},{1,9},{9,1},{2,10},{10,2},{3,11},{11,3},{4,12},{12,4},... | collective-permute-start | bytes 3145736 | tf_op jit(solution)/shard_map/ppermute | solution.py:464
  69.1 21.8 %copy-start.22 = (s32[196]{0:T(256)}, s32[196]{0:T(256)S(1)}, u32[]{:S(2)}) copy-start(s32[196]{0:T(256)S(1)} %broadcast_minimum_fusion.1.te) | copy-start | bytes 2356
  153.4 45.4 %collective-permute-start.2 = (f32[1024,512]{1,0:T(8,128)}, f32[1024,512]{1,0:T(8,128)S(1)}, u32[]{:S(2)}, u32[]{:S(2)}) collective-permute-start(f32[1024,512]{1,0:T(8,128)} %get-tuple-element.44), channel_id=1, source_target_pairs={{0,8},{8,0},{1,9},{9,1},{2,10},{10,2},{3,11},{11,3},{4,12},{12,4},... | collective-permute-start | bytes 6291464 | tf_op jit(solution)/shard_map/ppermute | solution.py:464
  198.7 3.6 copy-start.30
  203.1 25.0 %copy-start.7 = (bf16[1024,512]{1,0:T(8,128)(2,1)}, bf16[1024,512]{1,0:T(8,128)(2,1)S(1)}, u32[]{:S(2)}) copy-start(bf16[1024,512]{1,0:T(8,128)(2,1)S(1)} %add_convert_fusion.5) | copy-start | bytes 3145732
  204.4 263.3 %all-gather.21.cloned.1.call-start = ((), (), s32[]{:S(2)}) async-start(), calls=%async_computation.6 | async-start | bytes 9437184 | tf_op jit(solution)/shard_map/all_gather | solution.py:467
  204.5 22.0 %collective-permute-start.3 = (bf16[1024,4,128]{2,1,0:T(4,128)(2,1)}, bf16[1024,4,128]{2,1,0:T(4,128)(2,1)S(1)}, u32[]{:S(2)}, u32[]{:S(2)}) collective-permute-start(bf16[1024,4,128]{2,1,0:T(4,128)(2,1)} %reshape.502.u_own), channel_id=1, source_target_pairs={{0,8},{8,0},{1,9},{9,1},{2,10},{10,2},{3,11},{11,3},{4,12},{12,4},... | collective-permute-start | bytes 3145736 | tf_op jit(solution)/shard_map/ppermute | solution.py:464
  227.5 488.7 %all-gather.11.cloned.1.call-start = ((), (), s32[]{:S(2)}) async-start(), calls=%async_computation.1 | async-start | bytes 9437184 | tf_op jit(solution)/shard_map/all_gather | solution.py:467
  228.1 488.1 %all-gather.13.cloned.1.call-start = ((), (), s32[]{:S(2)}) async-start(), calls=%async_computation.2 | async-start | bytes 9437184 | tf_op jit(solution)/shard_map/all_gather | solution.py:467
  228.8 487.4 %all-gather.15.cloned.1.call-start = ((), (), s32[]{:S(2)}) async-start(), calls=%async_computation.3 | async-start | bytes 9437184 | tf_op jit(solution)/shard_map/all_gather | solution.py:467
  229.4 2.4 copy-start.23
  231.8 125.6 %copy-start.6 = (bf16[1024,512]{1,0:T(8,128)(2,1)S(1)}, bf16[1024,512]{1,0:T(8,128)(2,1)}, u32[]{:S(2)}) copy-start(bf16[1024,512]{1,0:T(8,128)(2,1)} %param.9) | copy-start | bytes 3145732
  311.2 46.2 %collective-permute-start.6 = (f32[1024,512]{1,0:T(8,128)}, f32[1024,512]{1,0:T(8,128)S(1)}, u32[]{:S(2)}, u32[]{:S(2)}) collective-permute-start(f32[1024,512]{1,0:T(8,128)} %get-tuple-element.47), channel_id=1, source_target_pairs={{0,8},{8,0},{1,9},{9,1},{2,10},{10,2},{3,11},{11,3},{4,12},{12,4},... | collective-permute-start | bytes 6291464 | tf_op jit(solution)/shard_map/ppermute | solution.py:464
  357.4 3.3 copy-start.31
  363.6 352.6 %all-gather.17.cloned.1.call-start = ((), (), s32[]{:S(2)}) async-start(), calls=%async_computation.4 | async-start | bytes 9437184 | tf_op jit(solution)/shard_map/all_gather | solution.py:467
  422.8 6.2 copy-start.4
  422.9 13.9 %copy-start = (f32[2,2,155648]{2,1,0:T(2,128)S(1)}, f32[2,2,155648]{2,1,0:T(2,128)}, u32[]{:S(2)}) copy-start(f32[2,2,155648]{2,1,0:T(2,128)} %all-gather.27.cloned.1.call-done) | copy-start | bytes 7471108
  429.1 38.4 %collective-permute-start.7 = (bf16[1024,4,128]{2,1,0:T(4,128)(2,1)S(1)}, bf16[1024,4,128]{2,1,0:T(4,128)(2,1)}, u32[]{:S(2)}, u32[]{:S(2)}) collective-permute-start(bf16[1024,4,128]{2,1,0:T(4,128)(2,1)S(1)} %copy-done.4), channel_id=1, source_target_pairs={{0,8},{8,0},{1,9},{9,1},{2,10},{10,2},{3,11},{11,3},{4,12},{12,4},... | collective-permute-start | bytes 3145736 | tf_op jit(solution)/shard_map/ppermute | solution.py:464
  434.3 5.7 copy-start.25
  436.1 3.8 copy-start.26
  467.5 519.4 %all-reduce.10.cloned.1.call-start = ((), (), s32[]{:S(2)}) async-start(), calls=%async_computation | async-start | bytes 2097152 | tf_op jit(solution)/shard_map/psum | solution.py:538
  603.4 89.0 %collective-permute-start.9 = (bf16[32,192,512]{2,1,0:T(8,128)(2,1)}, bf16[32,192,512]{2,1,0:T(8,128)(2,1)}, u32[]{:S(2)}, u32[]{:S(2)}) collective-permute-start(bf16[32,192,512]{2,1,0:T(8,128)(2,1)} %get-tuple-element.58), channel_id=1, source_target_pairs={{0,1},{1,0},{2,3},{3,2},{4,5},{5,4},{6,7},{7,6},{8,9},{9,8},{10,11... | collective-permute-start | bytes 18874376 | tf_op jit(solution)/shard_map/ppermute | solution.py:530
  606.6 85.8 %collective-permute-start.10 = (bf16[32,192,512]{2,1,0:T(8,128)(2,1)}, bf16[32,192,512]{2,1,0:T(8,128)(2,1)}, u32[]{:S(2)}, u32[]{:S(2)}) collective-permute-start(bf16[32,192,512]{2,1,0:T(8,128)(2,1)} %get-tuple-element.59), channel_id=1, source_target_pairs={{0,1},{1,0},{2,3},{3,2},{4,5},{5,4},{6,7},{7,6},{8,9},{9,8},{10,11... | collective-permute-start | bytes 18874376 | tf_op jit(solution)/shard_map/ppermute | solution.py:530
  606.6 85.2 %copy-start.27 = (s32[2,32]{1,0:T(2,128)S(1)}, s32[2,32]{1,0:T(2,128)}, u32[]{:S(2)}) copy-start(s32[2,32]{1,0:T(2,128)} %copy-done.26) | copy-start | bytes 772
  606.6 85.8 %collective-permute-start.11 = (bf16[32,192,512]{2,1,0:T(8,128)(2,1)}, bf16[32,192,512]{2,1,0:T(8,128)(2,1)}, u32[]{:S(2)}, u32[]{:S(2)}) collective-permute-start(bf16[32,192,512]{2,1,0:T(8,128)(2,1)} %get-tuple-element.60), channel_id=1, source_target_pairs={{0,1},{1,0},{2,3},{3,2},{4,5},{5,4},{6,7},{7,6},{8,9},{9,8},{10,11... | collective-permute-start | bytes 18874376 | tf_op jit(solution)/shard_map/ppermute | solution.py:530
  716.2 153.7 %copy-start.16 = (bf16[1024,512]{1,0:T(8,128)(2,1)S(1)}, bf16[1024,512]{1,0:T(8,128)(2,1)}, u32[]{:S(2)}) copy-start(bf16[1024,512]{1,0:T(8,128)(2,1)} %copy-done.15) | copy-start | bytes 3145732
  867.3 121.9 %collective-permute-start.12 = (bf16[32,192,512]{2,1,0:T(8,128)(2,1)}, bf16[32,192,512]{2,1,0:T(8,128)(2,1)}, u32[]{:S(2)}, u32[]{:S(2)}) collective-permute-start(bf16[32,192,512]{2,1,0:T(8,128)(2,1)} %get-tuple-element.67), channel_id=1, source_target_pairs={{0,1},{1,0},{2,3},{3,2},{4,5},{5,4},{6,7},{7,6},{8,9},{9,8},{10,11... | collective-permute-start | bytes 18874376 | tf_op jit(solution)/shard_map/ppermute | solution.py:530
  867.3 121.8 %collective-permute-start.13 = (bf16[32,192,512]{2,1,0:T(8,128)(2,1)}, bf16[32,192,512]{2,1,0:T(8,128)(2,1)}, u32[]{:S(2)}, u32[]{:S(2)}) collective-permute-start(bf16[32,192,512]{2,1,0:T(8,128)(2,1)} %get-tuple-element.68), channel_id=1, source_target_pairs={{0,1},{1,0},{2,3},{3,2},{4,5},{5,4},{6,7},{7,6},{8,9},{9,8},{10,11... | collective-permute-start | bytes 18874376 | tf_op jit(solution)/shard_map/ppermute | solution.py:530
  867.8 48.8 %copy-start.10 = (bf16[1024,512]{1,0:T(8,128)(2,1)S(1)}, bf16[1024,512]{1,0:T(8,128)(2,1)}, u32[]{:S(2)}) copy-start(bf16[1024,512]{1,0:T(8,128)(2,1)} %copy-done.9) | copy-start | bytes 3145732
  867.8 48.8 %copy-start.13 = (f32[1024,512]{1,0:T(8,128)S(1)}, f32[1024,512]{1,0:T(8,128)}, u32[]{:S(2)}) copy-start(f32[1024,512]{1,0:T(8,128)} %get-tuple-element.52) | copy-start | bytes 6291460
  867.8 121.4 %collective-permute-start.14 = (bf16[32,192,512]{2,1,0:T(8,128)(2,1)}, bf16[32,192,512]{2,1,0:T(8,128)(2,1)}, u32[]{:S(2)}, u32[]{:S(2)}) collective-permute-start(bf16[32,192,512]{2,1,0:T(8,128)(2,1)} %get-tuple-element.69), channel_id=1, source_target_pairs={{0,1},{1,0},{2,3},{3,2},{4,5},{5,4},{6,7},{7,6},{8,9},{9,8},{10,11... | collective-permute-start | bytes 18874376 | tf_op jit(solution)/shard_map/ppermute | solution.py:530
  867.9 48.7 %collective-permute-start.8 = (f32[1024,512]{1,0:T(8,128)}, f32[1024,512]{1,0:T(8,128)S(1)}, u32[]{:S(2)}, u32[]{:S(2)}) collective-permute-start(f32[1024,512]{1,0:T(8,128)} %get-tuple-element.53), channel_id=1, source_target_pairs={{0,8},{8,0},{1,9},{9,1},{2,10},{10,2},{3,11},{11,3},{4,12},{12,4},... | collective-permute-start | bytes 6291464 | tf_op jit(solution)/shard_map/ppermute | solution.py:464
  867.9 98.3 %collective-permute-start.5 = (f32[1024,512]{1,0:T(8,128)}, f32[1024,512]{1,0:T(8,128)}, u32[]{:S(2)}, u32[]{:S(2)}) collective-permute-start(f32[1024,512]{1,0:T(8,128)} %get-tuple-element.50), channel_id=1, source_target_pairs={{0,8},{8,0},{1,9},{9,1},{2,10},{10,2},{3,11},{11,3},{4,12},{12,4},... | collective-permute-start | bytes 6291464 | tf_op jit(solution)/shard_map/ppermute | solution.py:464
  918.8 47.3 %copy-start.8 = (bf16[1024,512]{1,0:T(8,128)(2,1)S(1)}, bf16[1024,512]{1,0:T(8,128)(2,1)}, u32[]{:S(2)}) copy-start(bf16[1024,512]{1,0:T(8,128)(2,1)} %copy-done.7) | copy-start | bytes 3145732
  918.8 47.3 %copy-start.12 = (f32[1024,512]{1,0:T(8,128)S(1)}, f32[1024,512]{1,0:T(8,128)}, u32[]{:S(2)}) copy-start(f32[1024,512]{1,0:T(8,128)} %get-tuple-element.49) | copy-start | bytes 6291460
  966.1 3.3 copy-start.19
  966.1 3.3 copy-start.32
  (10 other events, 9.7 us)
Sparse Core Ops, SparseCore 0:
  36.7 26.9 all-gather.26
  65.6 50.5 all-gather.22
  118.0 50.4 all-gather.24
  204.6 49.9 all-gather.18
  256.8 50.5 all-gather.20
  309.7 50.4 all-gather.10
  362.6 50.5 all-gather.12
  415.0 50.4 all-gather.14
  467.7 50.2 all-gather.16
Sparse Core Ops, SparseCore 1:
  919.9 66.9 all-reduce.9

commit v4 on v3

--- a/solution.py
+++ b/solution.py
@@ -13,7 +13,7 @@
 TILE = 128
 WTILE = 256
 BATCH = 16
-SLOTS = 4
+SLOTS = 6
 PAGE = 1024
 VMEM_LIMIT = 62 * 2**20
 
@@ -32,17 +32,21 @@
 
 def nn_dot(a, b):
     return lax.dot_general(a, b, (((1,), (0,)), ((), ())), preferred_element_type=jnp.float32)
+
+
+def clear(ref):
+    step = min(64, ref.shape[0])
+
+    def one(q, carry):
+        ref[pl.ds(pl.multiple_of(q * step, step), step), :] = jnp.zeros((step, ref.shape[1]), ref.dtype)
+        return carry
+
+    lax.fori_loop(0, ref.shape[0] // step, one, 0)
 
 
 def load_rows(ref, start, rows, parts):
     cols = [ref[pl.ds(start * parts + k, rows, stride=parts), :] for k in range(parts)]
     return jnp.concatenate(cols, axis=1).astype(jnp.bfloat16)
-
-
-def store_rows(ref, start, vals, parts):
-    rows = vals.shape[0]
-    for k in range(parts):
-        ref[pl.ds(start * parts + k, rows, stride=parts), :] = vals[:, k * LANES:(k + 1) * LANES]
 
 
 def fetch_pair(own, other, dst, sem):
@@ -51,14 +55,35 @@
             pltpu.make_async_copy(other, dst.at[pl.ds(n, n)], sem.at[1]))
 
 
-def add_rows(acc, vals_ref, idx, gat, row, parts):
+def add_rows(acc, vals_ref, idx, row, parts):
     for b in range(0, TILE, BATCH):
-        toks = [idx[row + b + r] for r in range(BATCH)]
-        gates = [gat[row + b + r] for r in range(BATCH)]
-        vals = [acc[pl.ds(toks[r] * parts, parts), :] + gates[r] * vals_ref[pl.ds((b + r) * parts, parts), :]
-                for r in range(BATCH)]
+        at = [pl.multiple_of(idx[row + b + r], parts) for r in range(BATCH)]
+        vals = [acc[pl.ds(at[r], parts), :] + vals_ref[pl.ds((b + r) * parts, parts), :] for r in range(BATCH)]
         for r in reversed(range(BATCH)):
-            acc[pl.ds(toks[r] * parts, parts), :] = vals[r]
+            acc[pl.ds(at[r], parts), :] = vals[r]
+
+
+def spread_column(row):
+    return jnp.broadcast_to(row, (LANES, LANES)).T
+
+
+def tile_gates(gates, row):
+    pair = gates[pl.ds(lax.div(row, LANES), 2), :]
+    skip = lax.rem(row, LANES)
+    pair = pltpu.roll(pair, lax.rem(LANES - skip, LANES), 1)
+    lane = lax.broadcasted_iota(jnp.int32, (1, LANES), 1)
+    return spread_column(jnp.where(lane < LANES - skip, pair[:1], pair[1:]))
+
+
+def widen(src, dst, parts):
+    step = 8
+
+    def one(q, carry):
+        for r in range(step):
+            dst[pl.ds((q * step + r) * parts, parts), :] = src[q * step + r].astype(jnp.float32)
+        return carry
+
+    lax.fori_loop(0, src.shape[0] // step, one, 0)
 
 
 def write_sums(acc, own_ref, other_ref, tok, parts):
@@ -82,91 +107,107 @@
             for k, w in enumerate(weights)]
 
 
-def run_tiles(step, weights, wbuf, wsem, tile_e, tile_first, n_steps, layer, copies):
+def run_tiles(step, weights, wbuf, wsem, tile_e, tile_first, n_steps, layer, prepare):
     n_local = weights[0].shape[1]
-    ahead = list(copies) + expert_copies(weights, wbuf, wsem, layer, 0)
-    for c in ahead:
-        c.start()
-    for e in range(1, min(SLOTS - 1, n_local)):
+    for e in range(min(SLOTS - 1, n_local)):
         for c in expert_copies(weights, wbuf, wsem, layer, e):
             c.start()
-    for c in ahead:
+    prepare()
+    for c in expert_copies(weights, wbuf, wsem, layer, 0):
         c.wait()
 
     def one(i, carry):
-        e = tile_e[i + 1]
-
-        @pl.when(tile_first[i + 1] == 1)
+        e = tile_e[i + 2]
+
+        @pl.when(tile_first[i + 2] == 1)
         def _():
             for c in expert_copies(weights, wbuf, wsem, layer, e):
                 c.wait()
 
-        @pl.when((tile_first[i + 1] == 1) & (e + SLOTS - 2 < n_local))
+        @pl.when((tile_first[i + 2] == 1) & (e + SLOTS - 2 < n_local))
         def _():
             for c in expert_copies(weights, wbuf, wsem, layer, e + SLOTS - 2):
                 c.start()
 
-        step(i, lax.rem(e, SLOTS))
+        step(i, lax.rem(e, SLOTS), lax.rem(tile_e[i + 1], SLOTS))
         return carry
 
     lax.fori_loop(0, n_steps, one, 0)
 
 
-def forward_body(te, tf, tr, tn, nt, idx, gat, u_own, u_oth, g_ref, up_ref, w_ref, own_ref, other_ref,
-                 usc, ut, ot, acc, wbuf, sem, wsem, *, layer, tok, parts):
+def forward_body(te, tf, tr, tn, nt, idx, gates, u_own, u_oth, g_ref, up_ref, w_ref, own_ref, other_ref,
+                 usc, uf, ut, ot, acc, ht, wbuf, sem, wsem, *, layer, tok, parts):
     ff = g_ref.shape[2]
-    acc[...] = jnp.zeros_like(acc)
-    ot[...] = jnp.zeros_like(ot)
-    ut[...] = jnp.zeros_like(ut)
-
-    def step(i, slot):
+
+    def prepare():
+        copies = fetch_pair(u_own, u_oth, usc, sem)
+        for c in copies:
+            c.start()
+        for ref in (acc, ot, ut, ht):
+            clear(ref)
+        for c in copies:
+            c.wait()
+        widen(usc, uf, parts)
+
+    def step(i, slot, slot_before):
+        o = tn_dot(ht[...], wbuf[slot_before, 2 * ff:]).astype(jnp.bfloat16).astype(jnp.float32)
         u = load_rows(ut, 0, TILE, parts)
         ab = nt_dot(wbuf[slot, :2 * ff], u)
-        add_rows(acc, ot, idx, gat, tr[i], parts)
-        row = tr[i + 2]
+        add_rows(acc, ot, idx, tr[i], parts)
+        row = tr[i + 3]
         for r in range(TILE):
-            ut[pl.ds(parts * r, parts), :] = usc[idx[row + r]].astype(jnp.float32)
+            ut[pl.ds(parts * r, parts), :] = uf[pl.ds(pl.multiple_of(idx[row + r], parts), parts), :]
+        live = lax.broadcasted_iota(jnp.int32, (TILE, LANES), 0) < tn[i + 1]
+        gate = tile_gates(gates, tr[i + 1])
+        for k in range(parts):
+            o_k = jnp.where(live, o[:, k * LANES:(k + 1) * LANES] * gate, 0.0)
+            ot[pl.ds(k, TILE, stride=parts), :] = o_k
         a, b = ab[:ff], ab[ff:]
-        h = (a * jax.nn.sigmoid(a) * b).astype(jnp.bfloat16)
-        o = tn_dot(h, wbuf[slot, 2 * ff:]).astype(jnp.bfloat16).astype(jnp.float32)
-        live = lax.broadcasted_iota(jnp.int32, o.shape, 0) < tn[i + 1]
-        store_rows(ot, 0, jnp.where(live, o, 0.0), parts)
-
-    run_tiles(step, (g_ref, up_ref, w_ref), wbuf, wsem, te, tf, nt[0] + 2, layer,
-              fetch_pair(u_own, u_oth, usc, sem))
+        ht[...] = (a * jax.nn.sigmoid(a) * b).astype(jnp.bfloat16)
+
+    run_tiles(step, (g_ref, up_ref, w_ref), wbuf, wsem, te, tf, nt[0] + 3, layer, prepare)
     write_sums(acc, own_ref, other_ref, tok, parts)
 
 
-def backward_body(te, tf, tr, tn, nt, idx, gat, u_own, u_oth, d_own, d_oth, g_ref, up_ref, w_ref, own_ref, other_ref,
-                  usc, dsc, ut, ct, vt, acc, wbuf, sem, wsem, *, layer, tok, parts):
+def backward_body(te, tf, tr, tn, nt, idx, gates, u_own, u_oth, d_own, d_oth, g_ref, up_ref, w_ref, own_ref, other_ref,
+                  usc, dsc, uf, df, ut, dt, vt, acc, da_t, wbuf, sem, wsem, *, layer, tok, parts):
     ff = g_ref.shape[2]
-    acc[...] = jnp.zeros_like(acc)
-    vt[...] = jnp.zeros_like(vt)
-    ut[...] = jnp.zeros_like(ut)
-    ct[...] = jnp.zeros_like(ct)
-
-    def step(i, slot):
+
+    def prepare():
+        copies = fetch_pair(u_own, u_oth, usc, sem.at[0]) + fetch_pair(d_own, d_oth, dsc, sem.at[1])
+        for c in copies:
+            c.start()
+        for ref in (acc, vt, ut, dt, da_t):
+            clear(ref)
+        for c in copies:
+            c.wait()
+        widen(usc, uf, parts)
+        widen(dsc, df, parts)
+
+    def step(i, slot, slot_before):
+        v = tn_dot(da_t[...], wbuf[slot_before, :2 * ff]).astype(jnp.bfloat16).astype(jnp.float32)
         u = load_rows(ut, 0, TILE, parts)
-        c = load_rows(ct, 0, TILE, parts)
-        gu = wbuf[slot, :2 * ff]
-        ab = nt_dot(gu, u)
+        gate = tile_gates(gates, tr[i + 2])
+        c = jnp.concatenate([(dt[pl.ds(k, TILE, stride=parts), :] * gate).astype(jnp.bfloat16) for k in range(parts)], axis=1)
+        ab = nt_dot(wbuf[slot, :2 * ff], u)
         dh = nt_dot(wbuf[slot, 2 * ff:], c)
-        add_rows(acc, vt, idx, gat, tr[i], parts)
-        row = tr[i + 2]
+        add_rows(acc, vt, idx, tr[i], parts)
+        row = tr[i + 3]
         for r in range(TILE):
-            t = idx[row + r]
-            ut[pl.ds(parts * r, parts), :] = usc[t].astype(jnp.float32)
-            ct[pl.ds(parts * r, parts), :] = gat[row + r] * dsc[t].astype(jnp.float32)
+            at = pl.multiple_of(idx[row + r], parts)
+            ut[pl.ds(parts * r, parts), :] = uf[pl.ds(at, parts), :]
+            dt[pl.ds(parts * r, parts), :] = df[pl.ds(at, parts), :]
+        live = lax.broadcasted_iota(jnp.int32, (TILE, LANES), 0) < tn[i + 1]
+        gate = tile_gates(gates, tr[i + 1])
+        for k in range(parts):
+            v_k = jnp.where(live, v[:, k * LANES:(k + 1) * LANES] * gate, 0.0)
+            vt[pl.ds(k, TILE, stride=parts), :] = v_k
         a, b = ab[:ff], ab[ff:]
         s = jax.nn.sigmoid(a)
-        da = (dh * b * (s * (1.0 + a * (1.0 - s)))).astype(jnp.bfloat16)
-        db = (dh * (a * s)).astype(jnp.bfloat16)
-        v = tn_dot(jnp.concatenate([da, db], axis=0), gu).astype(jnp.bfloat16).astype(jnp.float32)
-        live = lax.broadcasted_iota(jnp.int32, v.shape, 0) < tn[i + 1]
-        store_rows(vt, 0, jnp.where(live, v, 0.0), parts)
-
-    run_tiles(step, (g_ref, up_ref, w_ref), wbuf, wsem, te, tf, nt[0] + 2, layer,
-              fetch_pair(u_own, u_oth, usc, sem.at[0]) + fetch_pair(d_own, d_oth, dsc, sem.at[1]))
+        da_t[:ff] = (dh * b * (s * (1.0 + a * (1.0 - s)))).astype(jnp.bfloat16)
+        da_t[ff:] = (dh * (a * s)).astype(jnp.bfloat16)
+
+    run_tiles(step, (g_ref, up_ref, w_ref), wbuf, wsem, te, tf, nt[0] + 3, layer, prepare)
     write_sums(acc, own_ref, other_ref, tok, parts)
 
 
@@ -181,13 +222,15 @@
     return pl.pallas_call(
         functools.partial(body, layer=layer, tok=tok, parts=parts),
         grid_spec=pltpu.PrefetchScalarGridSpec(
-            num_scalar_prefetch=len(tables),
+            num_scalar_prefetch=len(tables) - 1,
             grid=(1,),
-            in_specs=[any_spec] * (len(slabs) + 3),
+            in_specs=[pl.BlockSpec(tables[-1].shape, lambda i, *_: (0, 0))] + [any_spec] * (len(slabs) + 3),
             out_specs=[rows_spec] * 2,
             scratch_shapes=[pltpu.VMEM((2 * tok, parts, LANES), jnp.bfloat16)] * n_pairs
+            + [pltpu.VMEM((2 * tok * parts, LANES), jnp.float32)] * n_pairs
             + [pltpu.VMEM((TILE * parts, LANES), jnp.float32)] * (n_pairs + 1)
-            + [pltpu.VMEM((2 * tok * parts, LANES), jnp.float32), pltpu.VMEM((SLOTS, 3 * ff, d_model), jnp.bfloat16),
+            + [pltpu.VMEM((2 * tok * parts, LANES), jnp.float32), pltpu.VMEM((n_pairs * ff, TILE), jnp.bfloat16),
+               pltpu.VMEM((SLOTS, 3 * ff, d_model), jnp.bfloat16),
                pltpu.SemaphoreType.DMA(sem_shape), pltpu.SemaphoreType.DMA((SLOTS,))],
         ),
         out_shape=[jax.ShapeDtypeStruct((tok, d_model), jnp.float32)] * 2,
@@ -197,10 +240,11 @@
     )(*tables, *slabs, *weights)
 
 
-def merge_tables_body(st, exps, table, idx_ref, gate_ref, buf, *, src, n_exp, src_rows, out_rows):
+def merge_tables_body(st, exps, table, idx_ref, gate_ref, buf, *, src, n_exp, src_rows, out_rows, pad_row):
     layer, e = pl.program_id(0), pl.program_id(1)
     exp = exps[layer * n_exp + e]
-    buf[...] = jnp.zeros_like(buf)
+    buf[0] = jnp.full(buf.shape[1:], float(pad_row), jnp.float32)
+    buf[1] = jnp.zeros(buf.shape[1:], jnp.float32)
     row = lax.broadcasted_iota(jnp.int32, (8, LANES), 0)
     lane = lax.broadcasted_iota(jnp.int32, (8, LANES), 1)
     off = 0
@@ -225,14 +269,15 @@
     gate_ref[0, 0] = buf[1, pl.ds(1, out_rows), :]
 
 
-def merge_tables(shared, starts, exps, out_rows):
+def merge_tables(shared, starts, exps, out_rows, pad_row):
     n_layers, _, src, rows = shared.shape
     n_exp = exps.shape[1]
     exps = exps.reshape(-1)
     src_rows = rows // LANES
     out = pl.BlockSpec((1, 1, out_rows, LANES), lambda l, e, *_: (l, e, 0, 0))
     return pl.pallas_call(
-        functools.partial(merge_tables_body, src=src, n_exp=n_exp, src_rows=src_rows, out_rows=out_rows),
+        functools.partial(merge_tables_body, src=src, n_exp=n_exp, src_rows=src_rows, out_rows=out_rows,
+                          pad_row=pad_row),
         grid_spec=pltpu.PrefetchScalarGridSpec(
             num_scalar_prefetch=2,
             grid=(n_layers, n_exp),
@@ -248,13 +293,14 @@
     )(starts, exps, shared.reshape(n_layers, 2, src * src_rows, LANES))
 
 
-def weight_grad_body(exps, tiles, u_own, u_oth, d_own, d_oth, idx_all, gate_ref, *refs, parts, n_exp, n_alias, layer, page):
+def weight_grad_body(exps, tiles, begins, ud_own, ud_oth, idx_all, gate_ref, *refs, parts, n_exp, n_alias, layer, page):
     g_ref, up_ref, w_ref = refs[:3]
     (dg_ref, du_ref, dw_ref, og_ref, ou_ref, ow_ref,
-     usc, dsc, ut, dt, ub, cb, gacc, wacc, idx_s, sem, tsem) = refs[3 + n_alias:]
+     uds, ut, dt, u0, c0, d0, h0, u1, c1, d1, h1, gacc, wacc, idx_s, sem, tsem) = refs[3 + n_alias:]
     e = pl.program_id(0)
     ff = g_ref.shape[2]
     slots = 3
+    both = ((u0, c0, d0, h0), (u1, c1, d1, h1))
 
     def table_copy(exp):
         slot = lax.rem(exp, slots)
@@ -263,17 +309,21 @@
         return pltpu.make_async_copy(idx_all.at[pl.ds(at, page)], idx_s.at[pl.ds(to, page)], tsem.at[slot])
 
     def gather_row(at, r):
-        t = idx_s[at]
-        ut[pl.ds(r * parts, parts), :] = usc[t].astype(jnp.float32)
-        dt[pl.ds(r * parts, parts), :] = dsc[t].astype(jnp.float32)
+        x = uds[idx_s[at]].astype(jnp.float32)
+        ut[pl.ds(r * parts, parts), :] = x[:parts]
+        dt[pl.ds(r * parts, parts), :] = x[parts:]
 
     @pl.when(e == 0)
     def _():
-        copies = fetch_pair(u_own, u_oth, usc, sem.at[0]) + fetch_pair(d_own, d_oth, dsc, sem.at[1])
+        copies = fetch_pair(ud_own, ud_oth, uds, sem)
         for c in copies:
             c.start()
         table_copy(0).start()
         table_copy(1).start()
+        n_rows = ud_own.shape[0] * 2
+        uds[pl.ds(n_rows, 8)] = jnp.zeros((8, 2 * parts, LANES), jnp.bfloat16)
+        for ref in (*both[0], *both[1], gacc, wacc):
+            clear(ref)
         table_copy(0).wait()
         for c in copies:
             c.wait()
@@ -293,76 +343,99 @@
     def _():
         table_copy(e + 2).start()
 
-    gacc[...] = jnp.zeros_like(gacc)
-    wacc[...] = jnp.zeros_like(wacc)
     here = lax.rem(e, slots) * page
     there = lax.rem(jnp.minimum(e + 1, n_exp - 1), slots) * page
-    n_tiles = tiles[layer * n_exp + e]
+    n_tiles = tiles[layer * (n_exp + 1) + e]
+    begin = begins[layer * (n_exp + 1) + e]
     gate_rows = WTILE // LANES
 
-    def tile(j, carry):
-        ub[...] = load_rows(ut, 0, WTILE, parts)
-        gates = [jnp.broadcast_to(gate_ref[0, 0, pl.ds(j * gate_rows + q, 1), :], (LANES, LANES)).T for q in range(gate_rows)]
+    def compute(j, new, old):
+        un, cn, dn, hn = new
+        uo, co, do, ho = old
+        gacc[...] += nn_dot(do[...], uo[...])
+        wacc[...] += nn_dot(ho[...], co[...])
+        un[...] = load_rows(ut, 0, WTILE, parts)
+        gates = [spread_column(gate_ref[0, 0, pl.ds(j * gate_rows + q, 1), :]) for q in range(gate_rows)]
         for k in range(parts):
             for q in range(gate_rows):
                 d = dt[pl.ds(q * LANES * parts + k, LANES, stride=parts), :]
-                cb[q * LANES:(q + 1) * LANES, k * LANES:(k + 1) * LANES] = (d * gates[q]).astype(jnp.bfloat16)
-        ab = nt_dot(jnp.concatenate([g_ref[0, 0], up_ref[0, 0]], axis=0), ub[...])
-        dh = nt_dot(w_ref[0, 0], cb[...])
+                cn[q * LANES:(q + 1) * LANES, k * LANES:(k + 1) * LANES] = (d * gates[q]).astype(jnp.bfloat16)
+        ab = nt_dot(jnp.concatenate([g_ref[0, 0], up_ref[0, 0]], axis=0), un[...])
+        dh = nt_dot(w_ref[0, 0], cn[...])
         nxt = jnp.where(j + 1 < n_tiles, here + (j + 1) * WTILE, there)
         for r in range(WTILE):
             gather_row(nxt + r, r)
         a, b = ab[:ff], ab[ff:]
         s = jax.nn.sigmoid(a)
         act = a * s
-        h = (act * b).astype(jnp.bfloat16)
-        da = (dh * b * (s * (1.0 + a * (1.0 - s)))).astype(jnp.bfloat16)
-        db = (dh * act).astype(jnp.bfloat16)
-        gacc[...] += nn_dot(jnp.concatenate([da, db], axis=0), ub[...])
-        wacc[...] += nn_dot(h, cb[...])
+        hn[...] = (act * b).astype(jnp.bfloat16)
+        dn[:ff] = (dh * b * (s * (1.0 + a * (1.0 - s)))).astype(jnp.bfloat16)
+        dn[ff:] = (dh * act).astype(jnp.bfloat16)
+
+    def tile(j, carry):
+        odd = lax.rem(begin + j, 2)
+
+        @pl.when(odd == 0)
+        def _():
+            compute(j, both[0], both[1])
+
+        @pl.when(odd == 1)
+        def _():
+            compute(j, both[1], both[0])
+
+        @pl.when(j == 0)
+        def _():
+            dg = gacc[:ff].astype(jnp.bfloat16)
+            du = gacc[ff:].astype(jnp.bfloat16)
+            dw = wacc[...].astype(jnp.bfloat16)
+            dg_ref[0, 0], du_ref[0, 0], dw_ref[0, 0] = dg, du, dw
+            og_ref[0], ou_ref[0], ow_ref[0] = dg, du, dw
+            gacc[...] = jnp.zeros_like(gacc)
+            wacc[...] = jnp.zeros_like(wacc)
+
         return carry
 
     lax.fori_loop(0, n_tiles, tile, 0)
-    dg = gacc[:ff].astype(jnp.bfloat16)
-    du = gacc[ff:].astype(jnp.bfloat16)
-    dw = wacc[...].astype(jnp.bfloat16)
-    dg_ref[0, 0], du_ref[0, 0], dw_ref[0, 0] = dg, du, dw
-    og_ref[0], ou_ref[0], ow_ref[0] = dg, du, dw
-
-
-def weight_grads(layer, exps, tiles, u_alls, d_alls, idx_all, gates, weights, full):
-    n_src, parts, _ = u_alls[0].shape
+
+
+def weight_grads(layer, exps, tiles, ud_alls, idx_all, gates, weights, full):
+    n_src, parts2, _ = ud_alls[0].shape
+    parts = parts2 // 2
     n_tok = 2 * n_src
     n_layers, n_local, ff, d_model = weights[0].shape
     n_exp = n_local // 2
     out_rows = gates.shape[2]
     page = out_rows * LANES
+    tiles = jnp.concatenate([tiles, jnp.ones((n_layers, 1), jnp.int32)], axis=1)
+    begins = jnp.cumsum(tiles, axis=1) - tiles
     any_spec = pl.BlockSpec(memory_space=pl.ANY)
-    mine = pl.BlockSpec((1, 1, ff, d_model), lambda e, exps, tiles: (layer, exps[e], 0, 0))
-    half = pl.BlockSpec((1, ff, d_model), lambda e, *_: (e, 0, 0))
-    gate_spec = pl.BlockSpec((1, 1, out_rows, LANES), lambda e, *_: (layer, e, 0, 0))
+    mine = pl.BlockSpec((1, 1, ff, d_model), lambda e, exps, *_: (layer, exps[jnp.minimum(e, n_exp - 1)], 0, 0))
+    done = pl.BlockSpec((1, 1, ff, d_model), lambda e, exps, *_: (layer, exps[jnp.maximum(e - 1, 0)], 0, 0))
+    half = pl.BlockSpec((1, ff, d_model), lambda e, *_: (jnp.maximum(e - 1, 0), 0, 0))
+    gate_spec = pl.BlockSpec((1, 1, out_rows, LANES), lambda e, *_: (layer, jnp.minimum(e, n_exp - 1), 0, 0))
     aliased = list(full) if full is not None else []
+    tile_set = [pltpu.VMEM((WTILE, d_model), jnp.bfloat16)] * 2 + [pltpu.VMEM((2 * ff, WTILE), jnp.bfloat16),
+                                                                 pltpu.VMEM((ff, WTILE), jnp.bfloat16)]
     outs = pl.pallas_call(
         functools.partial(weight_grad_body, parts=parts, n_exp=n_exp, n_alias=len(aliased), layer=layer, page=page),
         grid_spec=pltpu.PrefetchScalarGridSpec(
-            num_scalar_prefetch=2,
-            grid=(n_exp,),
-            in_specs=[any_spec] * 5 + [gate_spec] + [mine] * 3 + [any_spec] * len(aliased),
-            out_specs=[mine] * 3 + [half] * 3,
-            scratch_shapes=[pltpu.VMEM((n_tok, parts, LANES), jnp.bfloat16)] * 2
-            + [pltpu.VMEM((WTILE * parts, LANES), jnp.float32)] * 2
-            + [pltpu.VMEM((WTILE, d_model), jnp.bfloat16)] * 2
+            num_scalar_prefetch=3,
+            grid=(n_exp + 1,),
+            in_specs=[any_spec] * 3 + [gate_spec] + [mine] * 3 + [any_spec] * len(aliased),
+            out_specs=[done] * 3 + [half] * 3,
+            scratch_shapes=[pltpu.VMEM((n_tok + 8, parts2, LANES), jnp.bfloat16)]
+            + [pltpu.VMEM((WTILE * parts, LANES), jnp.float32)] * 2 + tile_set * 2
             + [pltpu.VMEM((2 * ff, d_model), jnp.float32), pltpu.VMEM((ff, d_model), jnp.float32),
-               pltpu.SMEM((3 * page,), jnp.int32), pltpu.SemaphoreType.DMA((2, 2)), pltpu.SemaphoreType.DMA((3,))],
+               pltpu.SMEM((3 * page,), jnp.int32), pltpu.SemaphoreType.DMA((2,)), pltpu.SemaphoreType.DMA((3,))],
         ),
         out_shape=[jax.ShapeDtypeStruct((n_layers, n_local, ff, d_model), jnp.bfloat16)] * 3
         + [jax.ShapeDtypeStruct((n_exp, ff, d_model), jnp.bfloat16)] * 3,
-        input_output_aliases={11 + k: k for k in range(len(aliased))},
+        input_output_aliases={10 + k: k for k in range(len(aliased))},
         compiler_params=pltpu.CompilerParams(dimension_semantics=("arbitrary",), vmem_limit_bytes=VMEM_LIMIT),
         cost_estimate=pl.CostEstimate(flops=6 * 2 * n_tok * 2 * d_model * ff * 4,
                                       bytes_accessed=n_tok * d_model * 4 + 9 * n_exp * ff * d_model * 2, transcendentals=0),
         name="weight_grads",
-    )(exps, tiles, *u_alls, *d_alls, idx_all, gates, *weights, *aliased)
+    )(exps, tiles.reshape(-1), begins.reshape(-1), *ud_alls, idx_all, gates, *weights, *aliased)
     return outs[:3], outs[3:]
 
 
@@ -402,7 +475,7 @@
     starts = ends - counts
     n_tiles = jnp.maximum((counts + TILE - 1) // TILE, 1)
     tile_end = jnp.cumsum(n_tiles)
-    tile_id = jnp.arange(n // TILE + n_local + 4, dtype=jnp.int32) - 2
+    tile_id = jnp.arange(n // TILE + n_local + 8, dtype=jnp.int32) - 3
     tile_e = jnp.minimum(jnp.sum((tile_end[None, :] <= tile_id[:, None]).astype(jnp.int32), axis=1), n_local - 1)
     pick = (tile_e[:, None] == jnp.arange(n_local)[None, :]).astype(jnp.int32)
     inside = (tile_id - jnp.sum(pick * (tile_end - n_tiles)[None, :], axis=1)) * TILE
@@ -477,15 +550,35 @@
         mine = jnp.stack([ids.astype(jnp.float32), gates])
         theirs = swap(mine)
         both = jnp.stack([mine, theirs], 2)
-        both_ids = both[0].astype(jnp.int32)
         tables, packed = [], []
-        for layer in range(n_layers):
-            table, bounds = route_tables(both_ids[layer], both[1, layer], ep_id, n_local)
-            tables.append(table)
+
+        def add_tables(pair):
+            table, bounds = route_tables(pair[0].astype(jnp.int32), pair[1], ep_id, n_local)
             token, gate = table[5], table[6]
+            tables.append((*table[:5], token * parts, gate.reshape(-1, LANES)))
             spot = lax.div(token, tok) * (dp_size * tok) + dp_id * tok + lax.rem(token, tok)
             packed.append(jnp.stack([jnp.concatenate([spot, jnp.pad(bounds, (0, PAGE - LANES))])
                                      .astype(jnp.float32), jnp.pad(gate, (0, PAGE))]))
+
+        add_tables(both[:, 0])
+
+        d_slab = slab(d_out)
+        d_other = swap(d_slab)
+
+        top = n_layers - 1
+        x_in, u_slabs, u_others, xs = tokens, [], [], []
+        for layer in range(n_layers):
+            u = mixed(x_in, layer)
+            u_slabs.append(slab(u))
+            u_others.append(swap(u_slabs[layer]))
+            xs.append(x_in)
+            if layer < top:
+                own, other = token_kernel(forward_body, layer, tables[layer],
+                                          (u_slabs[layer], u_others[layer]), weights)
+                sent = swap(other)
+                add_tables(after(both[:, layer + 1], other))
+                x_in = (u.astype(jnp.float32) + own + sent).astype(jnp.bfloat16)
+
         rows = packed[0].shape[1]
         shared = lax.all_gather(jnp.stack(packed), 'dp', axis=2)
         shared = shared.reshape(n_layers, 2, dp_size, rows)
@@ -493,29 +586,13 @@
         split = [split_experts(starts[layer, :, :n_local + 1], dp_id % 2) for layer in range(n_layers)]
         mine_e, theirs_e, tiles = (jnp.stack(x) for x in zip(*split))
         list_rows = cdiv(cdiv(dp_size * 2 * cap, LANES), 8) * 8 + 8
-        idx_all, gate_all = merge_tables(shared, starts.reshape(-1), mine_e, list_rows)
+        idx_all, gate_all = merge_tables(shared, starts.reshape(-1), mine_e, list_rows, dp_size * 2 * tok)
         idx_all = idx_all.reshape(-1)
-
-        d_slab = slab(d_out)
-        d_other = swap(d_slab)
-        d_spread = (spread(d_slab), spread(d_other))
-
-        top = n_layers - 1
-        x_in, u_slabs, u_others, xs, u_spreads = tokens, [], [], [], []
-        for layer in range(n_layers):
-            u = mixed(x_in, layer)
-            u_slabs.append(slab(u))
-            u_others.append(swap(u_slabs[layer]))
-            xs.append(x_in)
-            u_spreads.append((spread(u_slabs[layer]), spread(u_others[layer])))
-            if layer < top:
-                own, other = token_kernel(forward_body, layer, tables[layer],
-                                          (u_slabs[layer], u_others[layer]), weights)
-                x_in = (u.astype(jnp.float32) + own + swap(other)).astype(jnp.bfloat16)
 
         d_y, full = d_out, None
         d_mix = [None] * n_layers
         for layer in reversed(range(n_layers)):
+            spreads = [spread(jnp.concatenate(x, axis=1)) for x in ((u_slabs[layer], d_slab), (u_others[layer], d_other))]
             own, other = token_kernel(backward_body, layer, tables[layer],
                                       (u_slabs[layer], u_others[layer], d_slab, d_other), weights)
             d_u = (d_y.astype(jnp.float32) + own + swap(other)).astype(jnp.bfloat16)
@@ -525,8 +602,7 @@
                                               (after(u_slabs[top], other), u_others[top]), weights)
                 layer_out = (u.astype(jnp.float32) + y_own + swap(y_other)).astype(jnp.bfloat16)
                 last = y_other
-            full, half = weight_grads(layer, mine_e[layer], after(tiles, last).reshape(-1), u_spreads[layer], d_spread,
-                                      idx_all, gate_all, weights, full)
+            full, half = weight_grads(layer, mine_e[layer], after(tiles, last), spreads, idx_all, gate_all, weights, full)
             full = merge_half(layer, theirs_e[layer], [lax.ppermute(x, 'dp', core_pairs) for x in half], full)
             d_mix[layer] = jnp.einsum('td,te->de', xs[layer], d_u, preferred_element_type=jnp.float32).astype(jnp.bfloat16)
             d_y = (d_u.astype(jnp.float32)
@@ -534,7 +610,6 @@
             if layer:
                 d_slab = slab(d_y)
                 d_other = swap(d_slab)
-                d_spread = (spread(d_slab), spread(d_other))
         d_mix = lax.psum(jnp.stack(d_mix), ('dp', 'ep'))
         return (layer_out, d_y, d_mix, jnp.swapaxes(full[0], 2, 3), jnp.swapaxes(full[1], 2, 3), full[2])
 

time: 1020 us -> 904 us (0.89)
  Pallas kernels: 647 us -> 514 us
  waiting for transfers between devices: 262 us -> 273 us
    pallas_call x4, Pallas kernels: 286 us -> 210 us  [token_kernel(): pl.pallas_call(functools.partial(body, layer=layer, tok=tok, parts=parts)...]
    pallas_call x2, Pallas kernels: 287 us -> 229 us  [weight_grads(): pl.pallas_call(functools.partial(weight_grad_body, parts=parts, n_exp=n_e...]
    ppermute x9, waiting for transfers between devices: 245 us -> 256 us  [swap(): return lax.ppermute(x, 'ep', ep_pairs)]
  transfers between devices with their start and end apart: 25 -> 21, of which waited for: 9 -> 9; matrix products, arithmetic and copies ran while one was open for 4% -> 7% of each run, Pallas kernels for 46% -> 36%
where the time goes in v4:
time: 904 us; the launch traced here: 902 us
  Pallas kernels  514 us (57%)
  waiting for transfers between devices  273 us (30%)
  other arithmetic  47.7 us (5%)
  local copies, waits for them, and re-layouts  26.5 us (3%)
  starting transfers between devices  16.3 us (2%)
  between operations  15.9 us (2%)
    ppermute x9, waiting for transfers between devices, swap(): return lax.ppermute(x, 'ep', ep_pairs)  256 us
    pallas_call x2, Pallas kernels, weight_grads(): pl.pallas_call(functools.partial(weight_grad_body, parts=parts, n_exp=n_e...  229 us
    pallas_call x4, Pallas kernels, token_kernel(): pl.pallas_call(functools.partial(body, layer=layer, tok=tok, parts=parts)...  210 us
    pallas_call x2, Pallas kernels, merge_half(): pl.pallas_call(merge_body, grid_spec=pltpu.PrefetchScalarGridSpec(num_sca...  47.5 us
    pallas_call x1, Pallas kernels, merge_tables(): pl.pallas_call(functools.partial(merge_tables_body, src=src, n_exp=n_exp,...  27.6 us
  transfers between devices with their start and end apart: 21, of which 9 were waited for; matrix products, arithmetic and copies ran while one was open for 7% of the time, Pallas kernels for 36%

profile of v4, /device:TPU:0, one launch (start us, length us, event | category | flops | bytes accessed | tf_op | source)
XLA Modules:
  0.0 901.8 jit_solution(2272755737382666024)
XLA Ops:
  9.8 3.3 collective-permute-start
  13.1 2.4 add_convert_fusion.7
  18.8 6.4 sort.30
  26.0 1.2 and_convert_fusion.1.tf
  27.7 1.1 clamp_select_fusion.1
  29.6 11.8 %collective-permute-done.1.u_oth = bf16[1024,4,128]{2,1,0:T(4,128)(2,1)S(1)} collective-permute-done((bf16[1024,4,128]{2,1,0:T(4,128)(2,1)S(1)}, bf16[1024,4,128]{2,1,0:T(4,128)(2,1)S(1)}, u32[]{:S(2)}, u32[]{:S(2)}) %collective-permute-start.1) | collective-permute-done | bytes 1048608 | tf_op jit(solution)/shard_map/ppermute | solution.py:537
  41.4 1.0 copy-done.4
  42.4 48.9 %shard_map.127 = (f32[1024,512]{1,0:T(8,128)}, f32[1024,512]{1,0:T(8,128)}) custom-call(s32[200]{0:T(256)} %copy-done.28, s32[200]{0:T(256)} %and_convert_fusion.1.tf, s32[200]{0:T(256)} %get-tuple-element.139.tr, s32[200]{0:T(256)} %get-tuple-element.138.tn, s32[1]{0:T(128)} %bitcast.9.nt, s32[18432]{0:T(1024)} %get-tuple-element.123.idx, ...), custom_call_target="tpu_custom_call" | custom-call | flops 19327352832 | bytes 37748736 | tf_op jit(solution)/shard_map/pallas_call | solution.py:222
  92.9 6.4 sort.31
  104.1 46.2 %collective-permute-done.2 = f32[1024,512]{1,0:T(8,128)} collective-permute-done((f32[1024,512]{1,0:T(8,128)}, f32[1024,512]{1,0:T(8,128)}, u32[]{:S(2)}, u32[]{:S(2)}) %collective-permute-start.2) | collective-permute-done | bytes 2097184 | tf_op jit(solution)/shard_map/ppermute | solution.py:537
  150.3 2.9 add_convert_fusion.6
  153.2 1.0 copy-done.19
  155.2 2.4 pad_maximum_fusion.2
  158.0 1.7 collective-permute-start.3
  159.8 24.0 %collective-permute-done.4.d_oth = bf16[1024,4,128]{2,1,0:T(4,128)(2,1)S(1)} collective-permute-done((bf16[1024,4,128]{2,1,0:T(4,128)(2,1)S(1)}, bf16[1024,4,128]{2,1,0:T(4,128)(2,1)S(1)}, u32[]{:S(2)}, u32[]{:S(2)}) %collective-permute-start.4) | collective-permute-done | bytes 1048608 | tf_op jit(solution)/shard_map/ppermute | solution.py:537
  183.8 19.3 %collective-permute-done.3.u_oth = bf16[1024,4,128]{2,1,0:T(4,128)(2,1)S(1)} collective-permute-done((bf16[1024,4,128]{2,1,0:T(4,128)(2,1)S(1)}, bf16[1024,4,128]{2,1,0:T(4,128)(2,1)S(1)}, u32[]{:S(2)}, u32[]{:S(2)}) %collective-permute-start.3) | collective-permute-done | bytes 1048608 | tf_op jit(solution)/shard_map/ppermute | solution.py:537
  203.1 1.0 copy-done.6
  204.1 2.4 pad_maximum_fusion.3
  207.7 1.3 and_convert_fusion.tf
  209.0 1.2 clamp_select_fusion
  210.2 55.9 %shard_map.128 = (f32[1024,512]{1,0:T(8,128)}, f32[1024,512]{1,0:T(8,128)}) custom-call(s32[200]{0:T(256)} %copy-done.29, s32[200]{0:T(256)} %and_convert_fusion.tf, s32[200]{0:T(256)} %get-tuple-element.137.tr, s32[200]{0:T(256)} %get-tuple-element.136.tn, s32[1]{0:T(128)} %bitcast.17.nt, s32[18432]{0:T(1024)} %get-tuple-element.127.idx, ...), custom_call_target="tpu_custom_call" | custom-call | flops 38654705664 | bytes 37748736 | tf_op jit(solution)/shard_map/pallas_call | solution.py:222
  266.1 2.8 collective-permute-start.6
  268.8 43.3 %collective-permute-done.6 = f32[1024,512]{1,0:T(8,128)S(1)} collective-permute-done((f32[1024,512]{1,0:T(8,128)}, f32[1024,512]{1,0:T(8,128)S(1)}, u32[]{:S(2)}, u32[]{:S(2)}) %collective-permute-start.6) | collective-permute-done | bytes 2097184 | tf_op jit(solution)/shard_map/ppermute | solution.py:537
  312.1 2.3 add_convert_fusion.3
  316.6 2.4 pad_maximum_fusion
  319.1 1.8 collective-permute-start.7
  320.9 20.1 %collective-permute-done.7.d_oth = bf16[1024,4,128]{2,1,0:T(4,128)(2,1)S(1)} collective-permute-done((bf16[1024,4,128]{2,1,0:T(4,128)(2,1)S(1)}, bf16[1024,4,128]{2,1,0:T(4,128)(2,1)S(1)}, u32[]{:S(2)}, u32[]{:S(2)}) %collective-permute-start.7) | collective-permute-done | bytes 1048608 | tf_op jit(solution)/shard_map/ppermute | solution.py:537
  342.0 2.4 pad_maximum_fusion.1
  344.6 46.6 %shard_map.129 = (f32[1024,512]{1,0:T(8,128)}, f32[1024,512]{1,0:T(8,128)}) custom-call(s32[200]{0:T(256)} %copy-done.29, s32[200]{0:T(256)} %and_convert_fusion.tf, s32[200]{0:T(256)} %get-tuple-element.137.tr, s32[200]{0:T(256)} %get-tuple-element.136.tn, s32[1]{0:T(128)} %bitcast.17.nt, s32[18432]{0:T(1024)} %get-tuple-element.127.idx, ...), custom_call_target="tpu_custom_call" | custom-call | flops 19327352832 | bytes 37748736 | tf_op jit(solution)/shard_map/pallas_call | solution.py:222
  391.2 4.6 reshape.525
  395.8 1.3 fusion.48
  400.5 3.2 reshape.521.table
  403.7 27.6 %merge_tables.1 = (s32[2,32,32,128]{3,2,1,0:T(8,128)}, f32[2,32,32,128]{3,2,1,0:T(8,128)}) custom-call(s32[2048]{0:T(1024)} %get-tuple-element.118.st, s32[64]{0:T(128)} %reshape.520.exps, f32[2,2,1216,128]{3,2,1,0:T(8,128)} %reshape.521.table), custom_call_target="tpu_custom_call" | custom-call | flops 1000000000 | bytes 2490368 | tf_op jit(solution)/shard_map/merge_tables/pallas_call | solution.py:278
  431.4 108.3 %weight_grads.2 = (bf16[2,64,192,512]{3,2,1,0:T(8,128)(2,1)}, bf16[2,64,192,512]{3,2,1,0:T(8,128)(2,1)}, bf16[2,64,192,512]{3,2,1,0:T(8,128)(2,1)}, bf16[32,192,...) custom-call(s32[32]{0:T(128)} %copy-done.31, s32[66]{0:T(128)} %reshape.523.tiles, ...), custom_call_target="tpu_custom_call" | custom-call | flops 154618822656 | bytes 90177536 | tf_op jit(solution)/shard_map/weight_grads/pallas_call | solution.py:419
  539.6 2.7 collective-permute-start.9
  542.9 58.7 %shard_map.130 = (f32[1024,512]{1,0:T(8,128)}, f32[1024,512]{1,0:T(8,128)}) custom-call(s32[200]{0:T(256)} %copy-done.28, s32[200]{0:T(256)} %and_convert_fusion.1.tf, s32[200]{0:T(256)} %get-tuple-element.139.tr, s32[200]{0:T(256)} %get-tuple-element.138.tn, s32[1]{0:T(128)} %bitcast.9.nt, s32[18432]{0:T(1024)} %get-tuple-element.123.idx, ...), custom_call_target="tpu_custom_call" | custom-call | flops 38654705664 | bytes 37748736 | tf_op jit(solution)/shard_map/pallas_call | solution.py:222
  603.0 23.7 %merge_half.2 = (bf16[2,64,192,512]{3,2,1,0:T(8,128)(2,1)}, bf16[2,64,192,512]{3,2,1,0:T(8,128)(2,1)}, bf16[2,64,192,512]{3,2,1,0:T(8,128)(2,1)}) custom-call(s32[32]{0:T(128)} %get-tuple-element.112.exps, bf16[32,192,512]{2,1,0:T(8,128)(2,1)} %collective-permute-done.9.a, ...), custom_call_target="tpu_custom_call", output_to_operand_aliasing={{0}: (4, {}), {1}: (5, {}), {2}: (6, {})} | custom-call | bytes 37748736 | tf_op jit(solution)/shard_map/merge_half/pallas_call | solution.py:452
  626.8 120.4 %weight_grads.3 = (bf16[2,64,192,512]{3,2,1,0:T(8,128)(2,1)}, bf16[2,64,192,512]{3,2,1,0:T(8,128)(2,1)}, bf16[2,64,192,512]{3,2,1,0:T(8,128)(2,1)}, bf16[32,192,...) custom-call(s32[32]{0:T(128)} %copy-done.30, ...), custom_call_target="tpu_custom_call", output_to_operand_aliasing={{0}: (10, {}), {1}: (11, {}), {2}: (12, {})} | custom-call | flops 154618822656 | bytes 90177536 | tf_op jit(solution)/shard_map/weight_grads/pallas_call | solution.py:419
  747.8 2.0 collective-permute-start.5
  749.9 2.0 fusion.1
  751.9 44.7 %collective-permute-done.8 = f32[1024,512]{1,0:T(8,128)S(1)} collective-permute-done((f32[1024,512]{1,0:T(8,128)}, f32[1024,512]{1,0:T(8,128)S(1)}, u32[]{:S(2)}, u32[]{:S(2)}) %collective-permute-start.8) | collective-permute-done | bytes 2097184 | tf_op jit(solution)/shard_map/ppermute | solution.py:537
  798.8 1.1 pad_maximum_fusion.4
  799.9 46.2 %collective-permute-done.5 = f32[1024,512]{1,0:T(8,128)} collective-permute-done((f32[1024,512]{1,0:T(8,128)}, f32[1024,512]{1,0:T(8,128)}, u32[]{:S(2)}, u32[]{:S(2)}) %collective-permute-start.5) | collective-permute-done | bytes 2097184 | tf_op jit(solution)/shard_map/ppermute | solution.py:537
  846.1 3.4 add_convert_fusion.4
  849.4 1.7 add_convert_fusion
  851.1 17.5 %all-reduce.12.cloned.1.call-done = bf16[2,512,512]{1,2,0:T(8,128)(2,1)} async-done(((bf16[2,512,512]{1,2,0:T(8,128)(2,1)}), bf16[2,512,512]{1,2,0:T(8,128)(2,1)}) %all-reduce.12.cloned.1.call-update) | async-done | bytes 1048592 | tf_op jit(solution)/shard_map/psum | solution.py:613
  868.7 2.3 copy.58
  871.0 23.7 %merge_half.3 = (bf16[2,64,192,512]{3,2,1,0:T(8,128)(2,1)}, bf16[2,64,192,512]{3,2,1,0:T(8,128)(2,1)}, bf16[2,64,192,512]{3,2,1,0:T(8,128)(2,1)}) custom-call(s32[32]{0:T(128)} %get-tuple-element.113.exps, bf16[32,192,512]{2,1,0:T(8,128)(2,1)} %collective-permute-done.12.a, ...), custom_call_target="tpu_custom_call", output_to_operand_aliasing={{0}: (4, {}), {1}: (5, {}), {2}: (6, {})} | custom-call | bytes 37748736 | tf_op jit(solution)/shard_map/merge_half/pallas_call | solution.py:452
  (192 shorter events, 27.1 us)
Async XLA Ops:
  8.0 383.2 %all-gather.15.cloned.1.call-start = ((), (), s32[]{:S(2)}) async-start(), calls=%async_computation.5 | async-start | bytes 2801664 | tf_op jit(solution)/shard_map/all_gather | solution.py:583
  9.8 7.1 collective-permute-start
  16.8 25.6 %copy-start.1 = (bf16[1024,4,128]{2,1,0:T(4,128)(2,1)}, bf16[1024,4,128]{2,1,0:T(4,128)(2,1)S(1)}, u32[]{:S(2)}) copy-start(bf16[1024,4,128]{2,1,0:T(4,128)(2,1)S(1)} %reshape.512.u_own) | copy-start | bytes 3145732
  16.8 24.6 %collective-permute-start.1 = (bf16[1024,4,128]{2,1,0:T(4,128)(2,1)S(1)}, bf16[1024,4,128]{2,1,0:T(4,128)(2,1)S(1)}, u32[]{:S(2)}, u32[]{:S(2)}) collective-permute-start(bf16[1024,4,128]{2,1,0:T(4,128)(2,1)S(1)} %reshape.512.u_own), channel_id=1, source_target_pairs={{0,8},{8,0},{1,9},{9,1},{2,10},{10,2},{3,11},{11,3},{4,12},{12,4},... | collective-permute-start | bytes 3145736 | tf_op jit(solution)/shard_map/ppermute | solution.py:537
  18.4 24.0 %copy-start.28 = (s32[200]{0:T(256)}, s32[200]{0:T(256)S(1)}, u32[]{:S(2)}) copy-start(s32[200]{0:T(256)S(1)} %broadcast_minimum_fusion.1.te) | copy-start | bytes 2404
  91.3 12.4 %copy-start.7 = (bf16[1024,512]{1,0:T(8,128)(2,1)S(1)}, bf16[1024,512]{1,0:T(8,128)(2,1)}, u32[]{:S(2)}) copy-start(bf16[1024,512]{1,0:T(8,128)(2,1)} %param.9) | copy-start | bytes 3145732
  102.1 48.1 %copy-start.14 = (bf16[1024,512]{1,0:T(8,128)(2,1)S(1)}, bf16[1024,512]{1,0:T(8,128)(2,1)}, u32[]{:S(2)}) copy-start(bf16[1024,512]{1,0:T(8,128)(2,1)} %copy-done.13) | copy-start | bytes 3145732
  103.5 327.9 %all-gather.11.cloned.1.call-start = ((), (), s32[]{:S(2)}) async-start(), calls=%async_computation.3 | async-start | bytes 18874368 | tf_op jit(solution)/shard_map/all_gather | solution.py:540
  103.7 46.6 %collective-permute-start.2 = (f32[1024,512]{1,0:T(8,128)}, f32[1024,512]{1,0:T(8,128)}, u32[]{:S(2)}, u32[]{:S(2)}) collective-permute-start(f32[1024,512]{1,0:T(8,128)} %get-tuple-element.45), channel_id=1, source_target_pairs={{0,8},{8,0},{1,9},{9,1},{2,10},{10,2},{3,11},{11,3},{4,12},{12,4},... | collective-permute-start | bytes 6291464 | tf_op jit(solution)/shard_map/ppermute | solution.py:537
  104.1 53.6 %copy-start.16 = (bf16[1024,4,128]{2,1,0:T(4,128)(2,1)}, bf16[1024,4,128]{2,1,0:T(4,128)(2,1)S(1)}, u32[]{:S(2)}) copy-start(bf16[1024,4,128]{2,1,0:T(4,128)(2,1)S(1)} %reshape.516.d_own) | copy-start | bytes 3145732
  150.3 3.9 copy-start.33
  154.9 2.7 copy-start.9
  155.2 2.8 copy-start.3
  157.6 273.7 %all-gather.13.cloned.1.call-start = ((), (), s32[]{:S(2)}) async-start(), calls=%async_computation.4 | async-start | bytes 18874368 | tf_op jit(solution)/shard_map/all_gather | solution.py:540
  157.7 26.1 %collective-permute-start.4 = (bf16[1024,4,128]{2,1,0:T(4,128)(2,1)S(1)}, bf16[1024,4,128]{2,1,0:T(4,128)(2,1)S(1)}, u32[]{:S(2)}, u32[]{:S(2)}) collective-permute-start(bf16[1024,4,128]{2,1,0:T(4,128)(2,1)S(1)} %reshape.516.d_own), channel_id=1, source_target_pairs={{0,8},{8,0},{1,9},{9,1},{2,10},{10,2},{3,11},{11,3},{4,12},{12,4},... | collective-permute-start | bytes 3145736 | tf_op jit(solution)/shard_map/ppermute | solution.py:537
  158.0 45.0 %collective-permute-start.3 = (bf16[1024,4,128]{2,1,0:T(4,128)(2,1)S(1)}, bf16[1024,4,128]{2,1,0:T(4,128)(2,1)S(1)}, u32[]{:S(2)}, u32[]{:S(2)}) collective-permute-start(bf16[1024,4,128]{2,1,0:T(4,128)(2,1)S(1)} %reshape.515.u_own), channel_id=1, source_target_pairs={{0,8},{8,0},{1,9},{9,1},{2,10},{10,2},{3,11},{11,3},{4,12},{12,4},... | collective-permute-start | bytes 3145736 | tf_op jit(solution)/shard_map/ppermute | solution.py:537
  183.8 19.3 %copy-start.23 = (bf16[1024,4,128]{2,1,0:T(4,128)(2,1)}, bf16[1024,4,128]{2,1,0:T(4,128)(2,1)S(1)}, u32[]{:S(2)}) copy-start(bf16[1024,4,128]{2,1,0:T(4,128)(2,1)S(1)} %collective-permute-done.4.d_oth) | copy-start | bytes 3145732
  206.5 420.3 %all-gather.7.cloned.1.call-start = ((), (), s32[]{:S(2)}) async-start(), calls=%async_computation.1 | async-start | bytes 18874368 | tf_op jit(solution)/shard_map/all_gather | solution.py:540
  207.6 2.6 copy-start.29
  210.2 101.9 %copy-start.8 = (bf16[1024,512]{1,0:T(8,128)(2,1)S(1)}, bf16[1024,512]{1,0:T(8,128)(2,1)}, u32[]{:S(2)}) copy-start(bf16[1024,512]{1,0:T(8,128)(2,1)} %param.9) | copy-start | bytes 3145732
  266.1 46.0 %collective-permute-start.6 = (f32[1024,512]{1,0:T(8,128)}, f32[1024,512]{1,0:T(8,128)S(1)}, u32[]{:S(2)}, u32[]{:S(2)}) collective-permute-start(f32[1024,512]{1,0:T(8,128)} %get-tuple-element.49), channel_id=1, source_target_pairs={{0,8},{8,0},{1,9},{9,1},{2,10},{10,2},{3,11},{11,3},{4,12},{12,4},... | collective-permute-start | bytes 6291464 | tf_op jit(solution)/shard_map/ppermute | solution.py:537
  312.1 3.3 copy-start.34
  316.2 2.9 copy-start.11
  316.6 2.5 copy-start.15
  319.0 23.0 %copy-start.5 = (bf16[1024,4,128]{2,1,0:T(4,128)(2,1)S(1)}, bf16[1024,4,128]{2,1,0:T(4,128)(2,1)}, u32[]{:S(2)}) copy-start(bf16[1024,4,128]{2,1,0:T(4,128)(2,1)} %copy-done.4) | copy-start | bytes 3145732
  319.1 307.7 %all-gather.9.cloned.1.call-start = ((), (), s32[]{:S(2)}) async-start(), calls=%async_computation.2 | async-start | bytes 18874368 | tf_op jit(solution)/shard_map/all_gather | solution.py:540
  319.1 21.9 %collective-permute-start.7 = (bf16[1024,4,128]{2,1,0:T(4,128)(2,1)S(1)}, bf16[1024,4,128]{2,1,0:T(4,128)(2,1)S(1)}, u32[]{:S(2)}, u32[]{:S(2)}) collective-permute-start(bf16[1024,4,128]{2,1,0:T(4,128)(2,1)S(1)} %reshape.517.d_own), channel_id=1, source_target_pairs={{0,8},{8,0},{1,9},{9,1},{2,10},{10,2},{3,11},{11,3},{4,12},{12,4},... | collective-permute-start | bytes 3145736 | tf_op jit(solution)/shard_map/ppermute | solution.py:537
  344.5 524.2 %all-reduce.12.cloned.1.call-start = ((), (), s32[]{:S(2)}) async-start(), calls=%async_computation | async-start | bytes 2097152 | tf_op jit(solution)/shard_map/psum | solution.py:613
  391.2 9.3 %copy-start = (f32[2,2,155648]{2,1,0:T(2,128)S(1)}, f32[2,2,155648]{2,1,0:T(2,128)}, u32[]{:S(2)}) copy-start(f32[2,2,155648]{2,1,0:T(2,128)} %all-gather.15.cloned.1.call-done) | copy-start | bytes 7471108
  398.5 5.3 copy-start.30
  398.5 5.3 copy-start.31
  398.5 5.2 copy-start.26
  539.6 63.4 %collective-permute-start.9 = (bf16[32,192,512]{2,1,0:T(8,128)(2,1)}, bf16[32,192,512]{2,1,0:T(8,128)(2,1)}, u32[]{:S(2)}, u32[]{:S(2)}) collective-permute-start(bf16[32,192,512]{2,1,0:T(8,128)(2,1)} %get-tuple-element.60), channel_id=1, source_target_pairs={{0,1},{1,0},{2,3},{3,2},{4,5},{5,4},{6,7},{7,6},{8,9},{9,8},{10,11... | collective-permute-start | bytes 18874376 | tf_op jit(solution)/shard_map/ppermute | solution.py:606
  542.4 60.7 %collective-permute-start.10 = (bf16[32,192,512]{2,1,0:T(8,128)(2,1)}, bf16[32,192,512]{2,1,0:T(8,128)(2,1)}, u32[]{:S(2)}, u32[]{:S(2)}) collective-permute-start(bf16[32,192,512]{2,1,0:T(8,128)(2,1)} %get-tuple-element.61), channel_id=1, source_target_pairs={{0,1},{1,0},{2,3},{3,2},{4,5},{5,4},{6,7},{7,6},{8,9},{9,8},{10,11... | collective-permute-start | bytes 18874376 | tf_op jit(solution)/shard_map/ppermute | solution.py:606
  542.4 59.2 %copy-start.27 = (s32[2,32]{1,0:T(2,128)S(1)}, s32[2,32]{1,0:T(2,128)}, u32[]{:S(2)}) copy-start(s32[2,32]{1,0:T(2,128)} %copy-done.26) | copy-start | bytes 772
  542.4 60.6 %collective-permute-start.11 = (bf16[32,192,512]{2,1,0:T(8,128)(2,1)}, bf16[32,192,512]{2,1,0:T(8,128)(2,1)}, u32[]{:S(2)}, u32[]{:S(2)}) collective-permute-start(bf16[32,192,512]{2,1,0:T(8,128)(2,1)} %get-tuple-element.62), channel_id=1, source_target_pairs={{0,1},{1,0},{2,3},{3,2},{4,5},{5,4},{6,7},{7,6},{8,9},{9,8},{10,11... | collective-permute-start | bytes 18874376 | tf_op jit(solution)/shard_map/ppermute | solution.py:606
  626.8 123.1 %copy-start.20 = (bf16[1024,512]{1,0:T(8,128)(2,1)S(1)}, bf16[1024,512]{1,0:T(8,128)(2,1)}, u32[]{:S(2)}) copy-start(bf16[1024,512]{1,0:T(8,128)(2,1)} %copy-done.19) | copy-start | bytes 3145732
  747.2 123.8 %collective-permute-start.12 = (bf16[32,192,512]{2,1,0:T(8,128)(2,1)}, bf16[32,192,512]{2,1,0:T(8,128)(2,1)}, u32[]{:S(2)}, u32[]{:S(2)}) collective-permute-start(bf16[32,192,512]{2,1,0:T(8,128)(2,1)} %get-tuple-element.69), channel_id=1, source_target_pairs={{0,1},{1,0},{2,3},{3,2},{4,5},{5,4},{6,7},{7,6},{8,9},{9,8},{10,11... | collective-permute-start | bytes 18874376 | tf_op jit(solution)/shard_map/ppermute | solution.py:606
  747.3 123.6 %collective-permute-start.13 = (bf16[32,192,512]{2,1,0:T(8,128)(2,1)}, bf16[32,192,512]{2,1,0:T(8,128)(2,1)}, u32[]{:S(2)}, u32[]{:S(2)}) collective-permute-start(bf16[32,192,512]{2,1,0:T(8,128)(2,1)} %get-tuple-element.70), channel_id=1, source_target_pairs={{0,1},{1,0},{2,3},{3,2},{4,5},{5,4},{6,7},{7,6},{8,9},{9,8},{10,11... | collective-permute-start | bytes 18874376 | tf_op jit(solution)/shard_map/ppermute | solution.py:606
  747.7 48.8 %copy-start.12 = (bf16[1024,512]{1,0:T(8,128)(2,1)S(1)}, bf16[1024,512]{1,0:T(8,128)(2,1)}, u32[]{:S(2)}) copy-start(bf16[1024,512]{1,0:T(8,128)(2,1)} %copy-done.11) | copy-start | bytes 3145732
  747.7 48.8 %copy-start.18 = (f32[1024,512]{1,0:T(8,128)S(1)}, f32[1024,512]{1,0:T(8,128)}, u32[]{:S(2)}) copy-start(f32[1024,512]{1,0:T(8,128)} %get-tuple-element.54) | copy-start | bytes 6291460
  747.7 123.2 %collective-permute-start.14 = (bf16[32,192,512]{2,1,0:T(8,128)(2,1)}, bf16[32,192,512]{2,1,0:T(8,128)(2,1)}, u32[]{:S(2)}, u32[]{:S(2)}) collective-permute-start(bf16[32,192,512]{2,1,0:T(8,128)(2,1)} %get-tuple-element.71), channel_id=1, source_target_pairs={{0,1},{1,0},{2,3},{3,2},{4,5},{5,4},{6,7},{7,6},{8,9},{9,8},{10,11... | collective-permute-start | bytes 18874376 | tf_op jit(solution)/shard_map/ppermute | solution.py:606
  747.8 48.7 %collective-permute-start.8 = (f32[1024,512]{1,0:T(8,128)}, f32[1024,512]{1,0:T(8,128)S(1)}, u32[]{:S(2)}, u32[]{:S(2)}) collective-permute-start(f32[1024,512]{1,0:T(8,128)} %get-tuple-element.55), channel_id=1, source_target_pairs={{0,8},{8,0},{1,9},{9,1},{2,10},{10,2},{3,11},{11,3},{4,12},{12,4},... | collective-permute-start | bytes 6291464 | tf_op jit(solution)/shard_map/ppermute | solution.py:537
  747.8 98.2 %collective-permute-start.5 = (f32[1024,512]{1,0:T(8,128)}, f32[1024,512]{1,0:T(8,128)}, u32[]{:S(2)}, u32[]{:S(2)}) collective-permute-start(f32[1024,512]{1,0:T(8,128)} %get-tuple-element.52), channel_id=1, source_target_pairs={{0,8},{8,0},{1,9},{9,1},{2,10},{10,2},{3,11},{11,3},{4,12},{12,4},... | collective-permute-start | bytes 6291464 | tf_op jit(solution)/shard_map/ppermute | solution.py:537
  798.8 47.3 %copy-start.10 = (bf16[1024,512]{1,0:T(8,128)(2,1)S(1)}, bf16[1024,512]{1,0:T(8,128)(2,1)}, u32[]{:S(2)}) copy-start(bf16[1024,512]{1,0:T(8,128)(2,1)} %copy-done.9) | copy-start | bytes 3145732
  798.8 47.3 %copy-start.17 = (f32[1024,512]{1,0:T(8,128)S(1)}, f32[1024,512]{1,0:T(8,128)}, u32[]{:S(2)}) copy-start(f32[1024,512]{1,0:T(8,128)} %get-tuple-element.51) | copy-start | bytes 6291460
  846.1 3.4 copy-start.25
  846.1 3.4 copy-start.35
  (9 other events, 9.3 us)
Sparse Core Ops, SparseCore 0:
  103.6 25.7 all-gather.14
  157.8 86.0 all-gather.10
  245.7 85.9 all-gather.12
  333.4 85.9 all-gather.6
  421.1 85.9 all-gather.8
Sparse Core Ops, SparseCore 1:
  799.9 68.7 all-reduce.11

commit v5 on v4

--- a/solution.py
+++ b/solution.py
@@ -12,6 +12,7 @@
 LANES = 128
 TILE = 128
 WTILE = 256
+PITCH = 9
 BATCH = 16
 SLOTS = 6
 PAGE = 1024
@@ -47,6 +48,11 @@
 def load_rows(ref, start, rows, parts):
     cols = [ref[pl.ds(start * parts + k, rows, stride=parts), :] for k in range(parts)]
     return jnp.concatenate(cols, axis=1).astype(jnp.bfloat16)
+
+
+def fetch_rows(sources, halves, dst, sem):
+    n = sources[0].shape[0]
+    return [pltpu.make_async_copy(sources[k], dst.at[pl.ds(k * n, n)], sem.at[k]) for k in halves]
 
 
 def fetch_pair(own, other, dst, sem):
@@ -75,7 +81,7 @@
     return spread_column(jnp.where(lane < LANES - skip, pair[:1], pair[1:]))
 
 
-def widen(src, dst, parts):
+def widen(src, dst, parts, halves, tok):
     step = 8
 
     def one(q, carry):
@@ -83,18 +89,18 @@
             dst[pl.ds((q * step + r) * parts, parts), :] = src[q * step + r].astype(jnp.float32)
         return carry
 
-    lax.fori_loop(0, src.shape[0] // step, one, 0)
-
-
-def write_sums(acc, own_ref, other_ref, tok, parts):
+    lax.fori_loop(halves[0] * tok // step, (halves[-1] + 1) * tok // step, one, 0)
+
+
+def write_sums(acc, outs, tok, parts, halves):
     step = min(32, tok)
 
     def copy_out(q, carry):
         r0 = pl.multiple_of(q * step, step)
         for k in range(parts):
             cols = slice(k * LANES, (k + 1) * LANES)
-            own_ref[pl.ds(r0, step), cols] = acc[pl.ds(r0 * parts + k, step, stride=parts), :]
-            other_ref[pl.ds(r0, step), cols] = acc[pl.ds((tok + r0) * parts + k, step, stride=parts), :]
+            for out, half in zip(outs, halves):
+                out[pl.ds(r0, step), cols] = acc[pl.ds((half * tok + r0) * parts + k, step, stride=parts), :]
         return carry
 
     lax.fori_loop(0, tok // step, copy_out, 0)
@@ -135,19 +141,19 @@
     lax.fori_loop(0, n_steps, one, 0)
 
 
-def forward_body(te, tf, tr, tn, nt, idx, gates, u_own, u_oth, g_ref, up_ref, w_ref, own_ref, other_ref,
-                 usc, uf, ut, ot, acc, ht, wbuf, sem, wsem, *, layer, tok, parts):
+def forward_body(te, tf, tr, tn, nt, idx, gates, u_own, u_oth, g_ref, up_ref, w_ref, *refs, layer, tok, parts, halves):
     ff = g_ref.shape[2]
+    outs, (usc, uf, ut, ot, acc, ht, wbuf, sem, wsem) = refs[:len(halves)], refs[len(halves):]
 
     def prepare():
-        copies = fetch_pair(u_own, u_oth, usc, sem)
+        copies = fetch_rows((u_own, u_oth), halves, usc, sem)
         for c in copies:
             c.start()
         for ref in (acc, ot, ut, ht):
             clear(ref)
         for c in copies:
             c.wait()
-        widen(usc, uf, parts)
+        widen(usc, uf, parts, halves, tok)
 
     def step(i, slot, slot_before):
         o = tn_dot(ht[...], wbuf[slot_before, 2 * ff:]).astype(jnp.bfloat16).astype(jnp.float32)
@@ -166,23 +172,24 @@
         ht[...] = (a * jax.nn.sigmoid(a) * b).astype(jnp.bfloat16)
 
     run_tiles(step, (g_ref, up_ref, w_ref), wbuf, wsem, te, tf, nt[0] + 3, layer, prepare)
-    write_sums(acc, own_ref, other_ref, tok, parts)
-
-
-def backward_body(te, tf, tr, tn, nt, idx, gates, u_own, u_oth, d_own, d_oth, g_ref, up_ref, w_ref, own_ref, other_ref,
-                  usc, dsc, uf, df, ut, dt, vt, acc, da_t, wbuf, sem, wsem, *, layer, tok, parts):
+    write_sums(acc, outs, tok, parts, halves)
+
+
+def backward_body(te, tf, tr, tn, nt, idx, gates, u_own, u_oth, d_own, d_oth, g_ref, up_ref, w_ref, *refs, layer, tok, parts,
+                  halves):
     ff = g_ref.shape[2]
+    outs, (usc, dsc, uf, df, ut, dt, vt, acc, da_t, wbuf, sem, wsem) = refs[:len(halves)], refs[len(halves):]
 
     def prepare():
-        copies = fetch_pair(u_own, u_oth, usc, sem.at[0]) + fetch_pair(d_own, d_oth, dsc, sem.at[1])
+        copies = fetch_rows((u_own, u_oth), halves, usc, sem.at[0]) + fetch_rows((d_own, d_oth), halves, dsc, sem.at[1])
         for c in copies:
             c.start()
         for ref in (acc, vt, ut, dt, da_t):
             clear(ref)
         for c in copies:
             c.wait()
-        widen(usc, uf, parts)
-        widen(dsc, df, parts)
+        widen(usc, uf, parts, halves, tok)
+        widen(dsc, df, parts, halves, tok)
 
     def step(i, slot, slot_before):
         v = tn_dot(da_t[...], wbuf[slot_before, :2 * ff]).astype(jnp.bfloat16).astype(jnp.float32)
@@ -208,10 +215,10 @@
         da_t[ff:] = (dh * (a * s)).astype(jnp.bfloat16)
 
     run_tiles(step, (g_ref, up_ref, w_ref), wbuf, wsem, te, tf, nt[0] + 3, layer, prepare)
-    write_sums(acc, own_ref, other_ref, tok, parts)
-
-
-def token_kernel(body, layer, tables, slabs, weights):
+    write_sums(acc, outs, tok, parts, halves)
+
+
+def token_kernel(body, layer, tables, slabs, weights, halves=(0, 1)):
     tok, parts, _ = slabs[0].shape
     _, n_local, ff, d_model = weights[0].shape
     n_pairs = len(slabs) // 2
@@ -220,12 +227,12 @@
     sem_shape = (2,) if n_pairs == 1 else (2, 2)
     copies = 8 * tok
     return pl.pallas_call(
-        functools.partial(body, layer=layer, tok=tok, parts=parts),
+        functools.partial(body, layer=layer, tok=tok, parts=parts, halves=halves),
         grid_spec=pltpu.PrefetchScalarGridSpec(
             num_scalar_prefetch=len(tables) - 1,
             grid=(1,),
             in_specs=[pl.BlockSpec(tables[-1].shape, lambda i, *_: (0, 0))] + [any_spec] * (len(slabs) + 3),
-            out_specs=[rows_spec] * 2,
+            out_specs=[rows_spec] * len(halves),
             scratch_shapes=[pltpu.VMEM((2 * tok, parts, LANES), jnp.bfloat16)] * n_pairs
             + [pltpu.VMEM((2 * tok * parts, LANES), jnp.float32)] * n_pairs
             + [pltpu.VMEM((TILE * parts, LANES), jnp.float32)] * (n_pairs + 1)
@@ -233,23 +240,33 @@
                pltpu.VMEM((SLOTS, 3 * ff, d_model), jnp.bfloat16),
                pltpu.SemaphoreType.DMA(sem_shape), pltpu.SemaphoreType.DMA((SLOTS,))],
         ),
-        out_shape=[jax.ShapeDtypeStruct((tok, d_model), jnp.float32)] * 2,
+        out_shape=[jax.ShapeDtypeStruct((tok, d_model), jnp.float32)] * len(halves),
         compiler_params=pltpu.CompilerParams(dimension_semantics=("arbitrary",), vmem_limit_bytes=VMEM_LIMIT),
         cost_estimate=pl.CostEstimate(flops=(3 + 3 * (n_pairs - 1)) * 2 * copies * d_model * ff * 4,
                                       bytes_accessed=3 * n_local * ff * d_model * 2, transcendentals=0),
     )(*tables, *slabs, *weights)
 
 
-def merge_tables_body(st, exps, table, idx_ref, gate_ref, buf, *, src, n_exp, src_rows, out_rows, pad_row):
-    layer, e = pl.program_id(0), pl.program_id(1)
-    exp = exps[layer * n_exp + e]
+def merge_tables_body(st, exps, table, idx_ref, gate_ref, buf, *, src, n_exp, n_layers, out_rows, pad_row):
+    group = idx_ref.shape[1]
+    layer = pl.program_id(0)
+
+    def one(q, carry):
+        merge_expert(exps[layer * n_exp + pl.program_id(1) * group + q], layer, st, table, idx_ref.at[0, q], gate_ref.at[0, q],
+                     buf, src, n_layers, out_rows, pad_row)
+        return carry
+
+    lax.fori_loop(0, group, one, 0)
+
+
+def merge_expert(exp, layer, st, table, idx_out, gate_out, buf, src, n_layers, out_rows, pad_row):
     buf[0] = jnp.full(buf.shape[1:], float(pad_row), jnp.float32)
     buf[1] = jnp.zeros(buf.shape[1:], jnp.float32)
     row = lax.broadcasted_iota(jnp.int32, (8, LANES), 0)
     lane = lax.broadcasted_iota(jnp.int32, (8, LANES), 1)
     off = 0
     for d in range(src):
-        at = (layer * src + d) * LANES + exp
+        at = (d * n_layers + layer) * LANES + exp
         first = st[at]
         count = st[at + 1] - first
         to = lax.rem(off, LANES) + LANES
@@ -259,29 +276,28 @@
         place = row * LANES + lane
         take = (place >= to) & (place < to + count)
         for kind in range(2):
-            x = table[0, kind, pl.ds(d * src_rows + lax.div(first, LANES), 8), :]
+            x = table[d, 0, kind, pl.ds(lax.div(first, LANES), 8), :]
             x = pltpu.roll(pltpu.roll(x, over, 1), lax.div(shift, LANES), 0)
             x = jnp.where(lane >= over, x, pltpu.roll(x, 1, 0))
             old = buf[kind, pl.ds(start, 8), :]
             buf[kind, pl.ds(start, 8), :] = jnp.where(take, x, old)
         off = off + count
-    idx_ref[0, 0] = buf[0, pl.ds(1, out_rows), :].astype(jnp.int32)
-    gate_ref[0, 0] = buf[1, pl.ds(1, out_rows), :]
+    idx_out[...] = buf[0, pl.ds(1, out_rows), :].astype(jnp.int32)
+    gate_out[...] = buf[1, pl.ds(1, out_rows), :]
 
 
 def merge_tables(shared, starts, exps, out_rows, pad_row):
-    n_layers, _, src, rows = shared.shape
+    src, n_layers, _, rows, _ = shared.shape
     n_exp = exps.shape[1]
-    exps = exps.reshape(-1)
-    src_rows = rows // LANES
-    out = pl.BlockSpec((1, 1, out_rows, LANES), lambda l, e, *_: (l, e, 0, 0))
+    group = 8 if n_exp % 8 == 0 else 1
+    out = pl.BlockSpec((1, group, out_rows, LANES), lambda l, e, *_: (l, e, 0, 0))
     return pl.pallas_call(
-        functools.partial(merge_tables_body, src=src, n_exp=n_exp, src_rows=src_rows, out_rows=out_rows,
+        functools.partial(merge_tables_body, src=src, n_exp=n_exp, n_layers=n_layers, out_rows=out_rows,
                           pad_row=pad_row),
         grid_spec=pltpu.PrefetchScalarGridSpec(
             num_scalar_prefetch=2,
-            grid=(n_layers, n_exp),
-            in_specs=[pl.BlockSpec((1, 2, src * src_rows, LANES), lambda l, e, *_: (l, 0, 0, 0))],
+            grid=(n_layers, n_exp // group),
+            in_specs=[pl.BlockSpec((src, 1, 2, rows, LANES), lambda l, e, *_: (0, l, 0, 0, 0))],
             out_specs=[out] * 2,
             scratch_shapes=[pltpu.VMEM((2, out_rows + 16, LANES), jnp.float32)],
         ),
@@ -290,13 +306,13 @@
         compiler_params=pltpu.CompilerParams(dimension_semantics=("arbitrary", "arbitrary")),
         cost_estimate=pl.CostEstimate(flops=10**9, bytes_accessed=4 * shared.size, transcendentals=0),
         name="merge_tables",
-    )(starts, exps, shared.reshape(n_layers, 2, src * src_rows, LANES))
+    )(starts.reshape(-1), exps.reshape(-1), shared)
 
 
 def weight_grad_body(exps, tiles, begins, ud_own, ud_oth, idx_all, gate_ref, *refs, parts, n_exp, n_alias, layer, page):
     g_ref, up_ref, w_ref = refs[:3]
     (dg_ref, du_ref, dw_ref, og_ref, ou_ref, ow_ref,
-     uds, ut, dt, u0, c0, d0, h0, u1, c1, d1, h1, gacc, wacc, idx_s, sem, tsem) = refs[3 + n_alias:]
+     uds, rows, u0, c0, d0, h0, u1, c1, d1, h1, gacc, wacc, idx_s, sem, tsem) = refs[3 + n_alias:]
     e = pl.program_id(0)
     ff = g_ref.shape[2]
     slots = 3
@@ -309,9 +325,10 @@
         return pltpu.make_async_copy(idx_all.at[pl.ds(at, page)], idx_s.at[pl.ds(to, page)], tsem.at[slot])
 
     def gather_row(at, r):
-        x = uds[idx_s[at]].astype(jnp.float32)
-        ut[pl.ds(r * parts, parts), :] = x[:parts]
-        dt[pl.ds(r * parts, parts), :] = x[parts:]
+        rows[pl.ds(r * PITCH, 2 * parts), :] = uds[idx_s[at]].astype(jnp.float32)
+
+    def column(first, count, k):
+        return rows[pl.ds(first * PITCH + k, count, stride=PITCH), :]
 
     @pl.when(e == 0)
     def _():
@@ -354,11 +371,11 @@
         uo, co, do, ho = old
         gacc[...] += nn_dot(do[...], uo[...])
         wacc[...] += nn_dot(ho[...], co[...])
-        un[...] = load_rows(ut, 0, WTILE, parts)
+        un[...] = jnp.concatenate([column(0, WTILE, k) for k in range(parts)], axis=1).astype(jnp.bfloat16)
         gates = [spread_column(gate_ref[0, 0, pl.ds(j * gate_rows + q, 1), :]) for q in range(gate_rows)]
         for k in range(parts):
             for q in range(gate_rows):
-                d = dt[pl.ds(q * LANES * parts + k, LANES, stride=parts), :]
+                d = column(q * LANES, LANES, parts + k)
                 cn[q * LANES:(q + 1) * LANES, k * LANES:(k + 1) * LANES] = (d * gates[q]).astype(jnp.bfloat16)
         ab = nt_dot(jnp.concatenate([g_ref[0, 0], up_ref[0, 0]], axis=0), un[...])
         dh = nt_dot(w_ref[0, 0], cn[...])
@@ -424,7 +441,7 @@
             in_specs=[any_spec] * 3 + [gate_spec] + [mine] * 3 + [any_spec] * len(aliased),
             out_specs=[done] * 3 + [half] * 3,
             scratch_shapes=[pltpu.VMEM((n_tok + 8, parts2, LANES), jnp.bfloat16)]
-            + [pltpu.VMEM((WTILE * parts, LANES), jnp.float32)] * 2 + tile_set * 2
+            + [pltpu.VMEM((WTILE * PITCH + 16, LANES), jnp.float32)] + tile_set * 2
             + [pltpu.VMEM((2 * ff, d_model), jnp.float32), pltpu.VMEM((ff, d_model), jnp.float32),
                pltpu.SMEM((3 * page,), jnp.int32), pltpu.SemaphoreType.DMA((2,)), pltpu.SemaphoreType.DMA((3,))],
         ),
@@ -439,29 +456,50 @@
     return outs[:3], outs[3:]
 
 
-def merge_body(exps, a, b, c, f0, f1, f2, o0, o1, o2):
-    o0[0, 0], o1[0, 0], o2[0, 0] = a[0], b[0], c[0]
+def merge_body(exps, a, b, c, f0, f1, f2, o0, o1, o2, buf, in_sem, out_sem, *, layer, n_exp):
+    halves, wholes = (a, b, c), (o0, o1, o2)
+
+    def arrive(k, q):
+        return pltpu.make_async_copy(halves[k].at[q], buf.at[k, q], in_sem.at[k, q])
+
+    def leave(k, q):
+        return pltpu.make_async_copy(buf.at[k, q], wholes[k].at[layer, exps[q]], out_sem)
+
+    def each(act):
+        def one(q, carry):
+            for k in range(3):
+                act(k, q)
+            return carry
+
+        lax.fori_loop(0, n_exp, one, 0)
+
+    def pass_on(k, q):
+        arrive(k, q).wait()
+        leave(k, q).start()
+
+    each(lambda k, q: arrive(k, q).start())
+    each(pass_on)
+    each(lambda k, q: leave(k, q).wait())
 
 
 def merge_half(layer, exps, half, full):
-    _, n_local, ff, d_model = full[0].shape
-    n_exp = n_local // 2
+    n_exp, ff, d_model = half[0].shape
     any_spec = pl.BlockSpec(memory_space=pl.ANY)
-    part = pl.BlockSpec((1, ff, d_model), lambda e, exps: (e, 0, 0))
-    place = pl.BlockSpec((1, 1, ff, d_model), lambda e, exps: (layer, exps[e], 0, 0))
     return pl.pallas_call(
-        merge_body,
+        functools.partial(merge_body, layer=layer, n_exp=n_exp),
         grid_spec=pltpu.PrefetchScalarGridSpec(
-            num_scalar_prefetch=1, grid=(n_exp,), in_specs=[part] * 3 + [any_spec] * 3, out_specs=[place] * 3),
+            num_scalar_prefetch=1, grid=(1,), in_specs=[any_spec] * 6, out_specs=[any_spec] * 3,
+            scratch_shapes=[pltpu.VMEM((3, n_exp, ff, d_model), jnp.bfloat16), pltpu.SemaphoreType.DMA((3, n_exp)),
+                            pltpu.SemaphoreType.DMA]),
         out_shape=[jax.ShapeDtypeStruct(x.shape, x.dtype) for x in full],
         input_output_aliases={4: 0, 5: 1, 6: 2},
-        compiler_params=pltpu.CompilerParams(dimension_semantics=("arbitrary",)),
-        cost_estimate=pl.CostEstimate(flops=0, bytes_accessed=6 * n_exp * ff * d_model * 2, transcendentals=0),
+        compiler_params=pltpu.CompilerParams(dimension_semantics=("arbitrary",), vmem_limit_bytes=VMEM_LIMIT),
+        cost_estimate=pl.CostEstimate(flops=10**9, bytes_accessed=6 * n_exp * ff * d_model * 2, transcendentals=0),
         name="merge_half",
     )(exps, *half, *full)
 
 
-def route_tables(ids, gates, ep, n_local):
+def route_tables(ids, gates, ep, n_local, split):
     n_src, top_k, tok = ids.shape
     n = n_src * top_k * tok
     local = ids - ep * n_local
@@ -470,12 +508,27 @@
     key, gate = lax.sort((group * n + jnp.arange(n, dtype=jnp.int32), gates.reshape(-1)), num_keys=1, is_stable=False)
     copy = key % n
     token = copy // (top_k * tok) * tok + copy % tok
-    counts = jnp.sum((group[:, None] == jnp.arange(n_local)[None, :]).astype(jnp.int32), axis=0)
+    hits = (group.reshape(n_src, -1)[:, :, None] == jnp.arange(n_local)[None, None, :]).astype(jnp.int32)
+    half_counts = jnp.sum(hits, axis=1)
+    counts = jnp.sum(half_counts, axis=0)
     ends = jnp.cumsum(counts)
     starts = ends - counts
+    pad = cdiv(2 * PAGE, TILE) * TILE
+    token = jnp.pad(token, (0, pad))
+    gate = jnp.pad(gate, (0, pad))
+    bounds = jnp.concatenate([jnp.zeros((1,), jnp.int32), ends, jnp.full((LANES - 1 - n_local,), ends[-1], jnp.int32)])
+    whole = tile_list(starts, counts, n)
+    lists = (whole,)
+    if split:
+        lists = (tile_list(starts, half_counts[0], n // 2), tile_list(starts + half_counts[0], half_counts[1], n // 2))
+    return lists, whole, token, gate, bounds
+
+
+def tile_list(starts, counts, most):
+    n_local = starts.shape[0]
     n_tiles = jnp.maximum((counts + TILE - 1) // TILE, 1)
     tile_end = jnp.cumsum(n_tiles)
-    tile_id = jnp.arange(n // TILE + n_local + 8, dtype=jnp.int32) - 3
+    tile_id = jnp.arange(most // TILE + n_local + 8, dtype=jnp.int32) - 3
     tile_e = jnp.minimum(jnp.sum((tile_end[None, :] <= tile_id[:, None]).astype(jnp.int32), axis=1), n_local - 1)
     pick = (tile_e[:, None] == jnp.arange(n_local)[None, :]).astype(jnp.int32)
     inside = (tile_id - jnp.sum(pick * (tile_end - n_tiles)[None, :], axis=1)) * TILE
@@ -483,11 +536,7 @@
     tile_row = jnp.where(real, jnp.sum(pick * starts[None, :], axis=1) + inside, 0)
     tile_first = (real & (inside == 0) & (tile_e > 0)).astype(jnp.int32)
     tile_n = jnp.where(real, jnp.clip(jnp.sum(pick * counts[None, :], axis=1) - inside, 0, TILE), 0)
-    pad = cdiv(2 * PAGE, TILE) * TILE
-    token = jnp.pad(token, (0, pad))
-    gate = jnp.pad(gate, (0, pad))
-    bounds = jnp.concatenate([jnp.zeros((1,), jnp.int32), ends, jnp.full((LANES - 1 - n_local,), ends[-1], jnp.int32)])
-    return (tile_e, tile_first, tile_row, tile_n, tile_end[-1:], token, gate), bounds
+    return tile_e, tile_first, tile_row, tile_n, tile_end[-1:]
 
 
 def split_experts(bounds, core):
@@ -550,22 +599,24 @@
         mine = jnp.stack([ids.astype(jnp.float32), gates])
         theirs = swap(mine)
         both = jnp.stack([mine, theirs], 2)
-        tables, packed = [], []
-
-        def add_tables(pair):
-            table, bounds = route_tables(pair[0].astype(jnp.int32), pair[1], ep_id, n_local)
-            token, gate = table[5], table[6]
-            tables.append((*table[:5], token * parts, gate.reshape(-1, LANES)))
+        top = n_layers - 1
+        tables, combined, packed = [], [], []
+
+        def add_tables(layer, pair):
+            lists, whole, token, gate, bounds = route_tables(pair[0].astype(jnp.int32), pair[1], ep_id, n_local, layer < top)
+            gate_rows = gate.reshape(-1, LANES)
+            at = token * parts
+            tables.append([(*tiles, at, gate_rows) for tiles in lists])
+            combined.append(tables[layer][-1] if layer == top else (*whole, at, gate_rows))
             spot = lax.div(token, tok) * (dp_size * tok) + dp_id * tok + lax.rem(token, tok)
-            packed.append(jnp.stack([jnp.concatenate([spot, jnp.pad(bounds, (0, PAGE - LANES))])
-                                     .astype(jnp.float32), jnp.pad(gate, (0, PAGE))]))
-
-        add_tables(both[:, 0])
+            first = jnp.concatenate([spot.reshape(-1, LANES), jnp.pad(bounds.reshape(1, LANES), ((0, 7), (0, 0)))])
+            packed.append(jnp.stack([first.astype(jnp.float32), jnp.pad(gate_rows, ((0, 8), (0, 0)))]))
+
+        add_tables(0, both[:, 0])
 
         d_slab = slab(d_out)
         d_other = swap(d_slab)
 
-        top = n_layers - 1
         x_in, u_slabs, u_others, xs = tokens, [], [], []
         for layer in range(n_layers):
             u = mixed(x_in, layer)
@@ -573,43 +624,45 @@
             u_others.append(swap(u_slabs[layer]))
             xs.append(x_in)
             if layer < top:
-                own, other = token_kernel(forward_body, layer, tables[layer],
-                                          (u_slabs[layer], u_others[layer]), weights)
+                slabs = (u_slabs[layer], u_others[layer])
+                other, = token_kernel(forward_body, layer, tables[layer][1], slabs, weights, (1,))
                 sent = swap(other)
-                add_tables(after(both[:, layer + 1], other))
+                own, = token_kernel(forward_body, layer, tables[layer][0],
+                                    (after(u_slabs[layer], other), u_others[layer]), weights, (0,))
+                add_tables(layer + 1, after(both[:, layer + 1], other))
                 x_in = (u.astype(jnp.float32) + own + sent).astype(jnp.bfloat16)
 
-        rows = packed[0].shape[1]
-        shared = lax.all_gather(jnp.stack(packed), 'dp', axis=2)
-        shared = shared.reshape(n_layers, 2, dp_size, rows)
-        starts = shared[:, 0, :, rows - PAGE:rows - PAGE + LANES].astype(jnp.int32)
-        split = [split_experts(starts[layer, :, :n_local + 1], dp_id % 2) for layer in range(n_layers)]
+        shared = lax.all_gather(jnp.stack(packed), 'dp', axis=0)
+        starts = shared[:, :, 0, -8].astype(jnp.int32)
+        split = [split_experts(starts[:, layer, :n_local + 1], dp_id % 2) for layer in range(n_layers)]
         mine_e, theirs_e, tiles = (jnp.stack(x) for x in zip(*split))
         list_rows = cdiv(cdiv(dp_size * 2 * cap, LANES), 8) * 8 + 8
-        idx_all, gate_all = merge_tables(shared, starts.reshape(-1), mine_e, list_rows, dp_size * 2 * tok)
+        idx_all, gate_all = merge_tables(shared, starts, mine_e, list_rows, dp_size * 2 * tok)
         idx_all = idx_all.reshape(-1)
 
-        d_y, full = d_out, None
+        d_y, full, halves = d_out, None, []
         d_mix = [None] * n_layers
         for layer in reversed(range(n_layers)):
             spreads = [spread(jnp.concatenate(x, axis=1)) for x in ((u_slabs[layer], d_slab), (u_others[layer], d_other))]
-            own, other = token_kernel(backward_body, layer, tables[layer],
-                                      (u_slabs[layer], u_others[layer], d_slab, d_other), weights)
+            slabs = (u_slabs[layer], u_others[layer], d_slab, d_other)
+            own, other = token_kernel(backward_body, layer, combined[layer], slabs, weights)
             d_u = (d_y.astype(jnp.float32) + own + swap(other)).astype(jnp.bfloat16)
             last = other
             if layer == top:
-                y_own, y_other = token_kernel(forward_body, top, tables[top],
+                y_own, y_other = token_kernel(forward_body, top, combined[top],
                                               (after(u_slabs[top], other), u_others[top]), weights)
                 layer_out = (u.astype(jnp.float32) + y_own + swap(y_other)).astype(jnp.bfloat16)
                 last = y_other
             full, half = weight_grads(layer, mine_e[layer], after(tiles, last), spreads, idx_all, gate_all, weights, full)
-            full = merge_half(layer, theirs_e[layer], [lax.ppermute(x, 'dp', core_pairs) for x in half], full)
+            halves.append((layer, [lax.ppermute(x, 'dp', core_pairs) for x in half]))
             d_mix[layer] = jnp.einsum('td,te->de', xs[layer], d_u, preferred_element_type=jnp.float32).astype(jnp.bfloat16)
             d_y = (d_u.astype(jnp.float32)
                    + jnp.einsum('te,de->td', d_u, w_mix[layer], preferred_element_type=jnp.float32)).astype(jnp.bfloat16)
             if layer:
                 d_slab = slab(d_y)
                 d_other = swap(d_slab)
+        for layer, half in halves:
+            full = merge_half(layer, theirs_e[layer], half, full)
         d_mix = lax.psum(jnp.stack(d_mix), ('dp', 'ep'))
         return (layer_out, d_y, d_mix, jnp.swapaxes(full[0], 2, 3), jnp.swapaxes(full[1], 2, 3), full[2])
 

time: 904 us -> 803 us (0.89)
  waiting for transfers between devices: 273 us -> 181 us
    ppermute x9, waiting for transfers between devices: 256 us -> 119 us  [swap(): return lax.ppermute(x, 'ep', ep_pairs)]
    psum x1, waiting for transfers between devices: 17.5 us -> 61.9 us  [device_body(): d_mix = lax.psum(jnp.stack(d_mix), ('dp', 'ep'))]
    pallas_call x6 -> x7, Pallas kernels: 258 us -> 276 us  [the longest x5 247 us: token_kernel(): pl.pallas_call(functools.partial(body, layer=layer, tok=tok, parts=parts,...]
    pallas_call x1, Pallas kernels: 27.6 us -> 13.2 us  [merge_tables(): pl.pallas_call(functools.partial(merge_tables_body, src=src, n_exp=n_exp,...]
    pallas_call x2, Pallas kernels: 229 us -> 217 us  [weight_grads(): pl.pallas_call(functools.partial(weight_grad_body, parts=parts, n_exp=n_e...]
  transfers between devices with their start and end apart: 21 -> 21, of which waited for: 9 -> 7; matrix products, arithmetic and copies ran while one was open for 7% -> 8% of each run, Pallas kernels for 36% -> 56%
where the time goes in v5:
time: 803 us; the launch traced here: 802 us
  Pallas kernels  506 us (63%)
  waiting for transfers between devices  181 us (23%)
  other arithmetic  56.1 us (7%)
  local copies, waits for them, and re-layouts  18.1 us (2%)
  between operations  16 us (2%)
  starting transfers between devices  15.5 us (2%)
  matrix products  8.44 us (1%)
    pallas_call x5, Pallas kernels, token_kernel(): pl.pallas_call(functools.partial(body, layer=layer, tok=tok, parts=parts,...  247 us
    pallas_call x2, Pallas kernels, weight_grads(): pl.pallas_call(functools.partial(weight_grad_body, parts=parts, n_exp=n_e...  217 us
    ppermute x9, waiting for transfers between devices, swap(): return lax.ppermute(x, 'ep', ep_pairs)  119 us
    psum x1, waiting for transfers between devices, device_body(): d_mix = lax.psum(jnp.stack(d_mix), ('dp', 'ep'))  61.9 us
    pallas_call x2, Pallas kernels, merge_half(): pl.pallas_call(functools.partial(merge_body, layer=layer, n_exp=n_exp), g...  29.2 us
  transfers between devices with their start and end apart: 21, of which 7 were waited for; matrix products, arithmetic and copies ran while one was open for 8% of the time, Pallas kernels for 56%

profile of v5, /device:TPU:0, one launch (start us, length us, event | category | flops | bytes accessed | tf_op | source)
XLA Modules:
  0.0 802.1 jit_solution(11925035766019750708)
XLA Ops:
  9.8 3.3 collective-permute-start
  13.1 2.4 add_convert_fusion.7
  17.0 1.1 convert_reduce_fusion
  20.4 6.4 sort.30
  28.4 1.2 and_convert_fusion.2.tf
  29.6 1.2 clamp_select_fusion.2
  30.8 10.6 %collective-permute-done.1.u_oth = bf16[1024,4,128]{2,1,0:T(4,128)(2,1)S(1)} collective-permute-done((bf16[1024,4,128]{2,1,0:T(4,128)(2,1)S(1)}, bf16[1024,4,128]{2,1,0:T(4,128)(2,1)S(1)}, u32[]{:S(2)}, u32[]{:S(2)}) %collective-permute-start.1) | collective-permute-done | bytes 1048608 | tf_op jit(solution)/shard_map/ppermute | solution.py:586
  42.4 42.6 %shard_map.127 = f32[1024,512]{1,0:T(8,128)} custom-call(s32[136]{0:T(256)} %copy-done.28, s32[136]{0:T(256)} %and_convert_fusion.2.tf, s32[136]{0:T(256)} %get-tuple-element.150.tr, s32[136]{0:T(256)} %get-tuple-element.149.tn, s32[1]{0:T(128)} %bitcast.20.nt, s32[18432]{0:T(1024)} %get-tuple-element.133.idx, f32[144,128]{1,0:T(8,128)} %copy-done.17, ...), custom_call_target="tpu_custom_call" | custom-call | flops 19327352832 | bytes 37748736 | tf_op jit(solution)/shard_map/pallas_call | solution.py:229
  86.6 6.4 sort.31
  95.4 1.1 reshape.695.d_own
  97.5 1.2 and_convert_fusion.3.tf
  98.7 1.2 clamp_select_fusion.3
  99.9 42.4 %shard_map.128 = f32[1024,512]{1,0:T(8,128)} custom-call(s32[136]{0:T(256)} %copy-done.29, s32[136]{0:T(256)} %and_convert_fusion.3.tf, s32[136]{0:T(256)} %get-tuple-element.141.tr, s32[136]{0:T(256)} %get-tuple-element.140.tn, s32[1]{0:T(128)} %bitcast.12.nt, s32[18432]{0:T(1024)} %get-tuple-element.133.idx, f32[144,128]{1,0:T(8,128)} %copy-done.17, ...), custom_call_target="tpu_custom_call" | custom-call | flops 19327352832 | bytes 37748736 | tf_op jit(solution)/shard_map/pallas_call | solution.py:229
  142.3 1.7 collective-permute-done.2
  144.1 2.8 add_convert_fusion.6
  148.9 4.1 pad_maximum_fusion.2
  153.4 1.7 collective-permute-start.3
  155.1 24.2 %collective-permute-done.4.d_oth = bf16[1024,4,128]{2,1,0:T(4,128)(2,1)S(1)} collective-permute-done((bf16[1024,4,128]{2,1,0:T(4,128)(2,1)}, bf16[1024,4,128]{2,1,0:T(4,128)(2,1)S(1)}, u32[]{:S(2)}, u32[]{:S(2)}) %collective-permute-start.4) | collective-permute-done | bytes 1048608 | tf_op jit(solution)/shard_map/ppermute | solution.py:586
  179.3 19.3 %collective-permute-done.3.u_oth = bf16[1024,4,128]{2,1,0:T(4,128)(2,1)S(1)} collective-permute-done((bf16[1024,4,128]{2,1,0:T(4,128)(2,1)S(1)}, bf16[1024,4,128]{2,1,0:T(4,128)(2,1)S(1)}, u32[]{:S(2)}, u32[]{:S(2)}) %collective-permute-start.3) | collective-permute-done | bytes 1048608 | tf_op jit(solution)/shard_map/ppermute | solution.py:586
  198.6 2.4 pad_maximum_fusion.3
  202.3 1.2 and_convert_fusion.1.tf
  203.5 1.3 clamp_select_fusion.1
  204.8 56.1 %shard_map.129 = (f32[1024,512]{1,0:T(8,128)}, f32[1024,512]{1,0:T(8,128)}) custom-call(s32[200]{0:T(256)} %copy-done.27, s32[200]{0:T(256)} %and_convert_fusion.1.tf, s32[200]{0:T(256)} %get-tuple-element.148.tr, s32[200]{0:T(256)} %get-tuple-element.147.tn, s32[1]{0:T(128)} %bitcast.27.nt, s32[18432]{0:T(1024)} %get-tuple-element.135.idx, ...), custom_call_target="tpu_custom_call" | custom-call | flops 38654705664 | bytes 37748736 | tf_op jit(solution)/shard_map/pallas_call | solution.py:229
  260.9 2.8 collective-permute-start.6
  263.6 43.3 %collective-permute-done.6 = f32[1024,512]{1,0:T(8,128)S(1)} collective-permute-done((f32[1024,512]{1,0:T(8,128)}, f32[1024,512]{1,0:T(8,128)S(1)}, u32[]{:S(2)}, u32[]{:S(2)}) %collective-permute-start.6) | collective-permute-done | bytes 2097184 | tf_op jit(solution)/shard_map/ppermute | solution.py:586
  306.9 2.3 add_convert_fusion.3
  309.3 1.0 copy-done.20
  311.5 2.5 pad_maximum_fusion
  314.1 1.8 collective-permute-start.7
  315.9 20.1 %collective-permute-done.7.d_oth = bf16[1024,4,128]{2,1,0:T(4,128)(2,1)S(1)} collective-permute-done((bf16[1024,4,128]{2,1,0:T(4,128)(2,1)S(1)}, bf16[1024,4,128]{2,1,0:T(4,128)(2,1)S(1)}, u32[]{:S(2)}, u32[]{:S(2)}) %collective-permute-start.7) | collective-permute-done | bytes 1048608 | tf_op jit(solution)/shard_map/ppermute | solution.py:586
  336.0 2.4 pad_maximum_fusion.1
  339.1 1.1 and_convert_fusion.tf
  340.3 1.1 clamp_select_fusion
  341.4 46.3 %shard_map.130 = (f32[1024,512]{1,0:T(8,128)}, f32[1024,512]{1,0:T(8,128)}) custom-call(s32[200]{0:T(256)} %copy-done.27, s32[200]{0:T(256)} %and_convert_fusion.1.tf, s32[200]{0:T(256)} %get-tuple-element.148.tr, s32[200]{0:T(256)} %get-tuple-element.147.tn, s32[1]{0:T(128)} %bitcast.27.nt, s32[18432]{0:T(1024)} %get-tuple-element.135.idx, ...), custom_call_target="tpu_custom_call" | custom-call | flops 19327352832 | bytes 37748736 | tf_op jit(solution)/shard_map/pallas_call | solution.py:229
  387.7 3.3 collective-permute-start.5
  395.2 13.2 %merge_tables.1 = (s32[2,32,32,128]{3,2,1,0:T(8,128)}, f32[2,32,32,128]{3,2,1,0:T(8,128)}) custom-call(s32[2048]{0:T(1024)} %bitcast.213, s32[64]{0:T(128)} %reshape.701.exps, f32[8,2,2,152,128]{4,3,2,1,0:T(8,128)} %bitcast.219), custom_call_target="tpu_custom_call" | custom-call | flops 1000000000 | bytes 2490368 | tf_op jit(solution)/shard_map/merge_tables/pallas_call | solution.py:294
  408.5 59.3 %shard_map.131 = (f32[1024,512]{1,0:T(8,128)}, f32[1024,512]{1,0:T(8,128)}) custom-call(s32[200]{0:T(256)} %copy-done.30, s32[200]{0:T(256)} %and_convert_fusion.tf, s32[200]{0:T(256)} %get-tuple-element.139.tr, s32[200]{0:T(256)} %get-tuple-element.138.tn, s32[1]{0:T(128)} %bitcast.30.nt, s32[18432]{0:T(1024)} %get-tuple-element.133.idx, ...), custom_call_target="tpu_custom_call" | custom-call | flops 38654705664 | bytes 37748736 | tf_op jit(solution)/shard_map/pallas_call | solution.py:229
  469.2 103.2 %weight_grads.2 = (bf16[2,64,192,512]{3,2,1,0:T(8,128)(2,1)}, bf16[2,64,192,512]{3,2,1,0:T(8,128)(2,1)}, bf16[2,64,192,512]{3,2,1,0:T(8,128)(2,1)}, bf16[32,192,...) custom-call(s32[32]{0:T(128)} %copy-done.32, s32[66]{0:T(128)} %reshape.703.tiles, ...), custom_call_target="tpu_custom_call" | custom-call | flops 154618822656 | bytes 90177536 | tf_op jit(solution)/shard_map/weight_grads/pallas_call | solution.py:436
  573.8 114.2 %weight_grads.3 = (bf16[2,64,192,512]{3,2,1,0:T(8,128)(2,1)}, bf16[2,64,192,512]{3,2,1,0:T(8,128)(2,1)}, bf16[2,64,192,512]{3,2,1,0:T(8,128)(2,1)}, bf16[32,192,...) custom-call(s32[32]{0:T(128)} %copy-done.31, ...), custom_call_target="tpu_custom_call", output_to_operand_aliasing={{0}: (10, {}), {1}: (11, {}), {2}: (12, {})} | custom-call | flops 154618822656 | bytes 90177536 | tf_op jit(solution)/shard_map/weight_grads/pallas_call | solution.py:436
  688.7 2.1 fusion.1
  690.9 2.3 add_convert_fusion.1
  694.2 1.1 pad_maximum_fusion.4
  696.5 3.3 add_convert_fusion.4
  699.8 1.7 add_convert_fusion
  701.5 61.9 %all-reduce.12.cloned.1.call-done = bf16[2,512,512]{1,2,0:T(8,128)(2,1)} async-done(((bf16[2,512,512]{1,2,0:T(8,128)(2,1)}), bf16[2,512,512]{1,2,0:T(8,128)(2,1)}) %all-reduce.12.cloned.1.call-update) | async-done | bytes 1048592 | tf_op jit(solution)/shard_map/psum | solution.py:666
  763.4 2.3 copy.66
  765.7 14.6 %merge_half.2 = (bf16[2,64,192,512]{3,2,1,0:T(8,128)(2,1)}, bf16[2,64,192,512]{3,2,1,0:T(8,128)(2,1)}, bf16[2,64,192,512]{3,2,1,0:T(8,128)(2,1)}) custom-call(s32[32]{0:T(128)} %get-tuple-element.122.exps, bf16[32,192,512]{2,1,0:T(8,128)(2,1)} %collective-permute-done.12.a, ...), custom_call_target="tpu_custom_call", output_to_operand_aliasing={{0}: (4, {}), {1}: (5, {}), {2}: (6, {})} | custom-call | flops 1000000000 | bytes 37748736 | tf_op jit(solution)/shard_map/merge_half/pallas_call | solution.py:488
  780.3 14.6 %merge_half.3 = (bf16[2,64,192,512]{3,2,1,0:T(8,128)(2,1)}, bf16[2,64,192,512]{3,2,1,0:T(8,128)(2,1)}, bf16[2,64,192,512]{3,2,1,0:T(8,128)(2,1)}) custom-call(s32[32]{0:T(128)} %get-tuple-element.123.exps, bf16[32,192,512]{2,1,0:T(8,128)(2,1)} %collective-permute-done.9.a, ...), custom_call_target="tpu_custom_call", output_to_operand_aliasing={{0}: (4, {}), {1}: (5, {}), {2}: (6, {})} | custom-call | flops 1000000000 | bytes 37748736 | tf_op jit(solution)/shard_map/merge_half/pallas_call | solution.py:488
  (216 shorter events, 28.1 us)
Async XLA Ops:
  8.0 383.0 %all-gather.15.cloned.1.call-start = ((), (), s32[]{:S(2)}) async-start(), calls=%async_computation.5 | async-start | bytes 2801664 | tf_op jit(solution)/shard_map/all_gather | solution.py:635
  9.8 7.1 collective-permute-start
  16.8 25.6 %copy-start = (bf16[1024,4,128]{2,1,0:T(4,128)(2,1)}, bf16[1024,4,128]{2,1,0:T(4,128)(2,1)S(1)}, u32[]{:S(2)}) copy-start(bf16[1024,4,128]{2,1,0:T(4,128)(2,1)S(1)} %reshape.689.u_own) | copy-start | bytes 3145732
  16.8 24.6 %collective-permute-start.1 = (bf16[1024,4,128]{2,1,0:T(4,128)(2,1)S(1)}, bf16[1024,4,128]{2,1,0:T(4,128)(2,1)S(1)}, u32[]{:S(2)}, u32[]{:S(2)}) collective-permute-start(bf16[1024,4,128]{2,1,0:T(4,128)(2,1)S(1)} %reshape.689.u_own), channel_id=1, source_target_pairs={{0,8},{8,0},{1,9},{9,1},{2,10},{10,2},{3,11},{11,3},{4,12},{12,4},... | collective-permute-start | bytes 3145736 | tf_op jit(solution)/shard_map/ppermute | solution.py:586
  26.9 15.5 %copy-start.17 = (f32[144,128]{1,0:T(8,128)}, f32[144,128]{1,0:T(8,128)S(1)}, u32[]{:S(2)}) copy-start(f32[144,128]{1,0:T(8,128)S(1)} %pad_bitcast_fusion.3.gates) | copy-start | bytes 221188
  28.3 14.1 %copy-start.28 = (s32[136]{0:T(256)}, s32[136]{0:T(256)S(1)}, u32[]{:S(2)}) copy-start(s32[136]{0:T(256)S(1)} %broadcast_minimum_fusion.2.te) | copy-start | bytes 1636
  85.0 10.4 %copy-start.6 = (bf16[1024,512]{1,0:T(8,128)(2,1)S(1)}, bf16[1024,512]{1,0:T(8,128)(2,1)}, u32[]{:S(2)}) copy-start(bf16[1024,512]{1,0:T(8,128)(2,1)} %param.9) | copy-start | bytes 3145732
  93.9 48.4 %copy-start.25 = (f32[144,128]{1,0:T(8,128)}, f32[144,128]{1,0:T(8,128)S(1)}, u32[]{:S(2)}) copy-start(f32[144,128]{1,0:T(8,128)S(1)} %pad_bitcast_fusion.2.gates) | copy-start | bytes 221188
  95.4 373.8 %all-gather.11.cloned.1.call-start = ((), (), s32[]{:S(2)}) async-start(), calls=%async_computation.3 | async-start | bytes 18874368 | tf_op jit(solution)/shard_map/all_gather | solution.py:589
  97.3 2.5 copy-start.29
  97.5 46.6 %collective-permute-start.2 = (f32[1024,512]{1,0:T(8,128)}, f32[1024,512]{1,0:T(8,128)}, u32[]{:S(2)}, u32[]{:S(2)}) collective-permute-start(f32[1024,512]{1,0:T(8,128)} %shard_map.127), channel_id=1, source_target_pairs={{0,8},{8,0},{1,9},{9,1},{2,10},{10,2},{3,11},{11,3},{4,12},{12,4},... | collective-permute-start | bytes 6291464 | tf_op jit(solution)/shard_map/ppermute | solution.py:586
  99.9 44.2 %copy-start.13 = (bf16[1024,512]{1,0:T(8,128)(2,1)S(1)}, bf16[1024,512]{1,0:T(8,128)(2,1)}, u32[]{:S(2)}) copy-start(bf16[1024,512]{1,0:T(8,128)(2,1)} %copy-done.12) | copy-start | bytes 3145732
  142.3 5.6 copy-start.34
  148.6 4.4 copy-start.8
  148.9 4.5 copy-start.4
  153.0 316.2 %all-gather.13.cloned.1.call-start = ((), (), s32[]{:S(2)}) async-start(), calls=%async_computation.4 | async-start | bytes 18874368 | tf_op jit(solution)/shard_map/all_gather | solution.py:589
  153.0 26.3 %collective-permute-start.4 = (bf16[1024,4,128]{2,1,0:T(4,128)(2,1)}, bf16[1024,4,128]{2,1,0:T(4,128)(2,1)S(1)}, u32[]{:S(2)}, u32[]{:S(2)}) collective-permute-start(bf16[1024,4,128]{2,1,0:T(4,128)(2,1)} %reshape.695.d_own), channel_id=1, source_target_pairs={{0,8},{8,0},{1,9},{9,1},{2,10},{10,2},{3,11},{11,3},{4,12},{12,4},... | collective-permute-start | bytes 3145736 | tf_op jit(solution)/shard_map/ppermute | solution.py:586
  153.4 45.3 %collective-permute-start.3 = (bf16[1024,4,128]{2,1,0:T(4,128)(2,1)S(1)}, bf16[1024,4,128]{2,1,0:T(4,128)(2,1)S(1)}, u32[]{:S(2)}, u32[]{:S(2)}) collective-permute-start(bf16[1024,4,128]{2,1,0:T(4,128)(2,1)S(1)} %reshape.694.u_own), channel_id=1, source_target_pairs={{0,8},{8,0},{1,9},{9,1},{2,10},{10,2},{3,11},{11,3},{4,12},{12,4},... | collective-permute-start | bytes 3145736 | tf_op jit(solution)/shard_map/ppermute | solution.py:586
  179.3 19.3 %copy-start.22 = (bf16[1024,4,128]{2,1,0:T(4,128)(2,1)}, bf16[1024,4,128]{2,1,0:T(4,128)(2,1)S(1)}, u32[]{:S(2)}) copy-start(bf16[1024,4,128]{2,1,0:T(4,128)(2,1)S(1)} %collective-permute-done.4.d_oth) | copy-start | bytes 3145732
  198.6 2.4 copy-start.5
  201.1 372.7 %all-gather.7.cloned.1.call-start = ((), (), s32[]{:S(2)}) async-start(), calls=%async_computation.1 | async-start | bytes 18874368 | tf_op jit(solution)/shard_map/all_gather | solution.py:589
  202.2 2.6 copy-start.27
  204.8 102.2 %copy-start.7 = (bf16[1024,512]{1,0:T(8,128)(2,1)S(1)}, bf16[1024,512]{1,0:T(8,128)(2,1)}, u32[]{:S(2)}) copy-start(bf16[1024,512]{1,0:T(8,128)(2,1)} %param.9) | copy-start | bytes 3145732
  260.9 46.0 %collective-permute-start.6 = (f32[1024,512]{1,0:T(8,128)}, f32[1024,512]{1,0:T(8,128)S(1)}, u32[]{:S(2)}, u32[]{:S(2)}) collective-permute-start(f32[1024,512]{1,0:T(8,128)} %get-tuple-element.47), channel_id=1, source_target_pairs={{0,8},{8,0},{1,9},{9,1},{2,10},{10,2},{3,11},{11,3},{4,12},{12,4},... | collective-permute-start | bytes 6291464 | tf_op jit(solution)/shard_map/ppermute | solution.py:586
  306.9 3.4 copy-start.35
  311.1 3.0 copy-start.10
  311.5 2.6 copy-start.14
  314.0 22.0 %copy-start.3 = (bf16[1024,4,128]{2,1,0:T(4,128)(2,1)S(1)}, bf16[1024,4,128]{2,1,0:T(4,128)(2,1)}, u32[]{:S(2)}) copy-start(bf16[1024,4,128]{2,1,0:T(4,128)(2,1)} %copy-done.2) | copy-start | bytes 3145732
  314.0 259.8 %all-gather.9.cloned.1.call-start = ((), (), s32[]{:S(2)}) async-start(), calls=%async_computation.2 | async-start | bytes 18874368 | tf_op jit(solution)/shard_map/all_gather | solution.py:589
  314.1 21.9 %collective-permute-start.7 = (bf16[1024,4,128]{2,1,0:T(4,128)(2,1)S(1)}, bf16[1024,4,128]{2,1,0:T(4,128)(2,1)S(1)}, u32[]{:S(2)}, u32[]{:S(2)}) collective-permute-start(bf16[1024,4,128]{2,1,0:T(4,128)(2,1)S(1)} %reshape.696.d_own), channel_id=1, source_target_pairs={{0,8},{8,0},{1,9},{9,1},{2,10},{10,2},{3,11},{11,3},{4,12},{12,4},... | collective-permute-start | bytes 3145736 | tf_op jit(solution)/shard_map/ppermute | solution.py:586
  336.0 2.4 copy-start.21
  338.4 425.0 %all-reduce.12.cloned.1.call-start = ((), (), s32[]{:S(2)}) async-start(), calls=%async_computation | async-start | bytes 2097152 | tf_op jit(solution)/shard_map/psum | solution.py:666
  339.0 48.7 %copy-start.30 = (s32[200]{0:T(256)}, s32[200]{0:T(256)S(1)}, u32[]{:S(2)}) copy-start(s32[200]{0:T(256)S(1)} %broadcast_minimum_fusion.te) | copy-start | bytes 2404
  387.7 300.3 %collective-permute-start.5 = (f32[1024,512]{1,0:T(8,128)}, f32[1024,512]{1,0:T(8,128)}, u32[]{:S(2)}, u32[]{:S(2)}) collective-permute-start(f32[1024,512]{1,0:T(8,128)} %get-tuple-element.50), channel_id=1, source_target_pairs={{0,8},{8,0},{1,9},{9,1},{2,10},{10,2},{3,11},{11,3},{4,12},{12,4},... | collective-permute-start | bytes 6291464 | tf_op jit(solution)/shard_map/ppermute | solution.py:586
  391.8 3.4 copy-start.26
  393.1 15.3 %copy-start.31 = (s32[32]{0:T(128)}, s32[32]{0:T(128)S(1)}, u32[]{:S(2)}) copy-start(s32[32]{0:T(128)S(1)} %get-tuple-element.124.exps) | copy-start | bytes 388
  393.1 74.6 %copy-start.32 = (s32[32]{0:T(128)}, s32[32]{0:T(128)S(1)}, u32[]{:S(2)}) copy-start(s32[32]{0:T(128)S(1)} %get-tuple-element.127.exps) | copy-start | bytes 388
  468.6 219.5 %collective-permute-start.8 = (f32[1024,512]{1,0:T(8,128)}, f32[1024,512]{1,0:T(8,128)}, u32[]{:S(2)}, u32[]{:S(2)}) collective-permute-start(f32[1024,512]{1,0:T(8,128)} %get-tuple-element.53), channel_id=1, source_target_pairs={{0,8},{8,0},{1,9},{9,1},{2,10},{10,2},{3,11},{11,3},{4,12},{12,4},... | collective-permute-start | bytes 6291464 | tf_op jit(solution)/shard_map/ppermute | solution.py:586
  572.4 116.2 %collective-permute-start.12 = (bf16[32,192,512]{2,1,0:T(8,128)(2,1)}, bf16[32,192,512]{2,1,0:T(8,128)(2,1)}, u32[]{:S(2)}, u32[]{:S(2)}) collective-permute-start(bf16[32,192,512]{2,1,0:T(8,128)(2,1)} %get-tuple-element.64), channel_id=1, source_target_pairs={{0,1},{1,0},{2,3},{3,2},{4,5},{5,4},{6,7},{7,6},{8,9},{9,8},{10,11... | collective-permute-start | bytes 18874376 | tf_op jit(solution)/shard_map/ppermute | solution.py:657
  573.3 192.4 %collective-permute-start.13 = (bf16[32,192,512]{2,1,0:T(8,128)(2,1)}, bf16[32,192,512]{2,1,0:T(8,128)(2,1)}, u32[]{:S(2)}, u32[]{:S(2)}) collective-permute-start(bf16[32,192,512]{2,1,0:T(8,128)(2,1)} %get-tuple-element.65), channel_id=1, source_target_pairs={{0,1},{1,0},{2,3},{3,2},{4,5},{5,4},{6,7},{7,6},{8,9},{9,8},{10,11... | collective-permute-start | bytes 18874376 | tf_op jit(solution)/shard_map/ppermute | solution.py:657
  573.3 192.4 %collective-permute-start.14 = (bf16[32,192,512]{2,1,0:T(8,128)(2,1)}, bf16[32,192,512]{2,1,0:T(8,128)(2,1)}, u32[]{:S(2)}, u32[]{:S(2)}) collective-permute-start(bf16[32,192,512]{2,1,0:T(8,128)(2,1)} %get-tuple-element.66), channel_id=1, source_target_pairs={{0,1},{1,0},{2,3},{3,2},{4,5},{5,4},{6,7},{7,6},{8,9},{9,8},{10,11... | collective-permute-start | bytes 18874376 | tf_op jit(solution)/shard_map/ppermute | solution.py:657
  573.8 114.9 %copy-start.19 = (bf16[1024,512]{1,0:T(8,128)(2,1)S(1)}, bf16[1024,512]{1,0:T(8,128)(2,1)}, u32[]{:S(2)}) copy-start(bf16[1024,512]{1,0:T(8,128)(2,1)} %copy-done.18) | copy-start | bytes 3145732
  688.1 92.3 %collective-permute-start.9 = (bf16[32,192,512]{2,1,0:T(8,128)(2,1)}, bf16[32,192,512]{2,1,0:T(8,128)(2,1)}, u32[]{:S(2)}, u32[]{:S(2)}) collective-permute-start(bf16[32,192,512]{2,1,0:T(8,128)(2,1)} %get-tuple-element.61), channel_id=1, source_target_pairs={{0,1},{1,0},{2,3},{3,2},{4,5},{5,4},{6,7},{7,6},{8,9},{9,8},{10,11... | collective-permute-start | bytes 18874376 | tf_op jit(solution)/shard_map/ppermute | solution.py:657
  688.1 92.2 %collective-permute-start.10 = (bf16[32,192,512]{2,1,0:T(8,128)(2,1)}, bf16[32,192,512]{2,1,0:T(8,128)(2,1)}, u32[]{:S(2)}, u32[]{:S(2)}) collective-permute-start(bf16[32,192,512]{2,1,0:T(8,128)(2,1)} %get-tuple-element.62), channel_id=1, source_target_pairs={{0,1},{1,0},{2,3},{3,2},{4,5},{5,4},{6,7},{7,6},{8,9},{9,8},{10,11... | collective-permute-start | bytes 18874376 | tf_op jit(solution)/shard_map/ppermute | solution.py:657
  688.6 91.7 %collective-permute-start.11 = (bf16[32,192,512]{2,1,0:T(8,128)(2,1)}, bf16[32,192,512]{2,1,0:T(8,128)(2,1)}, u32[]{:S(2)}, u32[]{:S(2)}) collective-permute-start(bf16[32,192,512]{2,1,0:T(8,128)(2,1)} %get-tuple-element.63), channel_id=1, source_target_pairs={{0,1},{1,0},{2,3},{3,2},{4,5},{5,4},{6,7},{7,6},{8,9},{9,8},{10,11... | collective-permute-start | bytes 18874376 | tf_op jit(solution)/shard_map/ppermute | solution.py:657
  690.8 2.4 copy-start.33
  696.5 3.3 copy-start.24
  696.5 3.3 copy-start.36
  (10 other events, 14.5 us)
Sparse Core Ops, SparseCore 0:
  95.5 25.8 all-gather.14
  153.1 86.0 all-gather.10
  241.0 85.9 all-gather.12
  328.7 85.9 all-gather.6
  416.4 85.9 all-gather.8
Sparse Core Ops, SparseCore 1:
  695.4 68.0 all-reduce.11

commit v6 on v5

--- a/solution.py
+++ b/solution.py
@@ -10,8 +10,10 @@
 
 CAP_FACTOR = 3
 LANES = 128
-TILE = 128
+TILE = 96
+HALF_TILE = 64
 WTILE = 256
+PARTS = 2
 PITCH = 9
 BATCH = 16
 SLOTS = 6
@@ -36,7 +38,7 @@
 
 
 def clear(ref):
-    step = min(64, ref.shape[0])
+    step = next(n for n in (64, 48, 32, 16, 8) if ref.shape[0] % n == 0)
 
     def one(q, carry):
         ref[pl.ds(pl.multiple_of(q * step, step), step), :] = jnp.zeros((step, ref.shape[1]), ref.dtype)
@@ -55,18 +57,12 @@
     return [pltpu.make_async_copy(sources[k], dst.at[pl.ds(k * n, n)], sem.at[k]) for k in halves]
 
 
-def fetch_pair(own, other, dst, sem):
-    n = own.shape[0]
-    return (pltpu.make_async_copy(own, dst.at[pl.ds(0, n)], sem.at[0]),
-            pltpu.make_async_copy(other, dst.at[pl.ds(n, n)], sem.at[1]))
-
-
-def add_rows(acc, vals_ref, idx, row, parts):
-    for b in range(0, TILE, BATCH):
-        at = [pl.multiple_of(idx[row + b + r], parts) for r in range(BATCH)]
-        vals = [acc[pl.ds(at[r], parts), :] + vals_ref[pl.ds((b + r) * parts, parts), :] for r in range(BATCH)]
+def add_rows(acc, vals_ref, idx, row, tile, pitch, width):
+    for b in range(0, tile, BATCH):
+        at = [pl.multiple_of(idx[row + b + r], 4) for r in range(BATCH)]
+        vals = [acc[pl.ds(at[r], width), :] + vals_ref[pl.ds((b + r) * pitch, width), :] for r in range(BATCH)]
         for r in reversed(range(BATCH)):
-            acc[pl.ds(at[r], parts), :] = vals[r]
+            acc[pl.ds(at[r], width), :] = vals[r]
 
 
 def spread_column(row):
@@ -81,26 +77,27 @@
     return spread_column(jnp.where(lane < LANES - skip, pair[:1], pair[1:]))
 
 
-def widen(src, dst, parts, halves, tok):
+def widen(src, dst, pitch, halves, tok):
     step = 8
 
     def one(q, carry):
         for r in range(step):
-            dst[pl.ds((q * step + r) * parts, parts), :] = src[q * step + r].astype(jnp.float32)
+            dst[pl.ds((q * step + r) * pitch, pitch), :] = src[q * step + r].astype(jnp.float32)
         return carry
 
     lax.fori_loop(halves[0] * tok // step, (halves[-1] + 1) * tok // step, one, 0)
 
 
-def write_sums(acc, outs, tok, parts, halves):
+def write_sums(acc, outs, tok, parts, pitch, places):
     step = min(32, tok)
 
     def copy_out(q, carry):
         r0 = pl.multiple_of(q * step, step)
         for k in range(parts):
             cols = slice(k * LANES, (k + 1) * LANES)
-            for out, half in zip(outs, halves):
-                out[pl.ds(r0, step), cols] = acc[pl.ds((half * tok + r0) * parts + k, step, stride=parts), :]
+            for out, (half, part) in zip(outs, places):
+                first = (half * tok + r0) * pitch + part * parts + k
+                out[pl.ds(r0, step), cols] = acc[pl.ds(first, step, stride=pitch), :]
         return carry
 
     lax.fori_loop(0, tok // step, copy_out, 0)
@@ -141,7 +138,7 @@
     lax.fori_loop(0, n_steps, one, 0)
 
 
-def forward_body(te, tf, tr, tn, nt, idx, gates, u_own, u_oth, g_ref, up_ref, w_ref, *refs, layer, tok, parts, halves):
+def forward_body(te, tf, tr, tn, nt, idx, gates, u_own, u_oth, g_ref, up_ref, w_ref, *refs, layer, tok, parts, tile, halves):
     ff = g_ref.shape[2]
     outs, (usc, uf, ut, ot, acc, ht, wbuf, sem, wsem) = refs[:len(halves)], refs[len(halves):]
 
@@ -157,93 +154,117 @@
 
     def step(i, slot, slot_before):
         o = tn_dot(ht[...], wbuf[slot_before, 2 * ff:]).astype(jnp.bfloat16).astype(jnp.float32)
-        u = load_rows(ut, 0, TILE, parts)
+        u = load_rows(ut, 0, tile, parts)
         ab = nt_dot(wbuf[slot, :2 * ff], u)
-        add_rows(acc, ot, idx, tr[i], parts)
+        add_rows(acc, ot, idx, tr[i], tile, parts, parts)
         row = tr[i + 3]
-        for r in range(TILE):
+        for r in range(tile):
             ut[pl.ds(parts * r, parts), :] = uf[pl.ds(pl.multiple_of(idx[row + r], parts), parts), :]
-        live = lax.broadcasted_iota(jnp.int32, (TILE, LANES), 0) < tn[i + 1]
-        gate = tile_gates(gates, tr[i + 1])
+        live = lax.broadcasted_iota(jnp.int32, (tile, LANES), 0) < tn[i + 1]
+        gate = tile_gates(gates, tr[i + 1])[:tile]
         for k in range(parts):
             o_k = jnp.where(live, o[:, k * LANES:(k + 1) * LANES] * gate, 0.0)
-            ot[pl.ds(k, TILE, stride=parts), :] = o_k
+            ot[pl.ds(k, tile, stride=parts), :] = o_k
         a, b = ab[:ff], ab[ff:]
         ht[...] = (a * jax.nn.sigmoid(a) * b).astype(jnp.bfloat16)
 
     run_tiles(step, (g_ref, up_ref, w_ref), wbuf, wsem, te, tf, nt[0] + 3, layer, prepare)
-    write_sums(acc, outs, tok, parts, halves)
-
-
-def backward_body(te, tf, tr, tn, nt, idx, gates, u_own, u_oth, d_own, d_oth, g_ref, up_ref, w_ref, *refs, layer, tok, parts,
-                  halves):
+    write_sums(acc, outs, tok, parts, parts, [(half, 0) for half in halves])
+
+
+def backward_body(te, tf, tr, tn, nt, idx, gates, u_own, u_oth, d_own, d_oth, g_ref, up_ref, w_ref, *refs, layer, tok, parts, tile,
+                  forward):
     ff = g_ref.shape[2]
-    outs, (usc, dsc, uf, df, ut, dt, vt, acc, da_t, wbuf, sem, wsem) = refs[:len(halves)], refs[len(halves):]
+    n_out = 4 if forward else 2
+    outs, (uds, udf, rows, vt, acc, da_t, ht, wbuf, sem, wsem) = refs[:n_out], refs[n_out:]
+    pitch = 2 * parts
+    width = pitch if forward else parts
 
     def prepare():
-        copies = fetch_rows((u_own, u_oth), halves, usc, sem.at[0]) + fetch_rows((d_own, d_oth), halves, dsc, sem.at[1])
+        copies = [pltpu.make_async_copy(src, uds.at[pl.ds((k % 2) * tok, tok), pl.ds((k // 2) * parts, parts)], sem.at[k])
+                  for k, src in enumerate((u_own, u_oth, d_own, d_oth))]
         for c in copies:
             c.start()
-        for ref in (acc, vt, ut, dt, da_t):
+        for ref in (acc, vt, rows, da_t, ht):
             clear(ref)
         for c in copies:
             c.wait()
-        widen(usc, uf, parts, halves, tok)
-        widen(dsc, df, parts, halves, tok)
+        widen(uds, udf, pitch, (0, 1), tok)
+
+    def column(k):
+        return rows[pl.ds(k, tile, stride=PITCH), :]
 
     def step(i, slot, slot_before):
-        v = tn_dot(da_t[...], wbuf[slot_before, :2 * ff]).astype(jnp.bfloat16).astype(jnp.float32)
-        u = load_rows(ut, 0, TILE, parts)
-        gate = tile_gates(gates, tr[i + 2])
-        c = jnp.concatenate([(dt[pl.ds(k, TILE, stride=parts), :] * gate).astype(jnp.bfloat16) for k in range(parts)], axis=1)
+        results = [tn_dot(da_t[...], wbuf[slot_before, :2 * ff])]
+        if forward:
+            results.insert(0, tn_dot(ht[...], wbuf[slot_before, 2 * ff:]))
+        u = jnp.concatenate([column(k) for k in range(parts)], axis=1).astype(jnp.bfloat16)
+        gate = tile_gates(gates, tr[i + 2])[:tile]
+        c = jnp.concatenate([(column(parts + k) * gate).astype(jnp.bfloat16) for k in range(parts)], axis=1)
         ab = nt_dot(wbuf[slot, :2 * ff], u)
         dh = nt_dot(wbuf[slot, 2 * ff:], c)
-        add_rows(acc, vt, idx, tr[i], parts)
+        add_rows(acc, vt, idx, tr[i], tile, PITCH, width)
         row = tr[i + 3]
-        for r in range(TILE):
-            at = pl.multiple_of(idx[row + r], parts)
-            ut[pl.ds(parts * r, parts), :] = uf[pl.ds(at, parts), :]
-            dt[pl.ds(parts * r, parts), :] = df[pl.ds(at, parts), :]
-        live = lax.broadcasted_iota(jnp.int32, (TILE, LANES), 0) < tn[i + 1]
-        gate = tile_gates(gates, tr[i + 1])
-        for k in range(parts):
-            v_k = jnp.where(live, v[:, k * LANES:(k + 1) * LANES] * gate, 0.0)
-            vt[pl.ds(k, TILE, stride=parts), :] = v_k
+        for r in range(tile):
+            rows[pl.ds(PITCH * r, pitch), :] = udf[pl.ds(pl.multiple_of(idx[row + r], pitch), pitch), :]
+        live = lax.broadcasted_iota(jnp.int32, (tile, LANES), 0) < tn[i + 1]
+        gate = tile_gates(gates, tr[i + 1])[:tile]
+        for q, result in enumerate(results):
+            v = result.astype(jnp.bfloat16).astype(jnp.float32)
+            for k in range(parts):
+                v_k = jnp.where(live, v[:, k * LANES:(k + 1) * LANES] * gate, 0.0)
+                vt[pl.ds(q * parts + k, tile, stride=PITCH), :] = v_k
         a, b = ab[:ff], ab[ff:]
         s = jax.nn.sigmoid(a)
+        act = a * s
+        if forward:
+            ht[...] = (act * b).astype(jnp.bfloat16)
         da_t[:ff] = (dh * b * (s * (1.0 + a * (1.0 - s)))).astype(jnp.bfloat16)
-        da_t[ff:] = (dh * (a * s)).astype(jnp.bfloat16)
+        da_t[ff:] = (dh * act).astype(jnp.bfloat16)
 
     run_tiles(step, (g_ref, up_ref, w_ref), wbuf, wsem, te, tf, nt[0] + 3, layer, prepare)
-    write_sums(acc, outs, tok, parts, halves)
-
-
-def token_kernel(body, layer, tables, slabs, weights, halves=(0, 1)):
+    places = [(0, 0), (1, 0), (0, 1), (1, 1)] if forward else [(0, 0), (1, 0)]
+    write_sums(acc, outs, tok, parts, pitch, places)
+
+
+def token_kernel(layer, tables, slabs, weights, halves=(0, 1), forward=True):
     tok, parts, _ = slabs[0].shape
     _, n_local, ff, d_model = weights[0].shape
-    n_pairs = len(slabs) // 2
+    backward = len(slabs) == 4
+    tile = TILE if len(halves) == 2 else HALF_TILE
     rows_spec = pl.BlockSpec((tok, d_model), lambda i, *_: (0, 0))
     any_spec = pl.BlockSpec(memory_space=pl.ANY)
-    sem_shape = (2,) if n_pairs == 1 else (2, 2)
-    copies = 8 * tok
+    common = [pltpu.VMEM((SLOTS, 3 * ff, d_model), jnp.bfloat16)]
+    if backward:
+        body = functools.partial(backward_body, forward=forward)
+        n_out = 4 if forward else 2
+        scratch = [pltpu.VMEM((2 * tok, 2 * parts, LANES), jnp.bfloat16), pltpu.VMEM((2 * tok * 2 * parts, LANES), jnp.float32),
+                   pltpu.VMEM((tile * PITCH + 16, LANES), jnp.float32), pltpu.VMEM((tile * PITCH + 16, LANES), jnp.float32),
+                   pltpu.VMEM((2 * tok * 2 * parts, LANES), jnp.float32), pltpu.VMEM((2 * ff, tile), jnp.bfloat16),
+                   pltpu.VMEM((ff, tile), jnp.bfloat16)] + common
+        scratch += [pltpu.SemaphoreType.DMA((4,)), pltpu.SemaphoreType.DMA((SLOTS,))]
+    else:
+        body = functools.partial(forward_body, halves=halves)
+        n_out = len(halves)
+        scratch = [pltpu.VMEM((2 * tok, parts, LANES), jnp.bfloat16), pltpu.VMEM((2 * tok * parts, LANES), jnp.float32),
+                   pltpu.VMEM((tile * parts, LANES), jnp.float32), pltpu.VMEM((tile * parts, LANES), jnp.float32),
+                   pltpu.VMEM((2 * tok * parts, LANES), jnp.float32), pltpu.VMEM((ff, tile), jnp.bfloat16)] + common
+        scratch += [pltpu.SemaphoreType.DMA((2,)), pltpu.SemaphoreType.DMA((SLOTS,))]
+    work = (4 * backward + 3 * (not backward or forward)) * len(halves)
     return pl.pallas_call(
-        functools.partial(body, layer=layer, tok=tok, parts=parts, halves=halves),
+        functools.partial(body, layer=layer, tok=tok, parts=parts, tile=tile),
         grid_spec=pltpu.PrefetchScalarGridSpec(
             num_scalar_prefetch=len(tables) - 1,
             grid=(1,),
             in_specs=[pl.BlockSpec(tables[-1].shape, lambda i, *_: (0, 0))] + [any_spec] * (len(slabs) + 3),
-            out_specs=[rows_spec] * len(halves),
-            scratch_shapes=[pltpu.VMEM((2 * tok, parts, LANES), jnp.bfloat16)] * n_pairs
-            + [pltpu.VMEM((2 * tok * parts, LANES), jnp.float32)] * n_pairs
-            + [pltpu.VMEM((TILE * parts, LANES), jnp.float32)] * (n_pairs + 1)
-            + [pltpu.VMEM((2 * tok * parts, LANES), jnp.float32), pltpu.VMEM((n_pairs * ff, TILE), jnp.bfloat16),
-               pltpu.VMEM((SLOTS, 3 * ff, d_model), jnp.bfloat16),
-               pltpu.SemaphoreType.DMA(sem_shape), pltpu.SemaphoreType.DMA((SLOTS,))],
+            out_specs=[rows_spec] * n_out,
+            scratch_shapes=scratch,
         ),
-        out_shape=[jax.ShapeDtypeStruct((tok, d_model), jnp.float32)] * len(halves),
+        out_shape=[jax.ShapeDtypeStruct((tok, d_model), jnp.float32)] * n_out,
         compiler_params=pltpu.CompilerParams(dimension_semantics=("arbitrary",), vmem_limit_bytes=VMEM_LIMIT),
-        cost_estimate=pl.CostEstimate(flops=(3 + 3 * (n_pairs - 1)) * 2 * copies * d_model * ff * 4,
+        cost_estimate=pl.CostEstimate(flops=work * 2 * 8 * tok * d_model * ff * 4,
                                       bytes_accessed=3 * n_local * ff * d_model * 2, transcendentals=0),
+        name="experts_backward" if backward else "experts_forward",
     )(*tables, *slabs, *weights)
 
 
@@ -309,7 +330,8 @@
     )(starts.reshape(-1), exps.reshape(-1), shared)
 
 
-def weight_grad_body(exps, tiles, begins, ud_own, ud_oth, idx_all, gate_ref, *refs, parts, n_exp, n_alias, layer, page):
+def weight_grad_body(exps, tiles, begins, u_own, u_oth, d_own, d_oth, idx_all, gate_ref, *refs, parts, n_exp, n_alias, first_list,
+                     page):
     g_ref, up_ref, w_ref = refs[:3]
     (dg_ref, du_ref, dw_ref, og_ref, ou_ref, ow_ref,
      uds, rows, u0, c0, d0, h0, u1, c1, d1, h1, gacc, wacc, idx_s, sem, tsem) = refs[3 + n_alias:]
@@ -320,7 +342,7 @@
 
     def table_copy(exp):
         slot = lax.rem(exp, slots)
-        at = pl.multiple_of((layer * n_exp + exp) * page, PAGE)
+        at = pl.multiple_of((first_list + exp) * page, PAGE)
         to = pl.multiple_of(slot * page, PAGE)
         return pltpu.make_async_copy(idx_all.at[pl.ds(at, page)], idx_s.at[pl.ds(to, page)], tsem.at[slot])
 
@@ -332,12 +354,14 @@
 
     @pl.when(e == 0)
     def _():
-        copies = fetch_pair(ud_own, ud_oth, uds, sem)
+        n_half = u_own.shape[0]
+        copies = [pltpu.make_async_copy(src, uds.at[pl.ds((k % 2) * n_half, n_half), pl.ds((k // 2) * parts, parts)], sem.at[k])
+                  for k, src in enumerate((u_own, u_oth, d_own, d_oth))]
         for c in copies:
             c.start()
         table_copy(0).start()
         table_copy(1).start()
-        n_rows = ud_own.shape[0] * 2
+        n_rows = n_half * 2
         uds[pl.ds(n_rows, 8)] = jnp.zeros((8, 2 * parts, LANES), jnp.bfloat16)
         for ref in (*both[0], *both[1], gacc, wacc):
             clear(ref)
@@ -362,8 +386,8 @@
 
     here = lax.rem(e, slots) * page
     there = lax.rem(jnp.minimum(e + 1, n_exp - 1), slots) * page
-    n_tiles = tiles[layer * (n_exp + 1) + e]
-    begin = begins[layer * (n_exp + 1) + e]
+    n_tiles = tiles[e]
+    begin = begins[e]
     gate_rows = WTILE // LANES
 
     def compute(j, new, old):
@@ -415,44 +439,47 @@
     lax.fori_loop(0, n_tiles, tile, 0)
 
 
-def weight_grads(layer, exps, tiles, ud_alls, idx_all, gates, weights, full):
-    n_src, parts2, _ = ud_alls[0].shape
-    parts = parts2 // 2
-    n_tok = 2 * n_src
+def weight_grads(layer, part, exps, tiles, rows, idx_all, gates, weights, full):
+    n_half, parts, _ = rows[0].shape
+    n_tok = 2 * n_half
     n_layers, n_local, ff, d_model = weights[0].shape
-    n_exp = n_local // 2
+    n_own = exps.shape[1]
+    n_exp = n_own // PARTS
+    first = part * n_exp
     out_rows = gates.shape[2]
     page = out_rows * LANES
-    tiles = jnp.concatenate([tiles, jnp.ones((n_layers, 1), jnp.int32)], axis=1)
-    begins = jnp.cumsum(tiles, axis=1) - tiles
+    exps = lax.slice_in_dim(exps[layer], first, first + n_exp)
+    tiles = jnp.concatenate([lax.slice_in_dim(tiles[layer], first, first + n_exp), jnp.ones((1,), jnp.int32)])
+    begins = jnp.cumsum(tiles) - tiles
     any_spec = pl.BlockSpec(memory_space=pl.ANY)
     mine = pl.BlockSpec((1, 1, ff, d_model), lambda e, exps, *_: (layer, exps[jnp.minimum(e, n_exp - 1)], 0, 0))
     done = pl.BlockSpec((1, 1, ff, d_model), lambda e, exps, *_: (layer, exps[jnp.maximum(e - 1, 0)], 0, 0))
     half = pl.BlockSpec((1, ff, d_model), lambda e, *_: (jnp.maximum(e - 1, 0), 0, 0))
-    gate_spec = pl.BlockSpec((1, 1, out_rows, LANES), lambda e, *_: (layer, jnp.minimum(e, n_exp - 1), 0, 0))
+    gate_spec = pl.BlockSpec((1, 1, out_rows, LANES), lambda e, *_: (layer, first + jnp.minimum(e, n_exp - 1), 0, 0))
     aliased = list(full) if full is not None else []
     tile_set = [pltpu.VMEM((WTILE, d_model), jnp.bfloat16)] * 2 + [pltpu.VMEM((2 * ff, WTILE), jnp.bfloat16),
                                                                  pltpu.VMEM((ff, WTILE), jnp.bfloat16)]
     outs = pl.pallas_call(
-        functools.partial(weight_grad_body, parts=parts, n_exp=n_exp, n_alias=len(aliased), layer=layer, page=page),
+        functools.partial(weight_grad_body, parts=parts, n_exp=n_exp, n_alias=len(aliased), first_list=layer * n_own + first,
+                          page=page),
         grid_spec=pltpu.PrefetchScalarGridSpec(
             num_scalar_prefetch=3,
             grid=(n_exp + 1,),
-            in_specs=[any_spec] * 3 + [gate_spec] + [mine] * 3 + [any_spec] * len(aliased),
+            in_specs=[any_spec] * 5 + [gate_spec] + [mine] * 3 + [any_spec] * len(aliased),
             out_specs=[done] * 3 + [half] * 3,
-            scratch_shapes=[pltpu.VMEM((n_tok + 8, parts2, LANES), jnp.bfloat16)]
+            scratch_shapes=[pltpu.VMEM((n_tok + 8, 2 * parts, LANES), jnp.bfloat16)]
             + [pltpu.VMEM((WTILE * PITCH + 16, LANES), jnp.float32)] + tile_set * 2
             + [pltpu.VMEM((2 * ff, d_model), jnp.float32), pltpu.VMEM((ff, d_model), jnp.float32),
-               pltpu.SMEM((3 * page,), jnp.int32), pltpu.SemaphoreType.DMA((2,)), pltpu.SemaphoreType.DMA((3,))],
+               pltpu.SMEM((3 * page,), jnp.int32), pltpu.SemaphoreType.DMA((4,)), pltpu.SemaphoreType.DMA((3,))],
         ),
         out_shape=[jax.ShapeDtypeStruct((n_layers, n_local, ff, d_model), jnp.bfloat16)] * 3
         + [jax.ShapeDtypeStruct((n_exp, ff, d_model), jnp.bfloat16)] * 3,
-        input_output_aliases={10 + k: k for k in range(len(aliased))},
+        input_output_aliases={12 + k: k for k in range(len(aliased))},
         compiler_params=pltpu.CompilerParams(dimension_semantics=("arbitrary",), vmem_limit_bytes=VMEM_LIMIT),
-        cost_estimate=pl.CostEstimate(flops=6 * 2 * n_tok * 2 * d_model * ff * 4,
+        cost_estimate=pl.CostEstimate(flops=6 * 2 * n_tok * 2 * d_model * ff * 4 // PARTS,
                                       bytes_accessed=n_tok * d_model * 4 + 9 * n_exp * ff * d_model * 2, transcendentals=0),
         name="weight_grads",
-    )(exps, tiles.reshape(-1), begins.reshape(-1), *ud_alls, idx_all, gates, *weights, *aliased)
+    )(exps, tiles, begins, *rows, idx_all, gates, *weights, *aliased)
     return outs[:3], outs[3:]
 
 
@@ -513,29 +540,30 @@
     counts = jnp.sum(half_counts, axis=0)
     ends = jnp.cumsum(counts)
     starts = ends - counts
-    pad = cdiv(2 * PAGE, TILE) * TILE
+    pad = 2 * PAGE
     token = jnp.pad(token, (0, pad))
     gate = jnp.pad(gate, (0, pad))
     bounds = jnp.concatenate([jnp.zeros((1,), jnp.int32), ends, jnp.full((LANES - 1 - n_local,), ends[-1], jnp.int32)])
-    whole = tile_list(starts, counts, n)
+    whole = tile_list(starts, counts, n, TILE)
     lists = (whole,)
     if split:
-        lists = (tile_list(starts, half_counts[0], n // 2), tile_list(starts + half_counts[0], half_counts[1], n // 2))
+        lists = (tile_list(starts, half_counts[0], n // 2, HALF_TILE),
+                 tile_list(starts + half_counts[0], half_counts[1], n // 2, HALF_TILE))
     return lists, whole, token, gate, bounds
 
 
-def tile_list(starts, counts, most):
+def tile_list(starts, counts, most, tile):
     n_local = starts.shape[0]
-    n_tiles = jnp.maximum((counts + TILE - 1) // TILE, 1)
+    n_tiles = jnp.maximum((counts + tile - 1) // tile, 1)
     tile_end = jnp.cumsum(n_tiles)
-    tile_id = jnp.arange(most // TILE + n_local + 8, dtype=jnp.int32) - 3
+    tile_id = jnp.arange(most // tile + n_local + 8, dtype=jnp.int32) - 3
     tile_e = jnp.minimum(jnp.sum((tile_end[None, :] <= tile_id[:, None]).astype(jnp.int32), axis=1), n_local - 1)
     pick = (tile_e[:, None] == jnp.arange(n_local)[None, :]).astype(jnp.int32)
-    inside = (tile_id - jnp.sum(pick * (tile_end - n_tiles)[None, :], axis=1)) * TILE
+    inside = (tile_id - jnp.sum(pick * (tile_end - n_tiles)[None, :], axis=1)) * tile
     real = (tile_id >= 0) & (tile_id < tile_end[-1])
     tile_row = jnp.where(real, jnp.sum(pick * starts[None, :], axis=1) + inside, 0)
     tile_first = (real & (inside == 0) & (tile_e > 0)).astype(jnp.int32)
-    tile_n = jnp.where(real, jnp.clip(jnp.sum(pick * counts[None, :], axis=1) - inside, 0, TILE), 0)
+    tile_n = jnp.where(real, jnp.clip(jnp.sum(pick * counts[None, :], axis=1) - inside, 0, tile), 0)
     return tile_e, tile_first, tile_row, tile_n, tile_end[-1:]
 
 
@@ -545,7 +573,7 @@
     ids = jnp.arange(n_local, dtype=jnp.int32)
     ahead = (load[None, :] > load[:, None]) | ((load[None, :] == load[:, None]) & (ids[None, :] < ids[:, None]))
     rank = jnp.sum(ahead.astype(jnp.int32), axis=1)
-    turn = jnp.arange(n_local // 2, dtype=jnp.int32)
+    turn = jnp.concatenate([jnp.arange(k, n_local // 2, PARTS, dtype=jnp.int32) for k in range(PARTS)])
 
     def dealt(which):
         want = 2 * turn + (which + turn) % 2
@@ -597,7 +625,9 @@
         ids = jnp.swapaxes(expert_ids, 1, 2)
         gates = jnp.swapaxes(gate_vals, 1, 2)
         mine = jnp.stack([ids.astype(jnp.float32), gates])
-        theirs = swap(mine)
+        u = mixed(tokens, 0)
+        u_slab = slab(u)
+        theirs = swap(after(mine, u_slab))
         both = jnp.stack([mine, theirs], 2)
         top = n_layers - 1
         tables, combined, packed = [], [], []
@@ -605,9 +635,8 @@
         def add_tables(layer, pair):
             lists, whole, token, gate, bounds = route_tables(pair[0].astype(jnp.int32), pair[1], ep_id, n_local, layer < top)
             gate_rows = gate.reshape(-1, LANES)
-            at = token * parts
-            tables.append([(*tiles, at, gate_rows) for tiles in lists])
-            combined.append(tables[layer][-1] if layer == top else (*whole, at, gate_rows))
+            tables.append([(*tiles, token * parts, gate_rows) for tiles in lists])
+            combined.append((*whole, token * (2 * parts), gate_rows))
             spot = lax.div(token, tok) * (dp_size * tok) + dp_id * tok + lax.rem(token, tok)
             first = jnp.concatenate([spot.reshape(-1, LANES), jnp.pad(bounds.reshape(1, LANES), ((0, 7), (0, 0)))])
             packed.append(jnp.stack([first.astype(jnp.float32), jnp.pad(gate_rows, ((0, 8), (0, 0)))]))
@@ -616,20 +645,22 @@
 
         d_slab = slab(d_out)
         d_other = swap(d_slab)
-
-        x_in, u_slabs, u_others, xs = tokens, [], [], []
+        d_rows = (spread(d_slab), spread(d_other))
+
+        x_in, u_slabs, u_others, xs = tokens, [u_slab], [swap(u_slab)], []
         for layer in range(n_layers):
-            u = mixed(x_in, layer)
-            u_slabs.append(slab(u))
-            u_others.append(swap(u_slabs[layer]))
+            if layer:
+                u = mixed(x_in, layer)
+                u_slabs.append(slab(u))
+                u_others.append(swap(u_slabs[layer]))
             xs.append(x_in)
             if layer < top:
                 slabs = (u_slabs[layer], u_others[layer])
-                other, = token_kernel(forward_body, layer, tables[layer][1], slabs, weights, (1,))
+                other, = token_kernel(layer, tables[layer][1], slabs, weights, (1,))
                 sent = swap(other)
-                own, = token_kernel(forward_body, layer, tables[layer][0],
-                                    (after(u_slabs[layer], other), u_others[layer]), weights, (0,))
-                add_tables(layer + 1, after(both[:, layer + 1], other))
+                own, = token_kernel(layer, tables[layer][0], (after(u_slabs[layer], other, d_other), u_others[layer]), weights,
+                                    (0,))
+                add_tables(layer + 1, after(both[:, layer + 1], own))
                 x_in = (u.astype(jnp.float32) + own + sent).astype(jnp.bfloat16)
 
         shared = lax.all_gather(jnp.stack(packed), 'dp', axis=0)
@@ -643,26 +674,36 @@
         d_y, full, halves = d_out, None, []
         d_mix = [None] * n_layers
         for layer in reversed(range(n_layers)):
-            spreads = [spread(jnp.concatenate(x, axis=1)) for x in ((u_slabs[layer], d_slab), (u_others[layer], d_other))]
+            u_rows = tuple(spread(x) for x in (u_slabs[layer], u_others[layer]))
             slabs = (u_slabs[layer], u_others[layer], d_slab, d_other)
-            own, other = token_kernel(backward_body, layer, combined[layer], slabs, weights)
+            *sums, own, other = token_kernel(layer, combined[layer], slabs, weights, forward=layer == top)
+            if layer == top:
+                y_own, y_other = sums
             d_u = (d_y.astype(jnp.float32) + own + swap(other)).astype(jnp.bfloat16)
-            last = other
-            if layer == top:
-                y_own, y_other = token_kernel(forward_body, top, combined[top],
-                                              (after(u_slabs[top], other), u_others[top]), weights)
-                layer_out = (u.astype(jnp.float32) + y_own + swap(y_other)).astype(jnp.bfloat16)
-                last = y_other
-            full, half = weight_grads(layer, mine_e[layer], after(tiles, last), spreads, idx_all, gate_all, weights, full)
-            halves.append((layer, [lax.ppermute(x, 'dp', core_pairs) for x in half]))
+
+            def grads(part, full, *earlier):
+                full, half = weight_grads(layer, part, mine_e, after(tiles, *earlier), u_rows + d_rows, idx_all, gate_all, weights,
+                                          full)
+                halves.append((layer, part, [lax.ppermute(x, 'dp', core_pairs) for x in half]))
+                return full
+
+            full = grads(0, full, other)
             d_mix[layer] = jnp.einsum('td,te->de', xs[layer], d_u, preferred_element_type=jnp.float32).astype(jnp.bfloat16)
             d_y = (d_u.astype(jnp.float32)
                    + jnp.einsum('te,de->td', d_u, w_mix[layer], preferred_element_type=jnp.float32)).astype(jnp.bfloat16)
             if layer:
-                d_slab = slab(d_y)
-                d_other = swap(d_slab)
-        for layer, half in halves:
-            full = merge_half(layer, theirs_e[layer], half, full)
+                next_slab = slab(d_y)
+                next_other = swap(next_slab)
+                next_rows = (spread(next_slab), spread(next_other))
+                if layer == top:
+                    layer_out = (u.astype(jnp.float32) + y_own + swap(after(y_other, next_other))).astype(jnp.bfloat16)
+            for part in range(1, PARTS):
+                full = grads(part, full, d_y)
+            if layer:
+                d_slab, d_other, d_rows = next_slab, next_other, next_rows
+        for layer, part, half in halves:
+            n_exp = half[0].shape[0]
+            full = merge_half(layer, lax.slice_in_dim(theirs_e[layer], part * n_exp, (part + 1) * n_exp), half, full)
         d_mix = lax.psum(jnp.stack(d_mix), ('dp', 'ep'))
         return (layer_out, d_y, d_mix, jnp.swapaxes(full[0], 2, 3), jnp.swapaxes(full[1], 2, 3), full[2])
 

time: 803 us -> 854 us (1.064)
  waiting for transfers between devices: 181 us -> 224 us
  Pallas kernels: 506 us -> 482 us
  other arithmetic: 56.1 us -> 69.8 us
  local copies, waits for them, and re-layouts: 18.1 us -> 29.1 us
    pallas_call x5 -> x4, Pallas kernels: 247 us -> 188 us  [token_kernel(): pl.pallas_call(functools.partial(body, layer=layer, tok=tok, parts=parts,...]
    ppermute x9, waiting for transfers between devices: 119 us -> 160 us  [swap(): return lax.ppermute(x, 'ep', ep_pairs)]
    pallas_call x2 -> x4, Pallas kernels: 217 us -> 248 us  [weight_grads(): pl.pallas_call(functools.partial(weight_grad_body, parts=parts, n_exp=n_e...]
    concatenate x4 -> x0, other arithmetic: 11.3 us -> none  [device_body(): jnp.concatenate(x, axis=1)]
    another operation x14 -> x24, other arithmetic: 1.65 us -> 12.4 us
    pallas_call x2 -> x4, Pallas kernels: 29.2 us -> 32.7 us  [merge_half(): pl.pallas_call(functools.partial(merge_body, layer=layer, n_exp=n_exp), g...]
  transfers between devices with their start and end apart: 21 -> 31, of which waited for: 7 -> 7; matrix products, arithmetic and copies ran while one was open for 8% -> 10% of each run, Pallas kernels for 56% -> 51%
where the time goes in v6:
time: 854 us; the launch traced here: 851 us
  Pallas kernels  482 us (56%)
  waiting for transfers between devices  224 us (26%)
  other arithmetic  69.8 us (8%)
  local copies, waits for them, and re-layouts  29.1 us (3%)
  starting transfers between devices  22.6 us (3%)
  between operations  16.2 us (2%)
    pallas_call x4, Pallas kernels, weight_grads(): pl.pallas_call(functools.partial(weight_grad_body, parts=parts, n_exp=n_e...  248 us
    pallas_call x4, Pallas kernels, token_kernel(): pl.pallas_call(functools.partial(body, layer=layer, tok=tok, parts=parts,...  188 us
    ppermute x9, waiting for transfers between devices, swap(): return lax.ppermute(x, 'ep', ep_pairs)  160 us
    psum x1, waiting for transfers between devices, device_body(): d_mix = lax.psum(jnp.stack(d_mix), ('dp', 'ep'))  61.3 us
    pallas_call x4, Pallas kernels, merge_half(): pl.pallas_call(functools.partial(merge_body, layer=layer, n_exp=n_exp), g...  32.7 us
  transfers between devices with their start and end apart: 31, of which 7 were waited for; matrix products, arithmetic and copies ran while one was open for 10% of the time, Pallas kernels for 51%

profile of v6, /device:TPU:0, one launch (start us, length us, event | category | flops | bytes accessed | tf_op | source)
XLA Modules:
  0.0 851.3 jit_solution(60316703857870040)
XLA Ops:
  8.1 2.4 add_convert_fusion.7
  11.6 3.3 collective-permute-start
  14.9 1.3 reshape.760.d_own
  16.3 2.0 collective-permute-start.2
  21.4 1.4 reduce-window.67
  26.3 1.4 reduce-window.66
  28.6 1.4 copy.83
  30.0 1.4 reduce-window.68
  31.4 1.4 reduce.5
  34.0 1.4 convert_reduce_fusion.5
  36.1 7.9 sort.30
  45.8 1.4 copy.88
  47.2 1.4 reduce-window.71
  48.6 1.4 reduce.10
  56.1 1.3 slice.191
  59.4 1.9 and_convert_fusion.2.tf
  61.3 1.9 and_convert_fusion.3.tf
  66.7 36.8 %experts_forward.2 = f32[1024,512]{1,0:T(8,128)} custom-call(s32[200]{0:T(256)} %copy-done.23, s32[200]{0:T(256)} %and_convert_fusion.2.tf, s32[200]{0:T(256)} %get-tuple-element.188.tr, s32[200]{0:T(256)} %get-tuple-element.187.tn, s32[1]{0:T(128)} %bitcast.20.nt, s32[18432]{0:T(1024)} %get-tuple-element.176.idx, f32[144,128]{1,0:T(8,128)} %copy-done.10, ...), custom_call_target="tpu_custom_call" | custom-call | flops 19327352832 | bytes 37748736 | tf_op jit(solution)/shard_map/experts_forward/pallas_call | solution.py:254
  103.5 37.0 %experts_forward.3 = f32[1024,512]{1,0:T(8,128)} custom-call(s32[200]{0:T(256)} %copy-done.24, s32[200]{0:T(256)} %and_convert_fusion.3.tf, s32[200]{0:T(256)} %get-tuple-element.195.tr, s32[200]{0:T(256)} %get-tuple-element.194.tn, s32[1]{0:T(128)} %bitcast.12.nt, s32[18432]{0:T(1024)} %get-tuple-element.176.idx, f32[144,128]{1,0:T(8,128)} %copy-done.10, ...), custom_call_target="tpu_custom_call" | custom-call | flops 19327352832 | bytes 37748736 | tf_op jit(solution)/shard_map/experts_forward/pallas_call | solution.py:254
  144.1 7.1 sort.31
  155.2 46.2 %collective-permute-done.3 = f32[1024,512]{1,0:T(8,128)S(1)} collective-permute-done((f32[1024,512]{1,0:T(8,128)}, f32[1024,512]{1,0:T(8,128)S(1)}, u32[]{:S(2)}, u32[]{:S(2)}) %collective-permute-start.3) | collective-permute-done | bytes 2097184 | tf_op jit(solution)/shard_map/ppermute | solution.py:614
  203.8 1.3 reshape.763.u_own
  205.5 22.7 %collective-permute-done.4.u_oth = bf16[1024,4,128]{2,1,0:T(4,128)(2,1)S(1)} collective-permute-done((bf16[1024,4,128]{2,1,0:T(4,128)(2,1)}, bf16[1024,4,128]{2,1,0:T(4,128)(2,1)S(1)}, u32[]{:S(2)}, u32[]{:S(2)}) %collective-permute-start.4) | collective-permute-done | bytes 1048608 | tf_op jit(solution)/shard_map/ppermute | solution.py:614
  234.0 58.9 %experts_backward.2 = (f32[1024,512]{1,0:T(8,128)}, f32[1024,512]{1,0:T(8,128)}, f32[1024,512]{1,0:T(8,128)}, f32[1024,512]{1,0:T(8,128)}) custom-call(s32[242]{0:T(256)} %copy-done.33, s32[242]{0:T(256)} %and_convert_fusion.1.tf, s32[242]{0:T(256)} %get-tuple-element.186.tr, s32[242]{0:T(256)} %get-tuple-element.185.tn, s32[1]{0:T(128)} %bitcast.27.nt, ...), custom_call_target="tpu_custom_call" | custom-call | flops 90194313216 | bytes 37748736 | tf_op jit(solution)/shard_map/experts_backward/pallas_call | solution.py:254
  292.8 3.5 collective-permute-start.5
  296.3 42.8 %collective-permute-done.5 = f32[1024,512]{1,0:T(8,128)S(1)} collective-permute-done((f32[1024,512]{1,0:T(8,128)}, f32[1024,512]{1,0:T(8,128)S(1)}, u32[]{:S(2)}, u32[]{:S(2)}) %collective-permute-start.5) | collective-permute-done | bytes 2097184 | tf_op jit(solution)/shard_map/ppermute | solution.py:614
  339.0 2.3 add_convert_fusion.4
  349.4 1.8 collective-permute-start.6
  352.2 19.0 %collective-permute-done.6.d_oth = bf16[1024,4,128]{2,1,0:T(4,128)(2,1)} collective-permute-done((bf16[1024,4,128]{2,1,0:T(4,128)(2,1)}, bf16[1024,4,128]{2,1,0:T(4,128)(2,1)}, u32[]{:S(2)}, u32[]{:S(2)}) %collective-permute-start.6) | collective-permute-done | bytes 1048608 | tf_op jit(solution)/shard_map/ppermute | solution.py:614
  371.2 55.6 %experts_backward.3 = (f32[1024,512]{1,0:T(8,128)}, f32[1024,512]{1,0:T(8,128)}) custom-call(s32[242]{0:T(256)} %copy-done.32, s32[242]{0:T(256)} %and_convert_fusion.tf, s32[242]{0:T(256)} %get-tuple-element.184.tr, s32[242]{0:T(256)} %get-tuple-element.183.tn, s32[1]{0:T(128)} %bitcast.30.nt, s32[18432]{0:T(1024)} %get-tuple-element.175.idx, ...), custom_call_target="tpu_custom_call" | custom-call | flops 51539607552 | bytes 37748736 | tf_op jit(solution)/shard_map/experts_backward/pallas_call | solution.py:254
  427.9 13.1 %merge_tables.1 = (s32[2,32,32,128]{3,2,1,0:T(8,128)}, f32[2,32,32,128]{3,2,1,0:T(8,128)}) custom-call(s32[2048]{0:T(1024)} %bitcast.231, s32[64]{0:T(128)} %reshape.769.exps, f32[8,2,2,152,128]{4,3,2,1,0:T(8,128)} %bitcast.237), custom_call_target="tpu_custom_call" | custom-call | flops 1000000000 | bytes 2490368 | tf_op jit(solution)/shard_map/merge_tables/pallas_call | solution.py:315
  444.2 2.0 collective-permute-start.7
  447.2 28.4 %collective-permute-done.8 = f32[1024,512]{1,0:T(8,128)} collective-permute-done((f32[1024,512]{1,0:T(8,128)}, f32[1024,512]{1,0:T(8,128)}, u32[]{:S(2)}, u32[]{:S(2)}) %collective-permute-start.8) | collective-permute-done | bytes 2097184 | tf_op jit(solution)/shard_map/ppermute | solution.py:614
  475.7 2.9 add_convert_fusion.1
  479.6 1.7 add_convert_fusion
  482.4 62.0 %weight_grads.4 = (bf16[2,64,192,512]{3,2,1,0:T(8,128)(2,1)}, bf16[2,64,192,512]{3,2,1,0:T(8,128)(2,1)}, bf16[2,64,192,512]{3,2,1,0:T(8,128)(2,1)}, bf16[16,192,...) custom-call(s32[16]{0:T(128)} %get-tuple-element.204.exps, ...), custom_call_target="tpu_custom_call" | custom-call | flops 77309411328 | bytes 61865984 | tf_op jit(solution)/shard_map/weight_grads/pallas_call | solution.py:462
  545.1 57.0 %weight_grads.5 = (bf16[2,64,192,512]{3,2,1,0:T(8,128)(2,1)}, bf16[2,64,192,512]{3,2,1,0:T(8,128)(2,1)}, bf16[2,64,192,512]{3,2,1,0:T(8,128)(2,1)}, bf16[16,192,...) custom-call(s32[16]{0:T(128)} %get-tuple-element.205.exps, ...), custom_call_target="tpu_custom_call", output_to_operand_aliasing={{0}: (12, {}), {1}: (13, {}), {2}: (14, {})} | custom-call | flops 77309411328 | bytes 61865984 | tf_op jit(solution)/shard_map/weight_grads/pallas_call | solution.py:462
  602.0 6.2 collective-permute-start.15
  608.3 67.2 %weight_grads.6 = (bf16[2,64,192,512]{3,2,1,0:T(8,128)(2,1)}, bf16[2,64,192,512]{3,2,1,0:T(8,128)(2,1)}, bf16[2,64,192,512]{3,2,1,0:T(8,128)(2,1)}, bf16[16,192,...) custom-call(s32[16]{0:T(128)} %get-tuple-element.210.exps, ...), custom_call_target="tpu_custom_call", output_to_operand_aliasing={{0}: (12, {}), {1}: (13, {}), {2}: (14, {})} | custom-call | flops 77309411328 | bytes 61865984 | tf_op jit(solution)/shard_map/weight_grads/pallas_call | solution.py:462
  676.7 61.7 %weight_grads.7 = (bf16[2,64,192,512]{3,2,1,0:T(8,128)(2,1)}, bf16[2,64,192,512]{3,2,1,0:T(8,128)(2,1)}, bf16[2,64,192,512]{3,2,1,0:T(8,128)(2,1)}, bf16[16,192,...) custom-call(s32[16]{0:T(128)} %get-tuple-element.211.exps, ...), custom_call_target="tpu_custom_call", output_to_operand_aliasing={{0}: (12, {}), {1}: (13, {}), {2}: (14, {})} | custom-call | flops 77309411328 | bytes 61865984 | tf_op jit(solution)/shard_map/weight_grads/pallas_call | solution.py:462
  740.0 2.0 fusion.1
  744.5 3.3 add_convert_fusion.2
  747.8 61.3 %all-reduce.10.cloned.1.call-done = bf16[2,512,512]{1,2,0:T(8,128)(2,1)} async-done(((bf16[2,512,512]{1,2,0:T(8,128)(2,1)}), bf16[2,512,512]{1,2,0:T(8,128)(2,1)}) %all-reduce.10.cloned.1.call-update) | async-done | bytes 1048592 | tf_op jit(solution)/shard_map/psum | solution.py:707
  809.1 2.3 copy.94
  811.4 8.2 merge_half.4
  819.6 8.2 merge_half.5
  827.8 8.2 merge_half.6
  836.0 8.2 merge_half.7
  (262 shorter events, 61.8 us)
Async XLA Ops:
  8.0 340.2 %all-gather.27.cloned.1.call-start = ((), (), s32[]{:S(2)}) async-start(), calls=%async_computation.9 | async-start | bytes 2801664 | tf_op jit(solution)/shard_map/all_gather | solution.py:666
  10.8 45.3 %copy-start = (bf16[1024,4,128]{2,1,0:T(4,128)(2,1)}, bf16[1024,4,128]{2,1,0:T(4,128)(2,1)S(1)}, u32[]{:S(2)}) copy-start(bf16[1024,4,128]{2,1,0:T(4,128)(2,1)S(1)} %reshape.753.u_own) | copy-start | bytes 3145732
  11.6 7.8 collective-permute-start
  14.9 50.8 %collective-permute-start.1 = (bf16[1024,4,128]{2,1,0:T(4,128)(2,1)S(1)}, bf16[1024,4,128]{2,1,0:T(4,128)(2,1)S(1)}, u32[]{:S(2)}, u32[]{:S(2)}) collective-permute-start(bf16[1024,4,128]{2,1,0:T(4,128)(2,1)S(1)} %reshape.753.u_own), channel_id=1, source_target_pairs={{0,8},{8,0},{1,9},{9,1},{2,10},{10,2},{3,11},{11,3},{4,12},{12,4},... | collective-permute-start | bytes 3145736 | tf_op jit(solution)/shard_map/ppermute | solution.py:614
  16.3 87.2 %copy-start.3 = (bf16[1024,4,128]{2,1,0:T(4,128)(2,1)}, bf16[1024,4,128]{2,1,0:T(4,128)(2,1)S(1)}, u32[]{:S(2)}) copy-start(bf16[1024,4,128]{2,1,0:T(4,128)(2,1)S(1)} %reshape.760.d_own) | copy-start | bytes 3145732
  16.3 87.2 %collective-permute-start.2 = (bf16[1024,4,128]{2,1,0:T(4,128)(2,1)S(1)}, bf16[1024,4,128]{2,1,0:T(4,128)(2,1)}, u32[]{:S(2)}, u32[]{:S(2)}) collective-permute-start(bf16[1024,4,128]{2,1,0:T(4,128)(2,1)S(1)} %reshape.760.d_own), channel_id=1, source_target_pairs={{0,8},{8,0},{1,9},{9,1},{2,10},{10,2},{3,11},{11,3},{4,12},{12,4},... | collective-permute-start | bytes 3145736 | tf_op jit(solution)/shard_map/ppermute | solution.py:614
  23.7 21.2 %copy-start.26 = (s32[64]{0:T(128)}, s32[64]{0:T(128)S(1)}, u32[]{:S(2)}) copy-start(s32[64]{0:T(128)S(1)} %reduce.4) | copy-start | bytes 772
  35.4 31.3 %copy-start.23 = (s32[200]{0:T(256)}, s32[200]{0:T(256)S(1)}, u32[]{:S(2)}) copy-start(s32[200]{0:T(256)S(1)} %broadcast_minimum_fusion.2.te) | copy-start | bytes 2404
  103.5 37.0 %copy-start.18 = (f32[2,2,8,1024]{3,2,0,1:T(8,128)S(1)}, f32[2,2,8,1024]{3,2,0,1:T(8,128)}, u32[]{:S(2)}) copy-start(f32[2,2,8,1024]{3,2,0,1:T(8,128)} %fusion.19) | copy-start | bytes 393220
  103.5 49.4 %copy-start.17 = (f32[1,2,152,128]{3,2,1,0:T(8,128)S(1)}, f32[1,2,152,128]{3,2,1,0:T(8,128)}, u32[]{:S(2)}) copy-start(f32[1,2,152,128]{3,2,1,0:T(8,128)} %maximum_bitcast_fusion) | copy-start | bytes 466948
  140.5 60.9 %copy-start.2 = (f32[1024,512]{1,0:T(8,128)S(1)}, f32[1024,512]{1,0:T(8,128)}, u32[]{:S(2)}) copy-start(f32[1024,512]{1,0:T(8,128)} %experts_forward.3) | copy-start | bytes 6291460
  140.5 60.9 %copy-start.8 = (bf16[1024,512]{1,0:T(8,128)(2,1)S(1)}, bf16[1024,512]{1,0:T(8,128)(2,1)}, u32[]{:S(2)}) copy-start(bf16[1024,512]{1,0:T(8,128)(2,1)} %copy-done.7) | copy-start | bytes 3145732
  152.8 49.3 %copy-start.19 = (f32[144,128]{1,0:T(8,128)}, f32[144,128]{1,0:T(8,128)S(1)}, u32[]{:S(2)}) copy-start(f32[144,128]{1,0:T(8,128)S(1)} %pad_bitcast_fusion.2.gates) | copy-start | bytes 221188
  153.6 328.8 %all-gather.23.cloned.1.call-start = ((), (), s32[]{:S(2)}) async-start(), calls=%async_computation.7 | async-start | bytes 9437184 | tf_op jit(solution)/shard_map/all_gather | solution.py:617
  154.4 328.0 %all-gather.25.cloned.1.call-start = ((), (), s32[]{:S(2)}) async-start(), calls=%async_computation.8 | async-start | bytes 9437184 | tf_op jit(solution)/shard_map/all_gather | solution.py:617
  155.1 327.3 %all-gather.19.cloned.1.call-start = ((), (), s32[]{:S(2)}) async-start(), calls=%async_computation.5 | async-start | bytes 9437184 | tf_op jit(solution)/shard_map/all_gather | solution.py:617
  155.2 47.9 %copy-start.35 = (bf16[2,512,512]{2,1,0:T(8,128)(2,1)S(1)}, bf16[2,512,512]{2,1,0:T(8,128)(2,1)}, u32[]{:S(2)}) copy-start(bf16[2,512,512]{2,1,0:T(8,128)(2,1)} %param.12) | copy-start | bytes 3145732
  155.2 46.2 %collective-permute-start.3 = (f32[1024,512]{1,0:T(8,128)}, f32[1024,512]{1,0:T(8,128)S(1)}, u32[]{:S(2)}, u32[]{:S(2)}) collective-permute-start(f32[1024,512]{1,0:T(8,128)} %experts_forward.2), channel_id=1, source_target_pairs={{0,8},{8,0},{1,9},{9,1},{2,10},{10,2},{3,11},{11,3},{4,12},{12,4},... | collective-permute-start | bytes 6291464 | tf_op jit(solution)/shard_map/ppermute | solution.py:614
  203.8 26.7 %copy-start.5 = (bf16[1024,512]{1,0:T(8,128)(2,1)}, bf16[1024,512]{1,0:T(8,128)(2,1)S(1)}, u32[]{:S(2)}) copy-start(bf16[1024,512]{1,0:T(8,128)(2,1)S(1)} %add_convert_fusion.5) | copy-start | bytes 3145732
  203.8 27.6 %copy-start.27 = (s32[64]{0:T(128)S(1)}, s32[64]{0:T(128)}, u32[]{:S(2)}) copy-start(s32[64]{0:T(128)} %reduce.10) | copy-start | bytes 772
  205.1 277.3 %all-gather.21.cloned.1.call-start = ((), (), s32[]{:S(2)}) async-start(), calls=%async_computation.6 | async-start | bytes 9437184 | tf_op jit(solution)/shard_map/all_gather | solution.py:617
  205.2 23.0 %collective-permute-start.4 = (bf16[1024,4,128]{2,1,0:T(4,128)(2,1)}, bf16[1024,4,128]{2,1,0:T(4,128)(2,1)S(1)}, u32[]{:S(2)}, u32[]{:S(2)}) collective-permute-start(bf16[1024,4,128]{2,1,0:T(4,128)(2,1)} %reshape.763.u_own), channel_id=1, source_target_pairs={{0,8},{8,0},{1,9},{9,1},{2,10},{10,2},{3,11},{11,3},{4,12},{12,4},... | collective-permute-start | bytes 3145736 | tf_op jit(solution)/shard_map/ppermute | solution.py:614
  229.2 379.1 %all-gather.11.cloned.1.call-start = ((), (), s32[]{:S(2)}) async-start(), calls=%async_computation.1 | async-start | bytes 9437184 | tf_op jit(solution)/shard_map/all_gather | solution.py:617
  229.7 378.5 %all-gather.13.cloned.1.call-start = ((), (), s32[]{:S(2)}) async-start(), calls=%async_computation.2 | async-start | bytes 9437184 | tf_op jit(solution)/shard_map/all_gather | solution.py:617
  230.5 377.8 %all-gather.15.cloned.1.call-start = ((), (), s32[]{:S(2)}) async-start(), calls=%async_computation.3 | async-start | bytes 9437184 | tf_op jit(solution)/shard_map/all_gather | solution.py:617
  234.0 105.1 %copy-start.4 = (bf16[1024,512]{1,0:T(8,128)(2,1)S(1)}, bf16[1024,512]{1,0:T(8,128)(2,1)}, u32[]{:S(2)}) copy-start(bf16[1024,512]{1,0:T(8,128)(2,1)} %param.9) | copy-start | bytes 3145732
  292.8 46.2 %collective-permute-start.5 = (f32[1024,512]{1,0:T(8,128)}, f32[1024,512]{1,0:T(8,128)S(1)}, u32[]{:S(2)}, u32[]{:S(2)}) collective-permute-start(f32[1024,512]{1,0:T(8,128)} %get-tuple-element.72), channel_id=1, source_target_pairs={{0,8},{8,0},{1,9},{9,1},{2,10},{10,2},{3,11},{11,3},{4,12},{12,4},... | collective-permute-start | bytes 6291464 | tf_op jit(solution)/shard_map/ppermute | solution.py:614
  344.3 264.0 %all-gather.17.cloned.1.call-start = ((), (), s32[]{:S(2)}) async-start(), calls=%async_computation.4 | async-start | bytes 9437184 | tf_op jit(solution)/shard_map/all_gather | solution.py:617
  345.7 25.5 %copy-start.32 = (s32[242]{0:T(256)}, s32[242]{0:T(256)S(1)}, u32[]{:S(2)}) copy-start(s32[242]{0:T(256)S(1)} %broadcast_minimum_fusion.te) | copy-start | bytes 2908
  349.1 77.7 %copy-start.22 = (s32[8,2,1,1,128]{4,3,2,1,0:T(1,128)}, s32[8,2,1,1,128]{4,3,2,1,0:T(1,128)S(1)}, u32[]{:S(2)}) copy-start(s32[8,2,1,1,128]{4,3,2,1,0:T(1,128)S(1)} %slice_convert_fusion) | copy-start | bytes 24580
  349.4 21.8 %collective-permute-start.6 = (bf16[1024,4,128]{2,1,0:T(4,128)(2,1)}, bf16[1024,4,128]{2,1,0:T(4,128)(2,1)}, u32[]{:S(2)}, u32[]{:S(2)}) collective-permute-start(bf16[1024,4,128]{2,1,0:T(4,128)(2,1)} %reshape.764.d_own), channel_id=1, source_target_pairs={{0,8},{8,0},{1,9},{9,1},{2,10},{10,2},{3,11},{11,3},{4,12},{12,4},... | collective-permute-start | bytes 3145736 | tf_op jit(solution)/shard_map/ppermute | solution.py:614
  426.8 48.9 %collective-permute-start.8 = (f32[1024,512]{1,0:T(8,128)}, f32[1024,512]{1,0:T(8,128)}, u32[]{:S(2)}, u32[]{:S(2)}) collective-permute-start(f32[1024,512]{1,0:T(8,128)} %get-tuple-element.75), channel_id=1, source_target_pairs={{0,8},{8,0},{1,9},{9,1},{2,10},{10,2},{3,11},{11,3},{4,12},{12,4},... | collective-permute-start | bytes 6291464 | tf_op jit(solution)/shard_map/ppermute | solution.py:614
  444.2 231.3 %collective-permute-start.7 = (f32[1024,512]{1,0:T(8,128)}, f32[1024,512]{1,0:T(8,128)}, u32[]{:S(2)}, u32[]{:S(2)}) collective-permute-start(f32[1024,512]{1,0:T(8,128)} %get-tuple-element.73), channel_id=1, source_target_pairs={{0,8},{8,0},{1,9},{9,1},{2,10},{10,2},{3,11},{11,3},{4,12},{12,4},... | collective-permute-start | bytes 6291464 | tf_op jit(solution)/shard_map/ppermute | solution.py:614
  446.3 362.8 %all-reduce.10.cloned.1.call-start = ((), (), s32[]{:S(2)}) async-start(), calls=%async_computation | async-start | bytes 2097152 | tf_op jit(solution)/shard_map/psum | solution.py:707
  544.5 131.2 %collective-permute-start.18 = (bf16[16,192,512]{2,1,0:T(8,128)(2,1)}, bf16[16,192,512]{2,1,0:T(8,128)(2,1)}, u32[]{:S(2)}, u32[]{:S(2)}) collective-permute-start(bf16[16,192,512]{2,1,0:T(8,128)(2,1)} %get-tuple-element.100), channel_id=1, source_target_pairs={{0,1},{1,0},{2,3},{3,2},{4,5},{5,4},{6,7},{7,6},{8,9},{9,8},{10,11... | collective-permute-start | bytes 9437192 | tf_op jit(solution)/shard_map/ppermute | solution.py:687
  544.5 131.6 %collective-permute-start.19 = (bf16[16,192,512]{2,1,0:T(8,128)(2,1)}, bf16[16,192,512]{2,1,0:T(8,128)(2,1)}, u32[]{:S(2)}, u32[]{:S(2)}) collective-permute-start(bf16[16,192,512]{2,1,0:T(8,128)(2,1)} %get-tuple-element.101), channel_id=1, source_target_pairs={{0,1},{1,0},{2,3},{3,2},{4,5},{5,4},{6,7},{7,6},{8,9},{9,8},{10,11... | collective-permute-start | bytes 9437192 | tf_op jit(solution)/shard_map/ppermute | solution.py:687
  545.0 131.2 %collective-permute-start.20 = (bf16[16,192,512]{2,1,0:T(8,128)(2,1)}, bf16[16,192,512]{2,1,0:T(8,128)(2,1)}, u32[]{:S(2)}, u32[]{:S(2)}) collective-permute-start(bf16[16,192,512]{2,1,0:T(8,128)(2,1)} %get-tuple-element.102), channel_id=1, source_target_pairs={{0,1},{1,0},{2,3},{3,2},{4,5},{5,4},{6,7},{7,6},{8,9},{9,8},{10,11... | collective-permute-start | bytes 9437192 | tf_op jit(solution)/shard_map/ppermute | solution.py:687
  602.0 74.6 %collective-permute-start.15 = (bf16[16,192,512]{2,1,0:T(8,128)(2,1)}, bf16[16,192,512]{2,1,0:T(8,128)(2,1)}, u32[]{:S(2)}, u32[]{:S(2)}) collective-permute-start(bf16[16,192,512]{2,1,0:T(8,128)(2,1)} %get-tuple-element.97), channel_id=1, source_target_pairs={{0,1},{1,0},{2,3},{3,2},{4,5},{5,4},{6,7},{7,6},{8,9},{9,8},{10,11... | collective-permute-start | bytes 9437192 | tf_op jit(solution)/shard_map/ppermute | solution.py:687
  675.5 62.9 %collective-permute-start.16 = (bf16[16,192,512]{2,1,0:T(8,128)(2,1)}, bf16[16,192,512]{2,1,0:T(8,128)(2,1)}, u32[]{:S(2)}, u32[]{:S(2)}) collective-permute-start(bf16[16,192,512]{2,1,0:T(8,128)(2,1)} %get-tuple-element.98), channel_id=1, source_target_pairs={{0,1},{1,0},{2,3},{3,2},{4,5},{5,4},{6,7},{7,6},{8,9},{9,8},{10,11... | collective-permute-start | bytes 9437192 | tf_op jit(solution)/shard_map/ppermute | solution.py:687
  675.6 63.2 %collective-permute-start.17 = (bf16[16,192,512]{2,1,0:T(8,128)(2,1)}, bf16[16,192,512]{2,1,0:T(8,128)(2,1)}, u32[]{:S(2)}, u32[]{:S(2)}) collective-permute-start(bf16[16,192,512]{2,1,0:T(8,128)(2,1)} %get-tuple-element.99), channel_id=1, source_target_pairs={{0,1},{1,0},{2,3},{3,2},{4,5},{5,4},{6,7},{7,6},{8,9},{9,8},{10,11... | collective-permute-start | bytes 9437192 | tf_op jit(solution)/shard_map/ppermute | solution.py:687
  676.1 62.9 %collective-permute-start.12 = (bf16[16,192,512]{2,1,0:T(8,128)(2,1)}, bf16[16,192,512]{2,1,0:T(8,128)(2,1)}, u32[]{:S(2)}, u32[]{:S(2)}) collective-permute-start(bf16[16,192,512]{2,1,0:T(8,128)(2,1)} %get-tuple-element.94), channel_id=1, source_target_pairs={{0,1},{1,0},{2,3},{3,2},{4,5},{5,4},{6,7},{7,6},{8,9},{9,8},{10,11... | collective-permute-start | bytes 9437192 | tf_op jit(solution)/shard_map/ppermute | solution.py:687
  676.2 151.6 %collective-permute-start.13 = (bf16[16,192,512]{2,1,0:T(8,128)(2,1)}, bf16[16,192,512]{2,1,0:T(8,128)(2,1)}, u32[]{:S(2)}, u32[]{:S(2)}) collective-permute-start(bf16[16,192,512]{2,1,0:T(8,128)(2,1)} %get-tuple-element.95), channel_id=1, source_target_pairs={{0,1},{1,0},{2,3},{3,2},{4,5},{5,4},{6,7},{7,6},{8,9},{9,8},{10,11... | collective-permute-start | bytes 9437192 | tf_op jit(solution)/shard_map/ppermute | solution.py:687
  676.6 151.2 %collective-permute-start.14 = (bf16[16,192,512]{2,1,0:T(8,128)(2,1)}, bf16[16,192,512]{2,1,0:T(8,128)(2,1)}, u32[]{:S(2)}, u32[]{:S(2)}) collective-permute-start(bf16[16,192,512]{2,1,0:T(8,128)(2,1)} %get-tuple-element.96), channel_id=1, source_target_pairs={{0,1},{1,0},{2,3},{3,2},{4,5},{5,4},{6,7},{7,6},{8,9},{9,8},{10,11... | collective-permute-start | bytes 9437192 | tf_op jit(solution)/shard_map/ppermute | solution.py:687
  676.7 62.7 %copy-start.29 = (s32[32]{0:T(128)S(1)}, s32[32]{0:T(128)}, u32[]{:S(2)}) copy-start(s32[32]{0:T(128)} %get-tuple-element.164) | copy-start | bytes 388
  676.7 63.3 %copy-start.13 = (bf16[1024,512]{1,0:T(8,128)(2,1)S(1)}, bf16[1024,512]{1,0:T(8,128)(2,1)}, u32[]{:S(2)}) copy-start(bf16[1024,512]{1,0:T(8,128)(2,1)} %copy-done.12) | copy-start | bytes 3145732
  738.4 97.6 %collective-permute-start.10 = (bf16[16,192,512]{2,1,0:T(8,128)(2,1)}, bf16[16,192,512]{2,1,0:T(8,128)(2,1)}, u32[]{:S(2)}, u32[]{:S(2)}) collective-permute-start(bf16[16,192,512]{2,1,0:T(8,128)(2,1)} %get-tuple-element.92), channel_id=1, source_target_pairs={{0,1},{1,0},{2,3},{3,2},{4,5},{5,4},{6,7},{7,6},{8,9},{9,8},{10,11... | collective-permute-start | bytes 9437192 | tf_op jit(solution)/shard_map/ppermute | solution.py:687
  738.8 97.1 %collective-permute-start.11 = (bf16[16,192,512]{2,1,0:T(8,128)(2,1)}, bf16[16,192,512]{2,1,0:T(8,128)(2,1)}, u32[]{:S(2)}, u32[]{:S(2)}) collective-permute-start(bf16[16,192,512]{2,1,0:T(8,128)(2,1)} %get-tuple-element.93), channel_id=1, source_target_pairs={{0,1},{1,0},{2,3},{3,2},{4,5},{5,4},{6,7},{7,6},{8,9},{9,8},{10,11... | collective-permute-start | bytes 9437192 | tf_op jit(solution)/shard_map/ppermute | solution.py:687
  739.0 97.0 %collective-permute-start.9 = (bf16[16,192,512]{2,1,0:T(8,128)(2,1)}, bf16[16,192,512]{2,1,0:T(8,128)(2,1)}, u32[]{:S(2)}, u32[]{:S(2)}) collective-permute-start(bf16[16,192,512]{2,1,0:T(8,128)(2,1)} %get-tuple-element.91), channel_id=1, source_target_pairs={{0,1},{1,0},{2,3},{3,2},{4,5},{5,4},{6,7},{7,6},{8,9},{9,8},{10,11... | collective-permute-start | bytes 9437192 | tf_op jit(solution)/shard_map/ppermute | solution.py:687
  (22 other events, 99.6 us)
Sparse Core Ops, SparseCore 0:
  153.8 26.2 all-gather.26
  181.8 50.5 all-gather.22
  234.3 50.4 all-gather.24
  287.1 50.4 all-gather.18
  339.3 50.4 all-gather.20
  392.1 50.4 all-gather.10
  445.1 50.5 all-gather.12
  497.5 51.0 all-gather.14
  550.5 49.9 all-gather.16
Sparse Core Ops, SparseCore 1:
  743.9 65.1 all-reduce.9

commit v7 on v6

v7 whole, which is shorter than its diff:
```python
import functools
import math

import jax
import jax.numpy as jnp
from jax import lax
from jax.experimental import pallas as pl
from jax.experimental.pallas import tpu as pltpu
from jax.sharding import PartitionSpec as P


CAP_FACTOR = 3
LANES = 128
TILE = 96
HALF_TILE = 64
WTILE = 256
PITCH = 9
BATCH = 16
SLOTS = 8
PAGE = 1024
VMEM_LIMIT = 62 * 2**20


def cdiv(a, b):
    return (a + b - 1) // b


def nt_dot(a, b):
    return lax.dot_general(a, b, (((1,), (1,)), ((), ())), preferred_element_type=jnp.float32)


def tn_dot(a, b):
    return lax.dot_general(a, b, (((0,), (0,)), ((), ())), preferred_element_type=jnp.float32)


def nn_dot(a, b):
    return lax.dot_general(a, b, (((1,), (0,)), ((), ())), preferred_element_type=jnp.float32)


def clear(ref):
    step = next(n for n in (64, 48, 32, 16, 8) if ref.shape[0] % n == 0)

    def one(q, carry):
        ref[pl.ds(pl.multiple_of(q * step, step), step), :] = jnp.zeros((step, ref.shape[1]), ref.dtype)
        return carry

    lax.fori_loop(0, ref.shape[0] // step, one, 0)


def add_rows(acc, vals_ref, idx, row, tile, pitch, width):
    for b in range(0, tile, BATCH):
        at = [pl.multiple_of(idx[row + b + r], 4) for r in range(BATCH)]
        vals = [acc[pl.ds(at[r], width), :] + vals_ref[pl.ds((b + r) * pitch, width), :] for r in range(BATCH)]
        for r in reversed(range(BATCH)):
            acc[pl.ds(at[r], width), :] = vals[r]


def spread_column(row):
    return jnp.broadcast_to(row, (LANES, LANES)).T


def tile_gates(gates, row):
    pair = gates[pl.ds(lax.div(row, LANES), 2), :]
    skip = lax.rem(row, LANES)
    pair = pltpu.roll(pair, lax.rem(LANES - skip, LANES), 1)
    lane = lax.broadcasted_iota(jnp.int32, (1, LANES), 1)
    return spread_column(jnp.where(lane < LANES - skip, pair[:1], pair[1:]))


def widen(src, dst, pitch, halves, tok):
    step = 8

    def one(q, carry):
        for r in range(step):
            dst[pl.ds((q * step + r) * pitch, pitch), :] = src[q * step + r].astype(jnp.float32)
        return carry

    lax.fori_loop(halves[0] * tok // step, (halves[-1] + 1) * tok // step, one, 0)


def write_sums(acc, outs, tok, parts, pitch, halves):
    step = min(32, tok)

    def copy_out(q, carry):
        r0 = pl.multiple_of(q * step, step)
        for k in range(parts):
            for out, half in zip(outs, halves):
                first = (half * tok + r0) * pitch + k
                out[pl.ds(r0, step), k * LANES:(k + 1) * LANES] = acc[pl.ds(first, step, stride=pitch), :]
        return carry

    lax.fori_loop(0, tok // step, copy_out, 0)


def expert_copies(weights, buf, sem, layer, e):
    slot = lax.rem(e, SLOTS)
    ff = weights[0].shape[2]
    return [pltpu.make_async_copy(w.at[layer, e], buf.at[slot, pl.ds(k * ff, ff)], sem.at[slot])
            for k, w in enumerate(weights)]


def run_tiles(step, weights, wbuf, wsem, runs, tile, layer, prepare):
    n_local = weights[0].shape[1]
    for e in range(SLOTS - 1):
        for c in expert_copies(weights, wbuf, wsem, layer, e):
            c.start()
    prepare()
    for c in expert_copies(weights, wbuf, wsem, layer, 0):
        c.wait()

    def length(e):
        return runs[n_local + e] - runs[e]

    def add_tiles(e, total):
        return total + jnp.maximum(lax.div(length(e) + tile - 1, tile), 1)

    def one(i, carry):
        (e, row, left), (e1, row1, n1), (e2, row2, n2), row3 = carry

        @pl.when(e1 != e2)
        def _():
            for c in expert_copies(weights, wbuf, wsem, layer, e1):
                c.wait()

        @pl.when((e1 != e2) & (e1 + SLOTS - 2 < n_local))
        def _():
            for c in expert_copies(weights, wbuf, wsem, layer, e1 + SLOTS - 2):
                c.start()

        step(row, (lax.rem(e1, SLOTS), row1), (lax.rem(e2, SLOTS), row2, n2), row3)
        more = left > tile
        e_next = jnp.minimum(e + 1, n_local - 1)
        fresh = jnp.where(e + 1 < n_local, length(e_next), 0)
        ahead = (jnp.where(more, e, e_next), jnp.where(more, row + tile, runs[e_next]), jnp.where(more, left - tile, fresh))
        return ahead, (e, row, jnp.minimum(left, tile)), (e1, row1, n1), row2

    none = (0, 0, 0)
    lax.fori_loop(0, lax.fori_loop(0, n_local, add_tiles, 0) + 3, one, ((0, runs[0], length(0)), none, none, 0))


def token_body(runs, idx, gates, *refs, layer, tok, parts, tile, halves, backward):
    n_in = 4 if backward else 2
    sources, weights, outs, refs = refs[:n_in], refs[n_in:n_in + 3], refs[n_in + 3:n_in + 3 + len(halves)], refs[n_in + 3 + len(halves):]
    narrow, wide, rows, vt, acc, mid, wbuf, sem, wsem = refs
    ff = weights[0].shape[2]
    width = parts * n_in // 2
    pitch = width + 1

    def prepare():
        copies = [pltpu.make_async_copy(src, narrow.at[pl.ds(k % 2 * tok, tok), pl.ds(k // 2 * parts, parts)], sem.at[k])
                  for k, src in enumerate(sources) if k % 2 in halves]
        for c in copies:
            c.start()
        for ref in (acc, vt, rows, mid):
            clear(ref)
        for c in copies:
            c.wait()
        widen(narrow, wide, width, halves, tok)

    def column(k):
        return rows[pl.ds(k, tile, stride=pitch), :]

    def step(row, here, before, done):
        slot, row1 = here
        slot2, row2, n2 = before
        old = wbuf[slot2, :2 * ff] if backward else wbuf[slot2, 2 * ff:]
        v = tn_dot(mid[...], old).astype(jnp.bfloat16).astype(jnp.float32)
        u = jnp.concatenate([column(k) for k in range(parts)], axis=1).astype(jnp.bfloat16)
        ab = nt_dot(wbuf[slot, :2 * ff], u)
        if backward:
            gate = tile_gates(gates, row1)[:tile]
            c = jnp.concatenate([(column(parts + k) * gate).astype(jnp.bfloat16) for k in range(parts)], axis=1)
            dh = nt_dot(wbuf[slot, 2 * ff:], c)
        add_rows(acc, vt, idx, done, tile, parts + 1, parts)
        for r in range(tile):
            rows[pl.ds(pitch * r, width), :] = wide[pl.ds(pl.multiple_of(idx[row + r], width), width), :]
        live = lax.broadcasted_iota(jnp.int32, (tile, LANES), 0) < n2
        gate = tile_gates(gates, row2)[:tile]
        for k in range(parts):
            v_k = jnp.where(live, v[:, k * LANES:(k + 1) * LANES] * gate, 0.0)
            vt[pl.ds(k, tile, stride=parts + 1), :] = v_k
        a, b = ab[:ff], ab[ff:]
        s = jax.nn.sigmoid(a)
        act = a * s
        if backward:
            mid[:ff] = (dh * b * (s * (1.0 + a * (1.0 - s)))).astype(jnp.bfloat16)
            mid[ff:] = (dh * act).astype(jnp.bfloat16)
        else:
            mid[...] = (act * b).astype(jnp.bfloat16)

    run_tiles(step, weights, wbuf, wsem, runs, tile, layer, prepare)
    write_sums(acc, outs, tok, parts, width, halves)


def token_kernel(layer, runs, table, slabs, weights, halves=(0, 1)):
    idx, gates = table
    tok, parts, _ = slabs[0].shape
    _, n_local, ff, d_model = weights[0].shape
    backward = len(slabs) > 2
    tile = TILE if len(halves) == 2 else HALF_TILE
    width = parts * len(slabs) // 2
    rows_spec = pl.BlockSpec((tok, d_model), lambda i, *_: (0, 0))
    any_spec = pl.BlockSpec(memory_space=pl.ANY)
    tile_rows = cdiv(tile * (width + 1), 16) * 16
    work = (4 if backward else 3) * len(halves)
    return pl.pallas_call(
        functools.partial(token_body, layer=layer, tok=tok, parts=parts, tile=tile, halves=halves, backward=backward),
        grid_spec=pltpu.PrefetchScalarGridSpec(
            num_scalar_prefetch=2,
            grid=(1,),
            in_specs=[pl.BlockSpec(gates.shape, lambda i, *_: (0, 0))] + [any_spec] * (len(slabs) + 3),
            out_specs=[rows_spec] * len(halves),
            scratch_shapes=[pltpu.VMEM((2 * tok, width, LANES), jnp.bfloat16), pltpu.VMEM((2 * tok * width, LANES), jnp.float32),
                            pltpu.VMEM((tile_rows, LANES), jnp.float32), pltpu.VMEM((tile_rows, LANES), jnp.float32),
                            pltpu.VMEM((2 * tok * width, LANES), jnp.float32),
                            pltpu.VMEM((2 * ff if backward else ff, tile), jnp.bfloat16),
                            pltpu.VMEM((SLOTS, 3 * ff, d_model), jnp.bfloat16),
                            pltpu.SemaphoreType.DMA((len(slabs),)), pltpu.SemaphoreType.DMA((SLOTS,))],
        ),
        out_shape=[jax.ShapeDtypeStruct((tok, d_model), jnp.float32)] * len(halves),
        compiler_params=pltpu.CompilerParams(dimension_semantics=("arbitrary",), vmem_limit_bytes=VMEM_LIMIT),
        cost_estimate=pl.CostEstimate(flops=work * 2 * 8 * tok * d_model * ff * 4,
                                      bytes_accessed=3 * n_local * ff * d_model * 2, transcendentals=0),
        name="experts_backward" if backward else "experts_forward",
    )(runs, idx, gates, *slabs, *weights)


def merge_tables_body(st, exps, layers, table, idx_ref, gate_ref, buf, *, out_rows, pad_row):
    group = idx_ref.shape[0]

    def one(q, carry):
        item = pl.program_id(0) * group + q
        merge_expert(exps[item], layers[item], st, table, idx_ref.at[q], gate_ref.at[q], buf, out_rows, pad_row)
        return carry

    lax.fori_loop(0, group, one, 0)


def merge_expert(exp, layer, st, table, idx_out, gate_out, buf, out_rows, pad_row):
    src, n_layers = table.shape[:2]
    buf[0] = jnp.full(buf.shape[1:], float(pad_row), jnp.float32)
    buf[1] = jnp.zeros(buf.shape[1:], jnp.float32)
    row = lax.broadcasted_iota(jnp.int32, (8, LANES), 0)
    lane = lax.broadcasted_iota(jnp.int32, (8, LANES), 1)
    off = 0
    for d in range(src):
        at = (d * n_layers + layer) * LANES + exp
        first = st[at]
        count = st[at + 1] - first
        to = lax.rem(off, LANES) + LANES
        shift = to - lax.rem(first, LANES)
        over = lax.rem(shift, LANES)
        start = lax.div(off, LANES)
        place = row * LANES + lane
        take = (place >= to) & (place < to + count)
        for kind in range(2):
            x = table[d, layer, kind, pl.ds(lax.div(first, LANES), 8), :]
            x = pltpu.roll(pltpu.roll(x, over, 1), lax.div(shift, LANES), 0)
            x = jnp.where(lane >= over, x, pltpu.roll(x, 1, 0))
            old = buf[kind, pl.ds(start, 8), :]
            buf[kind, pl.ds(start, 8), :] = jnp.where(take, x, old)
        off = off + count
    idx_out[...] = buf[0, pl.ds(1, out_rows), :].astype(jnp.int32)
    gate_out[...] = buf[1, pl.ds(1, out_rows), :]


def merge_tables(shared, starts, exps, layers, out_rows, pad_row):
    n_items = exps.shape[0]
    group = math.gcd(n_items, 8)
    out = pl.BlockSpec((group, out_rows, LANES), lambda g, *_: (g, 0, 0))
    return pl.pallas_call(
        functools.partial(merge_tables_body, out_rows=out_rows, pad_row=pad_row),
        grid_spec=pltpu.PrefetchScalarGridSpec(
            num_scalar_prefetch=3,
            grid=(n_items // group,),
            in_specs=[pl.BlockSpec(shared.shape, lambda g, *_: (0,) * shared.ndim)],
            out_specs=[out] * 2,
            scratch_shapes=[pltpu.VMEM((2, out_rows + 16, LANES), jnp.float32)],
        ),
        out_shape=[jax.ShapeDtypeStruct((n_items, out_rows, LANES), jnp.int32),
                   jax.ShapeDtypeStruct((n_items, out_rows, LANES), jnp.float32)],
        compiler_params=pltpu.CompilerParams(dimension_semantics=("arbitrary",)),
        cost_estimate=pl.CostEstimate(flops=10**9, bytes_accessed=4 * shared.size, transcendentals=0),
        name="merge_tables",
    )(starts.reshape(-1), exps, layers, shared)


def weight_grad_body(exps, tiles, begins, u_own, u_oth, d_own, d_oth, idx_all, gate_ref, *refs, parts, n_exp, n_alias, first_list,
                     page):
    g_ref, up_ref, w_ref = refs[:3]
    (dg_ref, du_ref, dw_ref, og_ref, ou_ref, ow_ref,
     uds, rows, u0, c0, d0, h0, u1, c1, d1, h1, gacc, wacc, idx_s, sem, tsem) = refs[3 + n_alias:]
    e = pl.program_id(0)
    ff = g_ref.shape[2]
    slots = 3
    both = ((u0, c0, d0, h0), (u1, c1, d1, h1))

    def table_copy(exp):
        slot = lax.rem(exp, slots)
        at = pl.multiple_of((first_list + exp) * page, PAGE)
        to = pl.multiple_of(slot * page, PAGE)
        return pltpu.make_async_copy(idx_all.at[pl.ds(at, page)], idx_s.at[pl.ds(to, page)], tsem.at[slot])

    def gather_row(at, r):
        rows[pl.ds(r * PITCH, 2 * parts), :] = uds[idx_s[at]].astype(jnp.float32)

    def column(first, count, k):
        return rows[pl.ds(first * PITCH + k, count, stride=PITCH), :]

    @pl.when(e == 0)
    def _():
        n_half = u_own.shape[0]
        copies = [pltpu.make_async_copy(src, uds.at[pl.ds((k % 2) * n_half, n_half), pl.ds((k // 2) * parts, parts)], sem.at[k])
                  for k, src in enumerate((u_own, u_oth, d_own, d_oth))]
        for c in copies:
            c.start()
        table_copy(0).start()
        table_copy(1).start()
        n_rows = n_half * 2
        uds[pl.ds(n_rows, 8)] = jnp.zeros((8, 2 * parts, LANES), jnp.bfloat16)
        for ref in (*both[0], *both[1], gacc, wacc):
            clear(ref)
        table_copy(0).wait()
        for c in copies:
            c.wait()

        def first_rows(q, carry):
            for r in range(16):
                gather_row(q * 16 + r, q * 16 + r)
            return carry

        lax.fori_loop(0, WTILE // 16, first_rows, 0)

    @pl.when(e + 1 < n_exp)
    def _():
        table_copy(e + 1).wait()

    @pl.when(e + 2 < n_exp)
    def _():
        table_copy(e + 2).start()

    here = lax.rem(e, slots) * page
    there = lax.rem(jnp.minimum(e + 1, n_exp - 1), slots) * page
    n_tiles = tiles[e]
    begin = begins[e]
    gate_rows = WTILE // LANES

    def compute(j, new, old):
        un, cn, dn, hn = new
        uo, co, do, ho = old
        gacc[...] += nn_dot(do[...], uo[...])
        wacc[...] += nn_dot(ho[...], co[...])
        un[...] = jnp.concatenate([column(0, WTILE, k) for k in range(parts)], axis=1).astype(jnp.bfloat16)
        gates = [spread_column(gate_ref[0, pl.ds(j * gate_rows + q, 1), :]) for q in range(gate_rows)]
        for k in range(parts):
            for q in range(gate_rows):
                d = column(q * LANES, LANES, parts + k)
                cn[q * LANES:(q + 1) * LANES, k * LANES:(k + 1) * LANES] = (d * gates[q]).astype(jnp.bfloat16)
        ab = nt_dot(jnp.concatenate([g_ref[0, 0], up_ref[0, 0]], axis=0), un[...])
        dh = nt_dot(w_ref[0, 0], cn[...])
        nxt = jnp.where(j + 1 < n_tiles, here + (j + 1) * WTILE, there)
        for r in range(WTILE):
            gather_row(nxt + r, r)
        a, b = ab[:ff], ab[ff:]
        s = jax.nn.sigmoid(a)
        act = a * s
        hn[...] = (act * b).astype(jnp.bfloat16)
        dn[:ff] = (dh * b * (s * (1.0 + a * (1.0 - s)))).astype(jnp.bfloat16)
        dn[ff:] = (dh * act).astype(jnp.bfloat16)

    def tile(j, carry):
        odd = lax.rem(begin + j, 2)

        @pl.when(odd == 0)
        def _():
            compute(j, both[0], both[1])

        @pl.when(odd == 1)
        def _():
            compute(j, both[1], both[0])

        @pl.when(j == 0)
        def _():
            dg = gacc[:ff].astype(jnp.bfloat16)
            du = gacc[ff:].astype(jnp.bfloat16)
            dw = wacc[...].astype(jnp.bfloat16)
            dg_ref[0, 0], du_ref[0, 0], dw_ref[0, 0] = dg, du, dw
            og_ref[0], ou_ref[0], ow_ref[0] = dg, du, dw
            gacc[...] = jnp.zeros_like(gacc)
            wacc[...] = jnp.zeros_like(wacc)

        return carry

    lax.fori_loop(0, n_tiles, tile, 0)


def weight_grads(layer, first, exps, tiles, rows, idx_all, gates, weights, full):
    n_half, parts, _ = rows[0].shape
    n_tok = 2 * n_half
    n_layers, n_local, ff, d_model = weights[0].shape
    n_exp = exps.shape[0]
    out_rows = gates.shape[1]
    page = out_rows * LANES
    tiles = jnp.concatenate([tiles, jnp.ones((1,), jnp.int32)])
    begins = jnp.cumsum(tiles) - tiles
    any_spec = pl.BlockSpec(memory_space=pl.ANY)
    mine = pl.BlockSpec((1, 1, ff, d_model), lambda e, exps, *_: (layer, exps[jnp.minimum(e, n_exp - 1)], 0, 0))
    done = pl.BlockSpec((1, 1, ff, d_model), lambda e, exps, *_: (layer, exps[jnp.maximum(e - 1, 0)], 0, 0))
    half = pl.BlockSpec((1, ff, d_model), lambda e, *_: (jnp.maximum(e - 1, 0), 0, 0))
    gate_spec = pl.BlockSpec((1, out_rows, LANES), lambda e, *_: (first + jnp.minimum(e, n_exp - 1), 0, 0))
    aliased = list(full) if full is not None else []
    tile_set = [pltpu.VMEM((WTILE, d_model), jnp.bfloat16)] * 2 + [pltpu.VMEM((2 * ff, WTILE), jnp.bfloat16),
                                                                 pltpu.VMEM((ff, WTILE), jnp.bfloat16)]
    outs = pl.pallas_call(
        functools.partial(weight_grad_body, parts=parts, n_exp=n_exp, n_alias=len(aliased), first_list=first, page=page),
        grid_spec=pltpu.PrefetchScalarGridSpec(
            num_scalar_prefetch=3,
            grid=(n_exp + 1,),
            in_specs=[any_spec] * 5 + [gate_spec] + [mine] * 3 + [any_spec] * len(aliased),
            out_specs=[done] * 3 + [half] * 3,
            scratch_shapes=[pltpu.VMEM((n_tok + 8, 2 * parts, LANES), jnp.bfloat16)]
            + [pltpu.VMEM((WTILE * PITCH + 16, LANES), jnp.float32)] + tile_set * 2
            + [pltpu.VMEM((2 * ff, d_model), jnp.float32), pltpu.VMEM((ff, d_model), jnp.float32),
               pltpu.SMEM((3 * page,), jnp.int32), pltpu.SemaphoreType.DMA((4,)), pltpu.SemaphoreType.DMA((3,))],
        ),
        out_shape=[jax.ShapeDtypeStruct((n_layers, n_local, ff, d_model), jnp.bfloat16)] * 3
        + [jax.ShapeDtypeStruct((n_exp, ff, d_model), jnp.bfloat16)] * 3,
        input_output_aliases={12 + k: k for k in range(len(aliased))},
        compiler_params=pltpu.CompilerParams(dimension_semantics=("arbitrary",), vmem_limit_bytes=VMEM_LIMIT),
        cost_estimate=pl.CostEstimate(flops=6 * n_tok * n_exp * d_model * ff,
                                      bytes_accessed=n_tok * d_model * 4 + 9 * n_exp * ff * d_model * 2, transcendentals=0),
        name="weight_grads",
    )(exps, tiles, begins, *rows, idx_all, gates, *weights, *aliased)
    return outs[:3], outs[3:]


def merge_body(exps, a, b, c, f0, f1, f2, o0, o1, o2, buf, in_sem, out_sem, *, layer, n_exp):
    halves, wholes = (a, b, c), (o0, o1, o2)

    def arrive(k, q):
        return pltpu.make_async_copy(halves[k].at[q], buf.at[k, q], in_sem.at[k, q])

    def leave(k, q):
        return pltpu.make_async_copy(buf.at[k, q], wholes[k].at[layer, exps[q]], out_sem)

    def each(act):
        def one(q, carry):
            for k in range(3):
                act(k, q)
            return carry

        lax.fori_loop(0, n_exp, one, 0)

    def pass_on(k, q):
        arrive(k, q).wait()
        leave(k, q).start()

    each(lambda k, q: arrive(k, q).start())
    each(pass_on)
    each(lambda k, q: leave(k, q).wait())


def merge_half(layer, exps, half, full):
    n_exp, ff, d_model = half[0].shape
    any_spec = pl.BlockSpec(memory_space=pl.ANY)
    return pl.pallas_call(
        functools.partial(merge_body, layer=layer, n_exp=n_exp),
        grid_spec=pltpu.PrefetchScalarGridSpec(
            num_scalar_prefetch=1, grid=(1,), in_specs=[any_spec] * 6, out_specs=[any_spec] * 3,
            scratch_shapes=[pltpu.VMEM((3, n_exp, ff, d_model), jnp.bfloat16), pltpu.SemaphoreType.DMA((3, n_exp)),
                            pltpu.SemaphoreType.DMA]),
        out_shape=[jax.ShapeDtypeStruct(x.shape, x.dtype) for x in full],
        input_output_aliases={4: 0, 5: 1, 6: 2},
        compiler_params=pltpu.CompilerParams(dimension_semantics=("arbitrary",), vmem_limit_bytes=VMEM_LIMIT),
        cost_estimate=pl.CostEstimate(flops=10**9, bytes_accessed=6 * n_exp * ff * d_model * 2, transcendentals=0),
        name="merge_half",
    )(exps, *half, *full)


def route_tables(ids, gates, ep, n_local):
    n_src, top_k, tok = ids.shape
    n = n_src * top_k * tok
    local = ids - ep * n_local
    here = (local >= 0) & (local < n_local)
    group = jnp.where(here, local, n_local).reshape(-1)
    key, gate = lax.sort((group * n + jnp.arange(n, dtype=jnp.int32), gates.reshape(-1)), num_keys=1, is_stable=False)
    copy = key % n
    token = copy // (top_k * tok) * tok + copy % tok
    token = jnp.pad(token, (0, 2 * PAGE))
    gate = jnp.pad(gate, (0, 2 * PAGE)).reshape(-1, LANES)
    lane = jnp.arange(LANES, dtype=jnp.int32)
    bounds = jnp.sum((group[:, None] < lane[None, :]).astype(jnp.int32), axis=0)
    own = jnp.sum((group[:n // n_src, None] == lane[None, :]).astype(jnp.int32), axis=0)
    starts, ends = bounds[:n_local], bounds[1:n_local + 1]
    middle = starts + own[:n_local]
    runs = [jnp.concatenate(x) for x in ((starts, middle), (middle, ends), (starts, ends))]
    return runs, token, gate, bounds


def deal_experts(bounds, n_local, n_lists):
    load = jnp.sum(bounds[:, 1:n_local + 1] - bounds[:, :n_local], axis=0)
    ids = jnp.arange(n_local, dtype=jnp.int32)
    ahead = (load[None, :] > load[:, None]) | ((load[None, :] == load[:, None]) & (ids[None, :] < ids[:, None]))
    rank = jnp.sum(ahead.astype(jnp.int32), axis=1)
    turn, which = jnp.arange(n_local // n_lists)[None, :], jnp.arange(n_lists)[:, None]
    want = n_lists * turn + jnp.where(turn % 2 == 0, which, n_lists - 1 - which)
    pick = (rank[None, None, :] == want[:, :, None]).astype(jnp.int32)
    tiles = jnp.maximum((jnp.sum(pick * load, axis=2) + WTILE - 1) // WTILE, 1)
    return jnp.sum(pick * ids, axis=2), tiles


def after(x, *earlier):
    return lax.optimization_barrier((x, *earlier))[0]


def solution(mesh):
    ep_size = mesh.shape['ep']
    dp_size = mesh.shape['dp']
    tok_spec = P(('dp', 'ep'), None)
    route_spec = P(None, ('dp', 'ep'), None)
    whole_spec = P(None, None, None)
    expert_spec = P(None, 'ep', None, None)
    ep_pairs = [(i, 1 - i) for i in range(ep_size)]
    core_pairs = [(i, i ^ 1) for i in range(dp_size)]
    chip_pairs = [(i, i ^ (2 << i % 2)) for i in range(dp_size)]

    def device_body(tokens, d_out, expert_ids, gate_vals, w_mix, w_gate, w_up, w_down):
        n_layers = w_mix.shape[0]
        n_local = w_gate.shape[1]
        n_experts = n_local * ep_size
        tok, d_model = tokens.shape
        top_k = expert_ids.shape[2]
        parts = d_model // LANES
        cap = cdiv(CAP_FACTOR * tok * top_k, n_experts)
        ep_id = lax.axis_index('ep').astype(jnp.int32)
        dp_id = lax.axis_index('dp').astype(jnp.int32)
        weights = (jnp.swapaxes(w_gate, 2, 3), jnp.swapaxes(w_up, 2, 3), w_down)

        def swap(x):
            return lax.ppermute(x, 'ep', ep_pairs)

        def spread(x):
            return lax.all_gather(x, 'dp', axis=0, tiled=True)

        def trade(x, pairs):
            return [lax.ppermute(y, 'dp', pairs) for y in x]

        def slab(x):
            return x.reshape(tok, parts, LANES)

        def mixed(x, layer):
            return (x.astype(jnp.float32) + jnp.dot(x, w_mix[layer], preferred_element_type=jnp.float32)).astype(jnp.bfloat16)

        ids = jnp.swapaxes(expert_ids, 1, 2)
        gates = jnp.swapaxes(gate_vals, 1, 2)
        mine = jnp.stack([ids.astype(jnp.float32), gates])
        u = mixed(tokens, 0)
        u_slab = slab(u)
        theirs = swap(after(mine, u_slab))
        both = jnp.stack([mine, theirs], 2)
        top = n_layers - 1
        runs, tables, packed = [], [], []

        def add_tables(pair):
            run, token, gate, bounds = route_tables(pair[0].astype(jnp.int32), pair[1], ep_id, n_local)
            runs.append(run)
            tables.append([(token * parts, gate), (token * (2 * parts), gate)])
            spot = lax.div(token, tok) * (dp_size * tok) + dp_id * tok + lax.rem(token, tok)
            first = jnp.concatenate([spot.reshape(-1, LANES), jnp.pad(bounds.reshape(1, LANES), ((0, 7), (0, 0)))])
            packed.append(jnp.stack([first.astype(jnp.float32), jnp.pad(gate, ((0, 8), (0, 0)))]))

        add_tables(both[:, 0])

        x_in, u_slabs, u_others, xs = tokens, [u_slab], [swap(u_slab)], []
        d_slab = slab(d_out)
        d_other = swap(after(d_slab, u_others[0]))
        d_rows = (spread(d_slab), spread(d_other))
        for layer in range(n_layers):
            if layer:
                u = mixed(x_in, layer)
                u_slabs.append(slab(u))
                u_others.append(swap(u_slabs[layer]))
            xs.append(x_in)
            if layer < top:
                other, = token_kernel(layer, runs[layer][1], tables[layer][0], (u_slabs[layer], u_others[layer]), weights, (1,))
                sent = swap(other)
                own, = token_kernel(layer, runs[layer][0], tables[layer][0], (after(u_slabs[layer], other), u_others[layer]),
                                    weights, (0,))
                add_tables(after(both[:, layer + 1], own))
                x_in = (u.astype(jnp.float32) + own + sent).astype(jnp.bfloat16)

        shared = lax.all_gather(jnp.stack(packed), 'dp', axis=0)
        starts = shared[:, :, 0, -8].astype(jnp.int32)
        core = dp_id % 2
        kind = (dp_id // 2 + dp_id // 4) % 2
        dealt = [deal_experts(starts[:, layer], n_local, 4 if layer == top else 2) for layer in range(n_layers)]
        places = [2 * kind + core if layer == top else core for layer in range(n_layers)]
        mine = [lists[place] for (lists, _), place in zip(dealt, places)]
        firsts = [sum(x.shape[0] for x in mine[:layer]) for layer in range(n_layers)]
        list_rows = cdiv(cdiv(dp_size * 2 * cap, LANES), 8) * 8 + 8
        idx_all, gate_all = merge_tables(shared, starts, jnp.concatenate(mine),
                                         jnp.concatenate([jnp.full_like(x, layer) for layer, x in enumerate(mine)]),
                                         list_rows, dp_size * 2 * tok)
        idx_all = idx_all.reshape(-1)

        d_y, full, arrived = d_out, None, []
        d_mix = [None] * n_layers
        for layer in reversed(range(n_layers)):
            u_rows = tuple(spread(x) for x in (u_slabs[layer], u_others[layer]))
            slabs = (u_slabs[layer], u_others[layer], d_slab, d_other)
            own, other = token_kernel(layer, runs[layer][2], tables[layer][1], slabs, weights)
            d_u = (d_y.astype(jnp.float32) + own + swap(other)).astype(jnp.bfloat16)
            last = other
            if layer == top:
                y_own, last = token_kernel(top, runs[top][2], tables[top][0], (after(u_slabs[top], other), u_others[top]), weights)
            d_mix[layer] = jnp.einsum('td,te->de', xs[layer], d_u, preferred_element_type=jnp.float32).astype(jnp.bfloat16)
            d_y = (d_u.astype(jnp.float32)
                   + jnp.einsum('te,de->td', d_u, w_mix[layer], preferred_element_type=jnp.float32)).astype(jnp.bfloat16)
            tiles = dealt[layer][1][places[layer]]
            full, part = weight_grads(layer, firsts[layer], mine[layer], after(tiles, last), u_rows + d_rows, idx_all, gate_all,
                                      weights, full)
            lists = dealt[layer][0]
            if layer == top:
                far = trade(part, chip_pairs)
                near = trade(part, core_pairs)
                arrived.append((layer, lists[2 * kind + 1 - core], near))
                arrived.append((layer, lists[2 - 2 * kind + core], far))
                arrived.append((layer, lists[3 - 2 * kind - core], trade(far, core_pairs)))
            else:
                arrived.append((layer, lists[1 - core], trade(part, core_pairs)))
            if layer:
                d_slab = slab(d_y)
                d_other = swap(d_slab)
                d_rows = (spread(d_slab), spread(d_other))
                if layer == top:
                    layer_out = (u.astype(jnp.float32) + y_own + swap(after(last, d_other))).astype(jnp.bfloat16)
        for layer, names, part in arrived:
            full = merge_half(layer, names, part, full)
        d_mix = lax.psum(jnp.stack(d_mix), ('dp', 'ep'))
        return (layer_out, d_y, d_mix, jnp.swapaxes(full[0], 2, 3), jnp.swapaxes(full[1], 2, 3), full[2])

    return jax.shard_map(device_body, mesh=mesh,
                         in_specs=(tok_spec, tok_spec, route_spec, route_spec, whole_spec,
                                   expert_spec, expert_spec, expert_spec),
                         out_specs=(tok_spec, tok_spec, whole_spec, expert_spec, expert_spec, expert_spec),
                         check_vma=False)
```

time: 854 us -> 869 us (1.018)
  waiting for transfers between devices: 224 us -> 298 us
  Pallas kernels: 482 us -> 455 us
  other arithmetic: 69.8 us -> 51.5 us
  local copies, waits for them, and re-layouts: 29.1 us -> 13.5 us
    pallas_call x4 -> x2, Pallas kernels: 248 us -> 170 us  [weight_grads(): pl.pallas_call(functools.partial(weight_grad_body, parts=parts, n_exp=n_e...]
    ppermute x9, waiting for transfers between devices: 160 us -> 236 us  [swap(): return lax.ppermute(x, 'ep', ep_pairs)]
    pallas_call x5 -> x6, Pallas kernels: 201 us -> 245 us  [the longest x5 234 us: token_kernel(): pl.pallas_call(functools.partial(token_body, layer=layer, tok=tok, parts=...]
    reduce_sum x13 -> x9, other arithmetic: 6.07 us -> 19.9 us  [the longest x2 14.5 us: route_tables(): bounds = jnp.sum((group[:, None] < lane[None, :]).astype(jnp.int32), axis=0)]
    another operation x26 -> x6, other arithmetic: 12.4 us -> 0.48 us
  transfers between devices with their start and end apart: 31 -> 31, of which waited for: 7 -> 10; matrix products, arithmetic and copies ran while one was open for 10% -> 6% of each run, Pallas kernels for 51% -> 42%
where the time goes in v7:
time: 869 us; the launch traced here: 868 us
  Pallas kernels  455 us (52%)
  waiting for transfers between devices  298 us (34%)
  other arithmetic  51.5 us (6%)
  starting transfers between devices  24.2 us (3%)
  between operations  16.1 us (2%)
  local copies, waits for them, and re-layouts  13.5 us (2%)
  matrix products  10.2 us (1%)
    ppermute x9, waiting for transfers between devices, swap(): return lax.ppermute(x, 'ep', ep_pairs)  236 us
    pallas_call x5, Pallas kernels, token_kernel(): pl.pallas_call(functools.partial(token_body, layer=layer, tok=tok, parts=...  234 us
    pallas_call x2, Pallas kernels, weight_grads(): pl.pallas_call(functools.partial(weight_grad_body, parts=parts, n_exp=n_e...  170 us
    psum x1, waiting for transfers between devices, device_body(): d_mix = lax.psum(jnp.stack(d_mix), ('dp', 'ep'))  59.9 us
    pallas_call x4, Pallas kernels, merge_half(): pl.pallas_call(functools.partial(merge_body, layer=layer, n_exp=n_exp), g...  39.1 us
  transfers between devices with their start and end apart: 31, of which 10 were waited for; matrix products, arithmetic and copies ran while one was open for 6% of the time, Pallas kernels for 42%

profile of v7, /device:TPU:0, one launch (start us, length us, event | category | flops | bytes accessed | tf_op | source)
XLA Modules:
  0.0 868.1 jit_solution(10924452553742072057)
XLA Ops:
  8.9 2.4 add_convert_fusion.7
  12.3 3.3 collective-permute-start
  15.6 4.3 collective-permute-done
  20.0 3.7 convert_reduce_fusion.2
  23.8 7.3 convert_reduce_fusion.1
  31.1 6.4 sort.30
  39.0 2.5 collective-permute-done.1.refs_1_
  42.5 38.2 %experts_forward.3 = f32[1024,512]{1,0:T(8,128)} custom-call(s32[128]{0:T(128)} %get-tuple-element.147.runs, s32[18432]{0:T(1024)} %get-tuple-element.126.idx, f32[144,128]{1,0:T(8,128)} %copy-done.12, bf16[1024,4,128]{2,1,0:T(4,128)(2,1)} %copy-done, bf16[1024,4,128]{2,1,0:T(4,128)(2,1)} %copy-done.1, bf16[2,64,192,512]{3,2,1,0:T(8,128)(2,1)} %bitcast.117, ...), custom_call_target="tpu_custom_call" | custom-call | flops 19327352832 | bytes 37748736 | tf_op jit(solution)/shard_map/experts_forward/pallas_call | solution.py:206
  80.8 38.4 %experts_forward.4 = f32[1024,512]{1,0:T(8,128)} custom-call(s32[128]{0:T(128)} %get-tuple-element.148.runs, s32[18432]{0:T(1024)} %get-tuple-element.126.idx, f32[144,128]{1,0:T(8,128)} %copy-done.12, bf16[1024,4,128]{2,1,0:T(4,128)(2,1)} %copy-done, bf16[1024,4,128]{2,1,0:T(4,128)(2,1)} %copy-done.1, bf16[2,64,192,512]{3,2,1,0:T(8,128)(2,1)} %bitcast.118, ...), custom_call_target="tpu_custom_call" | custom-call | flops 19327352832 | bytes 37748736 | tf_op jit(solution)/shard_map/experts_forward/pallas_call | solution.py:206
  119.3 6.4 sort.31
  125.9 7.3 convert_reduce_fusion
  134.7 1.1 reshape.355.refs_2_
  136.0 24.6 %collective-permute-done.4.refs_3_ = bf16[1024,4,128]{2,1,0:T(4,128)(2,1)} collective-permute-done((bf16[1024,4,128]{2,1,0:T(4,128)(2,1)}, bf16[1024,4,128]{2,1,0:T(4,128)(2,1)}, u32[]{:S(2)}, u32[]{:S(2)}) %collective-permute-start.4) | collective-permute-done | bytes 1048608 | tf_op jit(solution)/shard_map/ppermute | solution.py:540
  161.0 45.8 %collective-permute-done.2 = f32[1024,512]{1,0:T(8,128)S(1)} collective-permute-done((f32[1024,512]{1,0:T(8,128)}, f32[1024,512]{1,0:T(8,128)S(1)}, u32[]{:S(2)}, u32[]{:S(2)}) %collective-permute-start.2) | collective-permute-done | bytes 2097184 | tf_op jit(solution)/shard_map/ppermute | solution.py:540
  206.8 1.9 add_convert_fusion.6
  208.7 1.0 copy-done.15
  210.4 1.3 reshape.354.refs_0_
  212.4 22.3 %collective-permute-done.3.refs_1_ = bf16[1024,4,128]{2,1,0:T(4,128)(2,1)S(1)} collective-permute-done((bf16[1024,4,128]{2,1,0:T(4,128)(2,1)}, bf16[1024,4,128]{2,1,0:T(4,128)(2,1)S(1)}, u32[]{:S(2)}, u32[]{:S(2)}) %collective-permute-start.3) | collective-permute-done | bytes 1048608 | tf_op jit(solution)/shard_map/ppermute | solution.py:540
  237.7 53.8 %experts_backward.2 = (f32[1024,512]{1,0:T(8,128)}, f32[1024,512]{1,0:T(8,128)}) custom-call(s32[128]{0:T(128)} %pad_add_fusion.2.runs, s32[18432]{0:T(1024)} %get-tuple-element.128.idx, f32[144,128]{1,0:T(8,128)} %copy-done.19, bf16[1024,4,128]{2,1,0:T(4,128)(2,1)} %reshape.354.refs_0_, bf16[1024,4,128]{2,1,0:T(4,128)(2,1)} %copy-done.13, ...), custom_call_target="tpu_custom_call" | custom-call | flops 51539607552 | bytes 37748736 | tf_op jit(solution)/shard_map/experts_backward/pallas_call | solution.py:206
  291.4 4.4 collective-permute-start.5
  295.8 43.0 %collective-permute-done.5 = f32[1024,512]{1,0:T(8,128)S(1)} collective-permute-done((f32[1024,512]{1,0:T(8,128)}, f32[1024,512]{1,0:T(8,128)S(1)}, u32[]{:S(2)}, u32[]{:S(2)}) %collective-permute-start.5) | collective-permute-done | bytes 2097184 | tf_op jit(solution)/shard_map/ppermute | solution.py:540
  338.9 2.3 add_convert_fusion.4
  342.0 1.3 reshape.356.refs_2_
  343.6 45.5 %experts_forward.5 = (f32[1024,512]{1,0:T(8,128)}, f32[1024,512]{1,0:T(8,128)}) custom-call(s32[128]{0:T(128)} %pad_add_fusion.2.runs, s32[18432]{0:T(1024)} %get-tuple-element.129.idx, f32[144,128]{1,0:T(8,128)} %copy-done.19, bf16[1024,4,128]{2,1,0:T(4,128)(2,1)} %reshape.354.refs_0_, bf16[1024,4,128]{2,1,0:T(4,128)(2,1)} %copy-done.13, ...), custom_call_target="tpu_custom_call" | custom-call | flops 38654705664 | bytes 37748736 | tf_op jit(solution)/shard_map/experts_forward/pallas_call | solution.py:206
  390.6 4.2 collective-permute-start.6
  397.8 11.0 %merge_tables.1 = (s32[48,32,128]{2,1,0:T(8,128)}, f32[48,32,128]{2,1,0:T(8,128)}) custom-call(s32[2048]{0:T(1024)} %bitcast.145, s32[48]{0:T(128)} %pad_add_fusion.4.exps, s32[48]{0:T(128)} %constant.196.clone.1.layers, f32[8,2,2,152,128]{4,3,2,1,0:T(8,128)} %bitcast.149), custom_call_target="tpu_custom_call" | custom-call | flops 1000000000 | bytes 2490368 | tf_op jit(solution)/shard_map/merge_tables/pallas_call | solution.py:271
  409.5 5.5 collective-permute-done.6.refs_3_
  415.0 1.0 copy-done.14
  416.4 56.2 %weight_grads.2 = (bf16[2,64,192,512]{3,2,1,0:T(8,128)(2,1)}, bf16[2,64,192,512]{3,2,1,0:T(8,128)(2,1)}, bf16[2,64,192,512]{3,2,1,0:T(8,128)(2,1)}, bf16[16,192,...) custom-call(s32[16]{0:T(128)} %copy-done.23, s32[17]{0:T(128)} %get-tuple-element.143.tiles, ...), custom_call_target="tpu_custom_call" | custom-call | flops 154618822656 | bytes 61865984 | tf_op jit(solution)/shard_map/weight_grads/pallas_call | solution.py:414
  472.6 2.2 collective-permute-start.18
  474.8 2.9 collective-permute-start.12
  477.7 58.5 %experts_backward.3 = (f32[1024,512]{1,0:T(8,128)}, f32[1024,512]{1,0:T(8,128)}) custom-call(s32[128]{0:T(128)} %get-tuple-element.146.runs, s32[18432]{0:T(1024)} %get-tuple-element.125.idx, f32[144,128]{1,0:T(8,128)} %copy-done.12, bf16[1024,4,128]{2,1,0:T(4,128)(2,1)} %copy-done, bf16[1024,4,128]{2,1,0:T(4,128)(2,1)} %copy-done.1, ...), custom_call_target="tpu_custom_call" | custom-call | flops 51539607552 | bytes 37748736 | tf_op jit(solution)/shard_map/experts_backward/pallas_call | solution.py:206
  536.3 1.7 collective-permute-start.8
  539.4 45.7 %collective-permute-done.8 = f32[1024,512]{1,0:T(8,128)} collective-permute-done((f32[1024,512]{1,0:T(8,128)}, f32[1024,512]{1,0:T(8,128)}, u32[]{:S(2)}, u32[]{:S(2)}) %collective-permute-start.8) | collective-permute-done | bytes 2097184 | tf_op jit(solution)/shard_map/ppermute | solution.py:540
  585.1 1.8 collective-permute-start.14
  587.0 42.7 %collective-permute-done.7 = f32[1024,512]{1,0:T(8,128)} collective-permute-done((f32[1024,512]{1,0:T(8,128)}, f32[1024,512]{1,0:T(8,128)}, u32[]{:S(2)}, u32[]{:S(2)}) %collective-permute-start.7) | collective-permute-done | bytes 2097184 | tf_op jit(solution)/shard_map/ppermute | solution.py:540
  630.2 114.2 %weight_grads.3 = (bf16[2,64,192,512]{3,2,1,0:T(8,128)(2,1)}, bf16[2,64,192,512]{3,2,1,0:T(8,128)(2,1)}, bf16[2,64,192,512]{3,2,1,0:T(8,128)(2,1)}, bf16[32,192,...) custom-call(s32[32]{0:T(128)} %copy-done.24, ...), custom_call_target="tpu_custom_call", output_to_operand_aliasing={{0}: (12, {}), {1}: (13, {}), {2}: (14, {})} | custom-call | flops 309237645312 | bytes 90177536 | tf_op jit(solution)/shard_map/weight_grads/pallas_call | solution.py:414
  745.6 2.0 fusion.1
  747.7 2.3 add_convert_fusion.1
  751.7 1.1 pad_maximum_fusion
  752.8 3.6 add_convert_fusion
  756.5 3.2 add_convert_fusion.2
  759.6 59.9 %all-reduce.10.cloned.1.call-done = bf16[2,512,512]{1,2,0:T(8,128)(2,1)} async-done(((bf16[2,512,512]{1,2,0:T(8,128)(2,1)}), bf16[2,512,512]{1,2,0:T(8,128)(2,1)}) %all-reduce.10.cloned.1.call-update) | async-done | bytes 1048592 | tf_op jit(solution)/shard_map/psum | solution.py:639
  819.5 2.3 copy.56
  821.8 8.2 merge_half.4
  829.9 8.2 merge_half.5
  838.1 8.2 merge_half.6
  846.4 14.6 %merge_half.7 = (bf16[2,64,192,512]{3,2,1,0:T(8,128)(2,1)}, bf16[2,64,192,512]{3,2,1,0:T(8,128)(2,1)}, bf16[2,64,192,512]{3,2,1,0:T(8,128)(2,1)}) custom-call(s32[32]{0:T(128)} %get-tuple-element.141.exps, bf16[32,192,512]{2,1,0:T(8,128)(2,1)} %collective-permute-done.9.a, ...), custom_call_target="tpu_custom_call", output_to_operand_aliasing={{0}: (4, {}), {1}: (5, {}), {2}: (6, {})} | custom-call | flops 1000000000 | bytes 37748736 | tf_op jit(solution)/shard_map/merge_half/pallas_call | solution.py:466
  (180 shorter events, 22.3 us)
Async XLA Ops:
  8.0 3.7 copy-start.20
  8.0 381.1 %all-gather.27.cloned.1.call-start = ((), (), s32[]{:S(2)}) async-start(), calls=%async_computation.9 | async-start | bytes 2801664 | tf_op jit(solution)/shard_map/all_gather | solution.py:592
  11.6 30.9 %copy-start = (bf16[1024,4,128]{2,1,0:T(4,128)(2,1)}, bf16[1024,4,128]{2,1,0:T(4,128)(2,1)S(1)}, u32[]{:S(2)}) copy-start(bf16[1024,4,128]{2,1,0:T(4,128)(2,1)S(1)} %reshape.351.refs_0_) | copy-start | bytes 3145732
  12.3 7.6 collective-permute-start
  15.6 26.0 %collective-permute-start.1 = (bf16[1024,4,128]{2,1,0:T(4,128)(2,1)S(1)}, bf16[1024,4,128]{2,1,0:T(4,128)(2,1)S(1)}, u32[]{:S(2)}, u32[]{:S(2)}) collective-permute-start(bf16[1024,4,128]{2,1,0:T(4,128)(2,1)S(1)} %reshape.351.refs_0_), channel_id=1, source_target_pairs={{0,8},{8,0},{1,9},{9,1},{2,10},{10,2},{3,11},{11,3},{4,12},{12,4},... | collective-permute-start | bytes 3145736 | tf_op jit(solution)/shard_map/ppermute | solution.py:540
  37.6 4.9 copy-start.12
  119.2 15.5 %copy-start.4 = (bf16[1024,512]{1,0:T(8,128)(2,1)S(1)}, bf16[1024,512]{1,0:T(8,128)(2,1)}, u32[]{:S(2)}) copy-start(bf16[1024,512]{1,0:T(8,128)(2,1)} %param.9) | copy-start | bytes 3145732
  125.8 80.9 %copy-start.2 = (f32[1024,512]{1,0:T(8,128)S(1)}, f32[1024,512]{1,0:T(8,128)}, u32[]{:S(2)}) copy-start(f32[1024,512]{1,0:T(8,128)} %experts_forward.4) | copy-start | bytes 6291460
  133.1 75.5 %copy-start.19 = (f32[144,128]{1,0:T(8,128)}, f32[144,128]{1,0:T(8,128)S(1)}, u32[]{:S(2)}) copy-start(f32[144,128]{1,0:T(8,128)S(1)} %pad_bitcast_fusion.2.gates) | copy-start | bytes 221188
  134.7 281.7 %all-gather.23.cloned.1.call-start = ((), (), s32[]{:S(2)}) async-start(), calls=%async_computation.7 | async-start | bytes 9437184 | tf_op jit(solution)/shard_map/all_gather | solution.py:543
  135.9 280.5 %all-gather.25.cloned.1.call-start = ((), (), s32[]{:S(2)}) async-start(), calls=%async_computation.8 | async-start | bytes 9437184 | tf_op jit(solution)/shard_map/all_gather | solution.py:543
  135.9 24.6 %collective-permute-start.4 = (bf16[1024,4,128]{2,1,0:T(4,128)(2,1)}, bf16[1024,4,128]{2,1,0:T(4,128)(2,1)}, u32[]{:S(2)}, u32[]{:S(2)}) collective-permute-start(bf16[1024,4,128]{2,1,0:T(4,128)(2,1)} %reshape.355.refs_2_), channel_id=1, source_target_pairs={{0,8},{8,0},{1,9},{9,1},{2,10},{10,2},{3,11},{11,3},{4,12},{12,4},... | collective-permute-start | bytes 3145736 | tf_op jit(solution)/shard_map/ppermute | solution.py:540
  160.6 255.8 %all-gather.19.cloned.1.call-start = ((), (), s32[]{:S(2)}) async-start(), calls=%async_computation.5 | async-start | bytes 9437184 | tf_op jit(solution)/shard_map/all_gather | solution.py:543
  160.6 49.0 %copy-start.26 = (bf16[2,512,512]{2,1,0:T(8,128)(2,1)S(1)}, bf16[2,512,512]{2,1,0:T(8,128)(2,1)}, u32[]{:S(2)}) copy-start(bf16[2,512,512]{2,1,0:T(8,128)(2,1)} %param.12) | copy-start | bytes 3145732
  160.6 46.1 %collective-permute-start.2 = (f32[1024,512]{1,0:T(8,128)}, f32[1024,512]{1,0:T(8,128)S(1)}, u32[]{:S(2)}, u32[]{:S(2)}) collective-permute-start(f32[1024,512]{1,0:T(8,128)} %experts_forward.3), channel_id=1, source_target_pairs={{0,8},{8,0},{1,9},{9,1},{2,10},{10,2},{3,11},{11,3},{4,12},{12,4},... | collective-permute-start | bytes 6291464 | tf_op jit(solution)/shard_map/ppermute | solution.py:540
  210.3 26.6 %copy-start.5 = (bf16[1024,512]{1,0:T(8,128)(2,1)}, bf16[1024,512]{1,0:T(8,128)(2,1)S(1)}, u32[]{:S(2)}) copy-start(bf16[1024,512]{1,0:T(8,128)(2,1)S(1)} %add_convert_fusion.5) | copy-start | bytes 3145732
  211.7 204.7 %all-gather.21.cloned.1.call-start = ((), (), s32[]{:S(2)}) async-start(), calls=%async_computation.6 | async-start | bytes 9437184 | tf_op jit(solution)/shard_map/all_gather | solution.py:543
  211.7 22.9 %collective-permute-start.3 = (bf16[1024,4,128]{2,1,0:T(4,128)(2,1)}, bf16[1024,4,128]{2,1,0:T(4,128)(2,1)S(1)}, u32[]{:S(2)}, u32[]{:S(2)}) collective-permute-start(bf16[1024,4,128]{2,1,0:T(4,128)(2,1)} %reshape.354.refs_0_), channel_id=1, source_target_pairs={{0,8},{8,0},{1,9},{9,1},{2,10},{10,2},{3,11},{11,3},{4,12},{12,4},... | collective-permute-start | bytes 3145736 | tf_op jit(solution)/shard_map/ppermute | solution.py:540
  235.6 394.6 %all-gather.11.cloned.1.call-start = ((), (), s32[]{:S(2)}) async-start(), calls=%async_computation.1 | async-start | bytes 9437184 | tf_op jit(solution)/shard_map/all_gather | solution.py:543
  236.2 394.0 %all-gather.13.cloned.1.call-start = ((), (), s32[]{:S(2)}) async-start(), calls=%async_computation.2 | async-start | bytes 9437184 | tf_op jit(solution)/shard_map/all_gather | solution.py:543
  237.0 393.2 %all-gather.15.cloned.1.call-start = ((), (), s32[]{:S(2)}) async-start(), calls=%async_computation.3 | async-start | bytes 9437184 | tf_op jit(solution)/shard_map/all_gather | solution.py:543
  291.4 47.4 %collective-permute-start.5 = (f32[1024,512]{1,0:T(8,128)}, f32[1024,512]{1,0:T(8,128)S(1)}, u32[]{:S(2)}, u32[]{:S(2)}) collective-permute-start(f32[1024,512]{1,0:T(8,128)} %get-tuple-element.58), channel_id=1, source_target_pairs={{0,8},{8,0},{1,9},{9,1},{2,10},{10,2},{3,11},{11,3},{4,12},{12,4},... | collective-permute-start | bytes 6291464 | tf_op jit(solution)/shard_map/ppermute | solution.py:540
  343.3 286.9 %all-gather.17.cloned.1.call-start = ((), (), s32[]{:S(2)}) async-start(), calls=%async_computation.4 | async-start | bytes 9437184 | tf_op jit(solution)/shard_map/all_gather | solution.py:543
  343.6 47.0 %copy-start.3 = (bf16[1024,4,128]{2,1,0:T(4,128)(2,1)S(1)}, bf16[1024,4,128]{2,1,0:T(4,128)(2,1)}, u32[]{:S(2)}) copy-start(bf16[1024,4,128]{2,1,0:T(4,128)(2,1)} %reshape.356.refs_2_) | copy-start | bytes 3145732
  390.0 7.9 copy-start.21
  390.6 24.3 %collective-permute-start.6 = (bf16[1024,4,128]{2,1,0:T(4,128)(2,1)S(1)}, bf16[1024,4,128]{2,1,0:T(4,128)(2,1)S(1)}, u32[]{:S(2)}, u32[]{:S(2)}) collective-permute-start(bf16[1024,4,128]{2,1,0:T(4,128)(2,1)S(1)} %copy-done.3), channel_id=1, source_target_pairs={{0,8},{8,0},{1,9},{9,1},{2,10},{10,2},{3,11},{11,3},{4,12},{12,4},... | collective-permute-start | bytes 3145736 | tf_op jit(solution)/shard_map/ppermute | solution.py:540
  396.7 19.4 %copy-start.24 = (s32[32]{0:T(128)}, s32[32]{0:T(128)S(1)}, u32[]{:S(2)}) copy-start(s32[32]{0:T(128)S(1)} %get-tuple-element.140.exps) | copy-start | bytes 388
  397.3 19.2 %copy-start.23 = (s32[16]{0:T(128)}, s32[16]{0:T(128)S(1)}, u32[]{:S(2)}) copy-start(s32[16]{0:T(128)S(1)} %get-tuple-element.139.exps) | copy-start | bytes 196
  416.0 403.5 %all-reduce.10.cloned.1.call-start = ((), (), s32[]{:S(2)}) async-start(), calls=%async_computation | async-start | bytes 2097152 | tf_op jit(solution)/shard_map/psum | solution.py:639
  472.6 157.0 %collective-permute-start.18 = (bf16[16,192,512]{2,1,0:T(8,128)(2,1)}, bf16[16,192,512]{2,1,0:T(8,128)(2,1)}, u32[]{:S(2)}, u32[]{:S(2)}) collective-permute-start(bf16[16,192,512]{2,1,0:T(8,128)(2,1)} %get-tuple-element.76), channel_id=1, source_target_pairs={{0,1},{1,0},{2,3},{3,2},{4,5},{5,4},{6,7},{7,6},{8,9},{9,8},{10,11... | collective-permute-start | bytes 9437192 | tf_op jit(solution)/shard_map/ppermute | solution.py:546
  474.8 154.9 %collective-permute-start.12 = (bf16[16,192,512]{2,1,0:T(8,128)(2,1)}, bf16[16,192,512]{2,1,0:T(8,128)(2,1)}, u32[]{:S(2)}, u32[]{:S(2)}) collective-permute-start(bf16[16,192,512]{2,1,0:T(8,128)(2,1)} %get-tuple-element.76), channel_id=1, source_target_pairs={{0,2},{1,5},{2,0},{3,7},{4,6},{5,1},{6,4},{7,3},{8,10},{9,13},{10,... | collective-permute-start | bytes 9437192 | tf_op jit(solution)/shard_map/ppermute | solution.py:546
  477.7 60.6 %copy-start.22 = (s32[2,32]{1,0:T(2,128)S(1)}, s32[2,32]{1,0:T(2,128)}, u32[]{:S(2)}) copy-start(s32[2,32]{1,0:T(2,128)} %get-tuple-element.120) | copy-start | bytes 772
  536.3 48.9 %collective-permute-start.8 = (f32[1024,512]{1,0:T(8,128)}, f32[1024,512]{1,0:T(8,128)}, u32[]{:S(2)}, u32[]{:S(2)}) collective-permute-start(f32[1024,512]{1,0:T(8,128)} %get-tuple-element.65), channel_id=1, source_target_pairs={{0,8},{8,0},{1,9},{9,1},{2,10},{10,2},{3,11},{11,3},{4,12},{12,4},... | collective-permute-start | bytes 6291464 | tf_op jit(solution)/shard_map/ppermute | solution.py:540
  538.0 91.6 %collective-permute-start.7 = (f32[1024,512]{1,0:T(8,128)}, f32[1024,512]{1,0:T(8,128)}, u32[]{:S(2)}, u32[]{:S(2)}) collective-permute-start(f32[1024,512]{1,0:T(8,128)} %get-tuple-element.63), channel_id=1, source_target_pairs={{0,8},{8,0},{1,9},{9,1},{2,10},{10,2},{3,11},{11,3},{4,12},{12,4},... | collective-permute-start | bytes 6291464 | tf_op jit(solution)/shard_map/ppermute | solution.py:540
  539.4 205.1 %collective-permute-start.19 = (bf16[16,192,512]{2,1,0:T(8,128)(2,1)}, bf16[16,192,512]{2,1,0:T(8,128)(2,1)}, u32[]{:S(2)}, u32[]{:S(2)}) collective-permute-start(bf16[16,192,512]{2,1,0:T(8,128)(2,1)} %get-tuple-element.77), channel_id=1, source_target_pairs={{0,1},{1,0},{2,3},{3,2},{4,5},{5,4},{6,7},{7,6},{8,9},{9,8},{10,11... | collective-permute-start | bytes 9437192 | tf_op jit(solution)/shard_map/ppermute | solution.py:546
  585.1 159.5 %collective-permute-start.14 = (bf16[16,192,512]{2,1,0:T(8,128)(2,1)}, bf16[16,192,512]{2,1,0:T(8,128)(2,1)}, u32[]{:S(2)}, u32[]{:S(2)}) collective-permute-start(bf16[16,192,512]{2,1,0:T(8,128)(2,1)} %get-tuple-element.77), channel_id=1, source_target_pairs={{0,2},{1,5},{2,0},{3,7},{4,6},{5,1},{6,4},{7,3},{8,10},{9,13},{10,... | collective-permute-start | bytes 9437192 | tf_op jit(solution)/shard_map/ppermute | solution.py:546
  629.7 115.4 %collective-permute-start.20 = (bf16[16,192,512]{2,1,0:T(8,128)(2,1)}, bf16[16,192,512]{2,1,0:T(8,128)(2,1)}, u32[]{:S(2)}, u32[]{:S(2)}) collective-permute-start(bf16[16,192,512]{2,1,0:T(8,128)(2,1)} %get-tuple-element.78), channel_id=1, source_target_pairs={{0,1},{1,0},{2,3},{3,2},{4,5},{5,4},{6,7},{7,6},{8,9},{9,8},{10,11... | collective-permute-start | bytes 9437192 | tf_op jit(solution)/shard_map/ppermute | solution.py:546
  629.7 115.5 %collective-permute-start.16 = (bf16[16,192,512]{2,1,0:T(8,128)(2,1)}, bf16[16,192,512]{2,1,0:T(8,128)(2,1)}, u32[]{:S(2)}, u32[]{:S(2)}) collective-permute-start(bf16[16,192,512]{2,1,0:T(8,128)(2,1)} %get-tuple-element.78), channel_id=1, source_target_pairs={{0,2},{1,5},{2,0},{3,7},{4,6},{5,1},{6,4},{7,3},{8,10},{9,13},{10,... | collective-permute-start | bytes 9437192 | tf_op jit(solution)/shard_map/ppermute | solution.py:546
  629.7 115.9 %collective-permute-start.13 = (bf16[16,192,512]{2,1,0:T(8,128)(2,1)}, bf16[16,192,512]{2,1,0:T(8,128)(2,1)}, u32[]{:S(2)}, u32[]{:S(2)}) collective-permute-start(bf16[16,192,512]{2,1,0:T(8,128)(2,1)} %collective-permute-done.12.a), channel_id=1, source_target_pairs={{0,1},{1,0},{2,3},{3,2},{4,5},{5,4},{6,7},{7,6},{8,9},{9,8},{10,11... | collective-permute-start | bytes 9437192 | tf_op jit(solution)/shard_map/ppermute | solution.py:546
  630.2 115.4 %copy-start.16 = (bf16[1024,512]{1,0:T(8,128)(2,1)S(1)}, bf16[1024,512]{1,0:T(8,128)(2,1)}, u32[]{:S(2)}) copy-start(bf16[1024,512]{1,0:T(8,128)(2,1)} %copy-done.15) | copy-start | bytes 3145732
  744.5 101.8 %collective-permute-start.9 = (bf16[32,192,512]{2,1,0:T(8,128)(2,1)}, bf16[32,192,512]{2,1,0:T(8,128)(2,1)}, u32[]{:S(2)}, u32[]{:S(2)}) collective-permute-start(bf16[32,192,512]{2,1,0:T(8,128)(2,1)} %get-tuple-element.73), channel_id=1, source_target_pairs={{0,1},{1,0},{2,3},{3,2},{4,5},{5,4},{6,7},{7,6},{8,9},{9,8},{10,11... | collective-permute-start | bytes 18874376 | tf_op jit(solution)/shard_map/ppermute | solution.py:546
  744.6 101.7 %collective-permute-start.10 = (bf16[32,192,512]{2,1,0:T(8,128)(2,1)}, bf16[32,192,512]{2,1,0:T(8,128)(2,1)}, u32[]{:S(2)}, u32[]{:S(2)}) collective-permute-start(bf16[32,192,512]{2,1,0:T(8,128)(2,1)} %get-tuple-element.74), channel_id=1, source_target_pairs={{0,1},{1,0},{2,3},{3,2},{4,5},{5,4},{6,7},{7,6},{8,9},{9,8},{10,11... | collective-permute-start | bytes 18874376 | tf_op jit(solution)/shard_map/ppermute | solution.py:546
  745.0 101.3 %collective-permute-start.11 = (bf16[32,192,512]{2,1,0:T(8,128)(2,1)}, bf16[32,192,512]{2,1,0:T(8,128)(2,1)}, u32[]{:S(2)}, u32[]{:S(2)}) collective-permute-start(bf16[32,192,512]{2,1,0:T(8,128)(2,1)} %get-tuple-element.75), channel_id=1, source_target_pairs={{0,1},{1,0},{2,3},{3,2},{4,5},{5,4},{6,7},{7,6},{8,9},{9,8},{10,11... | collective-permute-start | bytes 18874376 | tf_op jit(solution)/shard_map/ppermute | solution.py:546
  745.1 93.0 %collective-permute-start.15 = (bf16[16,192,512]{2,1,0:T(8,128)(2,1)}, bf16[16,192,512]{2,1,0:T(8,128)(2,1)}, u32[]{:S(2)}, u32[]{:S(2)}) collective-permute-start(bf16[16,192,512]{2,1,0:T(8,128)(2,1)} %collective-permute-done.14.b), channel_id=1, source_target_pairs={{0,1},{1,0},{2,3},{3,2},{4,5},{5,4},{6,7},{7,6},{8,9},{9,8},{10,11... | collective-permute-start | bytes 9437192 | tf_op jit(solution)/shard_map/ppermute | solution.py:546
  745.6 92.6 %collective-permute-start.17 = (bf16[16,192,512]{2,1,0:T(8,128)(2,1)}, bf16[16,192,512]{2,1,0:T(8,128)(2,1)}, u32[]{:S(2)}, u32[]{:S(2)}) collective-permute-start(bf16[16,192,512]{2,1,0:T(8,128)(2,1)} %collective-permute-done.16.c), channel_id=1, source_target_pairs={{0,1},{1,0},{2,3},{3,2},{4,5},{5,4},{6,7},{7,6},{8,9},{9,8},{10,11... | collective-permute-start | bytes 9437192 | tf_op jit(solution)/shard_map/ppermute | solution.py:546
  747.6 3.3 copy-start.25
  751.7 4.7 copy-start.6
  751.7 4.7 copy-start.10
  (11 other events, 18.4 us)
Sparse Core Ops, SparseCore 0:
  134.8 25.9 all-gather.26
  162.6 50.4 all-gather.22
  215.0 50.4 all-gather.24
  267.8 50.4 all-gather.18
  320.6 50.5 all-gather.20
  373.5 50.4 all-gather.10
  426.4 51.0 all-gather.12
  479.4 67.0 all-gather.14
  548.3 55.7 all-gather.16
Sparse Core Ops, SparseCore 1:
  752.9 66.5 all-reduce.9

commit v8 on v7

--- a/solution.py
+++ b/solution.py
@@ -13,7 +13,9 @@
 LANES = 128
 TILE = 96
 HALF_TILE = 64
-WTILE = 256
+WTILE = 768
+SOURCES = 8
+CHUNK = 256
 PITCH = 9
 BATCH = 16
 SLOTS = 8
@@ -101,7 +103,7 @@
 
 def run_tiles(step, weights, wbuf, wsem, runs, tile, layer, prepare):
     n_local = weights[0].shape[1]
-    for e in range(SLOTS - 1):
+    for e in range(SLOTS - 2):
         for c in expert_copies(weights, wbuf, wsem, layer, e):
             c.start()
     prepare()
@@ -117,14 +119,14 @@
     def one(i, carry):
         (e, row, left), (e1, row1, n1), (e2, row2, n2), row3 = carry
 
-        @pl.when(e1 != e2)
+        @pl.when(e != e1)
         def _():
-            for c in expert_copies(weights, wbuf, wsem, layer, e1):
+            for c in expert_copies(weights, wbuf, wsem, layer, e):
                 c.wait()
 
-        @pl.when((e1 != e2) & (e1 + SLOTS - 2 < n_local))
+        @pl.when((e != e1) & (e + SLOTS - 3 < n_local))
         def _():
-            for c in expert_copies(weights, wbuf, wsem, layer, e1 + SLOTS - 2):
+            for c in expert_copies(weights, wbuf, wsem, layer, e + SLOTS - 3):
                 c.start()
 
         step(row, (lax.rem(e1, SLOTS), row1), (lax.rem(e2, SLOTS), row2, n2), row3)
@@ -285,11 +287,11 @@
     )(starts.reshape(-1), exps, layers, shared)
 
 
-def weight_grad_body(exps, tiles, begins, u_own, u_oth, d_own, d_oth, idx_all, gate_ref, *refs, parts, n_exp, n_alias, first_list,
-                     page):
-    g_ref, up_ref, w_ref = refs[:3]
+def weight_grad_body(exps, tiles, begins, *refs, parts, n_exp, n_alias, n_rows, first_list, page):
+    rows_in, refs = refs[:sum(n_rows)], refs[sum(n_rows):]
+    idx_all, gate_ref, g_ref, up_ref, w_ref = refs[:5]
     (dg_ref, du_ref, dw_ref, og_ref, ou_ref, ow_ref,
-     uds, rows, u0, c0, d0, h0, u1, c1, d1, h1, gacc, wacc, idx_s, sem, tsem) = refs[3 + n_alias:]
+     uds, rows, u0, c0, d0, h0, u1, c1, d1, h1, gacc, wacc, idx_s, sem, tsem) = refs[5 + n_alias:]
     e = pl.program_id(0)
     ff = g_ref.shape[2]
     slots = 3
@@ -309,15 +311,22 @@
 
     @pl.when(e == 0)
     def _():
-        n_half = u_own.shape[0]
-        copies = [pltpu.make_async_copy(src, uds.at[pl.ds((k % 2) * n_half, n_half), pl.ds((k // 2) * parts, parts)], sem.at[k])
-                  for k, src in enumerate((u_own, u_oth, d_own, d_oth))]
+        n_tok = uds.shape[0] - 8
+        copies = []
+        for kind, arrays in enumerate((rows_in[:n_rows[0]], rows_in[n_rows[0]:])):
+            part = pl.ds(kind * parts, parts)
+            if len(arrays) == 1:
+                copies.append(pltpu.make_async_copy(arrays[0], uds.at[pl.ds(0, n_tok), part], sem.at[kind]))
+                continue
+            run = n_tok // (2 * SOURCES)
+            for q in range(2 * SOURCES):
+                copies.append(pltpu.make_async_copy(arrays[q % 2].at[pl.ds(q // 2 * run, run)],
+                                                    uds.at[pl.ds(q * run, run), part], sem.at[kind]))
         for c in copies:
             c.start()
         table_copy(0).start()
         table_copy(1).start()
-        n_rows = n_half * 2
-        uds[pl.ds(n_rows, 8)] = jnp.zeros((8, 2 * parts, LANES), jnp.bfloat16)
+        uds[pl.ds(n_tok, 8)] = jnp.zeros((8, 2 * parts, LANES), jnp.bfloat16)
         for ref in (*both[0], *both[1], gacc, wacc):
             clear(ref)
         table_copy(0).wait()
@@ -350,23 +359,26 @@
         uo, co, do, ho = old
         gacc[...] += nn_dot(do[...], uo[...])
         wacc[...] += nn_dot(ho[...], co[...])
-        un[...] = jnp.concatenate([column(0, WTILE, k) for k in range(parts)], axis=1).astype(jnp.bfloat16)
-        gates = [spread_column(gate_ref[0, pl.ds(j * gate_rows + q, 1), :]) for q in range(gate_rows)]
-        for k in range(parts):
-            for q in range(gate_rows):
-                d = column(q * LANES, LANES, parts + k)
-                cn[q * LANES:(q + 1) * LANES, k * LANES:(k + 1) * LANES] = (d * gates[q]).astype(jnp.bfloat16)
-        ab = nt_dot(jnp.concatenate([g_ref[0, 0], up_ref[0, 0]], axis=0), un[...])
-        dh = nt_dot(w_ref[0, 0], cn[...])
         nxt = jnp.where(j + 1 < n_tiles, here + (j + 1) * WTILE, there)
-        for r in range(WTILE):
-            gather_row(nxt + r, r)
-        a, b = ab[:ff], ab[ff:]
-        s = jax.nn.sigmoid(a)
-        act = a * s
-        hn[...] = (act * b).astype(jnp.bfloat16)
-        dn[:ff] = (dh * b * (s * (1.0 + a * (1.0 - s)))).astype(jnp.bfloat16)
-        dn[ff:] = (dh * act).astype(jnp.bfloat16)
+        gu = jnp.concatenate([g_ref[0, 0], up_ref[0, 0]], axis=0)
+        for q in range(0, WTILE, CHUNK):
+            part = slice(q, q + CHUNK)
+            un[part] = jnp.concatenate([column(q, CHUNK, k) for k in range(parts)], axis=1).astype(jnp.bfloat16)
+            for p in range(q, q + CHUNK, LANES):
+                gate = spread_column(gate_ref[0, pl.ds(j * gate_rows + p // LANES, 1), :])
+                for k in range(parts):
+                    d = column(p, LANES, parts + k)
+                    cn[p:p + LANES, k * LANES:(k + 1) * LANES] = (d * gate).astype(jnp.bfloat16)
+            ab = nt_dot(gu, un[part])
+            dh = nt_dot(w_ref[0, 0], cn[part])
+            for r in range(q, q + CHUNK):
+                gather_row(nxt + r, r)
+            a, b = ab[:ff], ab[ff:]
+            s = jax.nn.sigmoid(a)
+            act = a * s
+            hn[:, part] = (act * b).astype(jnp.bfloat16)
+            dn[:ff, part] = (dh * b * (s * (1.0 + a * (1.0 - s)))).astype(jnp.bfloat16)
+            dn[ff:, part] = (dh * act).astype(jnp.bfloat16)
 
     def tile(j, carry):
         odd = lax.rem(begin + j, 2)
@@ -395,8 +407,8 @@
 
 
 def weight_grads(layer, first, exps, tiles, rows, idx_all, gates, weights, full):
-    n_half, parts, _ = rows[0].shape
-    n_tok = 2 * n_half
+    parts = rows[0][0].shape[1]
+    n_tok = sum(x.shape[0] for x in rows[0])
     n_layers, n_local, ff, d_model = weights[0].shape
     n_exp = exps.shape[0]
     out_rows = gates.shape[1]
@@ -412,25 +424,26 @@
     tile_set = [pltpu.VMEM((WTILE, d_model), jnp.bfloat16)] * 2 + [pltpu.VMEM((2 * ff, WTILE), jnp.bfloat16),
                                                                  pltpu.VMEM((ff, WTILE), jnp.bfloat16)]
     outs = pl.pallas_call(
-        functools.partial(weight_grad_body, parts=parts, n_exp=n_exp, n_alias=len(aliased), first_list=first, page=page),
+        functools.partial(weight_grad_body, parts=parts, n_exp=n_exp, n_alias=len(aliased),
+                          n_rows=[len(x) for x in rows], first_list=first, page=page),
         grid_spec=pltpu.PrefetchScalarGridSpec(
             num_scalar_prefetch=3,
             grid=(n_exp + 1,),
-            in_specs=[any_spec] * 5 + [gate_spec] + [mine] * 3 + [any_spec] * len(aliased),
+            in_specs=[any_spec] * (sum(len(x) for x in rows) + 1) + [gate_spec] + [mine] * 3 + [any_spec] * len(aliased),
             out_specs=[done] * 3 + [half] * 3,
             scratch_shapes=[pltpu.VMEM((n_tok + 8, 2 * parts, LANES), jnp.bfloat16)]
             + [pltpu.VMEM((WTILE * PITCH + 16, LANES), jnp.float32)] + tile_set * 2
             + [pltpu.VMEM((2 * ff, d_model), jnp.float32), pltpu.VMEM((ff, d_model), jnp.float32),
-               pltpu.SMEM((3 * page,), jnp.int32), pltpu.SemaphoreType.DMA((4,)), pltpu.SemaphoreType.DMA((3,))],
+               pltpu.SMEM((3 * page,), jnp.int32), pltpu.SemaphoreType.DMA((2,)), pltpu.SemaphoreType.DMA((3,))],
         ),
         out_shape=[jax.ShapeDtypeStruct((n_layers, n_local, ff, d_model), jnp.bfloat16)] * 3
         + [jax.ShapeDtypeStruct((n_exp, ff, d_model), jnp.bfloat16)] * 3,
-        input_output_aliases={12 + k: k for k in range(len(aliased))},
+        input_output_aliases={sum(len(x) for x in rows) + 8 + k: k for k in range(len(aliased))},
         compiler_params=pltpu.CompilerParams(dimension_semantics=("arbitrary",), vmem_limit_bytes=VMEM_LIMIT),
         cost_estimate=pl.CostEstimate(flops=6 * n_tok * n_exp * d_model * ff,
                                       bytes_accessed=n_tok * d_model * 4 + 9 * n_exp * ff * d_model * 2, transcendentals=0),
         name="weight_grads",
-    )(exps, tiles, begins, *rows, idx_all, gates, *weights, *aliased)
+    )(exps, tiles, begins, *rows[0], *rows[1], idx_all, gates, *weights, *aliased)
     return outs[:3], outs[3:]
 
 
@@ -477,6 +490,26 @@
     )(exps, *half, *full)
 
 
+def join_body(a, b, out, sem):
+    n = a.shape[0]
+    copies = [pltpu.make_async_copy(x, out.at[pl.ds(k * n, n)], sem.at[k]) for k, x in enumerate((a, b))]
+    for c in copies:
+        c.start()
+    for c in copies:
+        c.wait()
+
+
+def join_rows(a, b):
+    n, parts, _ = a.shape
+    any_spec = pl.BlockSpec(memory_space=pl.ANY)
+    return pl.pallas_call(
+        join_body, in_specs=[any_spec] * 2, out_shape=jax.ShapeDtypeStruct((2 * n, parts, LANES), a.dtype),
+        out_specs=pl.BlockSpec(memory_space=pltpu.VMEM), scratch_shapes=[pltpu.SemaphoreType.DMA((2,))],
+        cost_estimate=pl.CostEstimate(flops=10**8, bytes_accessed=4 * a.size * a.dtype.itemsize, transcendentals=0),
+        name="join_rows",
+    )(a, b)
+
+
 def route_tables(ids, gates, ep, n_local):
     n_src, top_k, tok = ids.shape
     n = n_src * top_k * tok
@@ -488,11 +521,12 @@
     token = copy // (top_k * tok) * tok + copy % tok
     token = jnp.pad(token, (0, 2 * PAGE))
     gate = jnp.pad(gate, (0, 2 * PAGE)).reshape(-1, LANES)
-    lane = jnp.arange(LANES, dtype=jnp.int32)
-    bounds = jnp.sum((group[:, None] < lane[None, :]).astype(jnp.int32), axis=0)
-    own = jnp.sum((group[:n // n_src, None] == lane[None, :]).astype(jnp.int32), axis=0)
-    starts, ends = bounds[:n_local], bounds[1:n_local + 1]
-    middle = starts + own[:n_local]
+    ids = jnp.arange(n_local, dtype=jnp.int32)
+    hits = jnp.sum((group.reshape(n_src, -1)[:, :, None] == ids).astype(jnp.int32), axis=1)
+    starts = jnp.sum((ids[None, :] < ids[:, None]).astype(jnp.int32) * jnp.sum(hits, axis=0), axis=1)
+    ends = starts + jnp.sum(hits, axis=0)
+    middle = starts + hits[0]
+    bounds = jnp.pad(starts, (0, LANES - n_local), constant_values=0) + jnp.where(jnp.arange(LANES) < n_local, 0, ends[-1])
     runs = [jnp.concatenate(x) for x in ((starts, middle), (middle, ends), (starts, ends))]
     return runs, token, gate, bounds
 
@@ -522,7 +556,6 @@
     expert_spec = P(None, 'ep', None, None)
     ep_pairs = [(i, 1 - i) for i in range(ep_size)]
     core_pairs = [(i, i ^ 1) for i in range(dp_size)]
-    chip_pairs = [(i, i ^ (2 << i % 2)) for i in range(dp_size)]
 
     def device_body(tokens, d_out, expert_ids, gate_vals, w_mix, w_gate, w_up, w_down):
         n_layers = w_mix.shape[0]
@@ -565,7 +598,7 @@
             run, token, gate, bounds = route_tables(pair[0].astype(jnp.int32), pair[1], ep_id, n_local)
             runs.append(run)
             tables.append([(token * parts, gate), (token * (2 * parts), gate)])
-            spot = lax.div(token, tok) * (dp_size * tok) + dp_id * tok + lax.rem(token, tok)
+            spot = dp_id * (2 * tok) + token
             first = jnp.concatenate([spot.reshape(-1, LANES), jnp.pad(bounds.reshape(1, LANES), ((0, 7), (0, 0)))])
             packed.append(jnp.stack([first.astype(jnp.float32), jnp.pad(gate, ((0, 8), (0, 0)))]))
 
@@ -574,7 +607,7 @@
         x_in, u_slabs, u_others, xs = tokens, [u_slab], [swap(u_slab)], []
         d_slab = slab(d_out)
         d_other = swap(after(d_slab, u_others[0]))
-        d_rows = (spread(d_slab), spread(d_other))
+        d_rows = (spread(join_rows(d_slab, d_other)),)
         for layer in range(n_layers):
             if layer:
                 u = mixed(x_in, layer)
@@ -592,10 +625,8 @@
         shared = lax.all_gather(jnp.stack(packed), 'dp', axis=0)
         starts = shared[:, :, 0, -8].astype(jnp.int32)
         core = dp_id % 2
-        kind = (dp_id // 2 + dp_id // 4) % 2
-        dealt = [deal_experts(starts[:, layer], n_local, 4 if layer == top else 2) for layer in range(n_layers)]
-        places = [2 * kind + core if layer == top else core for layer in range(n_layers)]
-        mine = [lists[place] for (lists, _), place in zip(dealt, places)]
+        dealt = [deal_experts(starts[:, layer], n_local, 2) for layer in range(n_layers)]
+        mine = [lists[core] for lists, _ in dealt]
         firsts = [sum(x.shape[0] for x in mine[:layer]) for layer in range(n_layers)]
         list_rows = cdiv(cdiv(dp_size * 2 * cap, LANES), 8) * 8 + 8
         idx_all, gate_all = merge_tables(shared, starts, jnp.concatenate(mine),
@@ -606,7 +637,8 @@
         d_y, full, arrived = d_out, None, []
         d_mix = [None] * n_layers
         for layer in reversed(range(n_layers)):
-            u_rows = tuple(spread(x) for x in (u_slabs[layer], u_others[layer]))
+            both_u = (u_slabs[layer], u_others[layer])
+            u_rows = tuple(spread(x) for x in (both_u if layer < top else (join_rows(*both_u),)))
             slabs = (u_slabs[layer], u_others[layer], d_slab, d_other)
             own, other = token_kernel(layer, runs[layer][2], tables[layer][1], slabs, weights)
             d_u = (d_y.astype(jnp.float32) + own + swap(other)).astype(jnp.bfloat16)
@@ -616,22 +648,14 @@
             d_mix[layer] = jnp.einsum('td,te->de', xs[layer], d_u, preferred_element_type=jnp.float32).astype(jnp.bfloat16)
             d_y = (d_u.astype(jnp.float32)
                    + jnp.einsum('te,de->td', d_u, w_mix[layer], preferred_element_type=jnp.float32)).astype(jnp.bfloat16)
-            tiles = dealt[layer][1][places[layer]]
-            full, part = weight_grads(layer, firsts[layer], mine[layer], after(tiles, last), u_rows + d_rows, idx_all, gate_all,
-                                      weights, full)
-            lists = dealt[layer][0]
-            if layer == top:
-                far = trade(part, chip_pairs)
-                near = trade(part, core_pairs)
-                arrived.append((layer, lists[2 * kind + 1 - core], near))
-                arrived.append((layer, lists[2 - 2 * kind + core], far))
-                arrived.append((layer, lists[3 - 2 * kind - core], trade(far, core_pairs)))
-            else:
-                arrived.append((layer, lists[1 - core], trade(part, core_pairs)))
+            lists, tiles = dealt[layer]
+            full, part = weight_grads(layer, firsts[layer], mine[layer], after(tiles[core], last), (u_rows, d_rows), idx_all,
+                                      gate_all, weights, full)
+            arrived.append((layer, lists[1 - core], trade(part, core_pairs)))
             if layer:
                 d_slab = slab(d_y)
                 d_other = swap(d_slab)
-                d_rows = (spread(d_slab), spread(d_other))
+                d_rows = (spread(join_rows(d_slab, d_other)),)
                 if layer == top:
                     layer_out = (u.astype(jnp.float32) + y_own + swap(after(last, d_other))).astype(jnp.bfloat16)
         for layer, names, part in arrived:

time: 869 us -> 744 us (0.86)
  waiting for transfers between devices: 298 us -> 174 us
  Pallas kernels: 455 us -> 481 us
  other arithmetic: 51.5 us -> 36.6 us
  starting transfers between devices: 24.2 us -> 14.3 us
    ppermute x9, waiting for transfers between devices: 236 us -> 113 us  [swap(): return lax.ppermute(x, 'ep', ep_pairs)]
    pallas_call x2, Pallas kernels: 170 us -> 194 us  [weight_grads(): pl.pallas_call(functools.partial(weight_grad_body, parts=parts, n_exp=n_e...]
    reduce_sum x3 -> x4, other arithmetic: 18.3 us -> 1.8 us  [the longest x1 1.07 us: route_tables(): jnp.sum((group.reshape(n_src, -1)[:, :, None] == ids).astype(jnp.int32),...]
    pallas_call x4 -> x2, Pallas kernels: 39.1 us -> 29.2 us  [merge_half(): pl.pallas_call(functools.partial(merge_body, layer=layer, n_exp=n_exp), g...]
    pallas_call x0 -> x3, Pallas kernels: none -> 9.04 us  [join_rows(): pl.pallas_call(join_body, in_specs=[any_spec] * 2, out_shape=jax.ShapeDty...]
  transfers between devices with their start and end apart: 31 -> 22, of which waited for: 10 -> 7; matrix products, arithmetic and copies ran while one was open for 6% -> 5% of each run, Pallas kernels for 42% -> 52%
where the time goes in v8:
time: 744 us; the launch traced here: 743 us
  Pallas kernels  481 us (65%)
  waiting for transfers between devices  174 us (23%)
  other arithmetic  36.6 us (5%)
  between operations  16.3 us (2%)
  starting transfers between devices  14.3 us (2%)
  local copies, waits for them, and re-layouts  11.9 us (2%)
  matrix products  8.51 us (1%)
    pallas_call x5, Pallas kernels, token_kernel(): pl.pallas_call(functools.partial(token_body, layer=layer, tok=tok, parts=...  235 us
    pallas_call x2, Pallas kernels, weight_grads(): pl.pallas_call(functools.partial(weight_grad_body, parts=parts, n_exp=n_e...  194 us
    ppermute x9, waiting for transfers between devices, swap(): return lax.ppermute(x, 'ep', ep_pairs)  113 us
    psum x1, waiting for transfers between devices, device_body(): d_mix = lax.psum(jnp.stack(d_mix), ('dp', 'ep'))  60.2 us
    pallas_call x2, Pallas kernels, merge_half(): pl.pallas_call(functools.partial(merge_body, layer=layer, n_exp=n_exp), g...  29.2 us
  transfers between devices with their start and end apart: 22, of which 7 were waited for; matrix products, arithmetic and copies ran while one was open for 5% of the time, Pallas kernels for 52%

profile of v8, /device:TPU:0, one launch (start us, length us, event | category | flops | bytes accessed | tf_op | source)
XLA Modules:
  0.0 742.8 jit_solution(10962217849143555546)
XLA Ops:
  8.0 0.8 convert_bitcast_fusion
  8.9 2.4 add_convert_fusion.7
  12.3 3.3 collective-permute-start
  15.6 4.3 collective-permute-done
  20.1 1.1 convert_reduce_fusion
  21.9 6.4 sort.30
  28.4 1.3 fusion.48
  30.6 11.0 %collective-permute-done.1.refs_1_ = bf16[1024,4,128]{2,1,0:T(4,128)(2,1)S(1)} collective-permute-done((bf16[1024,4,128]{2,1,0:T(4,128)(2,1)S(1)}, bf16[1024,4,128]{2,1,0:T(4,128)(2,1)S(1)}, u32[]{:S(2)}, u32[]{:S(2)}) %collective-permute-start.1) | collective-permute-done | bytes 1048608 | tf_op jit(solution)/shard_map/ppermute | solution.py:573
  41.5 1.0 copy-done.1
  42.5 39.2 %experts_forward.3 = f32[1024,512]{1,0:T(8,128)} custom-call(s32[128]{0:T(128)} %get-tuple-element.136.runs, s32[18432]{0:T(1024)} %get-tuple-element.120.idx, f32[144,128]{1,0:T(8,128)} %copy-done.14, bf16[1024,4,128]{2,1,0:T(4,128)(2,1)} %copy-done, bf16[1024,4,128]{2,1,0:T(4,128)(2,1)} %copy-done.1, bf16[2,64,192,512]{3,2,1,0:T(8,128)(2,1)} %bitcast.120, ...), custom_call_target="tpu_custom_call" | custom-call | flops 19327352832 | bytes 37748736 | tf_op jit(solution)/shard_map/experts_forward/pallas_call | solution.py:208
  81.8 39.2 %experts_forward.4 = f32[1024,512]{1,0:T(8,128)} custom-call(s32[128]{0:T(128)} %get-tuple-element.137.runs, s32[18432]{0:T(1024)} %get-tuple-element.120.idx, f32[144,128]{1,0:T(8,128)} %copy-done.14, bf16[1024,4,128]{2,1,0:T(4,128)(2,1)} %copy-done, bf16[1024,4,128]{2,1,0:T(4,128)(2,1)} %copy-done.1, bf16[2,64,192,512]{3,2,1,0:T(8,128)(2,1)} %bitcast.121, ...), custom_call_target="tpu_custom_call" | custom-call | flops 19327352832 | bytes 37748736 | tf_op jit(solution)/shard_map/experts_forward/pallas_call | solution.py:208
  121.1 6.4 sort.31
  129.0 1.3 fusion.47
  131.0 0.7 pad_maximum_fusion.1
  132.4 24.2 %collective-permute-done.4.refs_3_.b = bf16[1024,4,128]{2,1,0:T(4,128)(2,1)S(1)} collective-permute-done((bf16[1024,4,128]{2,1,0:T(4,128)(2,1)S(1)}, bf16[1024,4,128]{2,1,0:T(4,128)(2,1)S(1)}, u32[]{:S(2)}, u32[]{:S(2)}) %collective-permute-start.4) | collective-permute-done | bytes 1048608 | tf_op jit(solution)/shard_map/ppermute | solution.py:573
  156.6 1.0 copy-done.18
  157.6 2.9 join_rows.5
  161.0 45.9 %collective-permute-done.2 = f32[1024,512]{1,0:T(8,128)S(1)} collective-permute-done((f32[1024,512]{1,0:T(8,128)}, f32[1024,512]{1,0:T(8,128)S(1)}, u32[]{:S(2)}, u32[]{:S(2)}) %collective-permute-start.2) | collective-permute-done | bytes 2097184 | tf_op jit(solution)/shard_map/ppermute | solution.py:573
  206.9 1.9 add_convert_fusion.6
  208.7 1.0 copy-done.15
  209.7 0.7 add_convert_fusion.5
  211.3 22.3 %collective-permute-done.3.refs_1_.b = bf16[1024,4,128]{2,1,0:T(4,128)(2,1)} collective-permute-done((bf16[1024,4,128]{2,1,0:T(4,128)(2,1)S(1)}, bf16[1024,4,128]{2,1,0:T(4,128)(2,1)}, u32[]{:S(2)}, u32[]{:S(2)}) %collective-permute-start.3) | collective-permute-done | bytes 1048608 | tf_op jit(solution)/shard_map/ppermute | solution.py:573
  233.6 3.1 join_rows.4
  238.0 53.5 %experts_backward.2 = (f32[1024,512]{1,0:T(8,128)}, f32[1024,512]{1,0:T(8,128)}) custom-call(s32[128]{0:T(128)} %get-tuple-element.139.runs, s32[18432]{0:T(1024)} %get-tuple-element.122.idx, f32[144,128]{1,0:T(8,128)} %copy-done.19, bf16[1024,4,128]{2,1,0:T(4,128)(2,1)} %copy-done.10, bf16[1024,4,128]{2,1,0:T(4,128)(2,1)} %collective-permute-done.3.refs_1_.b, ...), custom_call_target="tpu_custom_call" | custom-call | flops 51539607552 | bytes 37748736 | tf_op jit(solution)/shard_map/experts_backward/pallas_call | solution.py:208
  291.6 3.3 collective-permute-start.5
  294.9 45.6 %experts_forward.5 = (f32[1024,512]{1,0:T(8,128)}, f32[1024,512]{1,0:T(8,128)}) custom-call(s32[128]{0:T(128)} %get-tuple-element.139.runs, s32[18432]{0:T(1024)} %get-tuple-element.123.idx, f32[144,128]{1,0:T(8,128)} %copy-done.19, bf16[1024,4,128]{2,1,0:T(4,128)(2,1)} %copy-done.10, bf16[1024,4,128]{2,1,0:T(4,128)(2,1)} %collective-permute-done.3.refs_1_.b, ...), custom_call_target="tpu_custom_call" | custom-call | flops 38654705664 | bytes 37748736 | tf_op jit(solution)/shard_map/experts_forward/pallas_call | solution.py:208
  340.5 0.8 slice_convert_fusion
  342.2 3.3 add_convert_fusion.4
  345.6 1.0 copy-done.17
  346.6 0.7 add_convert_fusion.3
  347.7 2.5 collective-permute-start.6
  351.8 13.5 %merge_tables.1 = (s32[64,32,128]{2,1,0:T(8,128)}, f32[64,32,128]{2,1,0:T(8,128)}) custom-call(s32[2048]{0:T(1024)} %bitcast.151, s32[64]{0:T(128)} %pad_add_fusion.5.exps, s32[64]{0:T(128)} %constant.143.clone.1.layers, f32[8,2,2,152,128]{4,3,2,1,0:T(8,128)} %bitcast.153), custom_call_target="tpu_custom_call" | custom-call | flops 1000000000 | bytes 2490368 | tf_op jit(solution)/shard_map/merge_tables/pallas_call | solution.py:273
  365.4 5.0 collective-permute-done.6.refs_3_.b
  370.4 57.9 %experts_backward.3 = (f32[1024,512]{1,0:T(8,128)}, f32[1024,512]{1,0:T(8,128)}) custom-call(s32[128]{0:T(128)} %get-tuple-element.135.runs, s32[18432]{0:T(1024)} %get-tuple-element.119.idx, f32[144,128]{1,0:T(8,128)} %copy-done.14, bf16[1024,4,128]{2,1,0:T(4,128)(2,1)} %copy-done, bf16[1024,4,128]{2,1,0:T(4,128)(2,1)} %copy-done.1, ...), custom_call_target="tpu_custom_call" | custom-call | flops 51539607552 | bytes 37748736 | tf_op jit(solution)/shard_map/experts_backward/pallas_call | solution.py:208
  429.0 2.0 collective-permute-start.7
  431.1 3.0 join_rows.3
  435.4 92.6 %weight_grads.2 = (bf16[2,64,192,512]{3,2,1,0:T(8,128)(2,1)}, bf16[2,64,192,512]{3,2,1,0:T(8,128)(2,1)}, bf16[2,64,192,512]{3,2,1,0:T(8,128)(2,1)}, bf16[32,192,...) custom-call(s32[32]{0:T(128)} %copy-done.23, s32[33]{0:T(128)} %get-tuple-element.131.tiles, ...), custom_call_target="tpu_custom_call" | custom-call | flops 309237645312 | bytes 90177536 | tf_op jit(solution)/shard_map/weight_grads/pallas_call | solution.py:426
  528.7 101.5 %weight_grads.3 = (bf16[2,64,192,512]{3,2,1,0:T(8,128)(2,1)}, bf16[2,64,192,512]{3,2,1,0:T(8,128)(2,1)}, bf16[2,64,192,512]{3,2,1,0:T(8,128)(2,1)}, bf16[32,192,...) custom-call(s32[32]{0:T(128)} %copy-done.22, ...), custom_call_target="tpu_custom_call", output_to_operand_aliasing={{0}: (11, {}), {1}: (12, {}), {2}: (13, {})} | custom-call | flops 309237645312 | bytes 90177536 | tf_op jit(solution)/shard_map/weight_grads/pallas_call | solution.py:426
  631.2 2.2 fusion.1
  633.4 2.3 add_convert_fusion.1
  635.8 0.7 fusion
  636.5 1.1 pad_maximum_fusion
  638.1 1.7 add_convert_fusion
  640.4 3.2 add_convert_fusion.2
  643.7 60.2 %all-reduce.12.cloned.1.call-done = bf16[2,512,512]{1,2,0:T(8,128)(2,1)} async-done(((bf16[2,512,512]{1,2,0:T(8,128)(2,1)}), bf16[2,512,512]{1,2,0:T(8,128)(2,1)}) %all-reduce.12.cloned.1.call-update) | async-done | bytes 1048592 | tf_op jit(solution)/shard_map/psum | solution.py:663
  703.8 2.3 copy.50
  706.1 14.6 %merge_half.2 = (bf16[2,64,192,512]{3,2,1,0:T(8,128)(2,1)}, bf16[2,64,192,512]{3,2,1,0:T(8,128)(2,1)}, bf16[2,64,192,512]{3,2,1,0:T(8,128)(2,1)}) custom-call(s32[32]{0:T(128)} %get-tuple-element.126.exps, bf16[32,192,512]{2,1,0:T(8,128)(2,1)} %collective-permute-done.12.a, ...), custom_call_target="tpu_custom_call", output_to_operand_aliasing={{0}: (4, {}), {1}: (5, {}), {2}: (6, {})} | custom-call | flops 1000000000 | bytes 37748736 | tf_op jit(solution)/shard_map/merge_half/pallas_call | solution.py:479
  720.7 14.6 %merge_half.3 = (bf16[2,64,192,512]{3,2,1,0:T(8,128)(2,1)}, bf16[2,64,192,512]{3,2,1,0:T(8,128)(2,1)}, bf16[2,64,192,512]{3,2,1,0:T(8,128)(2,1)}) custom-call(s32[32]{0:T(128)} %get-tuple-element.129.exps, bf16[32,192,512]{2,1,0:T(8,128)(2,1)} %collective-permute-done.9.a, ...), custom_call_target="tpu_custom_call", output_to_operand_aliasing={{0}: (4, {}), {1}: (5, {}), {2}: (6, {})} | custom-call | flops 1000000000 | bytes 37748736 | tf_op jit(solution)/shard_map/merge_half/pallas_call | solution.py:479
  (159 shorter events, 15.6 us)
Async XLA Ops:
  8.0 332.5 %all-gather.18.cloned.1.call-start = ((), (), s32[]{:S(2)}) async-start(), calls=%async_computation.6 | async-start | bytes 2801664 | tf_op jit(solution)/shard_map/all_gather | solution.py:625
  8.9 2.8 copy-start.20
  11.3 1.0 copy-start.6
  11.6 30.9 %copy-start = (bf16[1024,4,128]{2,1,0:T(4,128)(2,1)}, bf16[1024,4,128]{2,1,0:T(4,128)(2,1)S(1)}, u32[]{:S(2)}) copy-start(bf16[1024,4,128]{2,1,0:T(4,128)(2,1)S(1)} %reshape.280.refs_0_) | copy-start | bytes 3145732
  12.3 7.6 %collective-permute-start = (f32[2,2,8,1024]{3,2,1,0:T(8,128)S(1)}, f32[2,2,8,1024]{3,2,1,0:T(8,128)S(1)}, u32[]{:S(2)}, u32[]{:S(2)}) collective-permute-start(f32[2,2,8,1024]{3,2,1,0:T(8,128)S(1)} %get-tuple-element.44), channel_id=1, source_target_pairs={{0,8},{8,0},{1,9},{9,1},{2,10},{10,2},{3,11},{11,3},{4,12},{12,4},... | collective-permute-start | bytes 393224 | tf_op jit(solution)/shard_map/ppermute | solution.py:573
  15.6 26.0 %collective-permute-start.1 = (bf16[1024,4,128]{2,1,0:T(4,128)(2,1)S(1)}, bf16[1024,4,128]{2,1,0:T(4,128)(2,1)S(1)}, u32[]{:S(2)}, u32[]{:S(2)}) collective-permute-start(bf16[1024,4,128]{2,1,0:T(4,128)(2,1)S(1)} %reshape.280.refs_0_), channel_id=1, source_target_pairs={{0,8},{8,0},{1,9},{9,1},{2,10},{10,2},{3,11},{11,3},{4,12},{12,4},... | collective-permute-start | bytes 3145736 | tf_op jit(solution)/shard_map/ppermute | solution.py:573
  28.4 14.1 %copy-start.14 = (f32[144,128]{1,0:T(8,128)}, f32[144,128]{1,0:T(8,128)S(1)}, u32[]{:S(2)}) copy-start(f32[144,128]{1,0:T(8,128)S(1)} %pad_bitcast_fusion.3.gates) | copy-start | bytes 221188
  121.0 11.1 %copy-start.3 = (bf16[1024,512]{1,0:T(8,128)(2,1)S(1)}, bf16[1024,512]{1,0:T(8,128)(2,1)}, u32[]{:S(2)}) copy-start(bf16[1024,512]{1,0:T(8,128)(2,1)} %param.9) | copy-start | bytes 3145732
  130.3 30.2 %copy-start.19 = (f32[144,128]{1,0:T(8,128)}, f32[144,128]{1,0:T(8,128)S(1)}, u32[]{:S(2)}) copy-start(f32[144,128]{1,0:T(8,128)S(1)} %pad_bitcast_fusion.2.gates) | copy-start | bytes 221188
  131.8 303.6 %all-gather.16.cloned.1.call-start = ((), (), s32[]{:S(2)}) async-start(), calls=%async_computation.5 | async-start | bytes 18874368 | tf_op jit(solution)/shard_map/all_gather | solution.py:576
  132.3 24.3 %copy-start.9 = (bf16[1024,4,128]{2,1,0:T(4,128)(2,1)}, bf16[1024,4,128]{2,1,0:T(4,128)(2,1)S(1)}, u32[]{:S(2)}) copy-start(bf16[1024,4,128]{2,1,0:T(4,128)(2,1)S(1)} %reshape.284.refs_2_.a) | copy-start | bytes 3145732
  132.4 24.3 %collective-permute-start.4 = (bf16[1024,4,128]{2,1,0:T(4,128)(2,1)S(1)}, bf16[1024,4,128]{2,1,0:T(4,128)(2,1)S(1)}, u32[]{:S(2)}, u32[]{:S(2)}) collective-permute-start(bf16[1024,4,128]{2,1,0:T(4,128)(2,1)S(1)} %reshape.284.refs_2_.a), channel_id=1, source_target_pairs={{0,8},{8,0},{1,9},{9,1},{2,10},{10,2},{3,11},{11,3},{4,12},{12,4},... | collective-permute-start | bytes 3145736 | tf_op jit(solution)/shard_map/ppermute | solution.py:573
  156.6 1.0 copy-start.18
  160.5 46.3 %copy-start.2 = (f32[1024,512]{1,0:T(8,128)S(1)}, f32[1024,512]{1,0:T(8,128)}, u32[]{:S(2)}) copy-start(f32[1024,512]{1,0:T(8,128)} %experts_forward.4) | copy-start | bytes 6291460
  160.6 274.8 %all-gather.14.cloned.1.call-start = ((), (), s32[]{:S(2)}) async-start(), calls=%async_computation.4 | async-start | bytes 18874368 | tf_op jit(solution)/shard_map/all_gather | solution.py:576
  160.6 49.1 %copy-start.25 = (bf16[2,512,512]{2,1,0:T(8,128)(2,1)S(1)}, bf16[2,512,512]{2,1,0:T(8,128)(2,1)}, u32[]{:S(2)}) copy-start(bf16[2,512,512]{2,1,0:T(8,128)(2,1)} %param.12) | copy-start | bytes 3145732
  160.6 46.2 %collective-permute-start.2 = (f32[1024,512]{1,0:T(8,128)}, f32[1024,512]{1,0:T(8,128)S(1)}, u32[]{:S(2)}, u32[]{:S(2)}) collective-permute-start(f32[1024,512]{1,0:T(8,128)} %experts_forward.3), channel_id=1, source_target_pairs={{0,8},{8,0},{1,9},{9,1},{2,10},{10,2},{3,11},{11,3},{4,12},{12,4},... | collective-permute-start | bytes 6291464 | tf_op jit(solution)/shard_map/ppermute | solution.py:573
  210.4 26.4 %copy-start.4 = (bf16[1024,512]{1,0:T(8,128)(2,1)}, bf16[1024,512]{1,0:T(8,128)(2,1)S(1)}, u32[]{:S(2)}) copy-start(bf16[1024,512]{1,0:T(8,128)(2,1)S(1)} %add_convert_fusion.5) | copy-start | bytes 3145732
  210.7 22.9 %copy-start.10 = (bf16[1024,4,128]{2,1,0:T(4,128)(2,1)}, bf16[1024,4,128]{2,1,0:T(4,128)(2,1)S(1)}, u32[]{:S(2)}) copy-start(bf16[1024,4,128]{2,1,0:T(4,128)(2,1)S(1)} %reshape.283.refs_0_.a) | copy-start | bytes 3145732
  210.7 22.9 %collective-permute-start.3 = (bf16[1024,4,128]{2,1,0:T(4,128)(2,1)S(1)}, bf16[1024,4,128]{2,1,0:T(4,128)(2,1)}, u32[]{:S(2)}, u32[]{:S(2)}) collective-permute-start(bf16[1024,4,128]{2,1,0:T(4,128)(2,1)S(1)} %reshape.283.refs_0_.a), channel_id=1, source_target_pairs={{0,8},{8,0},{1,9},{9,1},{2,10},{10,2},{3,11},{11,3},{4,12},{12,4},... | collective-permute-start | bytes 3145736 | tf_op jit(solution)/shard_map/ppermute | solution.py:573
  236.8 291.9 %all-gather.8.cloned.1.call-start = ((), (), s32[]{:S(2)}) async-start(), calls=%async_computation.1 | async-start | bytes 9437184 | tf_op jit(solution)/shard_map/all_gather | solution.py:576
  237.4 291.3 %all-gather.10.cloned.1.call-start = ((), (), s32[]{:S(2)}) async-start(), calls=%async_computation.2 | async-start | bytes 9437184 | tf_op jit(solution)/shard_map/all_gather | solution.py:576
  238.0 290.7 %all-gather.12.cloned.1.call-start = ((), (), s32[]{:S(2)}) async-start(), calls=%async_computation.3 | async-start | bytes 18874368 | tf_op jit(solution)/shard_map/all_gather | solution.py:576
  291.6 50.6 %collective-permute-start.5 = (f32[1024,512]{1,0:T(8,128)}, f32[1024,512]{1,0:T(8,128)}, u32[]{:S(2)}, u32[]{:S(2)}) collective-permute-start(f32[1024,512]{1,0:T(8,128)} %get-tuple-element.52), channel_id=1, source_target_pairs={{0,8},{8,0},{1,9},{9,1},{2,10},{10,2},{3,11},{11,3},{4,12},{12,4},... | collective-permute-start | bytes 6291464 | tf_op jit(solution)/shard_map/ppermute | solution.py:573
  341.4 4.2 copy-start.21
  342.2 4.4 copy-start.26
  345.6 1.0 copy-start.17
  347.3 18.0 %copy-start.7 = (bf16[1024,512]{1,0:T(8,128)(2,1)}, bf16[1024,512]{1,0:T(8,128)(2,1)S(1)}, u32[]{:S(2)}) copy-start(bf16[1024,512]{1,0:T(8,128)(2,1)S(1)} %add_convert_fusion.3) | copy-start | bytes 3145732
  347.6 22.8 %copy-start.11 = (bf16[1024,4,128]{2,1,0:T(4,128)(2,1)}, bf16[1024,4,128]{2,1,0:T(4,128)(2,1)S(1)}, u32[]{:S(2)}) copy-start(bf16[1024,4,128]{2,1,0:T(4,128)(2,1)S(1)} %reshape.285.refs_2_.a) | copy-start | bytes 3145732
  347.7 22.8 %collective-permute-start.6 = (bf16[1024,4,128]{2,1,0:T(4,128)(2,1)S(1)}, bf16[1024,4,128]{2,1,0:T(4,128)(2,1)}, u32[]{:S(2)}, u32[]{:S(2)}) collective-permute-start(bf16[1024,4,128]{2,1,0:T(4,128)(2,1)S(1)} %reshape.285.refs_2_.a), channel_id=1, source_target_pairs={{0,8},{8,0},{1,9},{9,1},{2,10},{10,2},{3,11},{11,3},{4,12},{12,4},... | collective-permute-start | bytes 3145736 | tf_op jit(solution)/shard_map/ppermute | solution.py:573
  350.7 77.6 %copy-start.23 = (s32[32]{0:T(128)}, s32[32]{0:T(128)S(1)}, u32[]{:S(2)}) copy-start(s32[32]{0:T(128)S(1)} %get-tuple-element.127.exps) | copy-start | bytes 388
  351.3 77.1 %copy-start.22 = (s32[32]{0:T(128)}, s32[32]{0:T(128)S(1)}, u32[]{:S(2)}) copy-start(s32[32]{0:T(128)S(1)} %get-tuple-element.128.exps) | copy-start | bytes 388
  428.4 201.9 %collective-permute-start.8 = (f32[1024,512]{1,0:T(8,128)}, f32[1024,512]{1,0:T(8,128)}, u32[]{:S(2)}, u32[]{:S(2)}) collective-permute-start(f32[1024,512]{1,0:T(8,128)} %get-tuple-element.59), channel_id=1, source_target_pairs={{0,8},{8,0},{1,9},{9,1},{2,10},{10,2},{3,11},{11,3},{4,12},{12,4},... | collective-permute-start | bytes 6291464 | tf_op jit(solution)/shard_map/ppermute | solution.py:573
  429.0 201.6 %collective-permute-start.7 = (f32[1024,512]{1,0:T(8,128)}, f32[1024,512]{1,0:T(8,128)}, u32[]{:S(2)}, u32[]{:S(2)}) collective-permute-start(f32[1024,512]{1,0:T(8,128)} %get-tuple-element.57), channel_id=1, source_target_pairs={{0,8},{8,0},{1,9},{9,1},{2,10},{10,2},{3,11},{11,3},{4,12},{12,4},... | collective-permute-start | bytes 6291464 | tf_op jit(solution)/shard_map/ppermute | solution.py:573
  434.1 269.7 %all-reduce.12.cloned.1.call-start = ((), (), s32[]{:S(2)}) async-start(), calls=%async_computation | async-start | bytes 2097152 | tf_op jit(solution)/shard_map/psum | solution.py:663
  528.0 102.8 %collective-permute-start.12 = (bf16[32,192,512]{2,1,0:T(8,128)(2,1)}, bf16[32,192,512]{2,1,0:T(8,128)(2,1)}, u32[]{:S(2)}, u32[]{:S(2)}) collective-permute-start(bf16[32,192,512]{2,1,0:T(8,128)(2,1)} %get-tuple-element.70), channel_id=1, source_target_pairs={{0,1},{1,0},{2,3},{3,2},{4,5},{5,4},{6,7},{7,6},{8,9},{9,8},{10,11... | collective-permute-start | bytes 18874376 | tf_op jit(solution)/shard_map/ppermute | solution.py:579
  528.2 177.9 %collective-permute-start.13 = (bf16[32,192,512]{2,1,0:T(8,128)(2,1)}, bf16[32,192,512]{2,1,0:T(8,128)(2,1)}, u32[]{:S(2)}, u32[]{:S(2)}) collective-permute-start(bf16[32,192,512]{2,1,0:T(8,128)(2,1)} %get-tuple-element.71), channel_id=1, source_target_pairs={{0,1},{1,0},{2,3},{3,2},{4,5},{5,4},{6,7},{7,6},{8,9},{9,8},{10,11... | collective-permute-start | bytes 18874376 | tf_op jit(solution)/shard_map/ppermute | solution.py:579
  528.5 177.6 %collective-permute-start.14 = (bf16[32,192,512]{2,1,0:T(8,128)(2,1)}, bf16[32,192,512]{2,1,0:T(8,128)(2,1)}, u32[]{:S(2)}, u32[]{:S(2)}) collective-permute-start(bf16[32,192,512]{2,1,0:T(8,128)(2,1)} %get-tuple-element.72), channel_id=1, source_target_pairs={{0,1},{1,0},{2,3},{3,2},{4,5},{5,4},{6,7},{7,6},{8,9},{9,8},{10,11... | collective-permute-start | bytes 18874376 | tf_op jit(solution)/shard_map/ppermute | solution.py:579
  528.7 102.5 %copy-start.16 = (bf16[1024,512]{1,0:T(8,128)(2,1)S(1)}, bf16[1024,512]{1,0:T(8,128)(2,1)}, u32[]{:S(2)}) copy-start(bf16[1024,512]{1,0:T(8,128)(2,1)} %copy-done.15) | copy-start | bytes 3145732
  630.3 90.5 %collective-permute-start.9 = (bf16[32,192,512]{2,1,0:T(8,128)(2,1)}, bf16[32,192,512]{2,1,0:T(8,128)(2,1)}, u32[]{:S(2)}, u32[]{:S(2)}) collective-permute-start(bf16[32,192,512]{2,1,0:T(8,128)(2,1)} %get-tuple-element.67), channel_id=1, source_target_pairs={{0,1},{1,0},{2,3},{3,2},{4,5},{5,4},{6,7},{7,6},{8,9},{9,8},{10,11... | collective-permute-start | bytes 18874376 | tf_op jit(solution)/shard_map/ppermute | solution.py:579
  630.7 90.0 %collective-permute-start.10 = (bf16[32,192,512]{2,1,0:T(8,128)(2,1)}, bf16[32,192,512]{2,1,0:T(8,128)(2,1)}, u32[]{:S(2)}, u32[]{:S(2)}) collective-permute-start(bf16[32,192,512]{2,1,0:T(8,128)(2,1)} %get-tuple-element.68), channel_id=1, source_target_pairs={{0,1},{1,0},{2,3},{3,2},{4,5},{5,4},{6,7},{7,6},{8,9},{9,8},{10,11... | collective-permute-start | bytes 18874376 | tf_op jit(solution)/shard_map/ppermute | solution.py:579
  630.8 2.6 copy-start.8
  630.8 2.6 copy-start.13
  630.8 89.9 %collective-permute-start.11 = (bf16[32,192,512]{2,1,0:T(8,128)(2,1)}, bf16[32,192,512]{2,1,0:T(8,128)(2,1)}, u32[]{:S(2)}, u32[]{:S(2)}) collective-permute-start(bf16[32,192,512]{2,1,0:T(8,128)(2,1)} %get-tuple-element.69), channel_id=1, source_target_pairs={{0,1},{1,0},{2,3},{3,2},{4,5},{5,4},{6,7},{7,6},{8,9},{9,8},{10,11... | collective-permute-start | bytes 18874376 | tf_op jit(solution)/shard_map/ppermute | solution.py:579
  633.4 2.4 copy-start.24
  636.5 1.6 copy-start.27
  638.1 1.7 copy-start.5
  638.1 2.3 copy-start.12
  (2 other events, 1.9 us)
Sparse Core Ops, SparseCore 0:
  131.9 25.8 all-gather.17
  160.7 86.0 all-gather.15
  249.2 85.9 all-gather.13
  337.5 50.4 all-gather.7
  390.3 50.5 all-gather.9
  442.5 85.9 all-gather.11
Sparse Core Ops, SparseCore 1:
  637.7 66.1 all-reduce.11

commit v9 on v8

--- a/solution.py
+++ b/solution.py
@@ -287,8 +287,8 @@
     )(starts.reshape(-1), exps, layers, shared)
 
 
-def weight_grad_body(exps, tiles, begins, *refs, parts, n_exp, n_alias, n_rows, first_list, page):
-    rows_in, refs = refs[:sum(n_rows)], refs[sum(n_rows):]
+def weight_grad_body(exps, tiles, begins, *refs, parts, n_exp, n_alias, first_list, page):
+    rows_in, refs = refs[:4], refs[4:]
     idx_all, gate_ref, g_ref, up_ref, w_ref = refs[:5]
     (dg_ref, du_ref, dw_ref, og_ref, ou_ref, ow_ref,
      uds, rows, u0, c0, d0, h0, u1, c1, d1, h1, gacc, wacc, idx_s, sem, tsem) = refs[5 + n_alias:]
@@ -312,16 +312,10 @@
     @pl.when(e == 0)
     def _():
         n_tok = uds.shape[0] - 8
-        copies = []
-        for kind, arrays in enumerate((rows_in[:n_rows[0]], rows_in[n_rows[0]:])):
-            part = pl.ds(kind * parts, parts)
-            if len(arrays) == 1:
-                copies.append(pltpu.make_async_copy(arrays[0], uds.at[pl.ds(0, n_tok), part], sem.at[kind]))
-                continue
-            run = n_tok // (2 * SOURCES)
-            for q in range(2 * SOURCES):
-                copies.append(pltpu.make_async_copy(arrays[q % 2].at[pl.ds(q // 2 * run, run)],
-                                                    uds.at[pl.ds(q * run, run), part], sem.at[kind]))
+        run = n_tok // (2 * SOURCES)
+        copies = [pltpu.make_async_copy(src.at[pl.ds(q * run, run)],
+                                        uds.at[pl.ds((2 * q + k % 2) * run, run), pl.ds(k // 2 * parts, parts)], sem.at[k])
+                  for q in range(SOURCES) for k, src in enumerate(rows_in)]
         for c in copies:
             c.start()
         table_copy(0).start()
@@ -407,8 +401,8 @@
 
 
 def weight_grads(layer, first, exps, tiles, rows, idx_all, gates, weights, full):
-    parts = rows[0][0].shape[1]
-    n_tok = sum(x.shape[0] for x in rows[0])
+    n_half, parts, _ = rows[0].shape
+    n_tok = 2 * n_half
     n_layers, n_local, ff, d_model = weights[0].shape
     n_exp = exps.shape[0]
     out_rows = gates.shape[1]
@@ -424,26 +418,25 @@
     tile_set = [pltpu.VMEM((WTILE, d_model), jnp.bfloat16)] * 2 + [pltpu.VMEM((2 * ff, WTILE), jnp.bfloat16),
                                                                  pltpu.VMEM((ff, WTILE), jnp.bfloat16)]
     outs = pl.pallas_call(
-        functools.partial(weight_grad_body, parts=parts, n_exp=n_exp, n_alias=len(aliased),
-                          n_rows=[len(x) for x in rows], first_list=first, page=page),
+        functools.partial(weight_grad_body, parts=parts, n_exp=n_exp, n_alias=len(aliased), first_list=first, page=page),
         grid_spec=pltpu.PrefetchScalarGridSpec(
             num_scalar_prefetch=3,
             grid=(n_exp + 1,),
-            in_specs=[any_spec] * (sum(len(x) for x in rows) + 1) + [gate_spec] + [mine] * 3 + [any_spec] * len(aliased),
+            in_specs=[any_spec] * 5 + [gate_spec] + [mine] * 3 + [any_spec] * len(aliased),
             out_specs=[done] * 3 + [half] * 3,
             scratch_shapes=[pltpu.VMEM((n_tok + 8, 2 * parts, LANES), jnp.bfloat16)]
             + [pltpu.VMEM((WTILE * PITCH + 16, LANES), jnp.float32)] + tile_set * 2
             + [pltpu.VMEM((2 * ff, d_model), jnp.float32), pltpu.VMEM((ff, d_model), jnp.float32),
-               pltpu.SMEM((3 * page,), jnp.int32), pltpu.SemaphoreType.DMA((2,)), pltpu.SemaphoreType.DMA((3,))],
+               pltpu.SMEM((3 * page,), jnp.int32), pltpu.SemaphoreType.DMA((4,)), pltpu.SemaphoreType.DMA((3,))],
         ),
         out_shape=[jax.ShapeDtypeStruct((n_layers, n_local, ff, d_model), jnp.bfloat16)] * 3
         + [jax.ShapeDtypeStruct((n_exp, ff, d_model), jnp.bfloat16)] * 3,
-        input_output_aliases={sum(len(x) for x in rows) + 8 + k: k for k in range(len(aliased))},
+        input_output_aliases={12 + k: k for k in range(len(aliased))},
         compiler_params=pltpu.CompilerParams(dimension_semantics=("arbitrary",), vmem_limit_bytes=VMEM_LIMIT),
         cost_estimate=pl.CostEstimate(flops=6 * n_tok * n_exp * d_model * ff,
                                       bytes_accessed=n_tok * d_model * 4 + 9 * n_exp * ff * d_model * 2, transcendentals=0),
         name="weight_grads",
-    )(exps, tiles, begins, *rows[0], *rows[1], idx_all, gates, *weights, *aliased)
+    )(exps, tiles, begins, *rows, idx_all, gates, *weights, *aliased)
     return outs[:3], outs[3:]
 
 
@@ -488,26 +481,6 @@
         cost_estimate=pl.CostEstimate(flops=10**9, bytes_accessed=6 * n_exp * ff * d_model * 2, transcendentals=0),
         name="merge_half",
     )(exps, *half, *full)
-
-
-def join_body(a, b, out, sem):
-    n = a.shape[0]
-    copies = [pltpu.make_async_copy(x, out.at[pl.ds(k * n, n)], sem.at[k]) for k, x in enumerate((a, b))]
-    for c in copies:
-        c.start()
-    for c in copies:
-        c.wait()
-
-
-def join_rows(a, b):
-    n, parts, _ = a.shape
-    any_spec = pl.BlockSpec(memory_space=pl.ANY)
-    return pl.pallas_call(
-        join_body, in_specs=[any_spec] * 2, out_shape=jax.ShapeDtypeStruct((2 * n, parts, LANES), a.dtype),
-        out_specs=pl.BlockSpec(memory_space=pltpu.VMEM), scratch_shapes=[pltpu.SemaphoreType.DMA((2,))],
-        cost_estimate=pl.CostEstimate(flops=10**8, bytes_accessed=4 * a.size * a.dtype.itemsize, transcendentals=0),
-        name="join_rows",
-    )(a, b)
 
 
 def route_tables(ids, gates, ep, n_local):
@@ -573,7 +546,7 @@
             return lax.ppermute(x, 'ep', ep_pairs)
 
         def spread(x):
-            return lax.all_gather(x, 'dp', axis=0, tiled=True)
+            return [lax.all_gather(y, 'dp', axis=0, tiled=True) for y in x]
 
         def trade(x, pairs):
             return [lax.ppermute(y, 'dp', pairs) for y in x]
@@ -607,19 +580,19 @@
         x_in, u_slabs, u_others, xs = tokens, [u_slab], [swap(u_slab)], []
         d_slab = slab(d_out)
         d_other = swap(after(d_slab, u_others[0]))
-        d_rows = (spread(join_rows(d_slab, d_other)),)
+        d_rows = spread((d_slab, d_other))
         for layer in range(n_layers):
             if layer:
                 u = mixed(x_in, layer)
                 u_slabs.append(slab(u))
                 u_others.append(swap(u_slabs[layer]))
+                add_tables(after(both[:, layer], u_slabs[layer]))
             xs.append(x_in)
             if layer < top:
                 other, = token_kernel(layer, runs[layer][1], tables[layer][0], (u_slabs[layer], u_others[layer]), weights, (1,))
                 sent = swap(other)
                 own, = token_kernel(layer, runs[layer][0], tables[layer][0], (after(u_slabs[layer], other), u_others[layer]),
                                     weights, (0,))
-                add_tables(after(both[:, layer + 1], own))
                 x_in = (u.astype(jnp.float32) + own + sent).astype(jnp.bfloat16)
 
         shared = lax.all_gather(jnp.stack(packed), 'dp', axis=0)
@@ -637,8 +610,7 @@
         d_y, full, arrived = d_out, None, []
         d_mix = [None] * n_layers
         for layer in reversed(range(n_layers)):
-            both_u = (u_slabs[layer], u_others[layer])
-            u_rows = tuple(spread(x) for x in (both_u if layer < top else (join_rows(*both_u),)))
+            u_rows = spread((u_slabs[layer], u_others[layer]))
             slabs = (u_slabs[layer], u_others[layer], d_slab, d_other)
             own, other = token_kernel(layer, runs[layer][2], tables[layer][1], slabs, weights)
             d_u = (d_y.astype(jnp.float32) + own + swap(other)).astype(jnp.bfloat16)
@@ -649,13 +621,13 @@
             d_y = (d_u.astype(jnp.float32)
                    + jnp.einsum('te,de->td', d_u, w_mix[layer], preferred_element_type=jnp.float32)).astype(jnp.bfloat16)
             lists, tiles = dealt[layer]
-            full, part = weight_grads(layer, firsts[layer], mine[layer], after(tiles[core], last), (u_rows, d_rows), idx_all,
+            full, part = weight_grads(layer, firsts[layer], mine[layer], after(tiles[core], last), u_rows + d_rows, idx_all,
                                       gate_all, weights, full)
             arrived.append((layer, lists[1 - core], trade(part, core_pairs)))
             if layer:
                 d_slab = slab(d_y)
                 d_other = swap(d_slab)
-                d_rows = (spread(join_rows(d_slab, d_other)),)
+                d_rows = spread((d_slab, d_other))
                 if layer == top:
                     layer_out = (u.astype(jnp.float32) + y_own + swap(after(last, d_other))).astype(jnp.bfloat16)
         for layer, names, part in arrived:

time: 744 us -> 808 us (1.086)
  waiting for transfers between devices: 174 us -> 238 us
    all_gather x5 -> x8, waiting for transfers between devices: 0.01 us -> 62.2 us  [spread(): return [lax.all_gather(y, 'dp', axis=0, tiled=True) for y in x]]
    pallas_call x3 -> x0, Pallas kernels: 9.04 us -> none  [join_rows(): pl.pallas_call(join_body, in_specs=[any_spec] * 2, out_shape=jax.ShapeDty...]
  transfers between devices with their start and end apart: 22 -> 25, of which waited for: 7 -> 9; matrix products, arithmetic and copies ran while one was open for 5% -> 4% of each run, Pallas kernels for 52% -> 52%
where the time goes in v9:
time: 808 us; the launch traced here: 807 us
  Pallas kernels  474 us (59%)
  waiting for transfers between devices  238 us (29%)
  other arithmetic  36.6 us (5%)
  local copies, waits for them, and re-layouts  18.2 us (2%)
  starting transfers between devices  16.2 us (2%)
  between operations  16 us (2%)
  matrix products  8.45 us (1%)
    pallas_call x5, Pallas kernels, token_kernel(): pl.pallas_call(functools.partial(token_body, layer=layer, tok=tok, parts=...  237 us
    pallas_call x2, Pallas kernels, weight_grads(): pl.pallas_call(functools.partial(weight_grad_body, parts=parts, n_exp=n_e...  195 us
    ppermute x9, waiting for transfers between devices, swap(): return lax.ppermute(x, 'ep', ep_pairs)  113 us
    all_gather x8, waiting for transfers between devices, spread(): return [lax.all_gather(y, 'dp', axis=0, tiled=True) for y in x]  62.2 us
    psum x1, waiting for transfers between devices, device_body(): d_mix = lax.psum(jnp.stack(d_mix), ('dp', 'ep'))  60.2 us
    pallas_call x2, Pallas kernels, merge_half(): pl.pallas_call(functools.partial(merge_body, layer=layer, n_exp=n_exp), g...  29.2 us
  transfers between devices with their start and end apart: 25, of which 9 were waited for; matrix products, arithmetic and copies ran while one was open for 4% of the time, Pallas kernels for 52%

profile of v9, /device:TPU:0, one launch (start us, length us, event | category | flops | bytes accessed | tf_op | source)
XLA Modules:
  0.0 807.2 jit_solution(4624942998828101014)
XLA Ops:
  8.9 2.4 add_convert_fusion.7
  12.3 3.3 collective-permute-start
  15.6 4.3 collective-permute-done
  20.1 1.1 convert_reduce_fusion
  21.9 6.4 sort.30
  28.4 1.3 fusion.48
  30.5 11.1 %collective-permute-done.1.refs_1_ = bf16[1024,4,128]{2,1,0:T(4,128)(2,1)S(1)} collective-permute-done((bf16[1024,4,128]{2,1,0:T(4,128)(2,1)S(1)}, bf16[1024,4,128]{2,1,0:T(4,128)(2,1)S(1)}, u32[]{:S(2)}, u32[]{:S(2)}) %collective-permute-start.1) | collective-permute-done | bytes 1048608 | tf_op jit(solution)/shard_map/ppermute | solution.py:546
  41.5 1.0 copy-done.1
  42.5 39.2 %experts_forward.3 = f32[1024,512]{1,0:T(8,128)} custom-call(s32[128]{0:T(128)} %get-tuple-element.136.runs, s32[18432]{0:T(1024)} %get-tuple-element.120.idx, f32[144,128]{1,0:T(8,128)} %copy-done.13, bf16[1024,4,128]{2,1,0:T(4,128)(2,1)} %copy-done, bf16[1024,4,128]{2,1,0:T(4,128)(2,1)} %copy-done.1, bf16[2,64,192,512]{3,2,1,0:T(8,128)(2,1)} %bitcast.120, ...), custom_call_target="tpu_custom_call" | custom-call | flops 19327352832 | bytes 37748736 | tf_op jit(solution)/shard_map/experts_forward/pallas_call | solution.py:208
  81.9 39.5 %experts_forward.4 = f32[1024,512]{1,0:T(8,128)} custom-call(s32[128]{0:T(128)} %get-tuple-element.137.runs, s32[18432]{0:T(1024)} %get-tuple-element.120.idx, f32[144,128]{1,0:T(8,128)} %copy-done.13, bf16[1024,4,128]{2,1,0:T(4,128)(2,1)} %copy-done, bf16[1024,4,128]{2,1,0:T(4,128)(2,1)} %copy-done.1, bf16[2,64,192,512]{3,2,1,0:T(8,128)(2,1)} %bitcast.121, ...), custom_call_target="tpu_custom_call" | custom-call | flops 19327352832 | bytes 37748736 | tf_op jit(solution)/shard_map/experts_forward/pallas_call | solution.py:208
  121.4 7.4 collective-permute-done.2
  128.8 2.8 add_convert_fusion.6
  131.7 1.0 copy-done.17
  133.4 1.0 copy-done.5
  134.3 1.1 reshape.282.refs_0_
  135.5 6.4 sort.31
  143.4 1.3 fusion.47
  146.3 1.1 reshape.284.refs_2_
  147.8 23.3 %collective-permute-done.4.refs_3_ = bf16[1024,4,128]{2,1,0:T(4,128)(2,1)S(1)} collective-permute-done((bf16[1024,4,128]{2,1,0:T(4,128)(2,1)}, bf16[1024,4,128]{2,1,0:T(4,128)(2,1)S(1)}, u32[]{:S(2)}, u32[]{:S(2)}) %collective-permute-start.4) | collective-permute-done | bytes 1048608 | tf_op jit(solution)/shard_map/ppermute | solution.py:546
  171.1 1.0 copy-done.14
  173.4 22.1 %collective-permute-done.3.refs_1_ = bf16[1024,4,128]{2,1,0:T(4,128)(2,1)S(1)} collective-permute-done((bf16[1024,4,128]{2,1,0:T(4,128)(2,1)S(1)}, bf16[1024,4,128]{2,1,0:T(4,128)(2,1)S(1)}, u32[]{:S(2)}, u32[]{:S(2)}) %collective-permute-start.3) | collective-permute-done | bytes 1048608 | tf_op jit(solution)/shard_map/ppermute | solution.py:546
  195.4 1.0 copy-done.15
  197.8 54.3 %experts_backward.2 = (f32[1024,512]{1,0:T(8,128)}, f32[1024,512]{1,0:T(8,128)}) custom-call(s32[128]{0:T(128)} %get-tuple-element.139.runs, s32[18432]{0:T(1024)} %get-tuple-element.122.idx, f32[144,128]{1,0:T(8,128)} %copy-done.20, bf16[1024,4,128]{2,1,0:T(4,128)(2,1)} %reshape.282.refs_0_, bf16[1024,4,128]{2,1,0:T(4,128)(2,1)} %copy-done.15, ...), custom_call_target="tpu_custom_call" | custom-call | flops 51539607552 | bytes 37748736 | tf_op jit(solution)/shard_map/experts_backward/pallas_call | solution.py:208
  252.1 3.1 collective-permute-start.5
  255.2 45.1 %collective-permute-done.5 = f32[1024,512]{1,0:T(8,128)S(1)} collective-permute-done((f32[1024,512]{1,0:T(8,128)}, f32[1024,512]{1,0:T(8,128)S(1)}, u32[]{:S(2)}, u32[]{:S(2)}) %collective-permute-start.5) | collective-permute-done | bytes 2097184 | tf_op jit(solution)/shard_map/ppermute | solution.py:546
  300.3 2.3 add_convert_fusion.4
  302.6 1.0 copy-done.19
  305.3 1.2 reshape.285.refs_2_
  306.7 1.7 collective-permute-start.6
  308.4 45.7 %experts_forward.5 = (f32[1024,512]{1,0:T(8,128)}, f32[1024,512]{1,0:T(8,128)}) custom-call(s32[128]{0:T(128)} %get-tuple-element.139.runs, s32[18432]{0:T(1024)} %get-tuple-element.123.idx, f32[144,128]{1,0:T(8,128)} %copy-done.20, bf16[1024,4,128]{2,1,0:T(4,128)(2,1)} %reshape.282.refs_0_, bf16[1024,4,128]{2,1,0:T(4,128)(2,1)} %copy-done.15, ...), custom_call_target="tpu_custom_call" | custom-call | flops 38654705664 | bytes 37748736 | tf_op jit(solution)/shard_map/experts_forward/pallas_call | solution.py:208
  354.2 1.0 copy-done.16
  355.1 57.8 %experts_backward.3 = (f32[1024,512]{1,0:T(8,128)}, f32[1024,512]{1,0:T(8,128)}) custom-call(s32[128]{0:T(128)} %get-tuple-element.135.runs, s32[18432]{0:T(1024)} %get-tuple-element.119.idx, f32[144,128]{1,0:T(8,128)} %copy-done.13, bf16[1024,4,128]{2,1,0:T(4,128)(2,1)} %copy-done, bf16[1024,4,128]{2,1,0:T(4,128)(2,1)} %copy-done.1, ...), custom_call_target="tpu_custom_call" | custom-call | flops 51539607552 | bytes 37748736 | tf_op jit(solution)/shard_map/experts_backward/pallas_call | solution.py:208
  413.0 2.0 collective-permute-start.7
  420.5 13.7 %merge_tables.1 = (s32[64,32,128]{2,1,0:T(8,128)}, f32[64,32,128]{2,1,0:T(8,128)}) custom-call(s32[2048]{0:T(1024)} %bitcast.151, s32[64]{0:T(128)} %pad_add_fusion.5.exps, s32[64]{0:T(128)} %constant.143.clone.1.layers, f32[8,2,2,152,128]{4,3,2,1,0:T(8,128)} %bitcast.153), custom_call_target="tpu_custom_call" | custom-call | flops 1000000000 | bytes 2490368 | tf_op jit(solution)/shard_map/merge_tables/pallas_call | solution.py:273
  434.4 93.3 %weight_grads.2 = (bf16[2,64,192,512]{3,2,1,0:T(8,128)(2,1)}, bf16[2,64,192,512]{3,2,1,0:T(8,128)(2,1)}, bf16[2,64,192,512]{3,2,1,0:T(8,128)(2,1)}, bf16[32,192,...) custom-call(s32[32]{0:T(128)} %copy-done.24, s32[33]{0:T(128)} %get-tuple-element.131.tiles, ...), custom_call_target="tpu_custom_call" | custom-call | flops 309237645312 | bytes 90177536 | tf_op jit(solution)/shard_map/weight_grads/pallas_call | solution.py:420
  527.6 3.4 collective-permute-start.12
  531.5 9.7 %all-gather.15.cloned.1.call-done.refs_2_ = bf16[8192,4,128]{2,1,0:T(4,128)(2,1)} async-done(((bf16[1024,4,128]{2,1,0:T(4,128)(2,1)}), bf16[8192,4,128]{2,1,0:T(4,128)(2,1)}) %all-gather.15.cloned.1.call-update) | async-done | bytes 8388624 | tf_op jit(solution)/shard_map/all_gather | solution.py:549
  541.3 52.4 %all-gather.17.cloned.1.call-done.refs_3_ = bf16[8192,4,128]{2,1,0:T(4,128)(2,1)} async-done(((bf16[1024,4,128]{2,1,0:T(4,128)(2,1)}), bf16[8192,4,128]{2,1,0:T(4,128)(2,1)}) %all-gather.17.cloned.1.call-update) | async-done | bytes 8388624 | tf_op jit(solution)/shard_map/all_gather | solution.py:549
  593.7 101.5 %weight_grads.3 = (bf16[2,64,192,512]{3,2,1,0:T(8,128)(2,1)}, bf16[2,64,192,512]{3,2,1,0:T(8,128)(2,1)}, bf16[2,64,192,512]{3,2,1,0:T(8,128)(2,1)}, bf16[32,192,...) custom-call(s32[32]{0:T(128)} %copy-done.23, ...), custom_call_target="tpu_custom_call", output_to_operand_aliasing={{0}: (12, {}), {1}: (13, {}), {2}: (14, {})} | custom-call | flops 309237645312 | bytes 90177536 | tf_op jit(solution)/shard_map/weight_grads/pallas_call | solution.py:420
  696.0 2.1 fusion.1
  698.1 2.3 add_convert_fusion.1
  701.2 1.1 pad_maximum_fusion
  702.8 1.7 add_convert_fusion
  705.1 3.2 add_convert_fusion.2
  708.4 60.2 %all-reduce.12.cloned.1.call-done = bf16[2,512,512]{1,2,0:T(8,128)(2,1)} async-done(((bf16[2,512,512]{1,2,0:T(8,128)(2,1)}), bf16[2,512,512]{1,2,0:T(8,128)(2,1)}) %all-reduce.12.cloned.1.call-update) | async-done | bytes 1048592 | tf_op jit(solution)/shard_map/psum | solution.py:635
  768.6 2.3 copy.50
  770.9 14.6 %merge_half.2 = (bf16[2,64,192,512]{3,2,1,0:T(8,128)(2,1)}, bf16[2,64,192,512]{3,2,1,0:T(8,128)(2,1)}, bf16[2,64,192,512]{3,2,1,0:T(8,128)(2,1)}) custom-call(s32[32]{0:T(128)} %get-tuple-element.126.exps, bf16[32,192,512]{2,1,0:T(8,128)(2,1)} %collective-permute-done.12.a, ...), custom_call_target="tpu_custom_call", output_to_operand_aliasing={{0}: (4, {}), {1}: (5, {}), {2}: (6, {})} | custom-call | flops 1000000000 | bytes 37748736 | tf_op jit(solution)/shard_map/merge_half/pallas_call | solution.py:472
  785.5 14.6 %merge_half.3 = (bf16[2,64,192,512]{3,2,1,0:T(8,128)(2,1)}, bf16[2,64,192,512]{3,2,1,0:T(8,128)(2,1)}, bf16[2,64,192,512]{3,2,1,0:T(8,128)(2,1)}) custom-call(s32[32]{0:T(128)} %get-tuple-element.129.exps, bf16[32,192,512]{2,1,0:T(8,128)(2,1)} %collective-permute-done.9.a, ...), custom_call_target="tpu_custom_call", output_to_operand_aliasing={{0}: (4, {}), {1}: (5, {}), {2}: (6, {})} | custom-call | flops 1000000000 | bytes 37748736 | tf_op jit(solution)/shard_map/merge_half/pallas_call | solution.py:472
  (167 shorter events, 20.8 us)
Async XLA Ops:
  8.0 407.1 %all-gather.27.cloned.1.call-start = ((), (), s32[]{:S(2)}) async-start(), calls=%async_computation.9 | async-start | bytes 2801664 | tf_op jit(solution)/shard_map/all_gather | solution.py:598
  8.9 2.8 copy-start.21
  11.6 30.9 %copy-start = (bf16[1024,4,128]{2,1,0:T(4,128)(2,1)}, bf16[1024,4,128]{2,1,0:T(4,128)(2,1)S(1)}, u32[]{:S(2)}) copy-start(bf16[1024,4,128]{2,1,0:T(4,128)(2,1)S(1)} %reshape.280.refs_0_) | copy-start | bytes 3145732
  12.3 7.6 collective-permute-start
  15.6 26.0 %collective-permute-start.1 = (bf16[1024,4,128]{2,1,0:T(4,128)(2,1)S(1)}, bf16[1024,4,128]{2,1,0:T(4,128)(2,1)S(1)}, u32[]{:S(2)}, u32[]{:S(2)}) collective-permute-start(bf16[1024,4,128]{2,1,0:T(4,128)(2,1)S(1)} %reshape.280.refs_0_), channel_id=1, source_target_pairs={{0,8},{8,0},{1,9},{9,1},{2,10},{10,2},{3,11},{11,3},{4,12},{12,4},... | collective-permute-start | bytes 3145736 | tf_op jit(solution)/shard_map/ppermute | solution.py:546
  29.7 12.8 %copy-start.13 = (f32[144,128]{1,0:T(8,128)}, f32[144,128]{1,0:T(8,128)S(1)}, u32[]{:S(2)}) copy-start(f32[144,128]{1,0:T(8,128)S(1)} %pad_bitcast_fusion.3.gates) | copy-start | bytes 221188
  81.8 47.1 %collective-permute-start.2 = (f32[1024,512]{1,0:T(8,128)}, f32[1024,512]{1,0:T(8,128)}, u32[]{:S(2)}, u32[]{:S(2)}) collective-permute-start(f32[1024,512]{1,0:T(8,128)} %experts_forward.3), channel_id=1, source_target_pairs={{0,8},{8,0},{1,9},{9,1},{2,10},{10,2},{3,11},{11,3},{4,12},{12,4},... | collective-permute-start | bytes 6291464 | tf_op jit(solution)/shard_map/ppermute | solution.py:546
  81.9 47.0 %copy-start.10 = (bf16[1024,512]{1,0:T(8,128)(2,1)S(1)}, bf16[1024,512]{1,0:T(8,128)(2,1)}, u32[]{:S(2)}) copy-start(bf16[1024,512]{1,0:T(8,128)(2,1)} %copy-done.9) | copy-start | bytes 3145732
  121.4 11.2 %copy-start.26 = (bf16[2,512,512]{2,1,0:T(8,128)(2,1)S(1)}, bf16[2,512,512]{2,1,0:T(8,128)(2,1)}, u32[]{:S(2)}) copy-start(bf16[2,512,512]{2,1,0:T(8,128)(2,1)} %param.12) | copy-start | bytes 3145732
  133.3 1.0 copy-start.5
  135.4 10.9 %copy-start.3 = (bf16[1024,512]{1,0:T(8,128)(2,1)S(1)}, bf16[1024,512]{1,0:T(8,128)(2,1)}, u32[]{:S(2)}) copy-start(bf16[1024,512]{1,0:T(8,128)(2,1)} %param.9) | copy-start | bytes 3145732
  144.7 2.7 copy-start.20
  146.3 288.0 %all-gather.23.cloned.1.call-start = ((), (), s32[]{:S(2)}) async-start(), calls=%async_computation.7 | async-start | bytes 9437184 | tf_op jit(solution)/shard_map/all_gather | solution.py:549
  147.4 25.3 %copy-start.2 = (bf16[1024,4,128]{2,1,0:T(4,128)(2,1)S(1)}, bf16[1024,4,128]{2,1,0:T(4,128)(2,1)}, u32[]{:S(2)}) copy-start(bf16[1024,4,128]{2,1,0:T(4,128)(2,1)} %reshape.282.refs_0_) | copy-start | bytes 3145732
  147.5 286.8 %all-gather.25.cloned.1.call-start = ((), (), s32[]{:S(2)}) async-start(), calls=%async_computation.8 | async-start | bytes 9437184 | tf_op jit(solution)/shard_map/all_gather | solution.py:549
  147.5 23.6 %collective-permute-start.4 = (bf16[1024,4,128]{2,1,0:T(4,128)(2,1)}, bf16[1024,4,128]{2,1,0:T(4,128)(2,1)S(1)}, u32[]{:S(2)}, u32[]{:S(2)}) collective-permute-start(bf16[1024,4,128]{2,1,0:T(4,128)(2,1)} %reshape.284.refs_2_), channel_id=1, source_target_pairs={{0,8},{8,0},{1,9},{9,1},{2,10},{10,2},{3,11},{11,3},{4,12},{12,4},... | collective-permute-start | bytes 3145736 | tf_op jit(solution)/shard_map/ppermute | solution.py:546
  172.1 262.2 %all-gather.19.cloned.1.call-start = ((), (), s32[]{:S(2)}) async-start(), calls=%async_computation.5 | async-start | bytes 9437184 | tf_op jit(solution)/shard_map/all_gather | solution.py:549
  172.7 261.6 %all-gather.21.cloned.1.call-start = ((), (), s32[]{:S(2)}) async-start(), calls=%async_computation.6 | async-start | bytes 9437184 | tf_op jit(solution)/shard_map/all_gather | solution.py:549
  172.8 22.7 %collective-permute-start.3 = (bf16[1024,4,128]{2,1,0:T(4,128)(2,1)S(1)}, bf16[1024,4,128]{2,1,0:T(4,128)(2,1)S(1)}, u32[]{:S(2)}, u32[]{:S(2)}) collective-permute-start(bf16[1024,4,128]{2,1,0:T(4,128)(2,1)S(1)} %copy-done.2), channel_id=1, source_target_pairs={{0,8},{8,0},{1,9},{9,1},{2,10},{10,2},{3,11},{11,3},{4,12},{12,4},... | collective-permute-start | bytes 3145736 | tf_op jit(solution)/shard_map/ppermute | solution.py:546
  196.4 335.1 %all-gather.11.cloned.1.call-start = ((), (), s32[]{:S(2)}) async-start(), calls=%async_computation.1 | async-start | bytes 9437184 | tf_op jit(solution)/shard_map/all_gather | solution.py:549
  197.0 334.5 %all-gather.13.cloned.1.call-start = ((), (), s32[]{:S(2)}) async-start(), calls=%async_computation.2 | async-start | bytes 9437184 | tf_op jit(solution)/shard_map/all_gather | solution.py:549
  197.8 343.5 %all-gather.15.cloned.1.call-start = ((), (), s32[]{:S(2)}) async-start(), calls=%async_computation.3 | async-start | bytes 9437184 | tf_op jit(solution)/shard_map/all_gather | solution.py:549
  197.8 102.5 %copy-start.4 = (bf16[1024,512]{1,0:T(8,128)(2,1)S(1)}, bf16[1024,512]{1,0:T(8,128)(2,1)}, u32[]{:S(2)}) copy-start(bf16[1024,512]{1,0:T(8,128)(2,1)} %param.9) | copy-start | bytes 3145732
  252.1 48.2 %collective-permute-start.5 = (f32[1024,512]{1,0:T(8,128)}, f32[1024,512]{1,0:T(8,128)S(1)}, u32[]{:S(2)}, u32[]{:S(2)}) collective-permute-start(f32[1024,512]{1,0:T(8,128)} %get-tuple-element.52), channel_id=1, source_target_pairs={{0,8},{8,0},{1,9},{9,1},{2,10},{10,2},{3,11},{11,3},{4,12},{12,4},... | collective-permute-start | bytes 6291464 | tf_op jit(solution)/shard_map/ppermute | solution.py:546
  300.3 3.3 copy-start.27
  302.6 1.0 copy-start.19
  306.5 287.2 %all-gather.17.cloned.1.call-start = ((), (), s32[]{:S(2)}) async-start(), calls=%async_computation.4 | async-start | bytes 9437184 | tf_op jit(solution)/shard_map/all_gather | solution.py:549
  306.7 47.5 %collective-permute-start.6 = (bf16[1024,4,128]{2,1,0:T(4,128)(2,1)}, bf16[1024,4,128]{2,1,0:T(4,128)(2,1)S(1)}, u32[]{:S(2)}, u32[]{:S(2)}) collective-permute-start(bf16[1024,4,128]{2,1,0:T(4,128)(2,1)} %reshape.285.refs_2_), channel_id=1, source_target_pairs={{0,8},{8,0},{1,9},{9,1},{2,10},{10,2},{3,11},{11,3},{4,12},{12,4},... | collective-permute-start | bytes 3145736 | tf_op jit(solution)/shard_map/ppermute | solution.py:546
  354.1 1.0 copy-start.16
  412.9 282.2 %collective-permute-start.8 = (f32[1024,512]{1,0:T(8,128)}, f32[1024,512]{1,0:T(8,128)}, u32[]{:S(2)}, u32[]{:S(2)}) collective-permute-start(f32[1024,512]{1,0:T(8,128)} %get-tuple-element.59), channel_id=1, source_target_pairs={{0,8},{8,0},{1,9},{9,1},{2,10},{10,2},{3,11},{11,3},{4,12},{12,4},... | collective-permute-start | bytes 6291464 | tf_op jit(solution)/shard_map/ppermute | solution.py:546
  413.0 282.4 %collective-permute-start.7 = (f32[1024,512]{1,0:T(8,128)}, f32[1024,512]{1,0:T(8,128)}, u32[]{:S(2)}, u32[]{:S(2)}) collective-permute-start(f32[1024,512]{1,0:T(8,128)} %get-tuple-element.57), channel_id=1, source_target_pairs={{0,8},{8,0},{1,9},{9,1},{2,10},{10,2},{3,11},{11,3},{4,12},{12,4},... | collective-permute-start | bytes 6291464 | tf_op jit(solution)/shard_map/ppermute | solution.py:546
  415.0 353.6 %all-reduce.12.cloned.1.call-start = ((), (), s32[]{:S(2)}) async-start(), calls=%async_computation | async-start | bytes 2097152 | tf_op jit(solution)/shard_map/psum | solution.py:635
  416.0 4.6 copy-start.22
  417.4 17.0 %copy-start.24 = (s32[32]{0:T(128)}, s32[32]{0:T(128)S(1)}, u32[]{:S(2)}) copy-start(s32[32]{0:T(128)S(1)} %get-tuple-element.127.exps) | copy-start | bytes 388
  418.0 16.3 %copy-start.23 = (s32[32]{0:T(128)}, s32[32]{0:T(128)S(1)}, u32[]{:S(2)}) copy-start(s32[32]{0:T(128)S(1)} %get-tuple-element.128.exps) | copy-start | bytes 388
  527.6 168.1 %collective-permute-start.12 = (bf16[32,192,512]{2,1,0:T(8,128)(2,1)}, bf16[32,192,512]{2,1,0:T(8,128)(2,1)}, u32[]{:S(2)}, u32[]{:S(2)}) collective-permute-start(bf16[32,192,512]{2,1,0:T(8,128)(2,1)} %get-tuple-element.70), channel_id=1, source_target_pairs={{0,1},{1,0},{2,3},{3,2},{4,5},{5,4},{6,7},{7,6},{8,9},{9,8},{10,11... | collective-permute-start | bytes 18874376 | tf_op jit(solution)/shard_map/ppermute | solution.py:552
  531.0 239.9 %collective-permute-start.13 = (bf16[32,192,512]{2,1,0:T(8,128)(2,1)}, bf16[32,192,512]{2,1,0:T(8,128)(2,1)}, u32[]{:S(2)}, u32[]{:S(2)}) collective-permute-start(bf16[32,192,512]{2,1,0:T(8,128)(2,1)} %get-tuple-element.71), channel_id=1, source_target_pairs={{0,1},{1,0},{2,3},{3,2},{4,5},{5,4},{6,7},{7,6},{8,9},{9,8},{10,11... | collective-permute-start | bytes 18874376 | tf_op jit(solution)/shard_map/ppermute | solution.py:552
  531.1 239.8 %collective-permute-start.14 = (bf16[32,192,512]{2,1,0:T(8,128)(2,1)}, bf16[32,192,512]{2,1,0:T(8,128)(2,1)}, u32[]{:S(2)}, u32[]{:S(2)}) collective-permute-start(bf16[32,192,512]{2,1,0:T(8,128)(2,1)} %get-tuple-element.72), channel_id=1, source_target_pairs={{0,1},{1,0},{2,3},{3,2},{4,5},{5,4},{6,7},{7,6},{8,9},{9,8},{10,11... | collective-permute-start | bytes 18874376 | tf_op jit(solution)/shard_map/ppermute | solution.py:552
  593.7 102.3 %copy-start.18 = (bf16[1024,512]{1,0:T(8,128)(2,1)S(1)}, bf16[1024,512]{1,0:T(8,128)(2,1)}, u32[]{:S(2)}) copy-start(bf16[1024,512]{1,0:T(8,128)(2,1)} %copy-done.17) | copy-start | bytes 3145732
  695.2 90.3 %collective-permute-start.9 = (bf16[32,192,512]{2,1,0:T(8,128)(2,1)}, bf16[32,192,512]{2,1,0:T(8,128)(2,1)}, u32[]{:S(2)}, u32[]{:S(2)}) collective-permute-start(bf16[32,192,512]{2,1,0:T(8,128)(2,1)} %get-tuple-element.67), channel_id=1, source_target_pairs={{0,1},{1,0},{2,3},{3,2},{4,5},{5,4},{6,7},{7,6},{8,9},{9,8},{10,11... | collective-permute-start | bytes 18874376 | tf_op jit(solution)/shard_map/ppermute | solution.py:552
  695.4 90.0 %collective-permute-start.10 = (bf16[32,192,512]{2,1,0:T(8,128)(2,1)}, bf16[32,192,512]{2,1,0:T(8,128)(2,1)}, u32[]{:S(2)}, u32[]{:S(2)}) collective-permute-start(bf16[32,192,512]{2,1,0:T(8,128)(2,1)} %get-tuple-element.68), channel_id=1, source_target_pairs={{0,1},{1,0},{2,3},{3,2},{4,5},{5,4},{6,7},{7,6},{8,9},{9,8},{10,11... | collective-permute-start | bytes 18874376 | tf_op jit(solution)/shard_map/ppermute | solution.py:552
  695.7 2.4 copy-start.8
  695.7 2.4 copy-start.12
  695.7 89.7 %collective-permute-start.11 = (bf16[32,192,512]{2,1,0:T(8,128)(2,1)}, bf16[32,192,512]{2,1,0:T(8,128)(2,1)}, u32[]{:S(2)}, u32[]{:S(2)}) collective-permute-start(bf16[32,192,512]{2,1,0:T(8,128)(2,1)} %get-tuple-element.69), channel_id=1, source_target_pairs={{0,1},{1,0},{2,3},{3,2},{4,5},{5,4},{6,7},{7,6},{8,9},{9,8},{10,11... | collective-permute-start | bytes 18874376 | tf_op jit(solution)/shard_map/ppermute | solution.py:552
  698.1 2.4 copy-start.25
  701.2 1.6 copy-start.28
  702.8 1.7 copy-start.6
  702.8 2.3 copy-start.11
  (6 other events, 5.8 us)
Sparse Core Ops, SparseCore 0:
  146.4 25.7 all-gather.26
  174.0 50.4 all-gather.22
  226.4 50.5 all-gather.24
  279.2 50.4 all-gather.18
  332.0 50.5 all-gather.20
  384.8 50.5 all-gather.10
  437.8 50.4 all-gather.12
  490.2 51.0 all-gather.14
  543.1 50.4 all-gather.16
Sparse Core Ops, SparseCore 1:
  702.4 66.1 all-reduce.11

commit v10 on v9

--- a/solution.py
+++ b/solution.py
@@ -14,6 +14,7 @@
 TILE = 96
 HALF_TILE = 64
 WTILE = 768
+PARTS = 2
 SOURCES = 8
 CHUNK = 256
 PITCH = 9
@@ -70,7 +71,7 @@
 
 
 def widen(src, dst, pitch, halves, tok):
-    step = 8
+    step = 32
 
     def one(q, carry):
         for r in range(step):
@@ -287,11 +288,12 @@
     )(starts.reshape(-1), exps, layers, shared)
 
 
-def weight_grad_body(exps, tiles, begins, *refs, parts, n_exp, n_alias, first_list, page):
+def weight_grad_body(exps, tiles, begins, offsets, names, *refs, parts, n_exp, n_alias, n_moved, first_list, page, layer):
     rows_in, refs = refs[:4], refs[4:]
     idx_all, gate_ref, g_ref, up_ref, w_ref = refs[:5]
+    moved, whole, refs = refs[5:5 + n_moved], refs[5 + n_moved:5 + n_moved + n_alias], refs[5 + n_moved + n_alias:]
     (dg_ref, du_ref, dw_ref, og_ref, ou_ref, ow_ref,
-     uds, rows, u0, c0, d0, h0, u1, c1, d1, h1, gacc, wacc, idx_s, sem, tsem) = refs[5 + n_alias:]
+     uds, rows, u0, c0, d0, h0, u1, c1, d1, h1, gacc, wacc, idx_s, seen, sem, tsem, *move_refs) = refs
     e = pl.program_id(0)
     ff = g_ref.shape[2]
     slots = 3
@@ -309,23 +311,41 @@
     def column(first, count, k):
         return rows[pl.ds(first * PITCH + k, count, stride=PITCH), :]
 
+    n_tok = uds.shape[0] - 8
+    run = n_tok // (2 * SOURCES)
+
+    def row_copies(q):
+        return [pltpu.make_async_copy(src.at[pl.ds(q * run, run)],
+                                      uds.at[pl.ds((2 * q + k % 2) * run, run), pl.ds(k // 2 * parts, parts)], sem.at[q])
+                for k, src in enumerate(rows_in)]
+
+    def wait_rows(limit):
+        def one(q, carry):
+            @pl.when((q >= seen[0]) & (offsets[q] < limit))
+            def _():
+                for c in row_copies(q):
+                    c.wait()
+                seen[0] = q + 1
+
+            return carry
+
+        @pl.when(seen[0] < SOURCES)
+        def _():
+            lax.fori_loop(0, SOURCES, one, 0)
+
     @pl.when(e == 0)
     def _():
-        n_tok = uds.shape[0] - 8
-        run = n_tok // (2 * SOURCES)
-        copies = [pltpu.make_async_copy(src.at[pl.ds(q * run, run)],
-                                        uds.at[pl.ds((2 * q + k % 2) * run, run), pl.ds(k // 2 * parts, parts)], sem.at[k])
-                  for q in range(SOURCES) for k, src in enumerate(rows_in)]
-        for c in copies:
-            c.start()
+        for q in range(SOURCES):
+            for c in row_copies(q):
+                c.start()
+        seen[0] = 0
         table_copy(0).start()
         table_copy(1).start()
         uds[pl.ds(n_tok, 8)] = jnp.zeros((8, 2 * parts, LANES), jnp.bfloat16)
         for ref in (*both[0], *both[1], gacc, wacc):
             clear(ref)
         table_copy(0).wait()
-        for c in copies:
-            c.wait()
+        wait_rows(WTILE)
 
         def first_rows(q, carry):
             for r in range(16):
@@ -333,6 +353,9 @@
             return carry
 
         lax.fori_loop(0, WTILE // 16, first_rows, 0)
+
+    if moved:
+        move_step(e, n_exp, layer + 1, names, moved, whole, *move_refs)
 
     @pl.when(e + 1 < n_exp)
     def _():
@@ -376,6 +399,7 @@
 
     def tile(j, carry):
         odd = lax.rem(begin + j, 2)
+        wait_rows(jnp.where((e == 0) & (j + 1 < n_tiles), (j + 2) * WTILE, page * SOURCES))
 
         @pl.when(odd == 0)
         def _():
@@ -400,7 +424,33 @@
     lax.fori_loop(0, n_tiles, tile, 0)
 
 
-def weight_grads(layer, first, exps, tiles, rows, idx_all, gates, weights, full):
+def move_step(e, n_steps, layer, names, arrived, whole, buf, in_sem, out_sem):
+    per = buf.shape[2]
+
+    def arrive(chunk):
+        slot = lax.rem(chunk, 2)
+        return [pltpu.make_async_copy(x.at[pl.ds(chunk * per, per)], buf.at[slot, k], in_sem.at[slot])
+                for k, x in enumerate(arrived)]
+
+    def leave(chunk):
+        slot = lax.rem(chunk, 2)
+        return [pltpu.make_async_copy(buf.at[slot, k, i], x.at[layer, names[chunk * per + i]], out_sem.at[slot])
+                for k, x in enumerate(whole) for i in range(per)]
+
+    def each(when, copies, act):
+        @pl.when(when)
+        def _():
+            for c in copies:
+                act(c)
+
+    each(e >= 2, leave(jnp.maximum(e - 2, 0)), lambda c: c.wait())
+    each(e < n_steps, arrive(jnp.minimum(e, n_steps - 1)), lambda c: c.start())
+    each(e >= 1, arrive(jnp.maximum(e - 1, 0)), lambda c: c.wait())
+    each(e >= 1, leave(jnp.maximum(e - 1, 0)), lambda c: c.start())
+    each(e == n_steps, leave(n_steps - 1), lambda c: c.wait())
+
+
+def weight_grads(layer, first, exps, tiles, offsets, rows, idx_all, gates, weights, full, moved=None):
     n_half, parts, _ = rows[0].shape
     n_tok = 2 * n_half
     n_layers, n_local, ff, d_model = weights[0].shape
@@ -417,26 +467,33 @@
     aliased = list(full) if full is not None else []
     tile_set = [pltpu.VMEM((WTILE, d_model), jnp.bfloat16)] * 2 + [pltpu.VMEM((2 * ff, WTILE), jnp.bfloat16),
                                                                  pltpu.VMEM((ff, WTILE), jnp.bfloat16)]
+    arrived, names = moved if moved else ([], exps)
+    scratch = []
+    if moved:
+        scratch = [pltpu.VMEM((2, 3, arrived[0].shape[0] // n_exp, ff, d_model), jnp.bfloat16), pltpu.SemaphoreType.DMA((2,)),
+                   pltpu.SemaphoreType.DMA((2,))]
     outs = pl.pallas_call(
-        functools.partial(weight_grad_body, parts=parts, n_exp=n_exp, n_alias=len(aliased), first_list=first, page=page),
+        functools.partial(weight_grad_body, parts=parts, n_exp=n_exp, n_alias=len(aliased), n_moved=len(arrived), first_list=first,
+                          page=page, layer=layer),
         grid_spec=pltpu.PrefetchScalarGridSpec(
-            num_scalar_prefetch=3,
+            num_scalar_prefetch=5,
             grid=(n_exp + 1,),
-            in_specs=[any_spec] * 5 + [gate_spec] + [mine] * 3 + [any_spec] * len(aliased),
+            in_specs=[any_spec] * 5 + [gate_spec] + [mine] * 3 + [any_spec] * (len(arrived) + len(aliased)),
             out_specs=[done] * 3 + [half] * 3,
             scratch_shapes=[pltpu.VMEM((n_tok + 8, 2 * parts, LANES), jnp.bfloat16)]
             + [pltpu.VMEM((WTILE * PITCH + 16, LANES), jnp.float32)] + tile_set * 2
             + [pltpu.VMEM((2 * ff, d_model), jnp.float32), pltpu.VMEM((ff, d_model), jnp.float32),
-               pltpu.SMEM((3 * page,), jnp.int32), pltpu.SemaphoreType.DMA((4,)), pltpu.SemaphoreType.DMA((3,))],
+               pltpu.SMEM((3 * page,), jnp.int32), pltpu.SMEM((1,), jnp.int32), pltpu.SemaphoreType.DMA((SOURCES,)),
+               pltpu.SemaphoreType.DMA((3,))] + scratch,
         ),
         out_shape=[jax.ShapeDtypeStruct((n_layers, n_local, ff, d_model), jnp.bfloat16)] * 3
         + [jax.ShapeDtypeStruct((n_exp, ff, d_model), jnp.bfloat16)] * 3,
-        input_output_aliases={12 + k: k for k in range(len(aliased))},
+        input_output_aliases={14 + len(arrived) + k: k for k in range(len(aliased))},
         compiler_params=pltpu.CompilerParams(dimension_semantics=("arbitrary",), vmem_limit_bytes=VMEM_LIMIT),
         cost_estimate=pl.CostEstimate(flops=6 * n_tok * n_exp * d_model * ff,
                                       bytes_accessed=n_tok * d_model * 4 + 9 * n_exp * ff * d_model * 2, transcendentals=0),
         name="weight_grads",
-    )(exps, tiles, begins, *rows, idx_all, gates, *weights, *aliased)
+    )(exps, tiles, begins, offsets, names, *rows, idx_all, gates, *weights, *arrived, *aliased)
     return outs[:3], outs[3:]
 
 
@@ -516,6 +573,13 @@
     return jnp.sum(pick * ids, axis=2), tiles
 
 
+def source_offsets(bounds, expert):
+    lane = jnp.arange(bounds.shape[1], dtype=jnp.int32)
+    counts = jnp.sum(bounds * ((lane == expert + 1).astype(jnp.int32) - (lane == expert).astype(jnp.int32)), axis=1)
+    place = jnp.arange(bounds.shape[0], dtype=jnp.int32)
+    return jnp.sum((place[None, :] < place[:, None]).astype(jnp.int32) * counts, axis=1)
+
+
 def after(x, *earlier):
     return lax.optimization_barrier((x, *earlier))[0]
 
@@ -547,9 +611,6 @@
 
         def spread(x):
             return [lax.all_gather(y, 'dp', axis=0, tiled=True) for y in x]
-
-        def trade(x, pairs):
-            return [lax.ppermute(y, 'dp', pairs) for y in x]
 
         def slab(x):
             return x.reshape(tok, parts, LANES)
@@ -598,12 +659,13 @@
         shared = lax.all_gather(jnp.stack(packed), 'dp', axis=0)
         starts = shared[:, :, 0, -8].astype(jnp.int32)
         core = dp_id % 2
-        dealt = [deal_experts(starts[:, layer], n_local, 2) for layer in range(n_layers)]
-        mine = [lists[core] for lists, _ in dealt]
-        firsts = [sum(x.shape[0] for x in mine[:layer]) for layer in range(n_layers)]
+        n_parts = [PARTS] * top + [1]
+        dealt = [deal_experts(starts[:, layer], n_local, 2 * n_parts[layer]) for layer in range(n_layers)]
+        mine = [dealt[layer][0][core * n_parts[layer] + part] for layer in range(n_layers) for part in range(n_parts[layer])]
+        of_layer = [layer for layer in range(n_layers) for _ in range(n_parts[layer])]
         list_rows = cdiv(cdiv(dp_size * 2 * cap, LANES), 8) * 8 + 8
         idx_all, gate_all = merge_tables(shared, starts, jnp.concatenate(mine),
-                                         jnp.concatenate([jnp.full_like(x, layer) for layer, x in enumerate(mine)]),
+                                         jnp.concatenate([jnp.full_like(x, layer) for x, layer in zip(mine, of_layer)]),
                                          list_rows, dp_size * 2 * tok)
         idx_all = idx_all.reshape(-1)
 
@@ -621,16 +683,21 @@
             d_y = (d_u.astype(jnp.float32)
                    + jnp.einsum('te,de->td', d_u, w_mix[layer], preferred_element_type=jnp.float32)).astype(jnp.bfloat16)
             lists, tiles = dealt[layer]
-            full, part = weight_grads(layer, firsts[layer], mine[layer], after(tiles[core], last), u_rows + d_rows, idx_all,
-                                      gate_all, weights, full)
-            arrived.append((layer, lists[1 - core], trade(part, core_pairs)))
+            for part in range(n_parts[layer]):
+                place = of_layer.index(layer) + part
+                own_list, its_list = core * n_parts[layer] + part, (1 - core) * n_parts[layer] + part
+                first = sum(x.shape[0] for x in mine[:place])
+                full, done = weight_grads(layer, first, mine[place], after(tiles[own_list], last),
+                                          source_offsets(starts[:, layer], mine[place][0]), u_rows + d_rows, idx_all, gate_all,
+                                          weights, full, arrived.pop(0)[2:] if part and arrived else None)
+                arrived.append((layer, part, [lax.ppermute(x, 'dp', core_pairs) for x in done], lists[its_list]))
             if layer:
                 d_slab = slab(d_y)
                 d_other = swap(d_slab)
                 d_rows = spread((d_slab, d_other))
                 if layer == top:
                     layer_out = (u.astype(jnp.float32) + y_own + swap(after(last, d_other))).astype(jnp.bfloat16)
-        for layer, names, part in arrived:
+        for layer, _, part, names in arrived:
             full = merge_half(layer, names, part, full)
         d_mix = lax.psum(jnp.stack(d_mix), ('dp', 'ep'))
         return (layer_out, d_y, d_mix, jnp.swapaxes(full[0], 2, 3), jnp.swapaxes(full[1], 2, 3), full[2])

time: 808 us -> 812 us (level)
    pallas_call x2, Pallas kernels: 29.2 us -> 16.3 us  [merge_half(): pl.pallas_call(functools.partial(merge_body, layer=layer, n_exp=n_exp), g...]
    pallas_call x2 -> x3, Pallas kernels: 195 us -> 207 us  [weight_grads(): pl.pallas_call(functools.partial(weight_grad_body, parts=parts, n_exp=n_e...]
  transfers between devices with their start and end apart: 25 -> 28, of which waited for: 9 -> 9; matrix products, arithmetic and copies ran while one was open for 4% -> 5% of each run, Pallas kernels for 52% -> 52%
where the time goes in v10:
time: 812 us; the launch traced here: 810 us
  Pallas kernels  470 us (58%)
  waiting for transfers between devices  242 us (30%)
  other arithmetic  40 us (5%)
  local copies, waits for them, and re-layouts  17.3 us (2%)
  between operations  16.3 us (2%)
  starting transfers between devices  13.9 us (2%)
  matrix products  10.5 us (1%)
    pallas_call x5, Pallas kernels, token_kernel(): pl.pallas_call(functools.partial(token_body, layer=layer, tok=tok, parts=...  233 us
    pallas_call x3, Pallas kernels, weight_grads(): pl.pallas_call(functools.partial(weight_grad_body, parts=parts, n_exp=n_e...  207 us
    ppermute x9, waiting for transfers between devices, swap(): return lax.ppermute(x, 'ep', ep_pairs)  113 us
    all_gather x8, waiting for transfers between devices, spread(): return [lax.all_gather(y, 'dp', axis=0, tiled=True) for y in x]  67.8 us
    psum x1, waiting for transfers between devices, device_body(): d_mix = lax.psum(jnp.stack(d_mix), ('dp', 'ep'))  59.5 us
    pallas_call x2, Pallas kernels, merge_half(): pl.pallas_call(functools.partial(merge_body, layer=layer, n_exp=n_exp), g...  16.3 us
  transfers between devices with their start and end apart: 28, of which 9 were waited for; matrix products, arithmetic and copies ran while one was open for 5% of the time, Pallas kernels for 52%

profile of v10, /device:TPU:0, one launch (start us, length us, event | category | flops | bytes accessed | tf_op | source)
XLA Modules:
  0.0 810.4 jit_solution(8622256913324213282)
XLA Ops:
  8.9 2.4 add_convert_fusion.7
  12.3 3.3 collective-permute-start
  15.6 4.3 collective-permute-done
  20.1 1.1 convert_reduce_fusion
  21.9 6.4 sort.30
  28.4 1.3 fusion.49
  30.5 11.1 %collective-permute-done.1.refs_1_ = bf16[1024,4,128]{2,1,0:T(4,128)(2,1)S(1)} collective-permute-done((bf16[1024,4,128]{2,1,0:T(4,128)(2,1)S(1)}, bf16[1024,4,128]{2,1,0:T(4,128)(2,1)S(1)}, u32[]{:S(2)}, u32[]{:S(2)}) %collective-permute-start.1) | collective-permute-done | bytes 1048608 | tf_op jit(solution)/shard_map/ppermute | solution.py:610
  41.6 1.0 copy-done.1
  42.5 38.7 %experts_forward.3 = f32[1024,512]{1,0:T(8,128)} custom-call(s32[128]{0:T(128)} %get-tuple-element.156.runs, s32[18432]{0:T(1024)} %get-tuple-element.134.idx, f32[144,128]{1,0:T(8,128)} %copy-done.13, bf16[1024,4,128]{2,1,0:T(4,128)(2,1)} %copy-done, bf16[1024,4,128]{2,1,0:T(4,128)(2,1)} %copy-done.1, bf16[2,64,192,512]{3,2,1,0:T(8,128)(2,1)} %bitcast.131, ...), custom_call_target="tpu_custom_call" | custom-call | flops 19327352832 | bytes 37748736 | tf_op jit(solution)/shard_map/experts_forward/pallas_call | solution.py:209
  81.3 38.9 %experts_forward.4 = f32[1024,512]{1,0:T(8,128)} custom-call(s32[128]{0:T(128)} %get-tuple-element.157.runs, s32[18432]{0:T(1024)} %get-tuple-element.134.idx, f32[144,128]{1,0:T(8,128)} %copy-done.13, bf16[1024,4,128]{2,1,0:T(4,128)(2,1)} %copy-done, bf16[1024,4,128]{2,1,0:T(4,128)(2,1)} %copy-done.1, bf16[2,64,192,512]{3,2,1,0:T(8,128)(2,1)} %bitcast.132, ...), custom_call_target="tpu_custom_call" | custom-call | flops 19327352832 | bytes 37748736 | tf_op jit(solution)/shard_map/experts_forward/pallas_call | solution.py:209
  120.3 8.0 collective-permute-done.2
  128.3 2.8 add_convert_fusion.6
  131.1 1.0 copy-done.17
  132.8 1.1 reshape.417.refs_0_
  134.0 6.4 sort.31
  141.9 1.3 fusion.48
  144.8 1.1 reshape.419.refs_2_
  146.4 23.3 %collective-permute-done.4.refs_3_ = bf16[1024,4,128]{2,1,0:T(4,128)(2,1)S(1)} collective-permute-done((bf16[1024,4,128]{2,1,0:T(4,128)(2,1)}, bf16[1024,4,128]{2,1,0:T(4,128)(2,1)S(1)}, u32[]{:S(2)}, u32[]{:S(2)}) %collective-permute-start.4) | collective-permute-done | bytes 1048608 | tf_op jit(solution)/shard_map/ppermute | solution.py:610
  169.7 1.0 copy-done.14
  171.9 22.1 %collective-permute-done.3.refs_1_ = bf16[1024,4,128]{2,1,0:T(4,128)(2,1)S(1)} collective-permute-done((bf16[1024,4,128]{2,1,0:T(4,128)(2,1)S(1)}, bf16[1024,4,128]{2,1,0:T(4,128)(2,1)S(1)}, u32[]{:S(2)}, u32[]{:S(2)}) %collective-permute-start.3) | collective-permute-done | bytes 1048608 | tf_op jit(solution)/shard_map/ppermute | solution.py:610
  194.0 1.0 copy-done.15
  196.4 52.8 %experts_backward.2 = (f32[1024,512]{1,0:T(8,128)}, f32[1024,512]{1,0:T(8,128)}) custom-call(s32[128]{0:T(128)} %get-tuple-element.159.runs, s32[18432]{0:T(1024)} %get-tuple-element.136.idx, f32[144,128]{1,0:T(8,128)} %copy-done.21, bf16[1024,4,128]{2,1,0:T(4,128)(2,1)} %reshape.417.refs_0_, bf16[1024,4,128]{2,1,0:T(4,128)(2,1)} %copy-done.15, ...), custom_call_target="tpu_custom_call" | custom-call | flops 51539607552 | bytes 37748736 | tf_op jit(solution)/shard_map/experts_backward/pallas_call | solution.py:209
  249.2 3.7 collective-permute-start.5
  252.9 44.4 %collective-permute-done.5 = f32[1024,512]{1,0:T(8,128)S(1)} collective-permute-done((f32[1024,512]{1,0:T(8,128)}, f32[1024,512]{1,0:T(8,128)S(1)}, u32[]{:S(2)}, u32[]{:S(2)}) %collective-permute-start.5) | collective-permute-done | bytes 2097184 | tf_op jit(solution)/shard_map/ppermute | solution.py:610
  297.3 2.3 add_convert_fusion.4
  299.7 1.0 copy-done.19
  301.4 1.0 copy-done.7
  302.4 1.1 reshape.420.refs_2_
  303.8 1.7 collective-permute-start.6
  305.5 44.4 %experts_forward.5 = (f32[1024,512]{1,0:T(8,128)}, f32[1024,512]{1,0:T(8,128)}) custom-call(s32[128]{0:T(128)} %get-tuple-element.159.runs, s32[18432]{0:T(1024)} %get-tuple-element.137.idx, f32[144,128]{1,0:T(8,128)} %copy-done.21, bf16[1024,4,128]{2,1,0:T(4,128)(2,1)} %reshape.417.refs_0_, bf16[1024,4,128]{2,1,0:T(4,128)(2,1)} %copy-done.15, ...), custom_call_target="tpu_custom_call" | custom-call | flops 38654705664 | bytes 37748736 | tf_op jit(solution)/shard_map/experts_forward/pallas_call | solution.py:209
  350.0 1.0 copy-done.16
  351.0 58.3 %experts_backward.3 = (f32[1024,512]{1,0:T(8,128)}, f32[1024,512]{1,0:T(8,128)}) custom-call(s32[128]{0:T(128)} %get-tuple-element.155.runs, s32[18432]{0:T(1024)} %get-tuple-element.133.idx, f32[144,128]{1,0:T(8,128)} %copy-done.13, bf16[1024,4,128]{2,1,0:T(4,128)(2,1)} %copy-done, bf16[1024,4,128]{2,1,0:T(4,128)(2,1)} %copy-done.1, ...), custom_call_target="tpu_custom_call" | custom-call | flops 51539607552 | bytes 37748736 | tf_op jit(solution)/shard_map/experts_backward/pallas_call | solution.py:209
  409.4 2.0 collective-permute-start.7
  420.6 13.8 %merge_tables.1 = (s32[64,32,128]{2,1,0:T(8,128)}, f32[64,32,128]{2,1,0:T(8,128)}) custom-call(s32[2048]{0:T(1024)} %bitcast.166, s32[64]{0:T(128)} %pad_add_fusion.5.exps, s32[64]{0:T(128)} %constant.166.clone.1.layers, f32[8,2,2,152,128]{4,3,2,1,0:T(8,128)} %bitcast.182), custom_call_target="tpu_custom_call" | custom-call | flops 1000000000 | bytes 2490368 | tf_op jit(solution)/shard_map/merge_tables/pallas_call | solution.py:274
  434.5 89.4 %weight_grads.3 = (bf16[2,64,192,512]{3,2,1,0:T(8,128)(2,1)}, bf16[2,64,192,512]{3,2,1,0:T(8,128)(2,1)}, bf16[2,64,192,512]{3,2,1,0:T(8,128)(2,1)}, bf16[32,192,...) custom-call(s32[32]{0:T(128)} %bitcast.179, s32[33]{0:T(128)} %get-tuple-element.151.tiles, ...), custom_call_target="tpu_custom_call" | custom-call | flops 309237645312 | bytes 90177536 | tf_op jit(solution)/shard_map/weight_grads/pallas_call | solution.py:475
  524.5 15.3 %all-gather.15.cloned.1.call-done.refs_2_ = bf16[8192,4,128]{2,1,0:T(4,128)(2,1)} async-done(((bf16[1024,4,128]{2,1,0:T(4,128)(2,1)}), bf16[8192,4,128]{2,1,0:T(4,128)(2,1)}) %all-gather.15.cloned.1.call-update) | async-done | bytes 8388624 | tf_op jit(solution)/shard_map/all_gather | solution.py:613
  539.8 52.4 %all-gather.17.cloned.1.call-done.refs_3_ = bf16[8192,4,128]{2,1,0:T(4,128)(2,1)} async-done(((bf16[1024,4,128]{2,1,0:T(4,128)(2,1)}), bf16[8192,4,128]{2,1,0:T(4,128)(2,1)}) %all-gather.17.cloned.1.call-update) | async-done | bytes 8388624 | tf_op jit(solution)/shard_map/all_gather | solution.py:613
  592.2 57.3 %weight_grads.4 = (bf16[2,64,192,512]{3,2,1,0:T(8,128)(2,1)}, bf16[2,64,192,512]{3,2,1,0:T(8,128)(2,1)}, bf16[2,64,192,512]{3,2,1,0:T(8,128)(2,1)}, bf16[16,192,...) custom-call(s32[16]{0:T(128)} %bitcast.174, ...), custom_call_target="tpu_custom_call", output_to_operand_aliasing={{0}: (14, {}), {1}: (15, {}), {2}: (16, {})} | custom-call | flops 154618822656 | bytes 61865984 | tf_op jit(solution)/shard_map/weight_grads/pallas_call | solution.py:475
  650.1 60.1 %weight_grads.5 = (bf16[2,64,192,512]{3,2,1,0:T(8,128)(2,1)}, bf16[2,64,192,512]{3,2,1,0:T(8,128)(2,1)}, bf16[2,64,192,512]{3,2,1,0:T(8,128)(2,1)}, bf16[16,192,...) custom-call(s32[16]{0:T(128)} %bitcast.170, ...), custom_call_target="tpu_custom_call", output_to_operand_aliasing={{0}: (17, {}), {1}: (18, {}), {2}: (19, {})} | custom-call | flops 154618822656 | bytes 61865984 | tf_op jit(solution)/shard_map/weight_grads/pallas_call | solution.py:475
  710.8 2.3 fusion.1
  713.1 2.3 add_convert_fusion.1
  717.2 1.1 pad_maximum_fusion
  718.3 3.6 add_convert_fusion
  721.9 3.2 add_convert_fusion.2
  725.1 59.5 %all-reduce.12.cloned.1.call-done = bf16[2,512,512]{1,2,0:T(8,128)(2,1)} async-done(((bf16[2,512,512]{1,2,0:T(8,128)(2,1)}), bf16[2,512,512]{1,2,0:T(8,128)(2,1)}) %all-reduce.12.cloned.1.call-update) | async-done | bytes 1048592 | tf_op jit(solution)/shard_map/psum | solution.py:702
  784.6 2.3 copy.57
  786.9 8.2 %merge_half.2 = (bf16[2,64,192,512]{3,2,1,0:T(8,128)(2,1)}, bf16[2,64,192,512]{3,2,1,0:T(8,128)(2,1)}, bf16[2,64,192,512]{3,2,1,0:T(8,128)(2,1)}) custom-call(s32[16]{0:T(128)} %get-tuple-element.140.exps, bf16[16,192,512]{2,1,0:T(8,128)(2,1)} %collective-permute-done.15.a, ...), custom_call_target="tpu_custom_call", output_to_operand_aliasing={{0}: (4, {}), {1}: (5, {}), {2}: (6, {})} | custom-call | flops 1000000000 | bytes 18874368 | tf_op jit(solution)/shard_map/merge_half/pallas_call | solution.py:529
  795.1 8.2 %merge_half.3 = (bf16[2,64,192,512]{3,2,1,0:T(8,128)(2,1)}, bf16[2,64,192,512]{3,2,1,0:T(8,128)(2,1)}, bf16[2,64,192,512]{3,2,1,0:T(8,128)(2,1)}) custom-call(s32[16]{0:T(128)} %get-tuple-element.143.exps, bf16[16,192,512]{2,1,0:T(8,128)(2,1)} %collective-permute-done.12.a, ...), custom_call_target="tpu_custom_call", output_to_operand_aliasing={{0}: (4, {}), {1}: (5, {}), {2}: (6, {})} | custom-call | flops 1000000000 | bytes 18874368 | tf_op jit(solution)/shard_map/merge_half/pallas_call | solution.py:529
  (193 shorter events, 23.9 us)
Async XLA Ops:
  8.0 3.7 copy-start.22
  8.0 403.5 %all-gather.27.cloned.1.call-start = ((), (), s32[]{:S(2)}) async-start(), calls=%async_computation.9 | async-start | bytes 2801664 | tf_op jit(solution)/shard_map/all_gather | solution.py:659
  11.6 30.9 %copy-start = (bf16[1024,4,128]{2,1,0:T(4,128)(2,1)}, bf16[1024,4,128]{2,1,0:T(4,128)(2,1)S(1)}, u32[]{:S(2)}) copy-start(bf16[1024,4,128]{2,1,0:T(4,128)(2,1)S(1)} %reshape.415.refs_0_) | copy-start | bytes 3145732
  12.3 7.6 collective-permute-start
  15.6 26.0 %collective-permute-start.1 = (bf16[1024,4,128]{2,1,0:T(4,128)(2,1)S(1)}, bf16[1024,4,128]{2,1,0:T(4,128)(2,1)S(1)}, u32[]{:S(2)}, u32[]{:S(2)}) collective-permute-start(bf16[1024,4,128]{2,1,0:T(4,128)(2,1)S(1)} %reshape.415.refs_0_), channel_id=1, source_target_pairs={{0,8},{8,0},{1,9},{9,1},{2,10},{10,2},{3,11},{11,3},{4,12},{12,4},... | collective-permute-start | bytes 3145736 | tf_op jit(solution)/shard_map/ppermute | solution.py:610
  29.7 12.8 %copy-start.13 = (f32[144,128]{1,0:T(8,128)}, f32[144,128]{1,0:T(8,128)S(1)}, u32[]{:S(2)}) copy-start(f32[144,128]{1,0:T(8,128)S(1)} %pad_bitcast_fusion.3.gates) | copy-start | bytes 221188
  81.2 47.1 %collective-permute-start.2 = (f32[1024,512]{1,0:T(8,128)}, f32[1024,512]{1,0:T(8,128)}, u32[]{:S(2)}, u32[]{:S(2)}) collective-permute-start(f32[1024,512]{1,0:T(8,128)} %experts_forward.3), channel_id=1, source_target_pairs={{0,8},{8,0},{1,9},{9,1},{2,10},{10,2},{3,11},{11,3},{4,12},{12,4},... | collective-permute-start | bytes 6291464 | tf_op jit(solution)/shard_map/ppermute | solution.py:610
  81.3 47.0 %copy-start.10 = (bf16[1024,512]{1,0:T(8,128)(2,1)S(1)}, bf16[1024,512]{1,0:T(8,128)(2,1)}, u32[]{:S(2)}) copy-start(bf16[1024,512]{1,0:T(8,128)(2,1)} %copy-done.9) | copy-start | bytes 3145732
  120.3 11.8 %copy-start.28 = (bf16[2,512,512]{2,1,0:T(8,128)(2,1)S(1)}, bf16[2,512,512]{2,1,0:T(8,128)(2,1)}, u32[]{:S(2)}) copy-start(bf16[2,512,512]{2,1,0:T(8,128)(2,1)} %param.12) | copy-start | bytes 3145732
  132.8 11.2 %copy-start.5 = (bf16[1024,512]{1,0:T(8,128)(2,1)}, bf16[1024,512]{1,0:T(8,128)(2,1)S(1)}, u32[]{:S(2)}) copy-start(bf16[1024,512]{1,0:T(8,128)(2,1)S(1)} %add_convert_fusion.5) | copy-start | bytes 3145732
  132.8 12.0 %copy-start.3 = (bf16[1024,512]{1,0:T(8,128)(2,1)S(1)}, bf16[1024,512]{1,0:T(8,128)(2,1)}, u32[]{:S(2)}) copy-start(bf16[1024,512]{1,0:T(8,128)(2,1)} %param.9) | copy-start | bytes 3145732
  143.2 28.0 %copy-start.21 = (f32[144,128]{1,0:T(8,128)}, f32[144,128]{1,0:T(8,128)S(1)}, u32[]{:S(2)}) copy-start(f32[144,128]{1,0:T(8,128)S(1)} %pad_bitcast_fusion.2.gates) | copy-start | bytes 221188
  144.0 27.3 %copy-start.2 = (bf16[1024,4,128]{2,1,0:T(4,128)(2,1)S(1)}, bf16[1024,4,128]{2,1,0:T(4,128)(2,1)}, u32[]{:S(2)}) copy-start(bf16[1024,4,128]{2,1,0:T(4,128)(2,1)} %reshape.417.refs_0_) | copy-start | bytes 3145732
  144.8 289.6 %all-gather.23.cloned.1.call-start = ((), (), s32[]{:S(2)}) async-start(), calls=%async_computation.7 | async-start | bytes 9437184 | tf_op jit(solution)/shard_map/all_gather | solution.py:613
  146.0 288.4 %all-gather.25.cloned.1.call-start = ((), (), s32[]{:S(2)}) async-start(), calls=%async_computation.8 | async-start | bytes 9437184 | tf_op jit(solution)/shard_map/all_gather | solution.py:613
  146.0 23.6 %collective-permute-start.4 = (bf16[1024,4,128]{2,1,0:T(4,128)(2,1)}, bf16[1024,4,128]{2,1,0:T(4,128)(2,1)S(1)}, u32[]{:S(2)}, u32[]{:S(2)}) collective-permute-start(bf16[1024,4,128]{2,1,0:T(4,128)(2,1)} %reshape.419.refs_2_), channel_id=1, source_target_pairs={{0,8},{8,0},{1,9},{9,1},{2,10},{10,2},{3,11},{11,3},{4,12},{12,4},... | collective-permute-start | bytes 3145736 | tf_op jit(solution)/shard_map/ppermute | solution.py:610
  170.7 263.8 %all-gather.19.cloned.1.call-start = ((), (), s32[]{:S(2)}) async-start(), calls=%async_computation.5 | async-start | bytes 9437184 | tf_op jit(solution)/shard_map/all_gather | solution.py:613
  171.3 263.2 %all-gather.21.cloned.1.call-start = ((), (), s32[]{:S(2)}) async-start(), calls=%async_computation.6 | async-start | bytes 9437184 | tf_op jit(solution)/shard_map/all_gather | solution.py:613
  171.3 22.7 %collective-permute-start.3 = (bf16[1024,4,128]{2,1,0:T(4,128)(2,1)S(1)}, bf16[1024,4,128]{2,1,0:T(4,128)(2,1)S(1)}, u32[]{:S(2)}, u32[]{:S(2)}) collective-permute-start(bf16[1024,4,128]{2,1,0:T(4,128)(2,1)S(1)} %copy-done.2), channel_id=1, source_target_pairs={{0,8},{8,0},{1,9},{9,1},{2,10},{10,2},{3,11},{11,3},{4,12},{12,4},... | collective-permute-start | bytes 3145736 | tf_op jit(solution)/shard_map/ppermute | solution.py:610
  195.0 329.5 %all-gather.11.cloned.1.call-start = ((), (), s32[]{:S(2)}) async-start(), calls=%async_computation.1 | async-start | bytes 9437184 | tf_op jit(solution)/shard_map/all_gather | solution.py:613
  195.6 328.9 %all-gather.13.cloned.1.call-start = ((), (), s32[]{:S(2)}) async-start(), calls=%async_computation.2 | async-start | bytes 9437184 | tf_op jit(solution)/shard_map/all_gather | solution.py:613
  196.3 343.5 %all-gather.15.cloned.1.call-start = ((), (), s32[]{:S(2)}) async-start(), calls=%async_computation.3 | async-start | bytes 9437184 | tf_op jit(solution)/shard_map/all_gather | solution.py:613
  196.4 101.0 %copy-start.4 = (bf16[1024,512]{1,0:T(8,128)(2,1)S(1)}, bf16[1024,512]{1,0:T(8,128)(2,1)}, u32[]{:S(2)}) copy-start(bf16[1024,512]{1,0:T(8,128)(2,1)} %param.9) | copy-start | bytes 3145732
  249.2 48.1 %collective-permute-start.5 = (f32[1024,512]{1,0:T(8,128)}, f32[1024,512]{1,0:T(8,128)S(1)}, u32[]{:S(2)}, u32[]{:S(2)}) collective-permute-start(f32[1024,512]{1,0:T(8,128)} %get-tuple-element.59), channel_id=1, source_target_pairs={{0,8},{8,0},{1,9},{9,1},{2,10},{10,2},{3,11},{11,3},{4,12},{12,4},... | collective-permute-start | bytes 6291464 | tf_op jit(solution)/shard_map/ppermute | solution.py:610
  297.3 3.3 copy-start.29
  303.5 288.7 %all-gather.17.cloned.1.call-start = ((), (), s32[]{:S(2)}) async-start(), calls=%async_computation.4 | async-start | bytes 9437184 | tf_op jit(solution)/shard_map/all_gather | solution.py:613
  303.8 46.2 %collective-permute-start.6 = (bf16[1024,4,128]{2,1,0:T(4,128)(2,1)}, bf16[1024,4,128]{2,1,0:T(4,128)(2,1)S(1)}, u32[]{:S(2)}, u32[]{:S(2)}) collective-permute-start(bf16[1024,4,128]{2,1,0:T(4,128)(2,1)} %reshape.420.refs_2_), channel_id=1, source_target_pairs={{0,8},{8,0},{1,9},{9,1},{2,10},{10,2},{3,11},{11,3},{4,12},{12,4},... | collective-permute-start | bytes 3145736 | tf_op jit(solution)/shard_map/ppermute | solution.py:610
  409.4 300.8 %collective-permute-start.8 = (f32[1024,512]{1,0:T(8,128)}, f32[1024,512]{1,0:T(8,128)}, u32[]{:S(2)}, u32[]{:S(2)}) collective-permute-start(f32[1024,512]{1,0:T(8,128)} %get-tuple-element.66), channel_id=1, source_target_pairs={{0,8},{8,0},{1,9},{9,1},{2,10},{10,2},{3,11},{11,3},{4,12},{12,4},... | collective-permute-start | bytes 6291464 | tf_op jit(solution)/shard_map/ppermute | solution.py:610
  409.4 300.8 %collective-permute-start.7 = (f32[1024,512]{1,0:T(8,128)}, f32[1024,512]{1,0:T(8,128)}, u32[]{:S(2)}, u32[]{:S(2)}) collective-permute-start(f32[1024,512]{1,0:T(8,128)} %get-tuple-element.64), channel_id=1, source_target_pairs={{0,8},{8,0},{1,9},{9,1},{2,10},{10,2},{3,11},{11,3},{4,12},{12,4},... | collective-permute-start | bytes 6291464 | tf_op jit(solution)/shard_map/ppermute | solution.py:610
  411.5 373.1 %all-reduce.12.cloned.1.call-start = ((), (), s32[]{:S(2)}) async-start(), calls=%async_computation | async-start | bytes 2097152 | tf_op jit(solution)/shard_map/psum | solution.py:702
  412.4 8.2 %copy-start.23 = (s32[8,2,1,1,128]{4,3,2,1,0:T(1,128)}, s32[8,2,1,1,128]{4,3,2,1,0:T(1,128)S(1)}, u32[]{:S(2)}) copy-start(s32[8,2,1,1,128]{4,3,2,1,0:T(1,128)S(1)} %slice_convert_fusion) | copy-start | bytes 24580
  413.6 20.9 %copy-start.26 = (s32[1,32]{1,0:T(1,128)}, s32[1,32]{1,0:T(1,128)S(1)}, u32[]{:S(2)}) copy-start(s32[1,32]{1,0:T(1,128)S(1)} %get-tuple-element.146) | copy-start | bytes 388
  415.6 18.8 %copy-start.24 = (s32[1,16]{1,0:T(1,128)}, s32[1,16]{1,0:T(1,128)S(1)}, u32[]{:S(2)}) copy-start(s32[1,16]{1,0:T(1,128)S(1)} %get-tuple-element.142) | copy-start | bytes 196
  415.6 18.8 %copy-start.25 = (s32[1,16]{1,0:T(1,128)}, s32[1,16]{1,0:T(1,128)S(1)}, u32[]{:S(2)}) copy-start(s32[1,16]{1,0:T(1,128)S(1)} %get-tuple-element.141) | copy-start | bytes 196
  523.9 125.6 %collective-permute-start.9 = (bf16[32,192,512]{2,1,0:T(8,128)(2,1)}, bf16[32,192,512]{2,1,0:T(8,128)(2,1)}, u32[]{:S(2)}, u32[]{:S(2)}) collective-permute-start(bf16[32,192,512]{2,1,0:T(8,128)(2,1)} %get-tuple-element.71), channel_id=1, source_target_pairs={{0,1},{1,0},{2,3},{3,2},{4,5},{5,4},{6,7},{7,6},{8,9},{9,8},{10,11... | collective-permute-start | bytes 18874376 | tf_op jit(solution)/shard_map/ppermute | solution.py:693
  523.9 125.6 %collective-permute-start.10 = (bf16[32,192,512]{2,1,0:T(8,128)(2,1)}, bf16[32,192,512]{2,1,0:T(8,128)(2,1)}, u32[]{:S(2)}, u32[]{:S(2)}) collective-permute-start(bf16[32,192,512]{2,1,0:T(8,128)(2,1)} %get-tuple-element.72), channel_id=1, source_target_pairs={{0,1},{1,0},{2,3},{3,2},{4,5},{5,4},{6,7},{7,6},{8,9},{9,8},{10,11... | collective-permute-start | bytes 18874376 | tf_op jit(solution)/shard_map/ppermute | solution.py:693
  524.4 125.6 %collective-permute-start.11 = (bf16[32,192,512]{2,1,0:T(8,128)(2,1)}, bf16[32,192,512]{2,1,0:T(8,128)(2,1)}, u32[]{:S(2)}, u32[]{:S(2)}) collective-permute-start(bf16[32,192,512]{2,1,0:T(8,128)(2,1)} %get-tuple-element.73), channel_id=1, source_target_pairs={{0,1},{1,0},{2,3},{3,2},{4,5},{5,4},{6,7},{7,6},{8,9},{9,8},{10,11... | collective-permute-start | bytes 18874376 | tf_op jit(solution)/shard_map/ppermute | solution.py:693
  649.5 61.3 %collective-permute-start.15 = (bf16[16,192,512]{2,1,0:T(8,128)(2,1)}, bf16[16,192,512]{2,1,0:T(8,128)(2,1)}, u32[]{:S(2)}, u32[]{:S(2)}) collective-permute-start(bf16[16,192,512]{2,1,0:T(8,128)(2,1)} %get-tuple-element.84), channel_id=1, source_target_pairs={{0,1},{1,0},{2,3},{3,2},{4,5},{5,4},{6,7},{7,6},{8,9},{9,8},{10,11... | collective-permute-start | bytes 9437192 | tf_op jit(solution)/shard_map/ppermute | solution.py:693
  649.5 137.3 %collective-permute-start.16 = (bf16[16,192,512]{2,1,0:T(8,128)(2,1)}, bf16[16,192,512]{2,1,0:T(8,128)(2,1)}, u32[]{:S(2)}, u32[]{:S(2)}) collective-permute-start(bf16[16,192,512]{2,1,0:T(8,128)(2,1)} %get-tuple-element.85), channel_id=1, source_target_pairs={{0,1},{1,0},{2,3},{3,2},{4,5},{5,4},{6,7},{7,6},{8,9},{9,8},{10,11... | collective-permute-start | bytes 9437192 | tf_op jit(solution)/shard_map/ppermute | solution.py:693
  650.0 136.8 %collective-permute-start.17 = (bf16[16,192,512]{2,1,0:T(8,128)(2,1)}, bf16[16,192,512]{2,1,0:T(8,128)(2,1)}, u32[]{:S(2)}, u32[]{:S(2)}) collective-permute-start(bf16[16,192,512]{2,1,0:T(8,128)(2,1)} %get-tuple-element.86), channel_id=1, source_target_pairs={{0,1},{1,0},{2,3},{3,2},{4,5},{5,4},{6,7},{7,6},{8,9},{9,8},{10,11... | collective-permute-start | bytes 9437192 | tf_op jit(solution)/shard_map/ppermute | solution.py:693
  650.1 60.7 %copy-start.18 = (bf16[1024,512]{1,0:T(8,128)(2,1)S(1)}, bf16[1024,512]{1,0:T(8,128)(2,1)}, u32[]{:S(2)}) copy-start(bf16[1024,512]{1,0:T(8,128)(2,1)} %copy-done.17) | copy-start | bytes 3145732
  710.2 2.9 copy-start.8
  710.2 84.8 %collective-permute-start.12 = (bf16[16,192,512]{2,1,0:T(8,128)(2,1)}, bf16[16,192,512]{2,1,0:T(8,128)(2,1)}, u32[]{:S(2)}, u32[]{:S(2)}) collective-permute-start(bf16[16,192,512]{2,1,0:T(8,128)(2,1)} %get-tuple-element.81), channel_id=1, source_target_pairs={{0,1},{1,0},{2,3},{3,2},{4,5},{5,4},{6,7},{7,6},{8,9},{9,8},{10,11... | collective-permute-start | bytes 9437192 | tf_op jit(solution)/shard_map/ppermute | solution.py:693
  710.3 84.8 %collective-permute-start.13 = (bf16[16,192,512]{2,1,0:T(8,128)(2,1)}, bf16[16,192,512]{2,1,0:T(8,128)(2,1)}, u32[]{:S(2)}, u32[]{:S(2)}) collective-permute-start(bf16[16,192,512]{2,1,0:T(8,128)(2,1)} %get-tuple-element.82), channel_id=1, source_target_pairs={{0,1},{1,0},{2,3},{3,2},{4,5},{5,4},{6,7},{7,6},{8,9},{9,8},{10,11... | collective-permute-start | bytes 9437192 | tf_op jit(solution)/shard_map/ppermute | solution.py:693
  710.7 84.3 %collective-permute-start.14 = (bf16[16,192,512]{2,1,0:T(8,128)(2,1)}, bf16[16,192,512]{2,1,0:T(8,128)(2,1)}, u32[]{:S(2)}, u32[]{:S(2)}) collective-permute-start(bf16[16,192,512]{2,1,0:T(8,128)(2,1)} %get-tuple-element.83), channel_id=1, source_target_pairs={{0,1},{1,0},{2,3},{3,2},{4,5},{5,4},{6,7},{7,6},{8,9},{9,8},{10,11... | collective-permute-start | bytes 9437192 | tf_op jit(solution)/shard_map/ppermute | solution.py:693
  713.1 3.3 copy-start.27
  717.2 4.7 copy-start.6
  717.2 4.7 copy-start.11
  (10 other events, 11.8 us)
Sparse Core Ops, SparseCore 0:
  144.9 25.6 all-gather.26
  172.5 50.4 all-gather.22
  224.9 50.4 all-gather.24
  277.7 50.4 all-gather.18
  330.5 50.5 all-gather.20
  383.3 50.5 all-gather.10
  436.3 50.5 all-gather.12
  488.7 51.0 all-gather.14
  541.6 50.4 all-gather.16
Sparse Core Ops, SparseCore 1:
  718.4 66.1 all-reduce.11

commit v11 on v10

--- a/solution.py
+++ b/solution.py
@@ -15,6 +15,7 @@
 HALF_TILE = 64
 WTILE = 768
 PARTS = 2
+AHEAD = 3
 SOURCES = 8
 CHUNK = 256
 PITCH = 9
@@ -26,6 +27,10 @@
 
 def cdiv(a, b):
     return (a + b - 1) // b
+
+
+def below(n):
+    return jnp.tri(n, k=-1, dtype=jnp.int32)
 
 
 def nt_dot(a, b):
@@ -327,6 +332,11 @@
                     c.wait()
                 seen[0] = q + 1
 
+                @pl.when(q + AHEAD < SOURCES)
+                def _():
+                    for c in row_copies(q + AHEAD):
+                        c.start()
+
             return carry
 
         @pl.when(seen[0] < SOURCES)
@@ -335,14 +345,15 @@
 
     @pl.when(e == 0)
     def _():
-        for q in range(SOURCES):
+        for q in range(AHEAD):
             for c in row_copies(q):
                 c.start()
         seen[0] = 0
+        seen[1] = 1
         table_copy(0).start()
         table_copy(1).start()
         uds[pl.ds(n_tok, 8)] = jnp.zeros((8, 2 * parts, LANES), jnp.bfloat16)
-        for ref in (*both[0], *both[1], gacc, wacc):
+        for ref in (*both[0], *both[1]):
             clear(ref)
         table_copy(0).wait()
         wait_rows(WTILE)
@@ -374,8 +385,9 @@
     def compute(j, new, old):
         un, cn, dn, hn = new
         uo, co, do, ho = old
-        gacc[...] += nn_dot(do[...], uo[...])
-        wacc[...] += nn_dot(ho[...], co[...])
+        fresh = seen[1] == 1
+        gacc[...] = jnp.where(fresh, 0.0, gacc[...]) + nn_dot(do[...], uo[...])
+        wacc[...] = jnp.where(fresh, 0.0, wacc[...]) + nn_dot(ho[...], co[...])
         nxt = jnp.where(j + 1 < n_tiles, here + (j + 1) * WTILE, there)
         gu = jnp.concatenate([g_ref[0, 0], up_ref[0, 0]], axis=0)
         for q in range(0, WTILE, CHUNK):
@@ -409,6 +421,8 @@
         def _():
             compute(j, both[1], both[0])
 
+        seen[1] = jnp.where(j == 0, 1, 0)
+
         @pl.when(j == 0)
         def _():
             dg = gacc[:ff].astype(jnp.bfloat16)
@@ -416,8 +430,6 @@
             dw = wacc[...].astype(jnp.bfloat16)
             dg_ref[0, 0], du_ref[0, 0], dw_ref[0, 0] = dg, du, dw
             og_ref[0], ou_ref[0], ow_ref[0] = dg, du, dw
-            gacc[...] = jnp.zeros_like(gacc)
-            wacc[...] = jnp.zeros_like(wacc)
 
         return carry
 
@@ -483,7 +495,7 @@
             scratch_shapes=[pltpu.VMEM((n_tok + 8, 2 * parts, LANES), jnp.bfloat16)]
             + [pltpu.VMEM((WTILE * PITCH + 16, LANES), jnp.float32)] + tile_set * 2
             + [pltpu.VMEM((2 * ff, d_model), jnp.float32), pltpu.VMEM((ff, d_model), jnp.float32),
-               pltpu.SMEM((3 * page,), jnp.int32), pltpu.SMEM((1,), jnp.int32), pltpu.SemaphoreType.DMA((SOURCES,)),
+               pltpu.SMEM((3 * page,), jnp.int32), pltpu.SMEM((2,), jnp.int32), pltpu.SemaphoreType.DMA((SOURCES,)),
                pltpu.SemaphoreType.DMA((3,))] + scratch,
         ),
         out_shape=[jax.ShapeDtypeStruct((n_layers, n_local, ff, d_model), jnp.bfloat16)] * 3
@@ -552,11 +564,12 @@
     token = jnp.pad(token, (0, 2 * PAGE))
     gate = jnp.pad(gate, (0, 2 * PAGE)).reshape(-1, LANES)
     ids = jnp.arange(n_local, dtype=jnp.int32)
-    hits = jnp.sum((group.reshape(n_src, -1)[:, :, None] == ids).astype(jnp.int32), axis=1)
-    starts = jnp.sum((ids[None, :] < ids[:, None]).astype(jnp.int32) * jnp.sum(hits, axis=0), axis=1)
+    hits = jnp.sum((group.reshape(n_src, -1, 1) == ids).astype(jnp.int32), axis=1)
+    starts = jnp.sum(below(n_local) * jnp.sum(hits, axis=0), axis=1)
     ends = starts + jnp.sum(hits, axis=0)
     middle = starts + hits[0]
-    bounds = jnp.pad(starts, (0, LANES - n_local), constant_values=0) + jnp.where(jnp.arange(LANES) < n_local, 0, ends[-1])
+    bounds = jnp.pad(starts, (0, LANES - n_local), mode='edge')
+    bounds = jnp.where(jnp.arange(LANES) < n_local, bounds, ends[-1])
     runs = [jnp.concatenate(x) for x in ((starts, middle), (middle, ends), (starts, ends))]
     return runs, token, gate, bounds
 
@@ -564,11 +577,11 @@
 def deal_experts(bounds, n_local, n_lists):
     load = jnp.sum(bounds[:, 1:n_local + 1] - bounds[:, :n_local], axis=0)
     ids = jnp.arange(n_local, dtype=jnp.int32)
-    ahead = (load[None, :] > load[:, None]) | ((load[None, :] == load[:, None]) & (ids[None, :] < ids[:, None]))
-    rank = jnp.sum(ahead.astype(jnp.int32), axis=1)
-    turn, which = jnp.arange(n_local // n_lists)[None, :], jnp.arange(n_lists)[:, None]
+    mine = load.reshape(-1, 1)
+    rank = jnp.sum((load > mine).astype(jnp.int32) + (load == mine).astype(jnp.int32) * below(n_local), axis=1)
+    turn, which = jnp.arange(n_local // n_lists), jnp.arange(n_lists).reshape(-1, 1)
     want = n_lists * turn + jnp.where(turn % 2 == 0, which, n_lists - 1 - which)
-    pick = (rank[None, None, :] == want[:, :, None]).astype(jnp.int32)
+    pick = (rank == jnp.expand_dims(want, 2)).astype(jnp.int32)
     tiles = jnp.maximum((jnp.sum(pick * load, axis=2) + WTILE - 1) // WTILE, 1)
     return jnp.sum(pick * ids, axis=2), tiles
 
@@ -576,8 +589,7 @@
 def source_offsets(bounds, expert):
     lane = jnp.arange(bounds.shape[1], dtype=jnp.int32)
     counts = jnp.sum(bounds * ((lane == expert + 1).astype(jnp.int32) - (lane == expert).astype(jnp.int32)), axis=1)
-    place = jnp.arange(bounds.shape[0], dtype=jnp.int32)
-    return jnp.sum((place[None, :] < place[:, None]).astype(jnp.int32) * counts, axis=1)
+    return jnp.sum(below(bounds.shape[0]) * counts, axis=1)
 
 
 def after(x, *earlier):
@@ -667,6 +679,7 @@
         idx_all, gate_all = merge_tables(shared, starts, jnp.concatenate(mine),
                                          jnp.concatenate([jnp.full_like(x, layer) for x, layer in zip(mine, of_layer)]),
                                          list_rows, dp_size * 2 * tok)
+        offsets = [source_offsets(starts[:, layer], x[0]) for x, layer in zip(mine, of_layer)]
         idx_all = idx_all.reshape(-1)
 
         d_y, full, arrived = d_out, None, []
@@ -688,8 +701,8 @@
                 own_list, its_list = core * n_parts[layer] + part, (1 - core) * n_parts[layer] + part
                 first = sum(x.shape[0] for x in mine[:place])
                 full, done = weight_grads(layer, first, mine[place], after(tiles[own_list], last),
-                                          source_offsets(starts[:, layer], mine[place][0]), u_rows + d_rows, idx_all, gate_all,
-                                          weights, full, arrived.pop(0)[2:] if part and arrived else None)
+                                          offsets[place], u_rows + d_rows, idx_all, gate_all, weights, full,
+                                          arrived.pop(0)[2:] if part and arrived else None)
                 arrived.append((layer, part, [lax.ppermute(x, 'dp', core_pairs) for x in done], lists[its_list]))
             if layer:
                 d_slab = slab(d_y)

time: 812 us -> 818 us (level)
  transfers between devices with their start and end apart: 28 -> 28, of which waited for: 9 -> 9; matrix products, arithmetic and copies ran while one was open for 5% -> 5% of each run, Pallas kernels for 52% -> 53%
where the time goes in v11:
time: 818 us; the launch traced here: 816 us
  Pallas kernels  477 us (58%)
  waiting for transfers between devices  239 us (29%)
  other arithmetic  40 us (5%)
  local copies, waits for them, and re-layouts  18.5 us (2%)
  between operations  16.3 us (2%)
  starting transfers between devices  14 us (2%)
  matrix products  10.5 us (1%)
    pallas_call x5, Pallas kernels, token_kernel(): pl.pallas_call(functools.partial(token_body, layer=layer, tok=tok, parts=...  233 us
    pallas_call x3, Pallas kernels, weight_grads(): pl.pallas_call(functools.partial(weight_grad_body, parts=parts, n_exp=n_e...  214 us
    ppermute x9, waiting for transfers between devices, swap(): return lax.ppermute(x, 'ep', ep_pairs)  112 us
    all_gather x8, waiting for transfers between devices, spread(): return [lax.all_gather(y, 'dp', axis=0, tiled=True) for y in x]  66.2 us
    psum x1, waiting for transfers between devices, device_body(): d_mix = lax.psum(jnp.stack(d_mix), ('dp', 'ep'))  59.4 us
  transfers between devices with their start and end apart: 28, of which 9 were waited for; matrix products, arithmetic and copies ran while one was open for 5% of the time, Pallas kernels for 53%

profile of v11, /device:TPU:0, one launch (start us, length us, event | category | flops | bytes accessed | tf_op | source)
XLA Modules:
  0.0 816.0 jit_solution(6463323433190254047)
XLA Ops:
  8.9 2.4 add_convert_fusion.7
  12.3 3.3 collective-permute-start
  15.6 4.3 collective-permute-done
  20.1 1.1 convert_reduce_fusion
  22.6 6.4 sort.30
  29.0 1.9 fusion.42
  31.7 9.8 %collective-permute-done.1.refs_1_ = bf16[1024,4,128]{2,1,0:T(4,128)(2,1)S(1)} collective-permute-done((bf16[1024,4,128]{2,1,0:T(4,128)(2,1)S(1)}, bf16[1024,4,128]{2,1,0:T(4,128)(2,1)S(1)}, u32[]{:S(2)}, u32[]{:S(2)}) %collective-permute-start.1) | collective-permute-done | bytes 1048608 | tf_op jit(solution)/shard_map/ppermute | solution.py:622
  41.6 1.0 copy-done.1
  42.5 38.7 %experts_forward.3 = f32[1024,512]{1,0:T(8,128)} custom-call(s32[128]{0:T(128)} %get-tuple-element.161.runs, s32[18432]{0:T(1024)} %get-tuple-element.139.idx, f32[144,128]{1,0:T(8,128)} %copy-done.13, bf16[1024,4,128]{2,1,0:T(4,128)(2,1)} %copy-done, bf16[1024,4,128]{2,1,0:T(4,128)(2,1)} %copy-done.1, bf16[2,64,192,512]{3,2,1,0:T(8,128)(2,1)} %bitcast.133, ...), custom_call_target="tpu_custom_call" | custom-call | flops 19327352832 | bytes 37748736 | tf_op jit(solution)/shard_map/experts_forward/pallas_call | solution.py:214
  81.3 38.9 %experts_forward.4 = f32[1024,512]{1,0:T(8,128)} custom-call(s32[128]{0:T(128)} %get-tuple-element.162.runs, s32[18432]{0:T(1024)} %get-tuple-element.139.idx, f32[144,128]{1,0:T(8,128)} %copy-done.13, bf16[1024,4,128]{2,1,0:T(4,128)(2,1)} %copy-done, bf16[1024,4,128]{2,1,0:T(4,128)(2,1)} %copy-done.1, bf16[2,64,192,512]{3,2,1,0:T(8,128)(2,1)} %bitcast.134, ...), custom_call_target="tpu_custom_call" | custom-call | flops 19327352832 | bytes 37748736 | tf_op jit(solution)/shard_map/experts_forward/pallas_call | solution.py:214
  120.3 8.0 collective-permute-done.2
  128.3 2.8 add_convert_fusion.6
  131.1 1.0 copy-done.17
  132.8 1.1 reshape.384.refs_0_
  135.4 6.4 sort.31
  142.6 2.0 fusion.43
  146.1 1.1 reshape.386.refs_2_
  147.7 23.3 %collective-permute-done.4.refs_3_ = bf16[1024,4,128]{2,1,0:T(4,128)(2,1)S(1)} collective-permute-done((bf16[1024,4,128]{2,1,0:T(4,128)(2,1)}, bf16[1024,4,128]{2,1,0:T(4,128)(2,1)S(1)}, u32[]{:S(2)}, u32[]{:S(2)}) %collective-permute-start.4) | collective-permute-done | bytes 1048608 | tf_op jit(solution)/shard_map/ppermute | solution.py:622
  171.0 1.0 copy-done.14
  173.2 22.1 %collective-permute-done.3.refs_1_ = bf16[1024,4,128]{2,1,0:T(4,128)(2,1)S(1)} collective-permute-done((bf16[1024,4,128]{2,1,0:T(4,128)(2,1)S(1)}, bf16[1024,4,128]{2,1,0:T(4,128)(2,1)S(1)}, u32[]{:S(2)}, u32[]{:S(2)}) %collective-permute-start.3) | collective-permute-done | bytes 1048608 | tf_op jit(solution)/shard_map/ppermute | solution.py:622
  195.3 1.0 copy-done.15
  197.7 52.8 %experts_backward.2 = (f32[1024,512]{1,0:T(8,128)}, f32[1024,512]{1,0:T(8,128)}) custom-call(s32[128]{0:T(128)} %get-tuple-element.164.runs, s32[18432]{0:T(1024)} %get-tuple-element.141.idx, f32[144,128]{1,0:T(8,128)} %copy-done.21, bf16[1024,4,128]{2,1,0:T(4,128)(2,1)} %reshape.384.refs_0_, bf16[1024,4,128]{2,1,0:T(4,128)(2,1)} %copy-done.15, ...), custom_call_target="tpu_custom_call" | custom-call | flops 51539607552 | bytes 37748736 | tf_op jit(solution)/shard_map/experts_backward/pallas_call | solution.py:214
  250.5 3.7 collective-permute-start.5
  254.2 44.4 %collective-permute-done.5 = f32[1024,512]{1,0:T(8,128)S(1)} collective-permute-done((f32[1024,512]{1,0:T(8,128)}, f32[1024,512]{1,0:T(8,128)S(1)}, u32[]{:S(2)}, u32[]{:S(2)}) %collective-permute-start.5) | collective-permute-done | bytes 2097184 | tf_op jit(solution)/shard_map/ppermute | solution.py:622
  298.6 2.3 add_convert_fusion.4
  301.0 1.0 copy-done.19
  302.7 1.0 copy-done.7
  303.7 1.1 reshape.387.refs_2_
  305.1 1.7 collective-permute-start.6
  306.9 44.4 %experts_forward.5 = (f32[1024,512]{1,0:T(8,128)}, f32[1024,512]{1,0:T(8,128)}) custom-call(s32[128]{0:T(128)} %get-tuple-element.164.runs, s32[18432]{0:T(1024)} %get-tuple-element.142.idx, f32[144,128]{1,0:T(8,128)} %copy-done.21, bf16[1024,4,128]{2,1,0:T(4,128)(2,1)} %reshape.384.refs_0_, bf16[1024,4,128]{2,1,0:T(4,128)(2,1)} %copy-done.15, ...), custom_call_target="tpu_custom_call" | custom-call | flops 38654705664 | bytes 37748736 | tf_op jit(solution)/shard_map/experts_forward/pallas_call | solution.py:214
  351.3 1.0 copy-done.16
  352.3 58.4 %experts_backward.3 = (f32[1024,512]{1,0:T(8,128)}, f32[1024,512]{1,0:T(8,128)}) custom-call(s32[128]{0:T(128)} %get-tuple-element.160.runs, s32[18432]{0:T(1024)} %get-tuple-element.138.idx, f32[144,128]{1,0:T(8,128)} %copy-done.13, bf16[1024,4,128]{2,1,0:T(4,128)(2,1)} %copy-done, bf16[1024,4,128]{2,1,0:T(4,128)(2,1)} %copy-done.1, ...), custom_call_target="tpu_custom_call" | custom-call | flops 51539607552 | bytes 37748736 | tf_op jit(solution)/shard_map/experts_backward/pallas_call | solution.py:214
  410.8 2.0 collective-permute-start.7
  419.7 13.7 %merge_tables.1 = (s32[64,32,128]{2,1,0:T(8,128)}, f32[64,32,128]{2,1,0:T(8,128)}) custom-call(s32[2048]{0:T(1024)} %bitcast.168, s32[64]{0:T(128)} %pad_add_fusion.5.exps, s32[64]{0:T(128)} %constant.170.clone.1.layers, f32[8,2,2,152,128]{4,3,2,1,0:T(8,128)} %bitcast.184), custom_call_target="tpu_custom_call" | custom-call | flops 1000000000 | bytes 2490368 | tf_op jit(solution)/shard_map/merge_tables/pallas_call | solution.py:279
  434.3 92.5 %weight_grads.3 = (bf16[2,64,192,512]{3,2,1,0:T(8,128)(2,1)}, bf16[2,64,192,512]{3,2,1,0:T(8,128)(2,1)}, bf16[2,64,192,512]{3,2,1,0:T(8,128)(2,1)}, bf16[32,192,...) custom-call(s32[32]{0:T(128)} %bitcast.181, s32[33]{0:T(128)} %get-tuple-element.156.tiles, ...), custom_call_target="tpu_custom_call" | custom-call | flops 309237645312 | bytes 90177536 | tf_op jit(solution)/shard_map/weight_grads/pallas_call | solution.py:487
  527.4 13.8 %all-gather.15.cloned.1.call-done.refs_2_ = bf16[8192,4,128]{2,1,0:T(4,128)(2,1)} async-done(((bf16[1024,4,128]{2,1,0:T(4,128)(2,1)}), bf16[8192,4,128]{2,1,0:T(4,128)(2,1)}) %all-gather.15.cloned.1.call-update) | async-done | bytes 8388624 | tf_op jit(solution)/shard_map/all_gather | solution.py:625
  541.1 52.4 %all-gather.17.cloned.1.call-done.refs_3_ = bf16[8192,4,128]{2,1,0:T(4,128)(2,1)} async-done(((bf16[1024,4,128]{2,1,0:T(4,128)(2,1)}), bf16[8192,4,128]{2,1,0:T(4,128)(2,1)}) %all-gather.17.cloned.1.call-update) | async-done | bytes 8388624 | tf_op jit(solution)/shard_map/all_gather | solution.py:625
  593.5 59.4 %weight_grads.4 = (bf16[2,64,192,512]{3,2,1,0:T(8,128)(2,1)}, bf16[2,64,192,512]{3,2,1,0:T(8,128)(2,1)}, bf16[2,64,192,512]{3,2,1,0:T(8,128)(2,1)}, bf16[16,192,...) custom-call(s32[16]{0:T(128)} %bitcast.176, ...), custom_call_target="tpu_custom_call", output_to_operand_aliasing={{0}: (14, {}), {1}: (15, {}), {2}: (16, {})} | custom-call | flops 154618822656 | bytes 61865984 | tf_op jit(solution)/shard_map/weight_grads/pallas_call | solution.py:487
  653.6 62.3 %weight_grads.5 = (bf16[2,64,192,512]{3,2,1,0:T(8,128)(2,1)}, bf16[2,64,192,512]{3,2,1,0:T(8,128)(2,1)}, bf16[2,64,192,512]{3,2,1,0:T(8,128)(2,1)}, bf16[16,192,...) custom-call(s32[16]{0:T(128)} %bitcast.172, ...), custom_call_target="tpu_custom_call", output_to_operand_aliasing={{0}: (17, {}), {1}: (18, {}), {2}: (19, {})} | custom-call | flops 154618822656 | bytes 61865984 | tf_op jit(solution)/shard_map/weight_grads/pallas_call | solution.py:487
  716.5 2.3 fusion.1
  718.8 2.3 add_convert_fusion.1
  722.9 1.1 pad_maximum_fusion
  724.0 3.6 add_convert_fusion
  727.6 3.2 add_convert_fusion.2
  730.8 59.4 %all-reduce.12.cloned.1.call-done = bf16[2,512,512]{1,2,0:T(8,128)(2,1)} async-done(((bf16[2,512,512]{1,2,0:T(8,128)(2,1)}), bf16[2,512,512]{1,2,0:T(8,128)(2,1)}) %all-reduce.12.cloned.1.call-update) | async-done | bytes 1048592 | tf_op jit(solution)/shard_map/psum | solution.py:715
  790.2 2.3 copy.57
  792.5 8.2 %merge_half.2 = (bf16[2,64,192,512]{3,2,1,0:T(8,128)(2,1)}, bf16[2,64,192,512]{3,2,1,0:T(8,128)(2,1)}, bf16[2,64,192,512]{3,2,1,0:T(8,128)(2,1)}) custom-call(s32[16]{0:T(128)} %get-tuple-element.145.exps, bf16[16,192,512]{2,1,0:T(8,128)(2,1)} %collective-permute-done.15.a, ...), custom_call_target="tpu_custom_call", output_to_operand_aliasing={{0}: (4, {}), {1}: (5, {}), {2}: (6, {})} | custom-call | flops 1000000000 | bytes 18874368 | tf_op jit(solution)/shard_map/merge_half/pallas_call | solution.py:541
  800.7 8.2 %merge_half.3 = (bf16[2,64,192,512]{3,2,1,0:T(8,128)(2,1)}, bf16[2,64,192,512]{3,2,1,0:T(8,128)(2,1)}, bf16[2,64,192,512]{3,2,1,0:T(8,128)(2,1)}) custom-call(s32[16]{0:T(128)} %get-tuple-element.148.exps, bf16[16,192,512]{2,1,0:T(8,128)(2,1)} %collective-permute-done.12.a, ...), custom_call_target="tpu_custom_call", output_to_operand_aliasing={{0}: (4, {}), {1}: (5, {}), {2}: (6, {})} | custom-call | flops 1000000000 | bytes 18874368 | tf_op jit(solution)/shard_map/merge_half/pallas_call | solution.py:541
  (198 shorter events, 23.7 us)
Async XLA Ops:
  8.0 3.7 copy-start.22
  8.0 404.9 %all-gather.27.cloned.1.call-start = ((), (), s32[]{:S(2)}) async-start(), calls=%async_computation.9 | async-start | bytes 2801664 | tf_op jit(solution)/shard_map/all_gather | solution.py:671
  11.6 30.9 %copy-start = (bf16[1024,4,128]{2,1,0:T(4,128)(2,1)}, bf16[1024,4,128]{2,1,0:T(4,128)(2,1)S(1)}, u32[]{:S(2)}) copy-start(bf16[1024,4,128]{2,1,0:T(4,128)(2,1)S(1)} %reshape.382.refs_0_) | copy-start | bytes 3145732
  12.3 7.6 collective-permute-start
  15.6 26.0 %collective-permute-start.1 = (bf16[1024,4,128]{2,1,0:T(4,128)(2,1)S(1)}, bf16[1024,4,128]{2,1,0:T(4,128)(2,1)S(1)}, u32[]{:S(2)}, u32[]{:S(2)}) collective-permute-start(bf16[1024,4,128]{2,1,0:T(4,128)(2,1)S(1)} %reshape.382.refs_0_), channel_id=1, source_target_pairs={{0,8},{8,0},{1,9},{9,1},{2,10},{10,2},{3,11},{11,3},{4,12},{12,4},... | collective-permute-start | bytes 3145736 | tf_op jit(solution)/shard_map/ppermute | solution.py:622
  15.6 119.0 %copy-start.27 = (s32[64]{0:T(128)}, s32[64]{0:T(128)S(1)}, u32[]{:S(2)}) copy-start(s32[64]{0:T(128)S(1)} %iota_add_fusion.3) | copy-start | bytes 772
  30.9 11.6 %copy-start.13 = (f32[144,128]{1,0:T(8,128)}, f32[144,128]{1,0:T(8,128)S(1)}, u32[]{:S(2)}) copy-start(f32[144,128]{1,0:T(8,128)S(1)} %pad_bitcast_fusion.3.gates) | copy-start | bytes 221188
  81.2 47.1 %collective-permute-start.2 = (f32[1024,512]{1,0:T(8,128)}, f32[1024,512]{1,0:T(8,128)}, u32[]{:S(2)}, u32[]{:S(2)}) collective-permute-start(f32[1024,512]{1,0:T(8,128)} %experts_forward.3), channel_id=1, source_target_pairs={{0,8},{8,0},{1,9},{9,1},{2,10},{10,2},{3,11},{11,3},{4,12},{12,4},... | collective-permute-start | bytes 6291464 | tf_op jit(solution)/shard_map/ppermute | solution.py:622
  81.3 47.0 %copy-start.10 = (bf16[1024,512]{1,0:T(8,128)(2,1)S(1)}, bf16[1024,512]{1,0:T(8,128)(2,1)}, u32[]{:S(2)}) copy-start(bf16[1024,512]{1,0:T(8,128)(2,1)} %copy-done.9) | copy-start | bytes 3145732
  120.3 11.8 %copy-start.30 = (bf16[2,512,512]{2,1,0:T(8,128)(2,1)S(1)}, bf16[2,512,512]{2,1,0:T(8,128)(2,1)}, u32[]{:S(2)}) copy-start(bf16[2,512,512]{2,1,0:T(8,128)(2,1)} %param.12) | copy-start | bytes 3145732
  132.8 12.4 %copy-start.5 = (bf16[1024,512]{1,0:T(8,128)(2,1)}, bf16[1024,512]{1,0:T(8,128)(2,1)S(1)}, u32[]{:S(2)}) copy-start(bf16[1024,512]{1,0:T(8,128)(2,1)S(1)} %add_convert_fusion.5) | copy-start | bytes 3145732
  132.8 13.3 %copy-start.3 = (bf16[1024,512]{1,0:T(8,128)(2,1)S(1)}, bf16[1024,512]{1,0:T(8,128)(2,1)}, u32[]{:S(2)}) copy-start(bf16[1024,512]{1,0:T(8,128)(2,1)} %param.9) | copy-start | bytes 3145732
  144.5 28.0 %copy-start.21 = (f32[144,128]{1,0:T(8,128)}, f32[144,128]{1,0:T(8,128)S(1)}, u32[]{:S(2)}) copy-start(f32[144,128]{1,0:T(8,128)S(1)} %pad_bitcast_fusion.2.gates) | copy-start | bytes 221188
  145.3 27.3 %copy-start.2 = (bf16[1024,4,128]{2,1,0:T(4,128)(2,1)S(1)}, bf16[1024,4,128]{2,1,0:T(4,128)(2,1)}, u32[]{:S(2)}) copy-start(bf16[1024,4,128]{2,1,0:T(4,128)(2,1)} %reshape.384.refs_0_) | copy-start | bytes 3145732
  146.1 288.2 %all-gather.23.cloned.1.call-start = ((), (), s32[]{:S(2)}) async-start(), calls=%async_computation.7 | async-start | bytes 9437184 | tf_op jit(solution)/shard_map/all_gather | solution.py:625
  147.3 287.0 %all-gather.25.cloned.1.call-start = ((), (), s32[]{:S(2)}) async-start(), calls=%async_computation.8 | async-start | bytes 9437184 | tf_op jit(solution)/shard_map/all_gather | solution.py:625
  147.3 23.6 %collective-permute-start.4 = (bf16[1024,4,128]{2,1,0:T(4,128)(2,1)}, bf16[1024,4,128]{2,1,0:T(4,128)(2,1)S(1)}, u32[]{:S(2)}, u32[]{:S(2)}) collective-permute-start(bf16[1024,4,128]{2,1,0:T(4,128)(2,1)} %reshape.386.refs_2_), channel_id=1, source_target_pairs={{0,8},{8,0},{1,9},{9,1},{2,10},{10,2},{3,11},{11,3},{4,12},{12,4},... | collective-permute-start | bytes 3145736 | tf_op jit(solution)/shard_map/ppermute | solution.py:622
  172.0 262.3 %all-gather.19.cloned.1.call-start = ((), (), s32[]{:S(2)}) async-start(), calls=%async_computation.5 | async-start | bytes 9437184 | tf_op jit(solution)/shard_map/all_gather | solution.py:625
  172.6 261.7 %all-gather.21.cloned.1.call-start = ((), (), s32[]{:S(2)}) async-start(), calls=%async_computation.6 | async-start | bytes 9437184 | tf_op jit(solution)/shard_map/all_gather | solution.py:625
  172.6 22.7 %collective-permute-start.3 = (bf16[1024,4,128]{2,1,0:T(4,128)(2,1)S(1)}, bf16[1024,4,128]{2,1,0:T(4,128)(2,1)S(1)}, u32[]{:S(2)}, u32[]{:S(2)}) collective-permute-start(bf16[1024,4,128]{2,1,0:T(4,128)(2,1)S(1)} %copy-done.2), channel_id=1, source_target_pairs={{0,8},{8,0},{1,9},{9,1},{2,10},{10,2},{3,11},{11,3},{4,12},{12,4},... | collective-permute-start | bytes 3145736 | tf_op jit(solution)/shard_map/ppermute | solution.py:622
  196.3 331.1 %all-gather.11.cloned.1.call-start = ((), (), s32[]{:S(2)}) async-start(), calls=%async_computation.1 | async-start | bytes 9437184 | tf_op jit(solution)/shard_map/all_gather | solution.py:625
  196.9 330.5 %all-gather.13.cloned.1.call-start = ((), (), s32[]{:S(2)}) async-start(), calls=%async_computation.2 | async-start | bytes 9437184 | tf_op jit(solution)/shard_map/all_gather | solution.py:625
  197.6 343.5 %all-gather.15.cloned.1.call-start = ((), (), s32[]{:S(2)}) async-start(), calls=%async_computation.3 | async-start | bytes 9437184 | tf_op jit(solution)/shard_map/all_gather | solution.py:625
  197.7 101.0 %copy-start.4 = (bf16[1024,512]{1,0:T(8,128)(2,1)S(1)}, bf16[1024,512]{1,0:T(8,128)(2,1)}, u32[]{:S(2)}) copy-start(bf16[1024,512]{1,0:T(8,128)(2,1)} %param.9) | copy-start | bytes 3145732
  250.5 48.1 %collective-permute-start.5 = (f32[1024,512]{1,0:T(8,128)}, f32[1024,512]{1,0:T(8,128)S(1)}, u32[]{:S(2)}, u32[]{:S(2)}) collective-permute-start(f32[1024,512]{1,0:T(8,128)} %get-tuple-element.59), channel_id=1, source_target_pairs={{0,8},{8,0},{1,9},{9,1},{2,10},{10,2},{3,11},{11,3},{4,12},{12,4},... | collective-permute-start | bytes 6291464 | tf_op jit(solution)/shard_map/ppermute | solution.py:622
  298.6 3.3 copy-start.31
  304.8 288.7 %all-gather.17.cloned.1.call-start = ((), (), s32[]{:S(2)}) async-start(), calls=%async_computation.4 | async-start | bytes 9437184 | tf_op jit(solution)/shard_map/all_gather | solution.py:625
  305.1 46.2 %collective-permute-start.6 = (bf16[1024,4,128]{2,1,0:T(4,128)(2,1)}, bf16[1024,4,128]{2,1,0:T(4,128)(2,1)S(1)}, u32[]{:S(2)}, u32[]{:S(2)}) collective-permute-start(bf16[1024,4,128]{2,1,0:T(4,128)(2,1)} %reshape.387.refs_2_), channel_id=1, source_target_pairs={{0,8},{8,0},{1,9},{9,1},{2,10},{10,2},{3,11},{11,3},{4,12},{12,4},... | collective-permute-start | bytes 3145736 | tf_op jit(solution)/shard_map/ppermute | solution.py:622
  352.3 61.6 %copy-start.28 = (s32[64]{0:T(128)S(1)}, s32[64]{0:T(128)}, u32[]{:S(2)}) copy-start(s32[64]{0:T(128)} %copy-done.27) | copy-start | bytes 772
  410.7 305.1 %collective-permute-start.8 = (f32[1024,512]{1,0:T(8,128)}, f32[1024,512]{1,0:T(8,128)}, u32[]{:S(2)}, u32[]{:S(2)}) collective-permute-start(f32[1024,512]{1,0:T(8,128)} %get-tuple-element.66), channel_id=1, source_target_pairs={{0,8},{8,0},{1,9},{9,1},{2,10},{10,2},{3,11},{11,3},{4,12},{12,4},... | collective-permute-start | bytes 6291464 | tf_op jit(solution)/shard_map/ppermute | solution.py:622
  410.8 305.2 %collective-permute-start.7 = (f32[1024,512]{1,0:T(8,128)}, f32[1024,512]{1,0:T(8,128)}, u32[]{:S(2)}, u32[]{:S(2)}) collective-permute-start(f32[1024,512]{1,0:T(8,128)} %get-tuple-element.64), channel_id=1, source_target_pairs={{0,8},{8,0},{1,9},{9,1},{2,10},{10,2},{3,11},{11,3},{4,12},{12,4},... | collective-permute-start | bytes 6291464 | tf_op jit(solution)/shard_map/ppermute | solution.py:622
  412.8 377.4 %all-reduce.12.cloned.1.call-start = ((), (), s32[]{:S(2)}) async-start(), calls=%async_computation | async-start | bytes 2097152 | tf_op jit(solution)/shard_map/psum | solution.py:715
  413.7 6.0 copy-start.23
  414.9 19.4 %copy-start.26 = (s32[1,32]{1,0:T(1,128)}, s32[1,32]{1,0:T(1,128)S(1)}, u32[]{:S(2)}) copy-start(s32[1,32]{1,0:T(1,128)S(1)} %get-tuple-element.152) | copy-start | bytes 388
  416.0 17.4 %copy-start.24 = (s32[1,16]{1,0:T(1,128)}, s32[1,16]{1,0:T(1,128)S(1)}, u32[]{:S(2)}) copy-start(s32[1,16]{1,0:T(1,128)S(1)} %get-tuple-element.147) | copy-start | bytes 196
  416.0 17.4 %copy-start.25 = (s32[1,16]{1,0:T(1,128)}, s32[1,16]{1,0:T(1,128)S(1)}, u32[]{:S(2)}) copy-start(s32[1,16]{1,0:T(1,128)S(1)} %get-tuple-element.146) | copy-start | bytes 196
  526.7 126.2 %collective-permute-start.9 = (bf16[32,192,512]{2,1,0:T(8,128)(2,1)}, bf16[32,192,512]{2,1,0:T(8,128)(2,1)}, u32[]{:S(2)}, u32[]{:S(2)}) collective-permute-start(bf16[32,192,512]{2,1,0:T(8,128)(2,1)} %get-tuple-element.71), channel_id=1, source_target_pairs={{0,1},{1,0},{2,3},{3,2},{4,5},{5,4},{6,7},{7,6},{8,9},{9,8},{10,11... | collective-permute-start | bytes 18874376 | tf_op jit(solution)/shard_map/ppermute | solution.py:706
  526.8 126.1 %collective-permute-start.10 = (bf16[32,192,512]{2,1,0:T(8,128)(2,1)}, bf16[32,192,512]{2,1,0:T(8,128)(2,1)}, u32[]{:S(2)}, u32[]{:S(2)}) collective-permute-start(bf16[32,192,512]{2,1,0:T(8,128)(2,1)} %get-tuple-element.72), channel_id=1, source_target_pairs={{0,1},{1,0},{2,3},{3,2},{4,5},{5,4},{6,7},{7,6},{8,9},{9,8},{10,11... | collective-permute-start | bytes 18874376 | tf_op jit(solution)/shard_map/ppermute | solution.py:706
  527.3 126.2 %collective-permute-start.11 = (bf16[32,192,512]{2,1,0:T(8,128)(2,1)}, bf16[32,192,512]{2,1,0:T(8,128)(2,1)}, u32[]{:S(2)}, u32[]{:S(2)}) collective-permute-start(bf16[32,192,512]{2,1,0:T(8,128)(2,1)} %get-tuple-element.73), channel_id=1, source_target_pairs={{0,1},{1,0},{2,3},{3,2},{4,5},{5,4},{6,7},{7,6},{8,9},{9,8},{10,11... | collective-permute-start | bytes 18874376 | tf_op jit(solution)/shard_map/ppermute | solution.py:706
  652.9 63.5 %collective-permute-start.15 = (bf16[16,192,512]{2,1,0:T(8,128)(2,1)}, bf16[16,192,512]{2,1,0:T(8,128)(2,1)}, u32[]{:S(2)}, u32[]{:S(2)}) collective-permute-start(bf16[16,192,512]{2,1,0:T(8,128)(2,1)} %get-tuple-element.84), channel_id=1, source_target_pairs={{0,1},{1,0},{2,3},{3,2},{4,5},{5,4},{6,7},{7,6},{8,9},{9,8},{10,11... | collective-permute-start | bytes 9437192 | tf_op jit(solution)/shard_map/ppermute | solution.py:706
  653.0 139.5 %collective-permute-start.16 = (bf16[16,192,512]{2,1,0:T(8,128)(2,1)}, bf16[16,192,512]{2,1,0:T(8,128)(2,1)}, u32[]{:S(2)}, u32[]{:S(2)}) collective-permute-start(bf16[16,192,512]{2,1,0:T(8,128)(2,1)} %get-tuple-element.85), channel_id=1, source_target_pairs={{0,1},{1,0},{2,3},{3,2},{4,5},{5,4},{6,7},{7,6},{8,9},{9,8},{10,11... | collective-permute-start | bytes 9437192 | tf_op jit(solution)/shard_map/ppermute | solution.py:706
  653.5 139.0 %collective-permute-start.17 = (bf16[16,192,512]{2,1,0:T(8,128)(2,1)}, bf16[16,192,512]{2,1,0:T(8,128)(2,1)}, u32[]{:S(2)}, u32[]{:S(2)}) collective-permute-start(bf16[16,192,512]{2,1,0:T(8,128)(2,1)} %get-tuple-element.86), channel_id=1, source_target_pairs={{0,1},{1,0},{2,3},{3,2},{4,5},{5,4},{6,7},{7,6},{8,9},{9,8},{10,11... | collective-permute-start | bytes 9437192 | tf_op jit(solution)/shard_map/ppermute | solution.py:706
  653.6 62.9 %copy-start.18 = (bf16[1024,512]{1,0:T(8,128)(2,1)S(1)}, bf16[1024,512]{1,0:T(8,128)(2,1)}, u32[]{:S(2)}) copy-start(bf16[1024,512]{1,0:T(8,128)(2,1)} %copy-done.17) | copy-start | bytes 3145732
  715.9 84.8 %collective-permute-start.12 = (bf16[16,192,512]{2,1,0:T(8,128)(2,1)}, bf16[16,192,512]{2,1,0:T(8,128)(2,1)}, u32[]{:S(2)}, u32[]{:S(2)}) collective-permute-start(bf16[16,192,512]{2,1,0:T(8,128)(2,1)} %get-tuple-element.81), channel_id=1, source_target_pairs={{0,1},{1,0},{2,3},{3,2},{4,5},{5,4},{6,7},{7,6},{8,9},{9,8},{10,11... | collective-permute-start | bytes 9437192 | tf_op jit(solution)/shard_map/ppermute | solution.py:706
  715.9 84.7 %collective-permute-start.13 = (bf16[16,192,512]{2,1,0:T(8,128)(2,1)}, bf16[16,192,512]{2,1,0:T(8,128)(2,1)}, u32[]{:S(2)}, u32[]{:S(2)}) collective-permute-start(bf16[16,192,512]{2,1,0:T(8,128)(2,1)} %get-tuple-element.82), channel_id=1, source_target_pairs={{0,1},{1,0},{2,3},{3,2},{4,5},{5,4},{6,7},{7,6},{8,9},{9,8},{10,11... | collective-permute-start | bytes 9437192 | tf_op jit(solution)/shard_map/ppermute | solution.py:706
  716.4 84.3 %collective-permute-start.14 = (bf16[16,192,512]{2,1,0:T(8,128)(2,1)}, bf16[16,192,512]{2,1,0:T(8,128)(2,1)}, u32[]{:S(2)}, u32[]{:S(2)}) collective-permute-start(bf16[16,192,512]{2,1,0:T(8,128)(2,1)} %get-tuple-element.83), channel_id=1, source_target_pairs={{0,1},{1,0},{2,3},{3,2},{4,5},{5,4},{6,7},{7,6},{8,9},{9,8},{10,11... | collective-permute-start | bytes 9437192 | tf_op jit(solution)/shard_map/ppermute | solution.py:706
  722.9 4.7 copy-start.6
  722.9 4.7 copy-start.11
  (12 other events, 18.1 us)
Sparse Core Ops, SparseCore 0:
  146.2 25.6 all-gather.26
  173.8 50.5 all-gather.22
  226.2 50.5 all-gather.24
  279.0 50.5 all-gather.18
  331.8 50.5 all-gather.20
  384.6 50.5 all-gather.10
  437.6 50.5 all-gather.12
  490.0 51.0 all-gather.14
  543.0 50.4 all-gather.16
Sparse Core Ops, SparseCore 1:
  724.1 66.1 all-reduce.11

commit v12 on v11

--- a/solution.py
+++ b/solution.py
@@ -15,7 +15,6 @@
 HALF_TILE = 64
 WTILE = 768
 PARTS = 2
-AHEAD = 3
 SOURCES = 8
 CHUNK = 256
 PITCH = 9
@@ -293,8 +292,8 @@
     )(starts.reshape(-1), exps, layers, shared)
 
 
-def weight_grad_body(exps, tiles, begins, offsets, names, *refs, parts, n_exp, n_alias, n_moved, first_list, page, layer):
-    rows_in, refs = refs[:4], refs[4:]
+def weight_grad_body(exps, tiles, begins, offsets, names, *refs, parts, n_exp, n_alias, n_moved, n_rows, first_list, page, layer):
+    u_rows, d_rows, refs = refs[:n_rows[0]], refs[n_rows[0]:sum(n_rows)], refs[sum(n_rows):]
     idx_all, gate_ref, g_ref, up_ref, w_ref = refs[:5]
     moved, whole, refs = refs[5:5 + n_moved], refs[5 + n_moved:5 + n_moved + n_alias], refs[5 + n_moved + n_alias:]
     (dg_ref, du_ref, dw_ref, og_ref, ou_ref, ow_ref,
@@ -317,12 +316,15 @@
         return rows[pl.ds(first * PITCH + k, count, stride=PITCH), :]
 
     n_tok = uds.shape[0] - 8
-    run = n_tok // (2 * SOURCES)
 
     def row_copies(q):
-        return [pltpu.make_async_copy(src.at[pl.ds(q * run, run)],
-                                      uds.at[pl.ds((2 * q + k % 2) * run, run), pl.ds(k // 2 * parts, parts)], sem.at[q])
-                for k, src in enumerate(rows_in)]
+        out = []
+        for kind, arrays in enumerate((u_rows, d_rows)):
+            run = n_tok // (SOURCES * len(arrays))
+            for k, src in enumerate(arrays):
+                place = uds.at[pl.ds((q * len(arrays) + k) * run, run), pl.ds(kind * parts, parts)]
+                out.append(pltpu.make_async_copy(src.at[pl.ds(q * run, run)], place, sem.at[q]))
+        return out
 
     def wait_rows(limit):
         def one(q, carry):
@@ -332,11 +334,6 @@
                     c.wait()
                 seen[0] = q + 1
 
-                @pl.when(q + AHEAD < SOURCES)
-                def _():
-                    for c in row_copies(q + AHEAD):
-                        c.start()
-
             return carry
 
         @pl.when(seen[0] < SOURCES)
@@ -345,15 +342,14 @@
 
     @pl.when(e == 0)
     def _():
-        for q in range(AHEAD):
+        for q in range(SOURCES):
             for c in row_copies(q):
                 c.start()
         seen[0] = 0
-        seen[1] = 1
         table_copy(0).start()
         table_copy(1).start()
         uds[pl.ds(n_tok, 8)] = jnp.zeros((8, 2 * parts, LANES), jnp.bfloat16)
-        for ref in (*both[0], *both[1]):
+        for ref in (*both[0], *both[1], gacc, wacc):
             clear(ref)
         table_copy(0).wait()
         wait_rows(WTILE)
@@ -385,9 +381,8 @@
     def compute(j, new, old):
         un, cn, dn, hn = new
         uo, co, do, ho = old
-        fresh = seen[1] == 1
-        gacc[...] = jnp.where(fresh, 0.0, gacc[...]) + nn_dot(do[...], uo[...])
-        wacc[...] = jnp.where(fresh, 0.0, wacc[...]) + nn_dot(ho[...], co[...])
+        gacc[...] += nn_dot(do[...], uo[...])
+        wacc[...] += nn_dot(ho[...], co[...])
         nxt = jnp.where(j + 1 < n_tiles, here + (j + 1) * WTILE, there)
         gu = jnp.concatenate([g_ref[0, 0], up_ref[0, 0]], axis=0)
         for q in range(0, WTILE, CHUNK):
@@ -421,8 +416,6 @@
         def _():
             compute(j, both[1], both[0])
 
-        seen[1] = jnp.where(j == 0, 1, 0)
-
         @pl.when(j == 0)
         def _():
             dg = gacc[:ff].astype(jnp.bfloat16)
@@ -430,6 +423,8 @@
             dw = wacc[...].astype(jnp.bfloat16)
             dg_ref[0, 0], du_ref[0, 0], dw_ref[0, 0] = dg, du, dw
             og_ref[0], ou_ref[0], ow_ref[0] = dg, du, dw
+            gacc[...] = jnp.zeros_like(gacc)
+            wacc[...] = jnp.zeros_like(wacc)
 
         return carry
 
@@ -463,8 +458,8 @@
 
 
 def weight_grads(layer, first, exps, tiles, offsets, rows, idx_all, gates, weights, full, moved=None):
-    n_half, parts, _ = rows[0].shape
-    n_tok = 2 * n_half
+    parts = rows[0][0].shape[1]
+    n_tok = sum(x.shape[0] for x in rows[0])
     n_layers, n_local, ff, d_model = weights[0].shape
     n_exp = exps.shape[0]
     out_rows = gates.shape[1]
@@ -485,27 +480,27 @@
         scratch = [pltpu.VMEM((2, 3, arrived[0].shape[0] // n_exp, ff, d_model), jnp.bfloat16), pltpu.SemaphoreType.DMA((2,)),
                    pltpu.SemaphoreType.DMA((2,))]
     outs = pl.pallas_call(
-        functools.partial(weight_grad_body, parts=parts, n_exp=n_exp, n_alias=len(aliased), n_moved=len(arrived), first_list=first,
-                          page=page, layer=layer),
+        functools.partial(weight_grad_body, parts=parts, n_exp=n_exp, n_alias=len(aliased), n_moved=len(arrived),
+                          n_rows=[len(x) for x in rows], first_list=first, page=page, layer=layer),
         grid_spec=pltpu.PrefetchScalarGridSpec(
             num_scalar_prefetch=5,
             grid=(n_exp + 1,),
-            in_specs=[any_spec] * 5 + [gate_spec] + [mine] * 3 + [any_spec] * (len(arrived) + len(aliased)),
+            in_specs=[any_spec] * (len(rows[0] + rows[1]) + 1) + [gate_spec] + [mine] * 3 + [any_spec] * (len(arrived) + len(aliased)),
             out_specs=[done] * 3 + [half] * 3,
             scratch_shapes=[pltpu.VMEM((n_tok + 8, 2 * parts, LANES), jnp.bfloat16)]
             + [pltpu.VMEM((WTILE * PITCH + 16, LANES), jnp.float32)] + tile_set * 2
             + [pltpu.VMEM((2 * ff, d_model), jnp.float32), pltpu.VMEM((ff, d_model), jnp.float32),
-               pltpu.SMEM((3 * page,), jnp.int32), pltpu.SMEM((2,), jnp.int32), pltpu.SemaphoreType.DMA((SOURCES,)),
+               pltpu.SMEM((3 * page,), jnp.int32), pltpu.SMEM((1,), jnp.int32), pltpu.SemaphoreType.DMA((SOURCES,)),
                pltpu.SemaphoreType.DMA((3,))] + scratch,
         ),
         out_shape=[jax.ShapeDtypeStruct((n_layers, n_local, ff, d_model), jnp.bfloat16)] * 3
         + [jax.ShapeDtypeStruct((n_exp, ff, d_model), jnp.bfloat16)] * 3,
-        input_output_aliases={14 + len(arrived) + k: k for k in range(len(aliased))},
+        input_output_aliases={10 + len(rows[0] + rows[1] + arrived) + k: k for k in range(len(aliased))},
         compiler_params=pltpu.CompilerParams(dimension_semantics=("arbitrary",), vmem_limit_bytes=VMEM_LIMIT),
         cost_estimate=pl.CostEstimate(flops=6 * n_tok * n_exp * d_model * ff,
                                       bytes_accessed=n_tok * d_model * 4 + 9 * n_exp * ff * d_model * 2, transcendentals=0),
         name="weight_grads",
-    )(exps, tiles, begins, offsets, names, *rows, idx_all, gates, *weights, *arrived, *aliased)
+    )(exps, tiles, begins, offsets, names, *rows[0], *rows[1], idx_all, gates, *weights, *arrived, *aliased)
     return outs[:3], outs[3:]
 
 
@@ -550,6 +545,24 @@
         cost_estimate=pl.CostEstimate(flops=10**9, bytes_accessed=6 * n_exp * ff * d_model * 2, transcendentals=0),
         name="merge_half",
     )(exps, *half, *full)
+
+
+def join_body(a, b, out, sem):
+    n = a.shape[0]
+    copies = [pltpu.make_async_copy(x, out.at[pl.ds(k * n, n)], sem.at[k]) for k, x in enumerate((a, b))]
+    for c in copies:
+        c.start()
+    for c in copies:
+        c.wait()
+
+
+def join_rows(a, b):
+    n, parts, _ = a.shape
+    any_spec = pl.BlockSpec(memory_space=pl.ANY)
+    return pl.pallas_call(
+        join_body, in_specs=[any_spec] * 2, out_shape=jax.ShapeDtypeStruct((2 * n, parts, LANES), a.dtype),
+        out_specs=pl.BlockSpec(memory_space=pltpu.VMEM), scratch_shapes=[pltpu.SemaphoreType.DMA((2,))], name="join_rows",
+    )(a, b)
 
 
 def route_tables(ids, gates, ep, n_local):
@@ -605,6 +618,7 @@
     expert_spec = P(None, 'ep', None, None)
     ep_pairs = [(i, 1 - i) for i in range(ep_size)]
     core_pairs = [(i, i ^ 1) for i in range(dp_size)]
+    chip_pairs = [(i, i ^ (2 << i % 2)) for i in range(dp_size)]
 
     def device_body(tokens, d_out, expert_ids, gate_vals, w_mix, w_gate, w_up, w_down):
         n_layers = w_mix.shape[0]
@@ -624,6 +638,9 @@
         def spread(x):
             return [lax.all_gather(y, 'dp', axis=0, tiled=True) for y in x]
 
+        def trade(x, pairs):
+            return [lax.ppermute(y, 'dp', pairs) for y in x]
+
         def slab(x):
             return x.reshape(tok, parts, LANES)
 
@@ -653,7 +670,7 @@
         x_in, u_slabs, u_others, xs = tokens, [u_slab], [swap(u_slab)], []
         d_slab = slab(d_out)
         d_other = swap(after(d_slab, u_others[0]))
-        d_rows = spread((d_slab, d_other))
+        d_rows = spread([join_rows(d_slab, d_other)])
         for layer in range(n_layers):
             if layer:
                 u = mixed(x_in, layer)
@@ -671,10 +688,11 @@
         shared = lax.all_gather(jnp.stack(packed), 'dp', axis=0)
         starts = shared[:, :, 0, -8].astype(jnp.int32)
         core = dp_id % 2
-        n_parts = [PARTS] * top + [1]
-        dealt = [deal_experts(starts[:, layer], n_local, 2 * n_parts[layer]) for layer in range(n_layers)]
-        mine = [dealt[layer][0][core * n_parts[layer] + part] for layer in range(n_layers) for part in range(n_parts[layer])]
-        of_layer = [layer for layer in range(n_layers) for _ in range(n_parts[layer])]
+        kind = (dp_id // 2 + dp_id // 4) % 2
+        dealt = [deal_experts(starts[:, layer], n_local, 2 * PARTS) for layer in range(n_layers)]
+        of_layer = [layer for layer in range(top) for _ in range(PARTS)] + [top]
+        places = [PARTS * core + part for _ in range(top) for part in range(PARTS)] + [PARTS * core + kind]
+        mine = [dealt[layer][0][place] for layer, place in zip(of_layer, places)]
         list_rows = cdiv(cdiv(dp_size * 2 * cap, LANES), 8) * 8 + 8
         idx_all, gate_all = merge_tables(shared, starts, jnp.concatenate(mine),
                                          jnp.concatenate([jnp.full_like(x, layer) for x, layer in zip(mine, of_layer)]),
@@ -685,7 +703,8 @@
         d_y, full, arrived = d_out, None, []
         d_mix = [None] * n_layers
         for layer in reversed(range(n_layers)):
-            u_rows = spread((u_slabs[layer], u_others[layer]))
+            both_u = [u_slabs[layer], u_others[layer]]
+            u_rows = spread(both_u if layer < top else [join_rows(*both_u)])
             slabs = (u_slabs[layer], u_others[layer], d_slab, d_other)
             own, other = token_kernel(layer, runs[layer][2], tables[layer][1], slabs, weights)
             d_u = (d_y.astype(jnp.float32) + own + swap(other)).astype(jnp.bfloat16)
@@ -696,22 +715,28 @@
             d_y = (d_u.astype(jnp.float32)
                    + jnp.einsum('te,de->td', d_u, w_mix[layer], preferred_element_type=jnp.float32)).astype(jnp.bfloat16)
             lists, tiles = dealt[layer]
-            for part in range(n_parts[layer]):
-                place = of_layer.index(layer) + part
-                own_list, its_list = core * n_parts[layer] + part, (1 - core) * n_parts[layer] + part
-                first = sum(x.shape[0] for x in mine[:place])
-                full, done = weight_grads(layer, first, mine[place], after(tiles[own_list], last),
-                                          offsets[place], u_rows + d_rows, idx_all, gate_all, weights, full,
-                                          arrived.pop(0)[2:] if part and arrived else None)
-                arrived.append((layer, part, [lax.ppermute(x, 'dp', core_pairs) for x in done], lists[its_list]))
+            theirs = PARTS * (1 - core)
+            for part in range(PARTS if layer < top else 1):
+                item = of_layer.index(layer) + part
+                first = sum(x.shape[0] for x in mine[:item])
+                full, done = weight_grads(layer, first, mine[item], after(tiles[places[item]], last), offsets[item],
+                                          (u_rows, d_rows), idx_all, gate_all, weights, full, moved if part else None)
+                got = trade(done, core_pairs)
+                if layer < top:
+                    arrived.insert(1 + 2 * part, (layer, got, lists[theirs + part]))
+                    continue
+                moved = got, lists[theirs + kind]
+                far = trade(done, chip_pairs)
+                arrived.append((layer, far, lists[PARTS * core + 1 - kind]))
+                arrived.append((layer, trade(far, core_pairs), lists[theirs + 1 - kind]))
             if layer:
                 d_slab = slab(d_y)
                 d_other = swap(d_slab)
-                d_rows = spread((d_slab, d_other))
+                d_rows = spread([join_rows(d_slab, d_other)])
                 if layer == top:
                     layer_out = (u.astype(jnp.float32) + y_own + swap(after(last, d_other))).astype(jnp.bfloat16)
-        for layer, _, part, names in arrived:
-            full = merge_half(layer, names, part, full)
+        for layer, got, names in arrived:
+            full = merge_half(layer, names, got, full)
         d_mix = lax.psum(jnp.stack(d_mix), ('dp', 'ep'))
         return (layer_out, d_y, d_mix, jnp.swapaxes(full[0], 2, 3), jnp.swapaxes(full[1], 2, 3), full[2])
 

time: 818 us -> 835 us (1.021)
  waiting for transfers between devices: 239 us -> 278 us
  Pallas kernels: 477 us -> 450 us
  starting transfers between devices: 14 us -> 23.1 us
    ppermute x9, waiting for transfers between devices: 112 us -> 217 us  [swap(): return lax.ppermute(x, 'ep', ep_pairs)]
    all_gather x8 -> x5, waiting for transfers between devices: 66.2 us -> 0.04 us  [spread(): return [lax.all_gather(y, 'dp', axis=0, tiled=True) for y in x]]
    pallas_call x3, Pallas kernels: 214 us -> 165 us  [weight_grads(): pl.pallas_call(functools.partial(weight_grad_body, parts=parts, n_exp=n_e...]
    pallas_call x2 -> x4, Pallas kernels: 16.3 us -> 32.7 us  [merge_half(): pl.pallas_call(functools.partial(merge_body, layer=layer, n_exp=n_exp), g...]
    ppermute x9 -> x15, starting transfers between devices: 1.79 us -> 10.7 us  [trade(): return [lax.ppermute(y, 'dp', pairs) for y in x]]
    pallas_call x0 -> x3, Pallas kernels: none -> 8.75 us  [join_rows(): pl.pallas_call(join_body, in_specs=[any_spec] * 2, out_shape=jax.ShapeDty...]
  transfers between devices with their start and end apart: 28 -> 31, of which waited for: 9 -> 10; matrix products, arithmetic and copies ran while one was open for 5% -> 5% of each run, Pallas kernels for 53% -> 48%
where the time goes in v12:
time: 835 us; the launch traced here: 834 us
  Pallas kernels  450 us (54%)
  waiting for transfers between devices  278 us (33%)
  other arithmetic  41 us (5%)
  starting transfers between devices  23.1 us (3%)
  between operations  16.6 us (2%)
  local copies, waits for them, and re-layouts  15.3 us (2%)
  matrix products  10.5 us (1%)
    pallas_call x5, Pallas kernels, token_kernel(): pl.pallas_call(functools.partial(token_body, layer=layer, tok=tok, parts=...  232 us
    ppermute x9, waiting for transfers between devices, swap(): return lax.ppermute(x, 'ep', ep_pairs)  217 us
    pallas_call x3, Pallas kernels, weight_grads(): pl.pallas_call(functools.partial(weight_grad_body, parts=parts, n_exp=n_e...  165 us
    psum x1, waiting for transfers between devices, device_body(): d_mix = lax.psum(jnp.stack(d_mix), ('dp', 'ep'))  59.5 us
    pallas_call x4, Pallas kernels, merge_half(): pl.pallas_call(functools.partial(merge_body, layer=layer, n_exp=n_exp), g...  32.7 us
  transfers between devices with their start and end apart: 31, of which 10 were waited for; matrix products, arithmetic and copies ran while one was open for 5% of the time, Pallas kernels for 48%

profile of v12, /device:TPU:0, one launch (start us, length us, event | category | flops | bytes accessed | tf_op | source)
XLA Modules:
  0.0 833.8 jit_solution(2970823333736394583)
XLA Ops:
  8.9 2.4 add_convert_fusion.7
  12.3 3.3 collective-permute-start
  15.6 4.3 collective-permute-done
  22.6 6.4 sort.30
  29.0 1.9 fusion.43
  31.7 9.8 %collective-permute-done.1.refs_1_ = bf16[1024,4,128]{2,1,0:T(4,128)(2,1)S(1)} collective-permute-done((bf16[1024,4,128]{2,1,0:T(4,128)(2,1)S(1)}, bf16[1024,4,128]{2,1,0:T(4,128)(2,1)S(1)}, u32[]{:S(2)}, u32[]{:S(2)}) %collective-permute-start.1) | collective-permute-done | bytes 1048608 | tf_op jit(solution)/shard_map/ppermute | solution.py:636
  42.5 38.7 %experts_forward.3 = f32[1024,512]{1,0:T(8,128)} custom-call(s32[128]{0:T(128)} %get-tuple-element.177.runs, s32[18432]{0:T(1024)} %get-tuple-element.153.idx, f32[144,128]{1,0:T(8,128)} %copy-done.13, bf16[1024,4,128]{2,1,0:T(4,128)(2,1)} %copy-done, bf16[1024,4,128]{2,1,0:T(4,128)(2,1)} %copy-done.1, bf16[2,64,192,512]{3,2,1,0:T(8,128)(2,1)} %bitcast.139, ...), custom_call_target="tpu_custom_call" | custom-call | flops 19327352832 | bytes 37748736 | tf_op jit(solution)/shard_map/experts_forward/pallas_call | solution.py:213
  81.3 38.9 %experts_forward.4 = f32[1024,512]{1,0:T(8,128)} custom-call(s32[128]{0:T(128)} %get-tuple-element.178.runs, s32[18432]{0:T(1024)} %get-tuple-element.153.idx, f32[144,128]{1,0:T(8,128)} %copy-done.13, bf16[1024,4,128]{2,1,0:T(4,128)(2,1)} %copy-done, bf16[1024,4,128]{2,1,0:T(4,128)(2,1)} %copy-done.1, bf16[2,64,192,512]{3,2,1,0:T(8,128)(2,1)} %bitcast.140, ...), custom_call_target="tpu_custom_call" | custom-call | flops 19327352832 | bytes 37748736 | tf_op jit(solution)/shard_map/experts_forward/pallas_call | solution.py:213
  120.3 8.0 collective-permute-done.2
  128.3 2.8 add_convert_fusion.6
  132.8 1.1 reshape.332.refs_0_.a
  136.0 6.4 sort.31
  143.3 1.9 fusion.44
  146.1 1.1 reshape.334.refs_2_.a
  147.5 23.4 %collective-permute-done.4.refs_3_.b = bf16[1024,4,128]{2,1,0:T(4,128)(2,1)} collective-permute-done((bf16[1024,4,128]{2,1,0:T(4,128)(2,1)}, bf16[1024,4,128]{2,1,0:T(4,128)(2,1)}, u32[]{:S(2)}, u32[]{:S(2)}) %collective-permute-start.4) | collective-permute-done | bytes 1048608 | tf_op jit(solution)/shard_map/ppermute | solution.py:636
  170.9 2.9 join_rows.5
  174.5 22.1 %collective-permute-done.3.refs_1_.b = bf16[1024,4,128]{2,1,0:T(4,128)(2,1)} collective-permute-done((bf16[1024,4,128]{2,1,0:T(4,128)(2,1)S(1)}, bf16[1024,4,128]{2,1,0:T(4,128)(2,1)}, u32[]{:S(2)}, u32[]{:S(2)}) %collective-permute-start.3) | collective-permute-done | bytes 1048608 | tf_op jit(solution)/shard_map/ppermute | solution.py:636
  196.6 2.9 join_rows.4
  200.8 52.7 %experts_backward.2 = (f32[1024,512]{1,0:T(8,128)}, f32[1024,512]{1,0:T(8,128)}) custom-call(s32[128]{0:T(128)} %get-tuple-element.180.runs, s32[18432]{0:T(1024)} %get-tuple-element.155.idx, f32[144,128]{1,0:T(8,128)} %copy-done.19, bf16[1024,4,128]{2,1,0:T(4,128)(2,1)} %reshape.332.refs_0_.a, bf16[1024,4,128]{2,1,0:T(4,128)(2,1)} %collective-permute-done.3.refs_1_.b, ...), custom_call_target="tpu_custom_call" | custom-call | flops 51539607552 | bytes 37748736 | tf_op jit(solution)/shard_map/experts_backward/pallas_call | solution.py:213
  253.4 3.6 collective-permute-start.5
  257.1 42.9 %collective-permute-done.5 = f32[1024,512]{1,0:T(8,128)S(1)} collective-permute-done((f32[1024,512]{1,0:T(8,128)}, f32[1024,512]{1,0:T(8,128)S(1)}, u32[]{:S(2)}, u32[]{:S(2)}) %collective-permute-start.5) | collective-permute-done | bytes 2097184 | tf_op jit(solution)/shard_map/ppermute | solution.py:636
  299.9 3.0 add_convert_fusion.4
  305.0 1.8 collective-permute-start.6
  306.8 19.0 %collective-permute-done.6.refs_3_.b = bf16[1024,4,128]{2,1,0:T(4,128)(2,1)S(1)} collective-permute-done((bf16[1024,4,128]{2,1,0:T(4,128)(2,1)S(1)}, bf16[1024,4,128]{2,1,0:T(4,128)(2,1)S(1)}, u32[]{:S(2)}, u32[]{:S(2)}) %collective-permute-start.6) | collective-permute-done | bytes 1048608 | tf_op jit(solution)/shard_map/ppermute | solution.py:636
  326.7 2.9 join_rows.3
  329.9 44.6 %experts_forward.5 = (f32[1024,512]{1,0:T(8,128)}, f32[1024,512]{1,0:T(8,128)}) custom-call(s32[128]{0:T(128)} %get-tuple-element.180.runs, s32[18432]{0:T(1024)} %get-tuple-element.156.idx, f32[144,128]{1,0:T(8,128)} %copy-done.19, bf16[1024,4,128]{2,1,0:T(4,128)(2,1)} %reshape.332.refs_0_.a, bf16[1024,4,128]{2,1,0:T(4,128)(2,1)} %collective-permute-done.3.refs_1_.b, ...), custom_call_target="tpu_custom_call" | custom-call | flops 38654705664 | bytes 37748736 | tf_op jit(solution)/shard_map/experts_forward/pallas_call | solution.py:213
  374.5 57.2 %experts_backward.3 = (f32[1024,512]{1,0:T(8,128)}, f32[1024,512]{1,0:T(8,128)}) custom-call(s32[128]{0:T(128)} %get-tuple-element.176.runs, s32[18432]{0:T(1024)} %get-tuple-element.152.idx, f32[144,128]{1,0:T(8,128)} %copy-done.13, bf16[1024,4,128]{2,1,0:T(4,128)(2,1)} %copy-done, bf16[1024,4,128]{2,1,0:T(4,128)(2,1)} %copy-done.1, ...), custom_call_target="tpu_custom_call" | custom-call | flops 51539607552 | bytes 37748736 | tf_op jit(solution)/shard_map/experts_backward/pallas_call | solution.py:213
  436.8 10.9 %merge_tables.1 = (s32[48,32,128]{2,1,0:T(8,128)}, f32[48,32,128]{2,1,0:T(8,128)}) custom-call(s32[2048]{0:T(1024)} %bitcast.172, s32[48]{0:T(128)} %pad_add_fusion.6.exps, s32[48]{0:T(128)} %constant.176.clone.1.layers, f32[8,2,2,152,128]{4,3,2,1,0:T(8,128)} %bitcast.188), custom_call_target="tpu_custom_call" | custom-call | flops 1000000000 | bytes 2490368 | tf_op jit(solution)/shard_map/merge_tables/pallas_call | solution.py:278
  449.5 49.0 %weight_grads.3 = (bf16[2,64,192,512]{3,2,1,0:T(8,128)(2,1)}, bf16[2,64,192,512]{3,2,1,0:T(8,128)(2,1)}, bf16[2,64,192,512]{3,2,1,0:T(8,128)(2,1)}, bf16[16,192,...) custom-call(s32[16]{0:T(128)} %bitcast.185, s32[17]{0:T(128)} %get-tuple-element.172.tiles, ...), custom_call_target="tpu_custom_call" | custom-call | flops 154618822656 | bytes 61865984 | tf_op jit(solution)/shard_map/weight_grads/pallas_call | solution.py:482
  498.6 4.6 collective-permute-start.15
  503.2 2.4 collective-permute-start.7
  507.7 44.7 %collective-permute-done.7 = f32[1024,512]{1,0:T(8,128)} collective-permute-done((f32[1024,512]{1,0:T(8,128)}, f32[1024,512]{1,0:T(8,128)}, u32[]{:S(2)}, u32[]{:S(2)}) %collective-permute-start.7) | collective-permute-done | bytes 2097184 | tf_op jit(solution)/shard_map/ppermute | solution.py:636
  552.4 1.9 collective-permute-start.17
  554.3 42.7 %collective-permute-done.8 = f32[1024,512]{1,0:T(8,128)} collective-permute-done((f32[1024,512]{1,0:T(8,128)}, f32[1024,512]{1,0:T(8,128)}, u32[]{:S(2)}, u32[]{:S(2)}) %collective-permute-start.8) | collective-permute-done | bytes 2097184 | tf_op jit(solution)/shard_map/ppermute | solution.py:636
  597.1 2.4 collective-permute-start.19
  599.5 57.3 %weight_grads.4 = (bf16[2,64,192,512]{3,2,1,0:T(8,128)(2,1)}, bf16[2,64,192,512]{3,2,1,0:T(8,128)(2,1)}, bf16[2,64,192,512]{3,2,1,0:T(8,128)(2,1)}, bf16[16,192,...) custom-call(s32[16]{0:T(128)} %bitcast.180, ...), custom_call_target="tpu_custom_call", output_to_operand_aliasing={{0}: (13, {}), {1}: (14, {}), {2}: (15, {})} | custom-call | flops 154618822656 | bytes 61865984 | tf_op jit(solution)/shard_map/weight_grads/pallas_call | solution.py:482
  657.9 59.0 %weight_grads.5 = (bf16[2,64,192,512]{3,2,1,0:T(8,128)(2,1)}, bf16[2,64,192,512]{3,2,1,0:T(8,128)(2,1)}, bf16[2,64,192,512]{3,2,1,0:T(8,128)(2,1)}, bf16[16,192,...) custom-call(s32[16]{0:T(128)} %bitcast.176, ...), custom_call_target="tpu_custom_call", output_to_operand_aliasing={{0}: (16, {}), {1}: (17, {}), {2}: (18, {})} | custom-call | flops 154618822656 | bytes 61865984 | tf_op jit(solution)/shard_map/weight_grads/pallas_call | solution.py:482
  717.6 2.3 fusion.1
  719.9 2.3 add_convert_fusion.1
  724.0 1.1 pad_maximum_fusion
  725.1 3.6 add_convert_fusion
  728.7 3.2 add_convert_fusion.2
  731.8 59.5 %all-reduce.12.cloned.1.call-done = bf16[2,512,512]{1,2,0:T(8,128)(2,1)} async-done(((bf16[2,512,512]{1,2,0:T(8,128)(2,1)}), bf16[2,512,512]{1,2,0:T(8,128)(2,1)}) %all-reduce.12.cloned.1.call-update) | async-done | bytes 1048592 | tf_op jit(solution)/shard_map/psum | solution.py:740
  791.4 2.3 copy.63
  793.6 8.2 merge_half.4
  801.8 8.2 merge_half.5
  810.0 8.2 merge_half.6
  818.2 8.2 merge_half.7
  (205 shorter events, 29.2 us)
Async XLA Ops:
  8.0 423.7 %all-gather.18.cloned.1.call-start = ((), (), s32[]{:S(2)}) async-start(), calls=%async_computation.6 | async-start | bytes 2801664 | tf_op jit(solution)/shard_map/all_gather | solution.py:688
  11.6 30.9 %copy-start = (bf16[1024,4,128]{2,1,0:T(4,128)(2,1)}, bf16[1024,4,128]{2,1,0:T(4,128)(2,1)S(1)}, u32[]{:S(2)}) copy-start(bf16[1024,4,128]{2,1,0:T(4,128)(2,1)S(1)} %reshape.330.refs_0_) | copy-start | bytes 3145732
  12.3 7.6 collective-permute-start
  15.6 26.0 %collective-permute-start.1 = (bf16[1024,4,128]{2,1,0:T(4,128)(2,1)S(1)}, bf16[1024,4,128]{2,1,0:T(4,128)(2,1)S(1)}, u32[]{:S(2)}, u32[]{:S(2)}) collective-permute-start(bf16[1024,4,128]{2,1,0:T(4,128)(2,1)S(1)} %reshape.330.refs_0_), channel_id=1, source_target_pairs={{0,8},{8,0},{1,9},{9,1},{2,10},{10,2},{3,11},{11,3},{4,12},{12,4},... | collective-permute-start | bytes 3145736 | tf_op jit(solution)/shard_map/ppermute | solution.py:636
  15.6 119.0 %copy-start.29 = (s32[64]{0:T(128)}, s32[64]{0:T(128)S(1)}, u32[]{:S(2)}) copy-start(s32[64]{0:T(128)S(1)} %iota_add_fusion.3) | copy-start | bytes 772
  81.2 47.1 %collective-permute-start.2 = (f32[1024,512]{1,0:T(8,128)}, f32[1024,512]{1,0:T(8,128)}, u32[]{:S(2)}, u32[]{:S(2)}) collective-permute-start(f32[1024,512]{1,0:T(8,128)} %experts_forward.3), channel_id=1, source_target_pairs={{0,8},{8,0},{1,9},{9,1},{2,10},{10,2},{3,11},{11,3},{4,12},{12,4},... | collective-permute-start | bytes 6291464 | tf_op jit(solution)/shard_map/ppermute | solution.py:636
  81.3 47.0 %copy-start.10 = (bf16[1024,512]{1,0:T(8,128)(2,1)S(1)}, bf16[1024,512]{1,0:T(8,128)(2,1)}, u32[]{:S(2)}) copy-start(bf16[1024,512]{1,0:T(8,128)(2,1)} %copy-done.9) | copy-start | bytes 3145732
  132.8 14.4 %copy-start.3 = (bf16[1024,512]{1,0:T(8,128)(2,1)}, bf16[1024,512]{1,0:T(8,128)(2,1)S(1)}, u32[]{:S(2)}) copy-start(bf16[1024,512]{1,0:T(8,128)(2,1)S(1)} %add_convert_fusion.5) | copy-start | bytes 3145732
  132.8 13.3 %copy-start.2 = (bf16[1024,512]{1,0:T(8,128)(2,1)S(1)}, bf16[1024,512]{1,0:T(8,128)(2,1)}, u32[]{:S(2)}) copy-start(bf16[1024,512]{1,0:T(8,128)(2,1)} %param.9) | copy-start | bytes 3145732
  143.2 30.6 %copy-start.19 = (f32[144,128]{1,0:T(8,128)}, f32[144,128]{1,0:T(8,128)S(1)}, u32[]{:S(2)}) copy-start(f32[144,128]{1,0:T(8,128)S(1)} %pad_bitcast_fusion.2.gates) | copy-start | bytes 221188
  146.0 303.5 %all-gather.16.cloned.1.call-start = ((), (), s32[]{:S(2)}) async-start(), calls=%async_computation.5 | async-start | bytes 18874368 | tf_op jit(solution)/shard_map/all_gather | solution.py:639
  147.2 23.7 %collective-permute-start.4 = (bf16[1024,4,128]{2,1,0:T(4,128)(2,1)}, bf16[1024,4,128]{2,1,0:T(4,128)(2,1)}, u32[]{:S(2)}, u32[]{:S(2)}) collective-permute-start(bf16[1024,4,128]{2,1,0:T(4,128)(2,1)} %reshape.334.refs_2_.a), channel_id=1, source_target_pairs={{0,8},{8,0},{1,9},{9,1},{2,10},{10,2},{3,11},{11,3},{4,12},{12,4},... | collective-permute-start | bytes 3145736 | tf_op jit(solution)/shard_map/ppermute | solution.py:636
  147.5 26.4 %copy-start.7 = (bf16[1024,4,128]{2,1,0:T(4,128)(2,1)S(1)}, bf16[1024,4,128]{2,1,0:T(4,128)(2,1)}, u32[]{:S(2)}) copy-start(bf16[1024,4,128]{2,1,0:T(4,128)(2,1)} %reshape.332.refs_0_.a) | copy-start | bytes 3145732
  173.9 275.6 %all-gather.14.cloned.1.call-start = ((), (), s32[]{:S(2)}) async-start(), calls=%async_computation.4 | async-start | bytes 18874368 | tf_op jit(solution)/shard_map/all_gather | solution.py:639
  173.9 22.7 %collective-permute-start.3 = (bf16[1024,4,128]{2,1,0:T(4,128)(2,1)S(1)}, bf16[1024,4,128]{2,1,0:T(4,128)(2,1)}, u32[]{:S(2)}, u32[]{:S(2)}) collective-permute-start(bf16[1024,4,128]{2,1,0:T(4,128)(2,1)S(1)} %copy-done.7), channel_id=1, source_target_pairs={{0,8},{8,0},{1,9},{9,1},{2,10},{10,2},{3,11},{11,3},{4,12},{12,4},... | collective-permute-start | bytes 3145736 | tf_op jit(solution)/shard_map/ppermute | solution.py:636
  199.5 399.9 %all-gather.8.cloned.1.call-start = ((), (), s32[]{:S(2)}) async-start(), calls=%async_computation.1 | async-start | bytes 9437184 | tf_op jit(solution)/shard_map/all_gather | solution.py:639
  200.1 399.3 %all-gather.10.cloned.1.call-start = ((), (), s32[]{:S(2)}) async-start(), calls=%async_computation.2 | async-start | bytes 9437184 | tf_op jit(solution)/shard_map/all_gather | solution.py:639
  200.7 398.8 %all-gather.12.cloned.1.call-start = ((), (), s32[]{:S(2)}) async-start(), calls=%async_computation.3 | async-start | bytes 18874368 | tf_op jit(solution)/shard_map/all_gather | solution.py:639
  253.4 46.5 %collective-permute-start.5 = (f32[1024,512]{1,0:T(8,128)}, f32[1024,512]{1,0:T(8,128)S(1)}, u32[]{:S(2)}, u32[]{:S(2)}) collective-permute-start(f32[1024,512]{1,0:T(8,128)} %get-tuple-element.65), channel_id=1, source_target_pairs={{0,8},{8,0},{1,9},{9,1},{2,10},{10,2},{3,11},{11,3},{4,12},{12,4},... | collective-permute-start | bytes 6291464 | tf_op jit(solution)/shard_map/ppermute | solution.py:636
  304.7 25.0 %copy-start.5 = (bf16[1024,512]{1,0:T(8,128)(2,1)}, bf16[1024,512]{1,0:T(8,128)(2,1)S(1)}, u32[]{:S(2)}) copy-start(bf16[1024,512]{1,0:T(8,128)(2,1)S(1)} %add_convert_fusion.3) | copy-start | bytes 3145732
  305.0 20.8 %copy-start.8 = (bf16[1024,4,128]{2,1,0:T(4,128)(2,1)}, bf16[1024,4,128]{2,1,0:T(4,128)(2,1)S(1)}, u32[]{:S(2)}) copy-start(bf16[1024,4,128]{2,1,0:T(4,128)(2,1)S(1)} %reshape.335.refs_2_.a) | copy-start | bytes 3145732
  305.0 20.8 %collective-permute-start.6 = (bf16[1024,4,128]{2,1,0:T(4,128)(2,1)S(1)}, bf16[1024,4,128]{2,1,0:T(4,128)(2,1)S(1)}, u32[]{:S(2)}, u32[]{:S(2)}) collective-permute-start(bf16[1024,4,128]{2,1,0:T(4,128)(2,1)S(1)} %reshape.335.refs_2_.a), channel_id=1, source_target_pairs={{0,8},{8,0},{1,9},{9,1},{2,10},{10,2},{3,11},{11,3},{4,12},{12,4},... | collective-permute-start | bytes 3145736 | tf_op jit(solution)/shard_map/ppermute | solution.py:636
  329.7 461.7 %all-reduce.12.cloned.1.call-start = ((), (), s32[]{:S(2)}) async-start(), calls=%async_computation | async-start | bytes 2097152 | tf_op jit(solution)/shard_map/psum | solution.py:740
  374.5 58.3 %copy-start.30 = (s32[64]{0:T(128)S(1)}, s32[64]{0:T(128)}, u32[]{:S(2)}) copy-start(s32[64]{0:T(128)} %copy-done.29) | copy-start | bytes 772
  434.6 14.9 %copy-start.24 = (s32[1,16]{1,0:T(1,128)}, s32[1,16]{1,0:T(1,128)S(1)}, u32[]{:S(2)}) copy-start(s32[1,16]{1,0:T(1,128)S(1)} %get-tuple-element.165) | copy-start | bytes 196
  434.6 14.9 %copy-start.25 = (s32[1,16]{1,0:T(1,128)}, s32[1,16]{1,0:T(1,128)S(1)}, u32[]{:S(2)}) copy-start(s32[1,16]{1,0:T(1,128)S(1)} %get-tuple-element.164) | copy-start | bytes 196
  435.3 14.2 %copy-start.28 = (s32[1,16]{1,0:T(1,128)}, s32[1,16]{1,0:T(1,128)S(1)}, u32[]{:S(2)}) copy-start(s32[1,16]{1,0:T(1,128)S(1)} %get-tuple-element.161) | copy-start | bytes 196
  449.5 56.1 %copy-start.26 = (s32[17,1]{0,1:T(1,128)S(1)}, s32[17,1]{0,1:T(1,128)}, u32[]{:S(2)}) copy-start(s32[17,1]{0,1:T(1,128)} %get-tuple-element.183) | copy-start | bytes 208
  449.5 56.4 %copy-start.27 = (s32[16]{0:T(128)S(1)}, s32[16]{0:T(128)}, u32[]{:S(2)}) copy-start(s32[16]{0:T(128)} %get-tuple-element.80) | copy-start | bytes 196
  449.5 56.7 %copy-start.23 = (s32[16]{0:T(128)S(1)}, s32[16]{0:T(128)}, u32[]{:S(2)}) copy-start(s32[16]{0:T(128)} %copy-done.22) | copy-start | bytes 196
  498.6 98.5 %collective-permute-start.9 = (bf16[16,192,512]{2,1,0:T(8,128)(2,1)}, bf16[16,192,512]{2,1,0:T(8,128)(2,1)}, u32[]{:S(2)}, u32[]{:S(2)}) collective-permute-start(bf16[16,192,512]{2,1,0:T(8,128)(2,1)} %get-tuple-element.77), channel_id=1, source_target_pairs={{0,1},{1,0},{2,3},{3,2},{4,5},{5,4},{6,7},{7,6},{8,9},{9,8},{10,11... | collective-permute-start | bytes 9437192 | tf_op jit(solution)/shard_map/ppermute | solution.py:642
  498.6 100.8 %collective-permute-start.15 = (bf16[16,192,512]{2,1,0:T(8,128)(2,1)}, bf16[16,192,512]{2,1,0:T(8,128)(2,1)}, u32[]{:S(2)}, u32[]{:S(2)}) collective-permute-start(bf16[16,192,512]{2,1,0:T(8,128)(2,1)} %get-tuple-element.77), channel_id=1, source_target_pairs={{0,2},{1,5},{2,0},{3,7},{4,6},{5,1},{6,4},{7,3},{8,10},{9,13},{10,... | collective-permute-start | bytes 9437192 | tf_op jit(solution)/shard_map/ppermute | solution.py:642
  503.2 49.2 %collective-permute-start.7 = (f32[1024,512]{1,0:T(8,128)}, f32[1024,512]{1,0:T(8,128)}, u32[]{:S(2)}, u32[]{:S(2)}) collective-permute-start(f32[1024,512]{1,0:T(8,128)} %get-tuple-element.70), channel_id=1, source_target_pairs={{0,8},{8,0},{1,9},{9,1},{2,10},{10,2},{3,11},{11,3},{4,12},{12,4},... | collective-permute-start | bytes 6291464 | tf_op jit(solution)/shard_map/ppermute | solution.py:636
  505.6 91.5 %collective-permute-start.8 = (f32[1024,512]{1,0:T(8,128)}, f32[1024,512]{1,0:T(8,128)}, u32[]{:S(2)}, u32[]{:S(2)}) collective-permute-start(f32[1024,512]{1,0:T(8,128)} %get-tuple-element.72), channel_id=1, source_target_pairs={{0,8},{8,0},{1,9},{9,1},{2,10},{10,2},{3,11},{11,3},{4,12},{12,4},... | collective-permute-start | bytes 6291464 | tf_op jit(solution)/shard_map/ppermute | solution.py:636
  507.6 149.2 %collective-permute-start.10 = (bf16[16,192,512]{2,1,0:T(8,128)(2,1)}, bf16[16,192,512]{2,1,0:T(8,128)(2,1)}, u32[]{:S(2)}, u32[]{:S(2)}) collective-permute-start(bf16[16,192,512]{2,1,0:T(8,128)(2,1)} %get-tuple-element.78), channel_id=1, source_target_pairs={{0,1},{1,0},{2,3},{3,2},{4,5},{5,4},{6,7},{7,6},{8,9},{9,8},{10,11... | collective-permute-start | bytes 9437192 | tf_op jit(solution)/shard_map/ppermute | solution.py:642
  552.4 104.9 %collective-permute-start.17 = (bf16[16,192,512]{2,1,0:T(8,128)(2,1)}, bf16[16,192,512]{2,1,0:T(8,128)(2,1)}, u32[]{:S(2)}, u32[]{:S(2)}) collective-permute-start(bf16[16,192,512]{2,1,0:T(8,128)(2,1)} %get-tuple-element.78), channel_id=1, source_target_pairs={{0,2},{1,5},{2,0},{3,7},{4,6},{5,1},{6,4},{7,3},{8,10},{9,13},{10,... | collective-permute-start | bytes 9437192 | tf_op jit(solution)/shard_map/ppermute | solution.py:642
  597.1 59.8 %collective-permute-start.11 = (bf16[16,192,512]{2,1,0:T(8,128)(2,1)}, bf16[16,192,512]{2,1,0:T(8,128)(2,1)}, u32[]{:S(2)}, u32[]{:S(2)}) collective-permute-start(bf16[16,192,512]{2,1,0:T(8,128)(2,1)} %get-tuple-element.79), channel_id=1, source_target_pairs={{0,1},{1,0},{2,3},{3,2},{4,5},{5,4},{6,7},{7,6},{8,9},{9,8},{10,11... | collective-permute-start | bytes 9437192 | tf_op jit(solution)/shard_map/ppermute | solution.py:642
  597.1 60.3 %collective-permute-start.19 = (bf16[16,192,512]{2,1,0:T(8,128)(2,1)}, bf16[16,192,512]{2,1,0:T(8,128)(2,1)}, u32[]{:S(2)}, u32[]{:S(2)}) collective-permute-start(bf16[16,192,512]{2,1,0:T(8,128)(2,1)} %get-tuple-element.79), channel_id=1, source_target_pairs={{0,2},{1,5},{2,0},{3,7},{4,6},{5,1},{6,4},{7,3},{8,10},{9,13},{10,... | collective-permute-start | bytes 9437192 | tf_op jit(solution)/shard_map/ppermute | solution.py:642
  599.4 58.4 %collective-permute-start.16 = (bf16[16,192,512]{2,1,0:T(8,128)(2,1)}, bf16[16,192,512]{2,1,0:T(8,128)(2,1)}, u32[]{:S(2)}, u32[]{:S(2)}) collective-permute-start(bf16[16,192,512]{2,1,0:T(8,128)(2,1)} %collective-permute-done.15.a), channel_id=1, source_target_pairs={{0,1},{1,0},{2,3},{3,2},{4,5},{5,4},{6,7},{7,6},{8,9},{9,8},{10,11... | collective-permute-start | bytes 9437192 | tf_op jit(solution)/shard_map/ppermute | solution.py:642
  656.8 60.1 %collective-permute-start.21 = (bf16[16,192,512]{2,1,0:T(8,128)(2,1)}, bf16[16,192,512]{2,1,0:T(8,128)(2,1)}, u32[]{:S(2)}, u32[]{:S(2)}) collective-permute-start(bf16[16,192,512]{2,1,0:T(8,128)(2,1)} %get-tuple-element.90), channel_id=1, source_target_pairs={{0,1},{1,0},{2,3},{3,2},{4,5},{5,4},{6,7},{7,6},{8,9},{9,8},{10,11... | collective-permute-start | bytes 9437192 | tf_op jit(solution)/shard_map/ppermute | solution.py:642
  656.9 60.1 %collective-permute-start.22 = (bf16[16,192,512]{2,1,0:T(8,128)(2,1)}, bf16[16,192,512]{2,1,0:T(8,128)(2,1)}, u32[]{:S(2)}, u32[]{:S(2)}) collective-permute-start(bf16[16,192,512]{2,1,0:T(8,128)(2,1)} %get-tuple-element.91), channel_id=1, source_target_pairs={{0,1},{1,0},{2,3},{3,2},{4,5},{5,4},{6,7},{7,6},{8,9},{9,8},{10,11... | collective-permute-start | bytes 9437192 | tf_op jit(solution)/shard_map/ppermute | solution.py:642
  657.3 60.2 %collective-permute-start.23 = (bf16[16,192,512]{2,1,0:T(8,128)(2,1)}, bf16[16,192,512]{2,1,0:T(8,128)(2,1)}, u32[]{:S(2)}, u32[]{:S(2)}) collective-permute-start(bf16[16,192,512]{2,1,0:T(8,128)(2,1)} %get-tuple-element.92), channel_id=1, source_target_pairs={{0,1},{1,0},{2,3},{3,2},{4,5},{5,4},{6,7},{7,6},{8,9},{9,8},{10,11... | collective-permute-start | bytes 9437192 | tf_op jit(solution)/shard_map/ppermute | solution.py:642
  657.4 152.6 %collective-permute-start.18 = (bf16[16,192,512]{2,1,0:T(8,128)(2,1)}, bf16[16,192,512]{2,1,0:T(8,128)(2,1)}, u32[]{:S(2)}, u32[]{:S(2)}) collective-permute-start(bf16[16,192,512]{2,1,0:T(8,128)(2,1)} %collective-permute-done.17.b), channel_id=1, source_target_pairs={{0,1},{1,0},{2,3},{3,2},{4,5},{5,4},{6,7},{7,6},{8,9},{9,8},{10,11... | collective-permute-start | bytes 9437192 | tf_op jit(solution)/shard_map/ppermute | solution.py:642
  657.9 152.1 %collective-permute-start.20 = (bf16[16,192,512]{2,1,0:T(8,128)(2,1)}, bf16[16,192,512]{2,1,0:T(8,128)(2,1)}, u32[]{:S(2)}, u32[]{:S(2)}) collective-permute-start(bf16[16,192,512]{2,1,0:T(8,128)(2,1)} %collective-permute-done.19.c), channel_id=1, source_target_pairs={{0,1},{1,0},{2,3},{3,2},{4,5},{5,4},{6,7},{7,6},{8,9},{9,8},{10,11... | collective-permute-start | bytes 9437192 | tf_op jit(solution)/shard_map/ppermute | solution.py:642
  657.9 59.6 %copy-start.15 = (bf16[1024,512]{1,0:T(8,128)(2,1)S(1)}, bf16[1024,512]{1,0:T(8,128)(2,1)}, u32[]{:S(2)}) copy-start(bf16[1024,512]{1,0:T(8,128)(2,1)} %copy-done.14) | copy-start | bytes 3145732
  716.9 101.2 %collective-permute-start.12 = (bf16[16,192,512]{2,1,0:T(8,128)(2,1)}, bf16[16,192,512]{2,1,0:T(8,128)(2,1)}, u32[]{:S(2)}, u32[]{:S(2)}) collective-permute-start(bf16[16,192,512]{2,1,0:T(8,128)(2,1)} %get-tuple-element.87), channel_id=1, source_target_pairs={{0,1},{1,0},{2,3},{3,2},{4,5},{5,4},{6,7},{7,6},{8,9},{9,8},{10,11... | collective-permute-start | bytes 9437192 | tf_op jit(solution)/shard_map/ppermute | solution.py:642
  717.0 101.2 %collective-permute-start.13 = (bf16[16,192,512]{2,1,0:T(8,128)(2,1)}, bf16[16,192,512]{2,1,0:T(8,128)(2,1)}, u32[]{:S(2)}, u32[]{:S(2)}) collective-permute-start(bf16[16,192,512]{2,1,0:T(8,128)(2,1)} %get-tuple-element.88), channel_id=1, source_target_pairs={{0,1},{1,0},{2,3},{3,2},{4,5},{5,4},{6,7},{7,6},{8,9},{9,8},{10,11... | collective-permute-start | bytes 9437192 | tf_op jit(solution)/shard_map/ppermute | solution.py:642
  717.5 100.7 %collective-permute-start.14 = (bf16[16,192,512]{2,1,0:T(8,128)(2,1)}, bf16[16,192,512]{2,1,0:T(8,128)(2,1)}, u32[]{:S(2)}, u32[]{:S(2)}) collective-permute-start(bf16[16,192,512]{2,1,0:T(8,128)(2,1)} %get-tuple-element.89), channel_id=1, source_target_pairs={{0,1},{1,0},{2,3},{3,2},{4,5},{5,4},{6,7},{7,6},{8,9},{9,8},{10,11... | collective-permute-start | bytes 9437192 | tf_op jit(solution)/shard_map/ppermute | solution.py:642
  (17 other events, 61.7 us)
Sparse Core Ops, SparseCore 0:
  146.1 25.6 all-gather.17
  174.0 85.8 all-gather.15
  262.3 85.9 all-gather.13
  350.6 50.5 all-gather.7
  403.4 50.5 all-gather.9
  455.7 103.2 all-gather.11
Sparse Core Ops, SparseCore 1:
  725.2 66.1 all-reduce.11

commit v13 on v12

--- a/solution.py
+++ b/solution.py
@@ -56,7 +56,7 @@
 
 def add_rows(acc, vals_ref, idx, row, tile, pitch, width):
     for b in range(0, tile, BATCH):
-        at = [pl.multiple_of(idx[row + b + r], 4) for r in range(BATCH)]
+        at = [idx[row + b + r] * width for r in range(BATCH)]
         vals = [acc[pl.ds(at[r], width), :] + vals_ref[pl.ds((b + r) * pitch, width), :] for r in range(BATCH)]
         for r in reversed(range(BATCH)):
             acc[pl.ds(at[r], width), :] = vals[r]
@@ -72,17 +72,6 @@
     pair = pltpu.roll(pair, lax.rem(LANES - skip, LANES), 1)
     lane = lax.broadcasted_iota(jnp.int32, (1, LANES), 1)
     return spread_column(jnp.where(lane < LANES - skip, pair[:1], pair[1:]))
-
-
-def widen(src, dst, pitch, halves, tok):
-    step = 32
-
-    def one(q, carry):
-        for r in range(step):
-            dst[pl.ds((q * step + r) * pitch, pitch), :] = src[q * step + r].astype(jnp.float32)
-        return carry
-
-    lax.fori_loop(halves[0] * tok // step, (halves[-1] + 1) * tok // step, one, 0)
 
 
 def write_sums(acc, outs, tok, parts, pitch, halves):
@@ -148,13 +137,13 @@
 def token_body(runs, idx, gates, *refs, layer, tok, parts, tile, halves, backward):
     n_in = 4 if backward else 2
     sources, weights, outs, refs = refs[:n_in], refs[n_in:n_in + 3], refs[n_in + 3:n_in + 3 + len(halves)], refs[n_in + 3 + len(halves):]
-    narrow, wide, rows, vt, acc, mid, wbuf, sem, wsem = refs
+    slabs, rows, vt, acc, mid, wbuf, sem, wsem = refs
     ff = weights[0].shape[2]
     width = parts * n_in // 2
     pitch = width + 1
 
     def prepare():
-        copies = [pltpu.make_async_copy(src, narrow.at[pl.ds(k % 2 * tok, tok), pl.ds(k // 2 * parts, parts)], sem.at[k])
+        copies = [pltpu.make_async_copy(src, slabs.at[pl.ds(k % 2 * tok, tok), pl.ds(k // 2 * parts, parts)], sem.at[k])
                   for k, src in enumerate(sources) if k % 2 in halves]
         for c in copies:
             c.start()
@@ -162,7 +151,6 @@
             clear(ref)
         for c in copies:
             c.wait()
-        widen(narrow, wide, width, halves, tok)
 
     def column(k):
         return rows[pl.ds(k, tile, stride=pitch), :]
@@ -180,7 +168,7 @@
             dh = nt_dot(wbuf[slot, 2 * ff:], c)
         add_rows(acc, vt, idx, done, tile, parts + 1, parts)
         for r in range(tile):
-            rows[pl.ds(pitch * r, width), :] = wide[pl.ds(pl.multiple_of(idx[row + r], width), width), :]
+            rows[pl.ds(pitch * r, width), :] = slabs[idx[row + r]].astype(jnp.float32)
         live = lax.broadcasted_iota(jnp.int32, (tile, LANES), 0) < n2
         gate = tile_gates(gates, row2)[:tile]
         for k in range(parts):
@@ -196,7 +184,7 @@
             mid[...] = (act * b).astype(jnp.bfloat16)
 
     run_tiles(step, weights, wbuf, wsem, runs, tile, layer, prepare)
-    write_sums(acc, outs, tok, parts, width, halves)
+    write_sums(acc, outs, tok, parts, parts, halves)
 
 
 def token_kernel(layer, runs, table, slabs, weights, halves=(0, 1)):
@@ -217,9 +205,9 @@
             grid=(1,),
             in_specs=[pl.BlockSpec(gates.shape, lambda i, *_: (0, 0))] + [any_spec] * (len(slabs) + 3),
             out_specs=[rows_spec] * len(halves),
-            scratch_shapes=[pltpu.VMEM((2 * tok, width, LANES), jnp.bfloat16), pltpu.VMEM((2 * tok * width, LANES), jnp.float32),
+            scratch_shapes=[pltpu.VMEM((2 * tok, width, LANES), jnp.bfloat16),
                             pltpu.VMEM((tile_rows, LANES), jnp.float32), pltpu.VMEM((tile_rows, LANES), jnp.float32),
-                            pltpu.VMEM((2 * tok * width, LANES), jnp.float32),
+                            pltpu.VMEM((2 * tok * parts, LANES), jnp.float32),
                             pltpu.VMEM((2 * ff if backward else ff, tile), jnp.bfloat16),
                             pltpu.VMEM((SLOTS, 3 * ff, d_model), jnp.bfloat16),
                             pltpu.SemaphoreType.DMA((len(slabs),)), pltpu.SemaphoreType.DMA((SLOTS,))],
@@ -504,47 +492,50 @@
     return outs[:3], outs[3:]
 
 
-def merge_body(exps, a, b, c, f0, f1, f2, o0, o1, o2, buf, in_sem, out_sem, *, layer, n_exp):
-    halves, wholes = (a, b, c), (o0, o1, o2)
-
-    def arrive(k, q):
-        return pltpu.make_async_copy(halves[k].at[q], buf.at[k, q], in_sem.at[k, q])
-
-    def leave(k, q):
-        return pltpu.make_async_copy(buf.at[k, q], wholes[k].at[layer, exps[q]], out_sem)
-
-    def each(act):
+def merge_body(exps, *refs, layers, n_exp):
+    n_in = 3 * len(layers)
+    wholes, (buf, in_sem, out_sem) = refs[n_in + 3:n_in + 6], refs[n_in + 6:]
+
+    def arrive(g, k, q):
+        return pltpu.make_async_copy(refs[3 * g + k].at[q], buf.at[g, k, q], in_sem.at[g, k, q])
+
+    def leave(g, k, q):
+        return pltpu.make_async_copy(buf.at[g, k, q], wholes[k].at[layers[g], exps[g * n_exp + q]], out_sem)
+
+    def each(g, act):
         def one(q, carry):
             for k in range(3):
-                act(k, q)
+                act(g, k, q)
             return carry
 
         lax.fori_loop(0, n_exp, one, 0)
 
-    def pass_on(k, q):
-        arrive(k, q).wait()
-        leave(k, q).start()
-
-    each(lambda k, q: arrive(k, q).start())
-    each(pass_on)
-    each(lambda k, q: leave(k, q).wait())
-
-
-def merge_half(layer, exps, half, full):
-    n_exp, ff, d_model = half[0].shape
+    def pass_on(*at):
+        arrive(*at).wait()
+        leave(*at).start()
+
+    for act in (lambda *at: arrive(*at).start(), pass_on, lambda *at: leave(*at).wait()):
+        for g in range(len(layers)):
+            each(g, act)
+
+
+def merge_lists(groups, full):
+    layers, arrays, names = zip(*groups)
+    n_exp, ff, d_model = arrays[0][0].shape
+    flat = [x for group in arrays for x in group]
     any_spec = pl.BlockSpec(memory_space=pl.ANY)
     return pl.pallas_call(
-        functools.partial(merge_body, layer=layer, n_exp=n_exp),
+        functools.partial(merge_body, layers=layers, n_exp=n_exp),
         grid_spec=pltpu.PrefetchScalarGridSpec(
-            num_scalar_prefetch=1, grid=(1,), in_specs=[any_spec] * 6, out_specs=[any_spec] * 3,
-            scratch_shapes=[pltpu.VMEM((3, n_exp, ff, d_model), jnp.bfloat16), pltpu.SemaphoreType.DMA((3, n_exp)),
-                            pltpu.SemaphoreType.DMA]),
+            num_scalar_prefetch=1, grid=(1,), in_specs=[any_spec] * (len(flat) + 3), out_specs=[any_spec] * 3,
+            scratch_shapes=[pltpu.VMEM((len(groups), 3, n_exp, ff, d_model), jnp.bfloat16),
+                            pltpu.SemaphoreType.DMA((len(groups), 3, n_exp)), pltpu.SemaphoreType.DMA]),
         out_shape=[jax.ShapeDtypeStruct(x.shape, x.dtype) for x in full],
-        input_output_aliases={4: 0, 5: 1, 6: 2},
-        compiler_params=pltpu.CompilerParams(dimension_semantics=("arbitrary",), vmem_limit_bytes=VMEM_LIMIT),
-        cost_estimate=pl.CostEstimate(flops=10**9, bytes_accessed=6 * n_exp * ff * d_model * 2, transcendentals=0),
-        name="merge_half",
-    )(exps, *half, *full)
+        input_output_aliases={len(flat) + 1 + k: k for k in range(3)},
+        compiler_params=pltpu.CompilerParams(vmem_limit_bytes=VMEM_LIMIT),
+        cost_estimate=pl.CostEstimate(flops=10**9, bytes_accessed=4 * len(flat) * flat[0].size, transcendentals=0),
+        name="merge_lists",
+    )(jnp.concatenate(names), *flat, *full)
 
 
 def join_body(a, b, out, sem):
@@ -660,7 +651,7 @@
         def add_tables(pair):
             run, token, gate, bounds = route_tables(pair[0].astype(jnp.int32), pair[1], ep_id, n_local)
             runs.append(run)
-            tables.append([(token * parts, gate), (token * (2 * parts), gate)])
+            tables.append((token, gate))
             spot = dp_id * (2 * tok) + token
             first = jnp.concatenate([spot.reshape(-1, LANES), jnp.pad(bounds.reshape(1, LANES), ((0, 7), (0, 0)))])
             packed.append(jnp.stack([first.astype(jnp.float32), jnp.pad(gate, ((0, 8), (0, 0)))]))
@@ -679,9 +670,9 @@
                 add_tables(after(both[:, layer], u_slabs[layer]))
             xs.append(x_in)
             if layer < top:
-                other, = token_kernel(layer, runs[layer][1], tables[layer][0], (u_slabs[layer], u_others[layer]), weights, (1,))
+                other, = token_kernel(layer, runs[layer][1], tables[layer], (u_slabs[layer], u_others[layer]), weights, (1,))
                 sent = swap(other)
-                own, = token_kernel(layer, runs[layer][0], tables[layer][0], (after(u_slabs[layer], other), u_others[layer]),
+                own, = token_kernel(layer, runs[layer][0], tables[layer], (after(u_slabs[layer], other), u_others[layer]),
                                     weights, (0,))
                 x_in = (u.astype(jnp.float32) + own + sent).astype(jnp.bfloat16)
 
@@ -706,11 +697,11 @@
             both_u = [u_slabs[layer], u_others[layer]]
             u_rows = spread(both_u if layer < top else [join_rows(*both_u)])
             slabs = (u_slabs[layer], u_others[layer], d_slab, d_other)
-            own, other = token_kernel(layer, runs[layer][2], tables[layer][1], slabs, weights)
+            own, other = token_kernel(layer, runs[layer][2], tables[layer], slabs, weights)
             d_u = (d_y.astype(jnp.float32) + own + swap(other)).astype(jnp.bfloat16)
             last = other
             if layer == top:
-                y_own, last = token_kernel(top, runs[top][2], tables[top][0], (after(u_slabs[top], other), u_others[top]), weights)
+                y_own, last = token_kernel(top, runs[top][2], tables[top], (after(u_slabs[top], other), u_others[top]), weights)
             d_mix[layer] = jnp.einsum('td,te->de', xs[layer], d_u, preferred_element_type=jnp.float32).astype(jnp.bfloat16)
             d_y = (d_u.astype(jnp.float32)
                    + jnp.einsum('te,de->td', d_u, w_mix[layer], preferred_element_type=jnp.float32)).astype(jnp.bfloat16)
@@ -735,8 +726,7 @@
                 d_rows = spread([join_rows(d_slab, d_other)])
                 if layer == top:
                     layer_out = (u.astype(jnp.float32) + y_own + swap(after(last, d_other))).astype(jnp.bfloat16)
-        for layer, got, names in arrived:
-            full = merge_half(layer, names, got, full)
+        full = merge_lists(arrived[-1:], merge_lists(arrived[:-1], full))
         d_mix = lax.psum(jnp.stack(d_mix), ('dp', 'ep'))
         return (layer_out, d_y, d_mix, jnp.swapaxes(full[0], 2, 3), jnp.swapaxes(full[1], 2, 3), full[2])
 

time: 835 us -> 879 us (1.053)
  waiting for transfers between devices: 278 us -> 326 us
    ppermute x15, waiting for transfers between devices: 0.04 us -> 100 us  [trade(): return [lax.ppermute(y, 'dp', pairs) for y in x]]
    ppermute x9, waiting for transfers between devices: 217 us -> 129 us  [swap(): return lax.ppermute(x, 'ep', ep_pairs)]
    all_gather x5, waiting for transfers between devices: 0.04 us -> 36.2 us  [spread(): return [lax.all_gather(y, 'dp', axis=0, tiled=True) for y in x]]
    pallas_call x4 -> x2, Pallas kernels: 32.7 us -> 28.9 us  [merge_lists(): pl.pallas_call(functools.partial(merge_body, layers=layers, n_exp=n_exp),...]
  transfers between devices with their start and end apart: 31 -> 31, of which waited for: 10 -> 12; matrix products, arithmetic and copies ran while one was open for 5% -> 5% of each run, Pallas kernels for 48% -> 46%
where the time goes in v13:
time: 879 us; the launch traced here: 878 us
  Pallas kernels  450 us (51%)
  waiting for transfers between devices  326 us (37%)
  other arithmetic  41.4 us (5%)
  starting transfers between devices  19.2 us (2%)
  between operations  16.6 us (2%)
  local copies, waits for them, and re-layouts  14.7 us (2%)
  matrix products  10.5 us (1%)
    pallas_call x5, Pallas kernels, token_kernel(): pl.pallas_call(functools.partial(token_body, layer=layer, tok=tok, parts=...  235 us
    pallas_call x3, Pallas kernels, weight_grads(): pl.pallas_call(functools.partial(weight_grad_body, parts=parts, n_exp=n_e...  166 us
    ppermute x9, waiting for transfers between devices, swap(): return lax.ppermute(x, 'ep', ep_pairs)  129 us
    ppermute x15, waiting for transfers between devices, trade(): return [lax.ppermute(y, 'dp', pairs) for y in x]  100 us
    psum x1, waiting for transfers between devices, device_body(): d_mix = lax.psum(jnp.stack(d_mix), ('dp', 'ep'))  59.5 us
    all_gather x5, waiting for transfers between devices, spread(): return [lax.all_gather(y, 'dp', axis=0, tiled=True) for y in x]  36.2 us
    pallas_call x2, Pallas kernels, merge_lists(): pl.pallas_call(functools.partial(merge_body, layers=layers, n_exp=n_exp),...  28.9 us
  transfers between devices with their start and end apart: 31, of which 12 were waited for; matrix products, arithmetic and copies ran while one was open for 5% of the time, Pallas kernels for 46%

profile of v13, /device:TPU:0, one launch (start us, length us, event | category | flops | bytes accessed | tf_op | source)
XLA Modules:
  0.0 878.2 jit_solution(4618441508125408790)
XLA Ops:
  8.9 2.4 add_convert_fusion.7
  12.3 3.3 collective-permute-start
  15.6 4.3 collective-permute-done
  20.1 1.1 convert_reduce_fusion
  22.6 6.4 sort.30
  29.0 1.9 fusion.43
  31.7 9.9 %collective-permute-done.1.refs_1_ = bf16[1024,4,128]{2,1,0:T(4,128)(2,1)S(1)} collective-permute-done((bf16[1024,4,128]{2,1,0:T(4,128)(2,1)S(1)}, bf16[1024,4,128]{2,1,0:T(4,128)(2,1)S(1)}, u32[]{:S(2)}, u32[]{:S(2)}) %collective-permute-start.1) | collective-permute-done | bytes 1048608 | tf_op jit(solution)/shard_map/ppermute | solution.py:627
  42.5 39.4 %experts_forward.3 = f32[1024,512]{1,0:T(8,128)} custom-call(s32[128]{0:T(128)} %get-tuple-element.163.runs, s32[18432]{0:T(1024)} %get-tuple-element.140.idx, f32[144,128]{1,0:T(8,128)} %copy-done.13, bf16[1024,4,128]{2,1,0:T(4,128)(2,1)} %copy-done, bf16[1024,4,128]{2,1,0:T(4,128)(2,1)} %copy-done.1, bf16[2,64,192,512]{3,2,1,0:T(8,128)(2,1)} %bitcast.137, ...), custom_call_target="tpu_custom_call" | custom-call | flops 19327352832 | bytes 37748736 | tf_op jit(solution)/shard_map/experts_forward/pallas_call | solution.py:201
  82.1 39.7 %experts_forward.4 = f32[1024,512]{1,0:T(8,128)} custom-call(s32[128]{0:T(128)} %get-tuple-element.164.runs, s32[18432]{0:T(1024)} %get-tuple-element.140.idx, f32[144,128]{1,0:T(8,128)} %copy-done.13, bf16[1024,4,128]{2,1,0:T(4,128)(2,1)} %copy-done, bf16[1024,4,128]{2,1,0:T(4,128)(2,1)} %copy-done.1, bf16[2,64,192,512]{3,2,1,0:T(8,128)(2,1)} %bitcast.138, ...), custom_call_target="tpu_custom_call" | custom-call | flops 19327352832 | bytes 37748736 | tf_op jit(solution)/shard_map/experts_forward/pallas_call | solution.py:201
  121.8 7.3 collective-permute-done.2
  129.1 2.8 add_convert_fusion.6
  133.6 1.1 reshape.332.refs_0_.a
  136.8 6.4 sort.31
  144.1 1.9 fusion.44
  146.8 1.1 reshape.334.refs_2_.a
  148.3 23.5 %collective-permute-done.4.refs_3_.b = bf16[1024,4,128]{2,1,0:T(4,128)(2,1)} collective-permute-done((bf16[1024,4,128]{2,1,0:T(4,128)(2,1)}, bf16[1024,4,128]{2,1,0:T(4,128)(2,1)}, u32[]{:S(2)}, u32[]{:S(2)}) %collective-permute-start.4) | collective-permute-done | bytes 1048608 | tf_op jit(solution)/shard_map/ppermute | solution.py:627
  171.8 2.9 join_rows.5
  175.4 22.1 %collective-permute-done.3.refs_1_.b = bf16[1024,4,128]{2,1,0:T(4,128)(2,1)} collective-permute-done((bf16[1024,4,128]{2,1,0:T(4,128)(2,1)S(1)}, bf16[1024,4,128]{2,1,0:T(4,128)(2,1)}, u32[]{:S(2)}, u32[]{:S(2)}) %collective-permute-start.3) | collective-permute-done | bytes 1048608 | tf_op jit(solution)/shard_map/ppermute | solution.py:627
  197.6 2.9 join_rows.4
  201.7 52.0 %experts_backward.2 = (f32[1024,512]{1,0:T(8,128)}, f32[1024,512]{1,0:T(8,128)}) custom-call(s32[128]{0:T(128)} %get-tuple-element.166.runs, s32[18432]{0:T(1024)} %get-tuple-element.142.idx, f32[144,128]{1,0:T(8,128)} %copy-done.19, bf16[1024,4,128]{2,1,0:T(4,128)(2,1)} %reshape.332.refs_0_.a, bf16[1024,4,128]{2,1,0:T(4,128)(2,1)} %collective-permute-done.3.refs_1_.b, ...), custom_call_target="tpu_custom_call" | custom-call | flops 51539607552 | bytes 37748736 | tf_op jit(solution)/shard_map/experts_backward/pallas_call | solution.py:201
  253.7 3.8 collective-permute-start.5
  257.5 42.9 %collective-permute-done.5 = f32[1024,512]{1,0:T(8,128)S(1)} collective-permute-done((f32[1024,512]{1,0:T(8,128)}, f32[1024,512]{1,0:T(8,128)S(1)}, u32[]{:S(2)}, u32[]{:S(2)}) %collective-permute-start.5) | collective-permute-done | bytes 2097184 | tf_op jit(solution)/shard_map/ppermute | solution.py:627
  300.4 3.0 add_convert_fusion.4
  305.4 1.8 collective-permute-start.6
  307.2 19.0 %collective-permute-done.6.refs_3_.b = bf16[1024,4,128]{2,1,0:T(4,128)(2,1)S(1)} collective-permute-done((bf16[1024,4,128]{2,1,0:T(4,128)(2,1)S(1)}, bf16[1024,4,128]{2,1,0:T(4,128)(2,1)S(1)}, u32[]{:S(2)}, u32[]{:S(2)}) %collective-permute-start.6) | collective-permute-done | bytes 1048608 | tf_op jit(solution)/shard_map/ppermute | solution.py:627
  327.2 2.9 join_rows.3
  330.4 46.9 %experts_forward.5 = (f32[1024,512]{1,0:T(8,128)}, f32[1024,512]{1,0:T(8,128)}) custom-call(s32[128]{0:T(128)} %get-tuple-element.166.runs, s32[18432]{0:T(1024)} %get-tuple-element.142.idx, f32[144,128]{1,0:T(8,128)} %copy-done.19, bf16[1024,4,128]{2,1,0:T(4,128)(2,1)} %reshape.332.refs_0_.a, bf16[1024,4,128]{2,1,0:T(4,128)(2,1)} %collective-permute-done.3.refs_1_.b, ...), custom_call_target="tpu_custom_call" | custom-call | flops 38654705664 | bytes 37748736 | tf_op jit(solution)/shard_map/experts_forward/pallas_call | solution.py:201
  377.3 3.3 collective-permute-start.7
  380.6 56.9 %experts_backward.3 = (f32[1024,512]{1,0:T(8,128)}, f32[1024,512]{1,0:T(8,128)}) custom-call(s32[128]{0:T(128)} %get-tuple-element.162.runs, s32[18432]{0:T(1024)} %get-tuple-element.140.idx, f32[144,128]{1,0:T(8,128)} %copy-done.13, bf16[1024,4,128]{2,1,0:T(4,128)(2,1)} %copy-done, bf16[1024,4,128]{2,1,0:T(4,128)(2,1)} %copy-done.1, ...), custom_call_target="tpu_custom_call" | custom-call | flops 51539607552 | bytes 37748736 | tf_op jit(solution)/shard_map/experts_backward/pallas_call | solution.py:201
  442.4 10.9 %merge_tables.1 = (s32[48,32,128]{2,1,0:T(8,128)}, f32[48,32,128]{2,1,0:T(8,128)}) custom-call(s32[2048]{0:T(1024)} %bitcast.172, s32[48]{0:T(128)} %pad_add_fusion.6.exps, s32[48]{0:T(128)} %constant.173.clone.1.layers, f32[8,2,2,152,128]{4,3,2,1,0:T(8,128)} %bitcast.188), custom_call_target="tpu_custom_call" | custom-call | flops 1000000000 | bytes 2490368 | tf_op jit(solution)/shard_map/merge_tables/pallas_call | solution.py:266
  455.8 49.9 %weight_grads.3 = (bf16[2,64,192,512]{3,2,1,0:T(8,128)(2,1)}, bf16[2,64,192,512]{3,2,1,0:T(8,128)(2,1)}, bf16[2,64,192,512]{3,2,1,0:T(8,128)(2,1)}, bf16[16,192,...) custom-call(s32[16]{0:T(128)} %bitcast.185, s32[17]{0:T(128)} %get-tuple-element.158.tiles, ...), custom_call_target="tpu_custom_call" | custom-call | flops 154618822656 | bytes 61865984 | tf_op jit(solution)/shard_map/weight_grads/pallas_call | solution.py:470
  506.3 36.2 %all-gather.12.cloned.1.call-done.refs_2_ = bf16[16384,4,128]{2,1,0:T(4,128)(2,1)} async-done(((bf16[2048,4,128]{2,1,0:T(4,128)(2,1)}), bf16[16384,4,128]{2,1,0:T(4,128)(2,1)}) %all-gather.12.cloned.1.call-update) | async-done | bytes 16777232 | tf_op jit(solution)/shard_map/all_gather | solution.py:630
  542.4 57.4 %weight_grads.4 = (bf16[2,64,192,512]{3,2,1,0:T(8,128)(2,1)}, bf16[2,64,192,512]{3,2,1,0:T(8,128)(2,1)}, bf16[2,64,192,512]{3,2,1,0:T(8,128)(2,1)}, bf16[16,192,...) custom-call(s32[16]{0:T(128)} %bitcast.180, ...), custom_call_target="tpu_custom_call", output_to_operand_aliasing={{0}: (13, {}), {1}: (14, {}), {2}: (15, {})} | custom-call | flops 154618822656 | bytes 61865984 | tf_op jit(solution)/shard_map/weight_grads/pallas_call | solution.py:470
  599.8 1.5 collective-permute-start.15
  601.9 1.5 collective-permute-start.17
  604.7 32.7 %collective-permute-done.15.refs_0_ = bf16[16,192,512]{2,1,0:T(8,128)(2,1)} collective-permute-done((bf16[16,192,512]{2,1,0:T(8,128)(2,1)}, bf16[16,192,512]{2,1,0:T(8,128)(2,1)}, u32[]{:S(2)}, u32[]{:S(2)}) %collective-permute-start.15) | collective-permute-done | bytes 3145760 | tf_op jit(solution)/shard_map/ppermute | solution.py:633
  637.5 33.7 %collective-permute-done.16.refs_1_ = bf16[16,192,512]{2,1,0:T(8,128)(2,1)} collective-permute-done((bf16[16,192,512]{2,1,0:T(8,128)(2,1)}, bf16[16,192,512]{2,1,0:T(8,128)(2,1)}, u32[]{:S(2)}, u32[]{:S(2)}) %collective-permute-start.16) | collective-permute-done | bytes 3145760 | tf_op jit(solution)/shard_map/ppermute | solution.py:633
  671.2 33.7 %collective-permute-done.17.refs_2_ = bf16[16,192,512]{2,1,0:T(8,128)(2,1)} collective-permute-done((bf16[16,192,512]{2,1,0:T(8,128)(2,1)}, bf16[16,192,512]{2,1,0:T(8,128)(2,1)}, u32[]{:S(2)}, u32[]{:S(2)}) %collective-permute-start.17) | collective-permute-done | bytes 3145760 | tf_op jit(solution)/shard_map/ppermute | solution.py:633
  705.4 59.0 %weight_grads.5 = (bf16[2,64,192,512]{3,2,1,0:T(8,128)(2,1)}, bf16[2,64,192,512]{3,2,1,0:T(8,128)(2,1)}, bf16[2,64,192,512]{3,2,1,0:T(8,128)(2,1)}, bf16[16,192,...) custom-call(s32[16]{0:T(128)} %bitcast.176, ...), custom_call_target="tpu_custom_call", output_to_operand_aliasing={{0}: (16, {}), {1}: (17, {}), {2}: (18, {})} | custom-call | flops 154618822656 | bytes 61865984 | tf_op jit(solution)/shard_map/weight_grads/pallas_call | solution.py:470
  765.1 2.3 fusion.1
  768.0 2.3 add_convert_fusion.1
  772.1 1.1 pad_maximum_fusion
  773.2 3.6 add_convert_fusion
  776.8 3.2 add_convert_fusion.2
  780.0 59.5 %all-reduce.12.cloned.1.call-done = bf16[2,512,512]{1,2,0:T(8,128)(2,1)} async-done(((bf16[2,512,512]{1,2,0:T(8,128)(2,1)}), bf16[2,512,512]{1,2,0:T(8,128)(2,1)}) %all-reduce.12.cloned.1.call-update) | async-done | bytes 1048592 | tf_op jit(solution)/shard_map/psum | solution.py:730
  839.5 2.3 copy.57
  841.7 20.7 %merge_lists.2 = (bf16[2,64,192,512]{3,2,1,0:T(8,128)(2,1)}, bf16[2,64,192,512]{3,2,1,0:T(8,128)(2,1)}, bf16[2,64,192,512]{3,2,1,0:T(8,128)(2,1)}) custom-call(s32[48]{0:T(128)} %pad_add_fusion.7.exps, bf16[16,192,512]{2,1,0:T(8,128)(2,1)} %collective-permute-done.15.refs_0_, ...), custom_call_target="tpu_custom_call", output_to_operand_aliasing={{0}: (10, {}), {1}: (11, {}), {2}: (12, {})} | custom-call | flops 1000000000 | bytes 56623104 | tf_op jit(solution)/shard_map/merge_lists/pallas_call | solution.py:527
  862.5 8.2 merge_lists.3
  (208 shorter events, 29.0 us)
Async XLA Ops:
  8.0 429.6 %all-gather.18.cloned.1.call-start = ((), (), s32[]{:S(2)}) async-start(), calls=%async_computation.6 | async-start | bytes 2801664 | tf_op jit(solution)/shard_map/all_gather | solution.py:679
  11.6 30.9 %copy-start = (bf16[1024,4,128]{2,1,0:T(4,128)(2,1)}, bf16[1024,4,128]{2,1,0:T(4,128)(2,1)S(1)}, u32[]{:S(2)}) copy-start(bf16[1024,4,128]{2,1,0:T(4,128)(2,1)S(1)} %reshape.330.refs_0_) | copy-start | bytes 3145732
  12.3 7.6 collective-permute-start
  15.6 26.0 %collective-permute-start.1 = (bf16[1024,4,128]{2,1,0:T(4,128)(2,1)S(1)}, bf16[1024,4,128]{2,1,0:T(4,128)(2,1)S(1)}, u32[]{:S(2)}, u32[]{:S(2)}) collective-permute-start(bf16[1024,4,128]{2,1,0:T(4,128)(2,1)S(1)} %reshape.330.refs_0_), channel_id=1, source_target_pairs={{0,8},{8,0},{1,9},{9,1},{2,10},{10,2},{3,11},{11,3},{4,12},{12,4},... | collective-permute-start | bytes 3145736 | tf_op jit(solution)/shard_map/ppermute | solution.py:627
  15.6 119.8 %copy-start.31 = (s32[64]{0:T(128)}, s32[64]{0:T(128)S(1)}, u32[]{:S(2)}) copy-start(s32[64]{0:T(128)S(1)} %iota_add_fusion.3) | copy-start | bytes 772
  30.9 11.6 %copy-start.13 = (f32[144,128]{1,0:T(8,128)}, f32[144,128]{1,0:T(8,128)S(1)}, u32[]{:S(2)}) copy-start(f32[144,128]{1,0:T(8,128)S(1)} %pad_bitcast_fusion.3.gates) | copy-start | bytes 221188
  82.0 47.2 %collective-permute-start.2 = (f32[1024,512]{1,0:T(8,128)}, f32[1024,512]{1,0:T(8,128)}, u32[]{:S(2)}, u32[]{:S(2)}) collective-permute-start(f32[1024,512]{1,0:T(8,128)} %experts_forward.3), channel_id=1, source_target_pairs={{0,8},{8,0},{1,9},{9,1},{2,10},{10,2},{3,11},{11,3},{4,12},{12,4},... | collective-permute-start | bytes 6291464 | tf_op jit(solution)/shard_map/ppermute | solution.py:627
  82.1 47.0 %copy-start.10 = (bf16[1024,512]{1,0:T(8,128)(2,1)S(1)}, bf16[1024,512]{1,0:T(8,128)(2,1)}, u32[]{:S(2)}) copy-start(bf16[1024,512]{1,0:T(8,128)(2,1)} %copy-done.9) | copy-start | bytes 3145732
  133.6 14.4 %copy-start.3 = (bf16[1024,512]{1,0:T(8,128)(2,1)}, bf16[1024,512]{1,0:T(8,128)(2,1)S(1)}, u32[]{:S(2)}) copy-start(bf16[1024,512]{1,0:T(8,128)(2,1)S(1)} %add_convert_fusion.5) | copy-start | bytes 3145732
  133.6 13.2 %copy-start.2 = (bf16[1024,512]{1,0:T(8,128)(2,1)S(1)}, bf16[1024,512]{1,0:T(8,128)(2,1)}, u32[]{:S(2)}) copy-start(bf16[1024,512]{1,0:T(8,128)(2,1)} %param.9) | copy-start | bytes 3145732
  144.0 30.6 %copy-start.19 = (f32[144,128]{1,0:T(8,128)}, f32[144,128]{1,0:T(8,128)S(1)}, u32[]{:S(2)}) copy-start(f32[144,128]{1,0:T(8,128)S(1)} %pad_bitcast_fusion.2.gates) | copy-start | bytes 221188
  146.8 309.0 %all-gather.16.cloned.1.call-start = ((), (), s32[]{:S(2)}) async-start(), calls=%async_computation.5 | async-start | bytes 18874368 | tf_op jit(solution)/shard_map/all_gather | solution.py:630
  148.0 23.8 %collective-permute-start.4 = (bf16[1024,4,128]{2,1,0:T(4,128)(2,1)}, bf16[1024,4,128]{2,1,0:T(4,128)(2,1)}, u32[]{:S(2)}, u32[]{:S(2)}) collective-permute-start(bf16[1024,4,128]{2,1,0:T(4,128)(2,1)} %reshape.334.refs_2_.a), channel_id=1, source_target_pairs={{0,8},{8,0},{1,9},{9,1},{2,10},{10,2},{3,11},{11,3},{4,12},{12,4},... | collective-permute-start | bytes 3145736 | tf_op jit(solution)/shard_map/ppermute | solution.py:627
  148.3 26.5 %copy-start.7 = (bf16[1024,4,128]{2,1,0:T(4,128)(2,1)S(1)}, bf16[1024,4,128]{2,1,0:T(4,128)(2,1)}, u32[]{:S(2)}) copy-start(bf16[1024,4,128]{2,1,0:T(4,128)(2,1)} %reshape.332.refs_0_.a) | copy-start | bytes 3145732
  174.7 281.1 %all-gather.14.cloned.1.call-start = ((), (), s32[]{:S(2)}) async-start(), calls=%async_computation.4 | async-start | bytes 18874368 | tf_op jit(solution)/shard_map/all_gather | solution.py:630
  174.8 22.8 %collective-permute-start.3 = (bf16[1024,4,128]{2,1,0:T(4,128)(2,1)S(1)}, bf16[1024,4,128]{2,1,0:T(4,128)(2,1)}, u32[]{:S(2)}, u32[]{:S(2)}) collective-permute-start(bf16[1024,4,128]{2,1,0:T(4,128)(2,1)S(1)} %copy-done.7), channel_id=1, source_target_pairs={{0,8},{8,0},{1,9},{9,1},{2,10},{10,2},{3,11},{11,3},{4,12},{12,4},... | collective-permute-start | bytes 3145736 | tf_op jit(solution)/shard_map/ppermute | solution.py:627
  200.5 305.8 %all-gather.8.cloned.1.call-start = ((), (), s32[]{:S(2)}) async-start(), calls=%async_computation.1 | async-start | bytes 9437184 | tf_op jit(solution)/shard_map/all_gather | solution.py:630
  201.0 305.2 %all-gather.10.cloned.1.call-start = ((), (), s32[]{:S(2)}) async-start(), calls=%async_computation.2 | async-start | bytes 9437184 | tf_op jit(solution)/shard_map/all_gather | solution.py:630
  201.6 340.8 %all-gather.12.cloned.1.call-start = ((), (), s32[]{:S(2)}) async-start(), calls=%async_computation.3 | async-start | bytes 18874368 | tf_op jit(solution)/shard_map/all_gather | solution.py:630
  253.7 46.7 %collective-permute-start.5 = (f32[1024,512]{1,0:T(8,128)}, f32[1024,512]{1,0:T(8,128)S(1)}, u32[]{:S(2)}, u32[]{:S(2)}) collective-permute-start(f32[1024,512]{1,0:T(8,128)} %get-tuple-element.59), channel_id=1, source_target_pairs={{0,8},{8,0},{1,9},{9,1},{2,10},{10,2},{3,11},{11,3},{4,12},{12,4},... | collective-permute-start | bytes 6291464 | tf_op jit(solution)/shard_map/ppermute | solution.py:627
  305.1 25.0 %copy-start.5 = (bf16[1024,512]{1,0:T(8,128)(2,1)}, bf16[1024,512]{1,0:T(8,128)(2,1)S(1)}, u32[]{:S(2)}) copy-start(bf16[1024,512]{1,0:T(8,128)(2,1)S(1)} %add_convert_fusion.3) | copy-start | bytes 3145732
  305.4 20.8 %copy-start.8 = (bf16[1024,4,128]{2,1,0:T(4,128)(2,1)}, bf16[1024,4,128]{2,1,0:T(4,128)(2,1)S(1)}, u32[]{:S(2)}) copy-start(bf16[1024,4,128]{2,1,0:T(4,128)(2,1)S(1)} %reshape.335.refs_2_.a) | copy-start | bytes 3145732
  305.4 20.8 %collective-permute-start.6 = (bf16[1024,4,128]{2,1,0:T(4,128)(2,1)S(1)}, bf16[1024,4,128]{2,1,0:T(4,128)(2,1)S(1)}, u32[]{:S(2)}, u32[]{:S(2)}) collective-permute-start(bf16[1024,4,128]{2,1,0:T(4,128)(2,1)S(1)} %reshape.335.refs_2_.a), channel_id=1, source_target_pairs={{0,8},{8,0},{1,9},{9,1},{2,10},{10,2},{3,11},{11,3},{4,12},{12,4},... | collective-permute-start | bytes 3145736 | tf_op jit(solution)/shard_map/ppermute | solution.py:627
  330.2 509.3 %all-reduce.12.cloned.1.call-start = ((), (), s32[]{:S(2)}) async-start(), calls=%async_computation | async-start | bytes 2097152 | tf_op jit(solution)/shard_map/psum | solution.py:730
  377.3 222.5 %collective-permute-start.7 = (f32[1024,512]{1,0:T(8,128)}, f32[1024,512]{1,0:T(8,128)}, u32[]{:S(2)}, u32[]{:S(2)}) collective-permute-start(f32[1024,512]{1,0:T(8,128)} %get-tuple-element.64), channel_id=1, source_target_pairs={{0,8},{8,0},{1,9},{9,1},{2,10},{10,2},{3,11},{11,3},{4,12},{12,4},... | collective-permute-start | bytes 6291464 | tf_op jit(solution)/shard_map/ppermute | solution.py:627
  380.6 58.0 %copy-start.32 = (s32[64]{0:T(128)S(1)}, s32[64]{0:T(128)}, u32[]{:S(2)}) copy-start(s32[64]{0:T(128)} %copy-done.31) | copy-start | bytes 772
  437.5 163.8 %collective-permute-start.8 = (f32[1024,512]{1,0:T(8,128)}, f32[1024,512]{1,0:T(8,128)}, u32[]{:S(2)}, u32[]{:S(2)}) collective-permute-start(f32[1024,512]{1,0:T(8,128)} %get-tuple-element.66), channel_id=1, source_target_pairs={{0,8},{8,0},{1,9},{9,1},{2,10},{10,2},{3,11},{11,3},{4,12},{12,4},... | collective-permute-start | bytes 6291464 | tf_op jit(solution)/shard_map/ppermute | solution.py:627
  439.9 13.8 %copy-start.24 = (s32[1,16]{1,0:T(1,128)}, s32[1,16]{1,0:T(1,128)S(1)}, u32[]{:S(2)}) copy-start(s32[1,16]{1,0:T(1,128)S(1)} %get-tuple-element.151) | copy-start | bytes 196
  439.9 13.8 %copy-start.25 = (s32[1,16]{1,0:T(1,128)}, s32[1,16]{1,0:T(1,128)S(1)}, u32[]{:S(2)}) copy-start(s32[1,16]{1,0:T(1,128)S(1)} %get-tuple-element.150) | copy-start | bytes 196
  440.6 15.2 %copy-start.30 = (s32[1,16]{1,0:T(1,128)}, s32[1,16]{1,0:T(1,128)S(1)}, u32[]{:S(2)}) copy-start(s32[1,16]{1,0:T(1,128)S(1)} %get-tuple-element.147) | copy-start | bytes 196
  505.7 96.2 %collective-permute-start.9 = (bf16[16,192,512]{2,1,0:T(8,128)(2,1)}, bf16[16,192,512]{2,1,0:T(8,128)(2,1)}, u32[]{:S(2)}, u32[]{:S(2)}) collective-permute-start(bf16[16,192,512]{2,1,0:T(8,128)(2,1)} %get-tuple-element.71), channel_id=1, source_target_pairs={{0,1},{1,0},{2,3},{3,2},{4,5},{5,4},{6,7},{7,6},{8,9},{9,8},{10,11... | collective-permute-start | bytes 9437192 | tf_op jit(solution)/shard_map/ppermute | solution.py:633
  505.7 97.7 %collective-permute-start.10 = (bf16[16,192,512]{2,1,0:T(8,128)(2,1)}, bf16[16,192,512]{2,1,0:T(8,128)(2,1)}, u32[]{:S(2)}, u32[]{:S(2)}) collective-permute-start(bf16[16,192,512]{2,1,0:T(8,128)(2,1)} %get-tuple-element.72), channel_id=1, source_target_pairs={{0,1},{1,0},{2,3},{3,2},{4,5},{5,4},{6,7},{7,6},{8,9},{9,8},{10,11... | collective-permute-start | bytes 9437192 | tf_op jit(solution)/shard_map/ppermute | solution.py:633
  506.2 98.0 %collective-permute-start.11 = (bf16[16,192,512]{2,1,0:T(8,128)(2,1)}, bf16[16,192,512]{2,1,0:T(8,128)(2,1)}, u32[]{:S(2)}, u32[]{:S(2)}) collective-permute-start(bf16[16,192,512]{2,1,0:T(8,128)(2,1)} %get-tuple-element.73), channel_id=1, source_target_pairs={{0,1},{1,0},{2,3},{3,2},{4,5},{5,4},{6,7},{7,6},{8,9},{9,8},{10,11... | collective-permute-start | bytes 9437192 | tf_op jit(solution)/shard_map/ppermute | solution.py:633
  542.4 61.0 %copy-start.26 = (s32[17,1]{0,1:T(1,128)S(1)}, s32[17,1]{0,1:T(1,128)}, u32[]{:S(2)}) copy-start(s32[17,1]{0,1:T(1,128)} %get-tuple-element.169) | copy-start | bytes 208
  542.4 61.2 %copy-start.23 = (s32[16]{0:T(128)S(1)}, s32[16]{0:T(128)}, u32[]{:S(2)}) copy-start(s32[16]{0:T(128)} %copy-done.22) | copy-start | bytes 196
  599.8 37.6 %collective-permute-start.15 = (bf16[16,192,512]{2,1,0:T(8,128)(2,1)}, bf16[16,192,512]{2,1,0:T(8,128)(2,1)}, u32[]{:S(2)}, u32[]{:S(2)}) collective-permute-start(bf16[16,192,512]{2,1,0:T(8,128)(2,1)} %get-tuple-element.71), channel_id=1, source_target_pairs={{0,2},{1,5},{2,0},{3,7},{4,6},{5,1},{6,4},{7,3},{8,10},{9,13},{10,... | collective-permute-start | bytes 9437192 | tf_op jit(solution)/shard_map/ppermute | solution.py:633
  601.3 69.8 %collective-permute-start.16 = (bf16[16,192,512]{2,1,0:T(8,128)(2,1)}, bf16[16,192,512]{2,1,0:T(8,128)(2,1)}, u32[]{:S(2)}, u32[]{:S(2)}) collective-permute-start(bf16[16,192,512]{2,1,0:T(8,128)(2,1)} %get-tuple-element.72), channel_id=1, source_target_pairs={{0,2},{1,5},{2,0},{3,7},{4,6},{5,1},{6,4},{7,3},{8,10},{9,13},{10,... | collective-permute-start | bytes 9437192 | tf_op jit(solution)/shard_map/ppermute | solution.py:633
  601.9 103.0 %collective-permute-start.17 = (bf16[16,192,512]{2,1,0:T(8,128)(2,1)}, bf16[16,192,512]{2,1,0:T(8,128)(2,1)}, u32[]{:S(2)}, u32[]{:S(2)}) collective-permute-start(bf16[16,192,512]{2,1,0:T(8,128)(2,1)} %get-tuple-element.73), channel_id=1, source_target_pairs={{0,2},{1,5},{2,0},{3,7},{4,6},{5,1},{6,4},{7,3},{8,10},{9,13},{10,... | collective-permute-start | bytes 9437192 | tf_op jit(solution)/shard_map/ppermute | solution.py:633
  603.4 101.5 %collective-permute-start.18 = (bf16[16,192,512]{2,1,0:T(8,128)(2,1)}, bf16[16,192,512]{2,1,0:T(8,128)(2,1)}, u32[]{:S(2)}, u32[]{:S(2)}) collective-permute-start(bf16[16,192,512]{2,1,0:T(8,128)(2,1)} %get-tuple-element.84), channel_id=1, source_target_pairs={{0,1},{1,0},{2,3},{3,2},{4,5},{5,4},{6,7},{7,6},{8,9},{9,8},{10,11... | collective-permute-start | bytes 9437192 | tf_op jit(solution)/shard_map/ppermute | solution.py:633
  604.2 160.2 %collective-permute-start.19 = (bf16[16,192,512]{2,1,0:T(8,128)(2,1)}, bf16[16,192,512]{2,1,0:T(8,128)(2,1)}, u32[]{:S(2)}, u32[]{:S(2)}) collective-permute-start(bf16[16,192,512]{2,1,0:T(8,128)(2,1)} %get-tuple-element.85), channel_id=1, source_target_pairs={{0,1},{1,0},{2,3},{3,2},{4,5},{5,4},{6,7},{7,6},{8,9},{9,8},{10,11... | collective-permute-start | bytes 9437192 | tf_op jit(solution)/shard_map/ppermute | solution.py:633
  637.5 127.0 %collective-permute-start.20 = (bf16[16,192,512]{2,1,0:T(8,128)(2,1)}, bf16[16,192,512]{2,1,0:T(8,128)(2,1)}, u32[]{:S(2)}, u32[]{:S(2)}) collective-permute-start(bf16[16,192,512]{2,1,0:T(8,128)(2,1)} %get-tuple-element.86), channel_id=1, source_target_pairs={{0,1},{1,0},{2,3},{3,2},{4,5},{5,4},{6,7},{7,6},{8,9},{9,8},{10,11... | collective-permute-start | bytes 9437192 | tf_op jit(solution)/shard_map/ppermute | solution.py:633
  671.2 93.8 %collective-permute-start.21 = (bf16[16,192,512]{2,1,0:T(8,128)(2,1)}, bf16[16,192,512]{2,1,0:T(8,128)(2,1)}, u32[]{:S(2)}, u32[]{:S(2)}) collective-permute-start(bf16[16,192,512]{2,1,0:T(8,128)(2,1)} %collective-permute-done.15.refs_0_), channel_id=1, source_target_pairs={{0,1},{1,0},{2,3},{3,2},{4,5},{5,4},{6,7},{7,6},{8,9},{9,8},{10,11... | collective-permute-start | bytes 9437192 | tf_op jit(solution)/shard_map/ppermute | solution.py:633
  704.9 136.9 %collective-permute-start.22 = (bf16[16,192,512]{2,1,0:T(8,128)(2,1)}, bf16[16,192,512]{2,1,0:T(8,128)(2,1)}, u32[]{:S(2)}, u32[]{:S(2)}) collective-permute-start(bf16[16,192,512]{2,1,0:T(8,128)(2,1)} %collective-permute-done.16.refs_1_), channel_id=1, source_target_pairs={{0,1},{1,0},{2,3},{3,2},{4,5},{5,4},{6,7},{7,6},{8,9},{9,8},{10,11... | collective-permute-start | bytes 9437192 | tf_op jit(solution)/shard_map/ppermute | solution.py:633
  704.9 136.9 %collective-permute-start.23 = (bf16[16,192,512]{2,1,0:T(8,128)(2,1)}, bf16[16,192,512]{2,1,0:T(8,128)(2,1)}, u32[]{:S(2)}, u32[]{:S(2)}) collective-permute-start(bf16[16,192,512]{2,1,0:T(8,128)(2,1)} %collective-permute-done.17.refs_2_), channel_id=1, source_target_pairs={{0,1},{1,0},{2,3},{3,2},{4,5},{5,4},{6,7},{7,6},{8,9},{9,8},{10,11... | collective-permute-start | bytes 9437192 | tf_op jit(solution)/shard_map/ppermute | solution.py:633
  705.4 59.7 %copy-start.15 = (bf16[1024,512]{1,0:T(8,128)(2,1)S(1)}, bf16[1024,512]{1,0:T(8,128)(2,1)}, u32[]{:S(2)}) copy-start(bf16[1024,512]{1,0:T(8,128)(2,1)} %copy-done.14) | copy-start | bytes 3145732
  764.4 98.0 %collective-permute-start.12 = (bf16[16,192,512]{2,1,0:T(8,128)(2,1)}, bf16[16,192,512]{2,1,0:T(8,128)(2,1)}, u32[]{:S(2)}, u32[]{:S(2)}) collective-permute-start(bf16[16,192,512]{2,1,0:T(8,128)(2,1)} %get-tuple-element.81), channel_id=1, source_target_pairs={{0,1},{1,0},{2,3},{3,2},{4,5},{5,4},{6,7},{7,6},{8,9},{9,8},{10,11... | collective-permute-start | bytes 9437192 | tf_op jit(solution)/shard_map/ppermute | solution.py:633
  764.5 98.0 %collective-permute-start.13 = (bf16[16,192,512]{2,1,0:T(8,128)(2,1)}, bf16[16,192,512]{2,1,0:T(8,128)(2,1)}, u32[]{:S(2)}, u32[]{:S(2)}) collective-permute-start(bf16[16,192,512]{2,1,0:T(8,128)(2,1)} %get-tuple-element.82), channel_id=1, source_target_pairs={{0,1},{1,0},{2,3},{3,2},{4,5},{5,4},{6,7},{7,6},{8,9},{9,8},{10,11... | collective-permute-start | bytes 9437192 | tf_op jit(solution)/shard_map/ppermute | solution.py:633
  765.0 97.5 %collective-permute-start.14 = (bf16[16,192,512]{2,1,0:T(8,128)(2,1)}, bf16[16,192,512]{2,1,0:T(8,128)(2,1)}, u32[]{:S(2)}, u32[]{:S(2)}) collective-permute-start(bf16[16,192,512]{2,1,0:T(8,128)(2,1)} %get-tuple-element.83), channel_id=1, source_target_pairs={{0,1},{1,0},{2,3},{3,2},{4,5},{5,4},{6,7},{7,6},{8,9},{9,8},{10,11... | collective-permute-start | bytes 9437192 | tf_op jit(solution)/shard_map/ppermute | solution.py:633
  (19 other events, 59.3 us)
Sparse Core Ops, SparseCore 0:
  146.9 25.6 all-gather.17
  174.8 85.7 all-gather.15
  263.1 85.9 all-gather.13
  351.4 50.4 all-gather.7
  404.2 50.5 all-gather.9
  456.4 85.9 all-gather.11
Sparse Core Ops, SparseCore 1:
  773.3 66.1 all-reduce.11

commit v14 on v13

--- a/solution.py
+++ b/solution.py
@@ -15,6 +15,7 @@
 HALF_TILE = 64
 WTILE = 768
 PARTS = 2
+AHEAD = 3
 SOURCES = 8
 CHUNK = 256
 PITCH = 9
@@ -56,7 +57,7 @@
 
 def add_rows(acc, vals_ref, idx, row, tile, pitch, width):
     for b in range(0, tile, BATCH):
-        at = [idx[row + b + r] * width for r in range(BATCH)]
+        at = [pl.multiple_of(idx[row + b + r], 4) for r in range(BATCH)]
         vals = [acc[pl.ds(at[r], width), :] + vals_ref[pl.ds((b + r) * pitch, width), :] for r in range(BATCH)]
         for r in reversed(range(BATCH)):
             acc[pl.ds(at[r], width), :] = vals[r]
@@ -72,6 +73,17 @@
     pair = pltpu.roll(pair, lax.rem(LANES - skip, LANES), 1)
     lane = lax.broadcasted_iota(jnp.int32, (1, LANES), 1)
     return spread_column(jnp.where(lane < LANES - skip, pair[:1], pair[1:]))
+
+
+def widen(src, dst, pitch, halves, tok):
+    step = 32
+
+    def one(q, carry):
+        for r in range(step):
+            dst[pl.ds((q * step + r) * pitch, pitch), :] = src[q * step + r].astype(jnp.float32)
+        return carry
+
+    lax.fori_loop(halves[0] * tok // step, (halves[-1] + 1) * tok // step, one, 0)
 
 
 def write_sums(acc, outs, tok, parts, pitch, halves):
@@ -137,13 +149,13 @@
 def token_body(runs, idx, gates, *refs, layer, tok, parts, tile, halves, backward):
     n_in = 4 if backward else 2
     sources, weights, outs, refs = refs[:n_in], refs[n_in:n_in + 3], refs[n_in + 3:n_in + 3 + len(halves)], refs[n_in + 3 + len(halves):]
-    slabs, rows, vt, acc, mid, wbuf, sem, wsem = refs
+    narrow, wide, rows, vt, acc, mid, wbuf, sem, wsem = refs
     ff = weights[0].shape[2]
     width = parts * n_in // 2
     pitch = width + 1
 
     def prepare():
-        copies = [pltpu.make_async_copy(src, slabs.at[pl.ds(k % 2 * tok, tok), pl.ds(k // 2 * parts, parts)], sem.at[k])
+        copies = [pltpu.make_async_copy(src, narrow.at[pl.ds(k % 2 * tok, tok), pl.ds(k // 2 * parts, parts)], sem.at[k])
                   for k, src in enumerate(sources) if k % 2 in halves]
         for c in copies:
             c.start()
@@ -151,6 +163,7 @@
             clear(ref)
         for c in copies:
             c.wait()
+        widen(narrow, wide, width, halves, tok)
 
     def column(k):
         return rows[pl.ds(k, tile, stride=pitch), :]
@@ -168,7 +181,7 @@
             dh = nt_dot(wbuf[slot, 2 * ff:], c)
         add_rows(acc, vt, idx, done, tile, parts + 1, parts)
         for r in range(tile):
-            rows[pl.ds(pitch * r, width), :] = slabs[idx[row + r]].astype(jnp.float32)
+            rows[pl.ds(pitch * r, width), :] = wide[pl.ds(pl.multiple_of(idx[row + r], width), width), :]
         live = lax.broadcasted_iota(jnp.int32, (tile, LANES), 0) < n2
         gate = tile_gates(gates, row2)[:tile]
         for k in range(parts):
@@ -184,7 +197,7 @@
             mid[...] = (act * b).astype(jnp.bfloat16)
 
     run_tiles(step, weights, wbuf, wsem, runs, tile, layer, prepare)
-    write_sums(acc, outs, tok, parts, parts, halves)
+    write_sums(acc, outs, tok, parts, width, halves)
 
 
 def token_kernel(layer, runs, table, slabs, weights, halves=(0, 1)):
@@ -205,9 +218,9 @@
             grid=(1,),
             in_specs=[pl.BlockSpec(gates.shape, lambda i, *_: (0, 0))] + [any_spec] * (len(slabs) + 3),
             out_specs=[rows_spec] * len(halves),
-            scratch_shapes=[pltpu.VMEM((2 * tok, width, LANES), jnp.bfloat16),
+            scratch_shapes=[pltpu.VMEM((2 * tok, width, LANES), jnp.bfloat16), pltpu.VMEM((2 * tok * width, LANES), jnp.float32),
                             pltpu.VMEM((tile_rows, LANES), jnp.float32), pltpu.VMEM((tile_rows, LANES), jnp.float32),
-                            pltpu.VMEM((2 * tok * parts, LANES), jnp.float32),
+                            pltpu.VMEM((2 * tok * width, LANES), jnp.float32),
                             pltpu.VMEM((2 * ff if backward else ff, tile), jnp.bfloat16),
                             pltpu.VMEM((SLOTS, 3 * ff, d_model), jnp.bfloat16),
                             pltpu.SemaphoreType.DMA((len(slabs),)), pltpu.SemaphoreType.DMA((SLOTS,))],
@@ -322,6 +335,11 @@
                     c.wait()
                 seen[0] = q + 1
 
+                @pl.when(q + AHEAD < SOURCES)
+                def _():
+                    for c in row_copies(q + AHEAD):
+                        c.start()
+
             return carry
 
         @pl.when(seen[0] < SOURCES)
@@ -330,7 +348,7 @@
 
     @pl.when(e == 0)
     def _():
-        for q in range(SOURCES):
+        for q in range(AHEAD):
             for c in row_copies(q):
                 c.start()
         seen[0] = 0
@@ -651,7 +669,7 @@
         def add_tables(pair):
             run, token, gate, bounds = route_tables(pair[0].astype(jnp.int32), pair[1], ep_id, n_local)
             runs.append(run)
-            tables.append((token, gate))
+            tables.append([(token * parts, gate), (token * (2 * parts), gate)])
             spot = dp_id * (2 * tok) + token
             first = jnp.concatenate([spot.reshape(-1, LANES), jnp.pad(bounds.reshape(1, LANES), ((0, 7), (0, 0)))])
             packed.append(jnp.stack([first.astype(jnp.float32), jnp.pad(gate, ((0, 8), (0, 0)))]))
@@ -670,9 +688,9 @@
                 add_tables(after(both[:, layer], u_slabs[layer]))
             xs.append(x_in)
             if layer < top:
-                other, = token_kernel(layer, runs[layer][1], tables[layer], (u_slabs[layer], u_others[layer]), weights, (1,))
+                other, = token_kernel(layer, runs[layer][1], tables[layer][0], (u_slabs[layer], u_others[layer]), weights, (1,))
                 sent = swap(other)
-                own, = token_kernel(layer, runs[layer][0], tables[layer], (after(u_slabs[layer], other), u_others[layer]),
+                own, = token_kernel(layer, runs[layer][0], tables[layer][0], (after(u_slabs[layer], other), u_others[layer]),
                                     weights, (0,))
                 x_in = (u.astype(jnp.float32) + own + sent).astype(jnp.bfloat16)
 
@@ -697,11 +715,11 @@
             both_u = [u_slabs[layer], u_others[layer]]
             u_rows = spread(both_u if layer < top else [join_rows(*both_u)])
             slabs = (u_slabs[layer], u_others[layer], d_slab, d_other)
-            own, other = token_kernel(layer, runs[layer][2], tables[layer], slabs, weights)
+            own, other = token_kernel(layer, runs[layer][2], tables[layer][1], slabs, weights)
             d_u = (d_y.astype(jnp.float32) + own + swap(other)).astype(jnp.bfloat16)
             last = other
             if layer == top:
-                y_own, last = token_kernel(top, runs[top][2], tables[top], (after(u_slabs[top], other), u_others[top]), weights)
+                y_own, last = token_kernel(top, runs[top][2], tables[top][0], (after(u_slabs[top], other), u_others[top]), weights)
             d_mix[layer] = jnp.einsum('td,te->de', xs[layer], d_u, preferred_element_type=jnp.float32).astype(jnp.bfloat16)
             d_y = (d_u.astype(jnp.float32)
                    + jnp.einsum('te,de->td', d_u, w_mix[layer], preferred_element_type=jnp.float32)).astype(jnp.bfloat16)

time: 879 us -> 879 us (level)
  no operation moved by 1% of the time
where the time goes in v14:
time: 879 us; the launch traced here: 878 us
  Pallas kernels  448 us (51%)
  waiting for transfers between devices  327 us (37%)
  other arithmetic  41.6 us (5%)
  starting transfers between devices  20 us (2%)
  between operations  16.6 us (2%)
  local copies, waits for them, and re-layouts  14.7 us (2%)
  matrix products  10.5 us (1%)
    pallas_call x5, Pallas kernels, token_kernel(): pl.pallas_call(functools.partial(token_body, layer=layer, tok=tok, parts=...  232 us
    pallas_call x3, Pallas kernels, weight_grads(): pl.pallas_call(functools.partial(weight_grad_body, parts=parts, n_exp=n_e...  167 us
    ppermute x9, waiting for transfers between devices, swap(): return lax.ppermute(x, 'ep', ep_pairs)  129 us
    ppermute x15, waiting for transfers between devices, trade(): return [lax.ppermute(y, 'dp', pairs) for y in x]  100 us
    psum x1, waiting for transfers between devices, device_body(): d_mix = lax.psum(jnp.stack(d_mix), ('dp', 'ep'))  59.5 us
    all_gather x5, waiting for transfers between devices, spread(): return [lax.all_gather(y, 'dp', axis=0, tiled=True) for y in x]  36.7 us
    pallas_call x2, Pallas kernels, merge_lists(): pl.pallas_call(functools.partial(merge_body, layers=layers, n_exp=n_exp),...  28.9 us
  transfers between devices with their start and end apart: 31, of which 12 were waited for; matrix products, arithmetic and copies ran while one was open for 5% of the time, Pallas kernels for 46%

profile of v14, /device:TPU:0, one launch (start us, length us, event | category | flops | bytes accessed | tf_op | source)
XLA Modules:
  0.0 878.2 jit_solution(14481031304359961892)
XLA Ops:
  8.9 2.4 add_convert_fusion.7
  12.3 3.3 collective-permute-start
  15.6 4.3 collective-permute-done
  20.1 1.1 convert_reduce_fusion
  22.6 6.4 sort.30
  29.0 2.0 fusion.43
  31.8 9.8 %collective-permute-done.1.refs_1_ = bf16[1024,4,128]{2,1,0:T(4,128)(2,1)S(1)} collective-permute-done((bf16[1024,4,128]{2,1,0:T(4,128)(2,1)S(1)}, bf16[1024,4,128]{2,1,0:T(4,128)(2,1)S(1)}, u32[]{:S(2)}, u32[]{:S(2)}) %collective-permute-start.1) | collective-permute-done | bytes 1048608 | tf_op jit(solution)/shard_map/ppermute | solution.py:645
  42.5 38.7 %experts_forward.3 = f32[1024,512]{1,0:T(8,128)} custom-call(s32[128]{0:T(128)} %get-tuple-element.165.runs, s32[18432]{0:T(1024)} %get-tuple-element.141.idx, f32[144,128]{1,0:T(8,128)} %copy-done.13, bf16[1024,4,128]{2,1,0:T(4,128)(2,1)} %copy-done, bf16[1024,4,128]{2,1,0:T(4,128)(2,1)} %copy-done.1, bf16[2,64,192,512]{3,2,1,0:T(8,128)(2,1)} %bitcast.137, ...), custom_call_target="tpu_custom_call" | custom-call | flops 19327352832 | bytes 37748736 | tf_op jit(solution)/shard_map/experts_forward/pallas_call | solution.py:214
  81.3 38.9 %experts_forward.4 = f32[1024,512]{1,0:T(8,128)} custom-call(s32[128]{0:T(128)} %get-tuple-element.166.runs, s32[18432]{0:T(1024)} %get-tuple-element.141.idx, f32[144,128]{1,0:T(8,128)} %copy-done.13, bf16[1024,4,128]{2,1,0:T(4,128)(2,1)} %copy-done, bf16[1024,4,128]{2,1,0:T(4,128)(2,1)} %copy-done.1, bf16[2,64,192,512]{3,2,1,0:T(8,128)(2,1)} %bitcast.138, ...), custom_call_target="tpu_custom_call" | custom-call | flops 19327352832 | bytes 37748736 | tf_op jit(solution)/shard_map/experts_forward/pallas_call | solution.py:214
  120.3 8.0 collective-permute-done.2
  128.3 2.8 add_convert_fusion.6
  132.8 1.1 reshape.332.refs_0_.a
  136.0 6.4 sort.31
  143.3 1.9 fusion.44
  146.0 1.1 reshape.334.refs_2_.a
  147.4 23.4 %collective-permute-done.4.refs_3_.b = bf16[1024,4,128]{2,1,0:T(4,128)(2,1)} collective-permute-done((bf16[1024,4,128]{2,1,0:T(4,128)(2,1)}, bf16[1024,4,128]{2,1,0:T(4,128)(2,1)}, u32[]{:S(2)}, u32[]{:S(2)}) %collective-permute-start.4) | collective-permute-done | bytes 1048608 | tf_op jit(solution)/shard_map/ppermute | solution.py:645
  170.9 2.9 join_rows.5
  174.5 22.1 %collective-permute-done.3.refs_1_.b = bf16[1024,4,128]{2,1,0:T(4,128)(2,1)} collective-permute-done((bf16[1024,4,128]{2,1,0:T(4,128)(2,1)S(1)}, bf16[1024,4,128]{2,1,0:T(4,128)(2,1)}, u32[]{:S(2)}, u32[]{:S(2)}) %collective-permute-start.3) | collective-permute-done | bytes 1048608 | tf_op jit(solution)/shard_map/ppermute | solution.py:645
  196.6 2.9 join_rows.4
  200.7 52.7 %experts_backward.2 = (f32[1024,512]{1,0:T(8,128)}, f32[1024,512]{1,0:T(8,128)}) custom-call(s32[128]{0:T(128)} %get-tuple-element.168.runs, s32[18432]{0:T(1024)} %get-tuple-element.143.idx, f32[144,128]{1,0:T(8,128)} %copy-done.19, bf16[1024,4,128]{2,1,0:T(4,128)(2,1)} %reshape.332.refs_0_.a, bf16[1024,4,128]{2,1,0:T(4,128)(2,1)} %collective-permute-done.3.refs_1_.b, ...), custom_call_target="tpu_custom_call" | custom-call | flops 51539607552 | bytes 37748736 | tf_op jit(solution)/shard_map/experts_backward/pallas_call | solution.py:214
  253.3 3.6 collective-permute-start.5
  257.0 42.9 %collective-permute-done.5 = f32[1024,512]{1,0:T(8,128)S(1)} collective-permute-done((f32[1024,512]{1,0:T(8,128)}, f32[1024,512]{1,0:T(8,128)S(1)}, u32[]{:S(2)}, u32[]{:S(2)}) %collective-permute-start.5) | collective-permute-done | bytes 2097184 | tf_op jit(solution)/shard_map/ppermute | solution.py:645
  299.9 3.0 add_convert_fusion.4
  304.9 1.8 collective-permute-start.6
  306.7 19.0 %collective-permute-done.6.refs_3_.b = bf16[1024,4,128]{2,1,0:T(4,128)(2,1)S(1)} collective-permute-done((bf16[1024,4,128]{2,1,0:T(4,128)(2,1)S(1)}, bf16[1024,4,128]{2,1,0:T(4,128)(2,1)S(1)}, u32[]{:S(2)}, u32[]{:S(2)}) %collective-permute-start.6) | collective-permute-done | bytes 1048608 | tf_op jit(solution)/shard_map/ppermute | solution.py:645
  326.6 2.9 join_rows.3
  329.8 44.4 %experts_forward.5 = (f32[1024,512]{1,0:T(8,128)}, f32[1024,512]{1,0:T(8,128)}) custom-call(s32[128]{0:T(128)} %get-tuple-element.168.runs, s32[18432]{0:T(1024)} %get-tuple-element.144.idx, f32[144,128]{1,0:T(8,128)} %copy-done.19, bf16[1024,4,128]{2,1,0:T(4,128)(2,1)} %reshape.332.refs_0_.a, bf16[1024,4,128]{2,1,0:T(4,128)(2,1)} %collective-permute-done.3.refs_1_.b, ...), custom_call_target="tpu_custom_call" | custom-call | flops 38654705664 | bytes 37748736 | tf_op jit(solution)/shard_map/experts_forward/pallas_call | solution.py:214
  374.2 4.3 collective-permute-start.7
  378.5 57.4 %experts_backward.3 = (f32[1024,512]{1,0:T(8,128)}, f32[1024,512]{1,0:T(8,128)}) custom-call(s32[128]{0:T(128)} %get-tuple-element.164.runs, s32[18432]{0:T(1024)} %get-tuple-element.140.idx, f32[144,128]{1,0:T(8,128)} %copy-done.13, bf16[1024,4,128]{2,1,0:T(4,128)(2,1)} %copy-done, bf16[1024,4,128]{2,1,0:T(4,128)(2,1)} %copy-done.1, ...), custom_call_target="tpu_custom_call" | custom-call | flops 51539607552 | bytes 37748736 | tf_op jit(solution)/shard_map/experts_backward/pallas_call | solution.py:214
  440.8 10.9 %merge_tables.1 = (s32[48,32,128]{2,1,0:T(8,128)}, f32[48,32,128]{2,1,0:T(8,128)}) custom-call(s32[2048]{0:T(1024)} %bitcast.172, s32[48]{0:T(128)} %pad_add_fusion.6.exps, s32[48]{0:T(128)} %constant.176.clone.1.layers, f32[8,2,2,152,128]{4,3,2,1,0:T(8,128)} %bitcast.188), custom_call_target="tpu_custom_call" | custom-call | flops 1000000000 | bytes 2490368 | tf_op jit(solution)/shard_map/merge_tables/pallas_call | solution.py:279
  454.2 50.1 %weight_grads.3 = (bf16[2,64,192,512]{3,2,1,0:T(8,128)(2,1)}, bf16[2,64,192,512]{3,2,1,0:T(8,128)(2,1)}, bf16[2,64,192,512]{3,2,1,0:T(8,128)(2,1)}, bf16[16,192,...) custom-call(s32[16]{0:T(128)} %bitcast.185, s32[17]{0:T(128)} %get-tuple-element.160.tiles, ...), custom_call_target="tpu_custom_call" | custom-call | flops 154618822656 | bytes 61865984 | tf_op jit(solution)/shard_map/weight_grads/pallas_call | solution.py:488
  504.9 36.7 %all-gather.12.cloned.1.call-done.refs_2_ = bf16[16384,4,128]{2,1,0:T(4,128)(2,1)} async-done(((bf16[2048,4,128]{2,1,0:T(4,128)(2,1)}), bf16[16384,4,128]{2,1,0:T(4,128)(2,1)}) %all-gather.12.cloned.1.call-update) | async-done | bytes 16777232 | tf_op jit(solution)/shard_map/all_gather | solution.py:648
  541.6 57.7 %weight_grads.4 = (bf16[2,64,192,512]{3,2,1,0:T(8,128)(2,1)}, bf16[2,64,192,512]{3,2,1,0:T(8,128)(2,1)}, bf16[2,64,192,512]{3,2,1,0:T(8,128)(2,1)}, bf16[16,192,...) custom-call(s32[16]{0:T(128)} %bitcast.180, ...), custom_call_target="tpu_custom_call", output_to_operand_aliasing={{0}: (13, {}), {1}: (14, {}), {2}: (15, {})} | custom-call | flops 154618822656 | bytes 61865984 | tf_op jit(solution)/shard_map/weight_grads/pallas_call | solution.py:488
  599.3 1.5 collective-permute-start.15
  601.4 1.5 collective-permute-start.17
  604.2 32.7 %collective-permute-done.15.refs_0_ = bf16[16,192,512]{2,1,0:T(8,128)(2,1)} collective-permute-done((bf16[16,192,512]{2,1,0:T(8,128)(2,1)}, bf16[16,192,512]{2,1,0:T(8,128)(2,1)}, u32[]{:S(2)}, u32[]{:S(2)}) %collective-permute-start.15) | collective-permute-done | bytes 3145760 | tf_op jit(solution)/shard_map/ppermute | solution.py:651
  637.0 33.7 %collective-permute-done.16.refs_1_ = bf16[16,192,512]{2,1,0:T(8,128)(2,1)} collective-permute-done((bf16[16,192,512]{2,1,0:T(8,128)(2,1)}, bf16[16,192,512]{2,1,0:T(8,128)(2,1)}, u32[]{:S(2)}, u32[]{:S(2)}) %collective-permute-start.16) | collective-permute-done | bytes 3145760 | tf_op jit(solution)/shard_map/ppermute | solution.py:651
  670.7 33.7 %collective-permute-done.17.refs_2_ = bf16[16,192,512]{2,1,0:T(8,128)(2,1)} collective-permute-done((bf16[16,192,512]{2,1,0:T(8,128)(2,1)}, bf16[16,192,512]{2,1,0:T(8,128)(2,1)}, u32[]{:S(2)}, u32[]{:S(2)}) %collective-permute-start.17) | collective-permute-done | bytes 3145760 | tf_op jit(solution)/shard_map/ppermute | solution.py:651
  704.9 59.5 %weight_grads.5 = (bf16[2,64,192,512]{3,2,1,0:T(8,128)(2,1)}, bf16[2,64,192,512]{3,2,1,0:T(8,128)(2,1)}, bf16[2,64,192,512]{3,2,1,0:T(8,128)(2,1)}, bf16[16,192,...) custom-call(s32[16]{0:T(128)} %bitcast.176, ...), custom_call_target="tpu_custom_call", output_to_operand_aliasing={{0}: (16, {}), {1}: (17, {}), {2}: (18, {})} | custom-call | flops 154618822656 | bytes 61865984 | tf_op jit(solution)/shard_map/weight_grads/pallas_call | solution.py:488
  765.0 2.3 fusion.1
  768.0 2.3 add_convert_fusion.1
  772.1 1.1 pad_maximum_fusion
  773.2 3.6 add_convert_fusion
  776.8 3.2 add_convert_fusion.2
  780.0 59.5 %all-reduce.12.cloned.1.call-done = bf16[2,512,512]{1,2,0:T(8,128)(2,1)} async-done(((bf16[2,512,512]{1,2,0:T(8,128)(2,1)}), bf16[2,512,512]{1,2,0:T(8,128)(2,1)}) %all-reduce.12.cloned.1.call-update) | async-done | bytes 1048592 | tf_op jit(solution)/shard_map/psum | solution.py:748
  839.5 2.3 copy.57
  841.8 20.7 %merge_lists.2 = (bf16[2,64,192,512]{3,2,1,0:T(8,128)(2,1)}, bf16[2,64,192,512]{3,2,1,0:T(8,128)(2,1)}, bf16[2,64,192,512]{3,2,1,0:T(8,128)(2,1)}) custom-call(s32[48]{0:T(128)} %pad_add_fusion.7.exps, bf16[16,192,512]{2,1,0:T(8,128)(2,1)} %collective-permute-done.15.refs_0_, ...), custom_call_target="tpu_custom_call", output_to_operand_aliasing={{0}: (10, {}), {1}: (11, {}), {2}: (12, {})} | custom-call | flops 1000000000 | bytes 56623104 | tf_op jit(solution)/shard_map/merge_lists/pallas_call | solution.py:545
  862.5 8.2 merge_lists.3
  (208 shorter events, 29.0 us)
Async XLA Ops:
  8.0 428.0 %all-gather.18.cloned.1.call-start = ((), (), s32[]{:S(2)}) async-start(), calls=%async_computation.6 | async-start | bytes 2801664 | tf_op jit(solution)/shard_map/all_gather | solution.py:697
  11.6 30.9 %copy-start = (bf16[1024,4,128]{2,1,0:T(4,128)(2,1)}, bf16[1024,4,128]{2,1,0:T(4,128)(2,1)S(1)}, u32[]{:S(2)}) copy-start(bf16[1024,4,128]{2,1,0:T(4,128)(2,1)S(1)} %reshape.330.refs_0_) | copy-start | bytes 3145732
  12.3 7.6 collective-permute-start
  15.6 26.0 %collective-permute-start.1 = (bf16[1024,4,128]{2,1,0:T(4,128)(2,1)S(1)}, bf16[1024,4,128]{2,1,0:T(4,128)(2,1)S(1)}, u32[]{:S(2)}, u32[]{:S(2)}) collective-permute-start(bf16[1024,4,128]{2,1,0:T(4,128)(2,1)S(1)} %reshape.330.refs_0_), channel_id=1, source_target_pairs={{0,8},{8,0},{1,9},{9,1},{2,10},{10,2},{3,11},{11,3},{4,12},{12,4},... | collective-permute-start | bytes 3145736 | tf_op jit(solution)/shard_map/ppermute | solution.py:645
  15.6 118.9 %copy-start.31 = (s32[64]{0:T(128)}, s32[64]{0:T(128)S(1)}, u32[]{:S(2)}) copy-start(s32[64]{0:T(128)S(1)} %iota_add_fusion.3) | copy-start | bytes 772
  81.2 47.1 %collective-permute-start.2 = (f32[1024,512]{1,0:T(8,128)}, f32[1024,512]{1,0:T(8,128)}, u32[]{:S(2)}, u32[]{:S(2)}) collective-permute-start(f32[1024,512]{1,0:T(8,128)} %experts_forward.3), channel_id=1, source_target_pairs={{0,8},{8,0},{1,9},{9,1},{2,10},{10,2},{3,11},{11,3},{4,12},{12,4},... | collective-permute-start | bytes 6291464 | tf_op jit(solution)/shard_map/ppermute | solution.py:645
  81.3 47.0 %copy-start.10 = (bf16[1024,512]{1,0:T(8,128)(2,1)S(1)}, bf16[1024,512]{1,0:T(8,128)(2,1)}, u32[]{:S(2)}) copy-start(bf16[1024,512]{1,0:T(8,128)(2,1)} %copy-done.9) | copy-start | bytes 3145732
  120.3 11.8 %copy-start.34 = (bf16[2,512,512]{2,1,0:T(8,128)(2,1)S(1)}, bf16[2,512,512]{2,1,0:T(8,128)(2,1)}, u32[]{:S(2)}) copy-start(bf16[2,512,512]{2,1,0:T(8,128)(2,1)} %param.12) | copy-start | bytes 3145732
  132.8 14.4 %copy-start.3 = (bf16[1024,512]{1,0:T(8,128)(2,1)}, bf16[1024,512]{1,0:T(8,128)(2,1)S(1)}, u32[]{:S(2)}) copy-start(bf16[1024,512]{1,0:T(8,128)(2,1)S(1)} %add_convert_fusion.5) | copy-start | bytes 3145732
  132.8 13.2 %copy-start.2 = (bf16[1024,512]{1,0:T(8,128)(2,1)S(1)}, bf16[1024,512]{1,0:T(8,128)(2,1)}, u32[]{:S(2)}) copy-start(bf16[1024,512]{1,0:T(8,128)(2,1)} %param.9) | copy-start | bytes 3145732
  143.2 30.5 %copy-start.19 = (f32[144,128]{1,0:T(8,128)}, f32[144,128]{1,0:T(8,128)S(1)}, u32[]{:S(2)}) copy-start(f32[144,128]{1,0:T(8,128)S(1)} %pad_bitcast_fusion.2.gates) | copy-start | bytes 221188
  146.0 308.3 %all-gather.16.cloned.1.call-start = ((), (), s32[]{:S(2)}) async-start(), calls=%async_computation.5 | async-start | bytes 18874368 | tf_op jit(solution)/shard_map/all_gather | solution.py:648
  147.2 23.7 %collective-permute-start.4 = (bf16[1024,4,128]{2,1,0:T(4,128)(2,1)}, bf16[1024,4,128]{2,1,0:T(4,128)(2,1)}, u32[]{:S(2)}, u32[]{:S(2)}) collective-permute-start(bf16[1024,4,128]{2,1,0:T(4,128)(2,1)} %reshape.334.refs_2_.a), channel_id=1, source_target_pairs={{0,8},{8,0},{1,9},{9,1},{2,10},{10,2},{3,11},{11,3},{4,12},{12,4},... | collective-permute-start | bytes 3145736 | tf_op jit(solution)/shard_map/ppermute | solution.py:645
  147.4 26.4 %copy-start.7 = (bf16[1024,4,128]{2,1,0:T(4,128)(2,1)S(1)}, bf16[1024,4,128]{2,1,0:T(4,128)(2,1)}, u32[]{:S(2)}) copy-start(bf16[1024,4,128]{2,1,0:T(4,128)(2,1)} %reshape.332.refs_0_.a) | copy-start | bytes 3145732
  173.8 280.4 %all-gather.14.cloned.1.call-start = ((), (), s32[]{:S(2)}) async-start(), calls=%async_computation.4 | async-start | bytes 18874368 | tf_op jit(solution)/shard_map/all_gather | solution.py:648
  173.8 22.7 %collective-permute-start.3 = (bf16[1024,4,128]{2,1,0:T(4,128)(2,1)S(1)}, bf16[1024,4,128]{2,1,0:T(4,128)(2,1)}, u32[]{:S(2)}, u32[]{:S(2)}) collective-permute-start(bf16[1024,4,128]{2,1,0:T(4,128)(2,1)S(1)} %copy-done.7), channel_id=1, source_target_pairs={{0,8},{8,0},{1,9},{9,1},{2,10},{10,2},{3,11},{11,3},{4,12},{12,4},... | collective-permute-start | bytes 3145736 | tf_op jit(solution)/shard_map/ppermute | solution.py:645
  199.5 305.4 %all-gather.8.cloned.1.call-start = ((), (), s32[]{:S(2)}) async-start(), calls=%async_computation.1 | async-start | bytes 9437184 | tf_op jit(solution)/shard_map/all_gather | solution.py:648
  200.0 304.9 %all-gather.10.cloned.1.call-start = ((), (), s32[]{:S(2)}) async-start(), calls=%async_computation.2 | async-start | bytes 9437184 | tf_op jit(solution)/shard_map/all_gather | solution.py:648
  200.6 341.0 %all-gather.12.cloned.1.call-start = ((), (), s32[]{:S(2)}) async-start(), calls=%async_computation.3 | async-start | bytes 18874368 | tf_op jit(solution)/shard_map/all_gather | solution.py:648
  253.3 46.5 %collective-permute-start.5 = (f32[1024,512]{1,0:T(8,128)}, f32[1024,512]{1,0:T(8,128)S(1)}, u32[]{:S(2)}, u32[]{:S(2)}) collective-permute-start(f32[1024,512]{1,0:T(8,128)} %get-tuple-element.59), channel_id=1, source_target_pairs={{0,8},{8,0},{1,9},{9,1},{2,10},{10,2},{3,11},{11,3},{4,12},{12,4},... | collective-permute-start | bytes 6291464 | tf_op jit(solution)/shard_map/ppermute | solution.py:645
  304.6 25.0 %copy-start.5 = (bf16[1024,512]{1,0:T(8,128)(2,1)}, bf16[1024,512]{1,0:T(8,128)(2,1)S(1)}, u32[]{:S(2)}) copy-start(bf16[1024,512]{1,0:T(8,128)(2,1)S(1)} %add_convert_fusion.3) | copy-start | bytes 3145732
  304.9 20.8 %copy-start.8 = (bf16[1024,4,128]{2,1,0:T(4,128)(2,1)}, bf16[1024,4,128]{2,1,0:T(4,128)(2,1)S(1)}, u32[]{:S(2)}) copy-start(bf16[1024,4,128]{2,1,0:T(4,128)(2,1)S(1)} %reshape.335.refs_2_.a) | copy-start | bytes 3145732
  304.9 20.8 %collective-permute-start.6 = (bf16[1024,4,128]{2,1,0:T(4,128)(2,1)S(1)}, bf16[1024,4,128]{2,1,0:T(4,128)(2,1)S(1)}, u32[]{:S(2)}, u32[]{:S(2)}) collective-permute-start(bf16[1024,4,128]{2,1,0:T(4,128)(2,1)S(1)} %reshape.335.refs_2_.a), channel_id=1, source_target_pairs={{0,8},{8,0},{1,9},{9,1},{2,10},{10,2},{3,11},{11,3},{4,12},{12,4},... | collective-permute-start | bytes 3145736 | tf_op jit(solution)/shard_map/ppermute | solution.py:645
  329.6 509.9 %all-reduce.12.cloned.1.call-start = ((), (), s32[]{:S(2)}) async-start(), calls=%async_computation | async-start | bytes 2097152 | tf_op jit(solution)/shard_map/psum | solution.py:748
  374.2 225.1 %collective-permute-start.7 = (f32[1024,512]{1,0:T(8,128)}, f32[1024,512]{1,0:T(8,128)}, u32[]{:S(2)}, u32[]{:S(2)}) collective-permute-start(f32[1024,512]{1,0:T(8,128)} %get-tuple-element.64), channel_id=1, source_target_pairs={{0,8},{8,0},{1,9},{9,1},{2,10},{10,2},{3,11},{11,3},{4,12},{12,4},... | collective-permute-start | bytes 6291464 | tf_op jit(solution)/shard_map/ppermute | solution.py:645
  378.5 58.5 %copy-start.32 = (s32[64]{0:T(128)S(1)}, s32[64]{0:T(128)}, u32[]{:S(2)}) copy-start(s32[64]{0:T(128)} %copy-done.31) | copy-start | bytes 772
  435.9 164.9 %collective-permute-start.8 = (f32[1024,512]{1,0:T(8,128)}, f32[1024,512]{1,0:T(8,128)}, u32[]{:S(2)}, u32[]{:S(2)}) collective-permute-start(f32[1024,512]{1,0:T(8,128)} %get-tuple-element.66), channel_id=1, source_target_pairs={{0,8},{8,0},{1,9},{9,1},{2,10},{10,2},{3,11},{11,3},{4,12},{12,4},... | collective-permute-start | bytes 6291464 | tf_op jit(solution)/shard_map/ppermute | solution.py:645
  438.3 13.8 %copy-start.24 = (s32[1,16]{1,0:T(1,128)}, s32[1,16]{1,0:T(1,128)S(1)}, u32[]{:S(2)}) copy-start(s32[1,16]{1,0:T(1,128)S(1)} %get-tuple-element.153) | copy-start | bytes 196
  438.3 13.8 %copy-start.25 = (s32[1,16]{1,0:T(1,128)}, s32[1,16]{1,0:T(1,128)S(1)}, u32[]{:S(2)}) copy-start(s32[1,16]{1,0:T(1,128)S(1)} %get-tuple-element.152) | copy-start | bytes 196
  439.0 15.2 %copy-start.30 = (s32[1,16]{1,0:T(1,128)}, s32[1,16]{1,0:T(1,128)S(1)}, u32[]{:S(2)}) copy-start(s32[1,16]{1,0:T(1,128)S(1)} %get-tuple-element.149) | copy-start | bytes 196
  504.3 97.1 %collective-permute-start.9 = (bf16[16,192,512]{2,1,0:T(8,128)(2,1)}, bf16[16,192,512]{2,1,0:T(8,128)(2,1)}, u32[]{:S(2)}, u32[]{:S(2)}) collective-permute-start(bf16[16,192,512]{2,1,0:T(8,128)(2,1)} %get-tuple-element.71), channel_id=1, source_target_pairs={{0,1},{1,0},{2,3},{3,2},{4,5},{5,4},{6,7},{7,6},{8,9},{9,8},{10,11... | collective-permute-start | bytes 9437192 | tf_op jit(solution)/shard_map/ppermute | solution.py:651
  504.3 98.5 %collective-permute-start.10 = (bf16[16,192,512]{2,1,0:T(8,128)(2,1)}, bf16[16,192,512]{2,1,0:T(8,128)(2,1)}, u32[]{:S(2)}, u32[]{:S(2)}) collective-permute-start(bf16[16,192,512]{2,1,0:T(8,128)(2,1)} %get-tuple-element.72), channel_id=1, source_target_pairs={{0,1},{1,0},{2,3},{3,2},{4,5},{5,4},{6,7},{7,6},{8,9},{9,8},{10,11... | collective-permute-start | bytes 9437192 | tf_op jit(solution)/shard_map/ppermute | solution.py:651
  504.8 98.9 %collective-permute-start.11 = (bf16[16,192,512]{2,1,0:T(8,128)(2,1)}, bf16[16,192,512]{2,1,0:T(8,128)(2,1)}, u32[]{:S(2)}, u32[]{:S(2)}) collective-permute-start(bf16[16,192,512]{2,1,0:T(8,128)(2,1)} %get-tuple-element.73), channel_id=1, source_target_pairs={{0,1},{1,0},{2,3},{3,2},{4,5},{5,4},{6,7},{7,6},{8,9},{9,8},{10,11... | collective-permute-start | bytes 9437192 | tf_op jit(solution)/shard_map/ppermute | solution.py:651
  541.6 61.3 %copy-start.26 = (s32[17,1]{0,1:T(1,128)S(1)}, s32[17,1]{0,1:T(1,128)}, u32[]{:S(2)}) copy-start(s32[17,1]{0,1:T(1,128)} %get-tuple-element.171) | copy-start | bytes 208
  541.6 61.6 %copy-start.23 = (s32[16]{0:T(128)S(1)}, s32[16]{0:T(128)}, u32[]{:S(2)}) copy-start(s32[16]{0:T(128)} %copy-done.22) | copy-start | bytes 196
  599.3 37.6 %collective-permute-start.15 = (bf16[16,192,512]{2,1,0:T(8,128)(2,1)}, bf16[16,192,512]{2,1,0:T(8,128)(2,1)}, u32[]{:S(2)}, u32[]{:S(2)}) collective-permute-start(bf16[16,192,512]{2,1,0:T(8,128)(2,1)} %get-tuple-element.71), channel_id=1, source_target_pairs={{0,2},{1,5},{2,0},{3,7},{4,6},{5,1},{6,4},{7,3},{8,10},{9,13},{10,... | collective-permute-start | bytes 9437192 | tf_op jit(solution)/shard_map/ppermute | solution.py:651
  600.8 69.8 %collective-permute-start.16 = (bf16[16,192,512]{2,1,0:T(8,128)(2,1)}, bf16[16,192,512]{2,1,0:T(8,128)(2,1)}, u32[]{:S(2)}, u32[]{:S(2)}) collective-permute-start(bf16[16,192,512]{2,1,0:T(8,128)(2,1)} %get-tuple-element.72), channel_id=1, source_target_pairs={{0,2},{1,5},{2,0},{3,7},{4,6},{5,1},{6,4},{7,3},{8,10},{9,13},{10,... | collective-permute-start | bytes 9437192 | tf_op jit(solution)/shard_map/ppermute | solution.py:651
  601.4 103.0 %collective-permute-start.17 = (bf16[16,192,512]{2,1,0:T(8,128)(2,1)}, bf16[16,192,512]{2,1,0:T(8,128)(2,1)}, u32[]{:S(2)}, u32[]{:S(2)}) collective-permute-start(bf16[16,192,512]{2,1,0:T(8,128)(2,1)} %get-tuple-element.73), channel_id=1, source_target_pairs={{0,2},{1,5},{2,0},{3,7},{4,6},{5,1},{6,4},{7,3},{8,10},{9,13},{10,... | collective-permute-start | bytes 9437192 | tf_op jit(solution)/shard_map/ppermute | solution.py:651
  602.9 101.5 %collective-permute-start.18 = (bf16[16,192,512]{2,1,0:T(8,128)(2,1)}, bf16[16,192,512]{2,1,0:T(8,128)(2,1)}, u32[]{:S(2)}, u32[]{:S(2)}) collective-permute-start(bf16[16,192,512]{2,1,0:T(8,128)(2,1)} %get-tuple-element.84), channel_id=1, source_target_pairs={{0,1},{1,0},{2,3},{3,2},{4,5},{5,4},{6,7},{7,6},{8,9},{9,8},{10,11... | collective-permute-start | bytes 9437192 | tf_op jit(solution)/shard_map/ppermute | solution.py:651
  603.7 160.7 %collective-permute-start.19 = (bf16[16,192,512]{2,1,0:T(8,128)(2,1)}, bf16[16,192,512]{2,1,0:T(8,128)(2,1)}, u32[]{:S(2)}, u32[]{:S(2)}) collective-permute-start(bf16[16,192,512]{2,1,0:T(8,128)(2,1)} %get-tuple-element.85), channel_id=1, source_target_pairs={{0,1},{1,0},{2,3},{3,2},{4,5},{5,4},{6,7},{7,6},{8,9},{9,8},{10,11... | collective-permute-start | bytes 9437192 | tf_op jit(solution)/shard_map/ppermute | solution.py:651
  637.0 127.5 %collective-permute-start.20 = (bf16[16,192,512]{2,1,0:T(8,128)(2,1)}, bf16[16,192,512]{2,1,0:T(8,128)(2,1)}, u32[]{:S(2)}, u32[]{:S(2)}) collective-permute-start(bf16[16,192,512]{2,1,0:T(8,128)(2,1)} %get-tuple-element.86), channel_id=1, source_target_pairs={{0,1},{1,0},{2,3},{3,2},{4,5},{5,4},{6,7},{7,6},{8,9},{9,8},{10,11... | collective-permute-start | bytes 9437192 | tf_op jit(solution)/shard_map/ppermute | solution.py:651
  670.7 94.3 %collective-permute-start.21 = (bf16[16,192,512]{2,1,0:T(8,128)(2,1)}, bf16[16,192,512]{2,1,0:T(8,128)(2,1)}, u32[]{:S(2)}, u32[]{:S(2)}) collective-permute-start(bf16[16,192,512]{2,1,0:T(8,128)(2,1)} %collective-permute-done.15.refs_0_), channel_id=1, source_target_pairs={{0,1},{1,0},{2,3},{3,2},{4,5},{5,4},{6,7},{7,6},{8,9},{9,8},{10,11... | collective-permute-start | bytes 9437192 | tf_op jit(solution)/shard_map/ppermute | solution.py:651
  704.4 137.4 %collective-permute-start.22 = (bf16[16,192,512]{2,1,0:T(8,128)(2,1)}, bf16[16,192,512]{2,1,0:T(8,128)(2,1)}, u32[]{:S(2)}, u32[]{:S(2)}) collective-permute-start(bf16[16,192,512]{2,1,0:T(8,128)(2,1)} %collective-permute-done.16.refs_1_), channel_id=1, source_target_pairs={{0,1},{1,0},{2,3},{3,2},{4,5},{5,4},{6,7},{7,6},{8,9},{9,8},{10,11... | collective-permute-start | bytes 9437192 | tf_op jit(solution)/shard_map/ppermute | solution.py:651
  704.4 137.4 %collective-permute-start.23 = (bf16[16,192,512]{2,1,0:T(8,128)(2,1)}, bf16[16,192,512]{2,1,0:T(8,128)(2,1)}, u32[]{:S(2)}, u32[]{:S(2)}) collective-permute-start(bf16[16,192,512]{2,1,0:T(8,128)(2,1)} %collective-permute-done.17.refs_2_), channel_id=1, source_target_pairs={{0,1},{1,0},{2,3},{3,2},{4,5},{5,4},{6,7},{7,6},{8,9},{9,8},{10,11... | collective-permute-start | bytes 9437192 | tf_op jit(solution)/shard_map/ppermute | solution.py:651
  704.9 60.2 %copy-start.15 = (bf16[1024,512]{1,0:T(8,128)(2,1)S(1)}, bf16[1024,512]{1,0:T(8,128)(2,1)}, u32[]{:S(2)}) copy-start(bf16[1024,512]{1,0:T(8,128)(2,1)} %copy-done.14) | copy-start | bytes 3145732
  764.4 98.1 %collective-permute-start.12 = (bf16[16,192,512]{2,1,0:T(8,128)(2,1)}, bf16[16,192,512]{2,1,0:T(8,128)(2,1)}, u32[]{:S(2)}, u32[]{:S(2)}) collective-permute-start(bf16[16,192,512]{2,1,0:T(8,128)(2,1)} %get-tuple-element.81), channel_id=1, source_target_pairs={{0,1},{1,0},{2,3},{3,2},{4,5},{5,4},{6,7},{7,6},{8,9},{9,8},{10,11... | collective-permute-start | bytes 9437192 | tf_op jit(solution)/shard_map/ppermute | solution.py:651
  764.5 98.0 %collective-permute-start.13 = (bf16[16,192,512]{2,1,0:T(8,128)(2,1)}, bf16[16,192,512]{2,1,0:T(8,128)(2,1)}, u32[]{:S(2)}, u32[]{:S(2)}) collective-permute-start(bf16[16,192,512]{2,1,0:T(8,128)(2,1)} %get-tuple-element.82), channel_id=1, source_target_pairs={{0,1},{1,0},{2,3},{3,2},{4,5},{5,4},{6,7},{7,6},{8,9},{9,8},{10,11... | collective-permute-start | bytes 9437192 | tf_op jit(solution)/shard_map/ppermute | solution.py:651
  765.0 97.5 %collective-permute-start.14 = (bf16[16,192,512]{2,1,0:T(8,128)(2,1)}, bf16[16,192,512]{2,1,0:T(8,128)(2,1)}, u32[]{:S(2)}, u32[]{:S(2)}) collective-permute-start(bf16[16,192,512]{2,1,0:T(8,128)(2,1)} %get-tuple-element.83), channel_id=1, source_target_pairs={{0,1},{1,0},{2,3},{3,2},{4,5},{5,4},{6,7},{7,6},{8,9},{9,8},{10,11... | collective-permute-start | bytes 9437192 | tf_op jit(solution)/shard_map/ppermute | solution.py:651
  (19 other events, 59.8 us)
Sparse Core Ops, SparseCore 0:
  146.1 25.6 all-gather.17
  173.9 85.8 all-gather.15
  262.2 85.9 all-gather.13
  350.5 50.5 all-gather.7
  403.3 50.5 all-gather.9
  455.6 85.8 all-gather.11
Sparse Core Ops, SparseCore 1:
  773.3 66.1 all-reduce.11
